TPU v7x, 256 devices: a whole 4x4x8 slice. The times are simulated.
256 devices in a mesh: blk: 64 (over x_lo, y, z), mp: 4 (over x_hi, core).
Axes of the slice: x: 4 (x_hi: 2, x_lo: 2; x = x_hi * 2 + x_lo), y: 4, z: 8, core: 2. Of those that a mesh axis runs over, the one named last changes fastest.
Arguments:
- tokens: bfloat16 [8192, 2048], P('blk', 'mp'), may hold values from -16 to 16
- grad_out: bfloat16 [8192, 2048], P('blk', 'mp'), may hold values from -0.29882812 to 0.29882812
- w_gate: bfloat16 [2048, 2560], P(None, 'mp'), may hold values from -0.125 to 0.125
- w_lin: bfloat16 [2048, 2560], P(None, 'mp'), may hold values from -0.125 to 0.125
- w_out_t: bfloat16 [2048, 2560], P(None, 'mp'), may hold values from -0.125 to 0.125
- code: float32 [64, 5], P('blk'), may hold values from 0.5 to 2
- decode: float32 [64], P('blk'), may hold values from 0.05 to 0.2
- stragglers: int32 [4], replicated, may hold values from 0 to 63, as said below
Outputs:
- grads: float32 [2048, 3, 2560], P('blk', None, 'mp')
Inputs may be any that keep to these rules, and one draw needn't show every extreme that they name: `stragglers`: 4 distinct worker indices; worker 0 and worker 64 - 1 are always among them.
All inputs are finite; a program needn't handle non-finite values.
Results may differ from a plain program's by a relative error of at most 0.0042.
Values may be sent and summed in bfloat16 or wider, within the bound.
No kernel may reach another device: no remote copies, remote signals or barrier semaphores. Data moves between devices by JAX's collectives and lax.ppermute only.
A program may use at most 128 MiB of HBM per device.

v0:
```python
from functools import partial

import jax
import jax.numpy as jnp
from jax import lax
from jax.sharding import PartitionSpec as P


def from_behind(block, axis, distance):
    devices = range(lax.axis_size(axis))
    route = [((i - distance) % len(devices), i) for i in devices]
    return lax.ppermute(block, axis, route)


def sent_to_all(shard, axis):
    copies = jnp.broadcast_to(shard, (lax.axis_size(axis), *shard.shape))
    return lax.all_to_all(copies, axis, split_axis=0, concat_axis=0, tiled=True)


def laid_out(blocks, dim):
    blocks = jnp.moveaxis(blocks, 0, dim)
    dims = blocks.shape
    return blocks.reshape(*dims[:dim], dims[dim] * dims[dim + 1], *dims[dim + 2 :])


def gathered_copies(shard, axis, dim):
    blocks = sent_to_all(shard, axis)
    return laid_out(blocks, dim)


def in_blocks(shard, dim, peers):
    before, after = (shard.shape[:dim], shard.shape[dim + 1 :])
    return jnp.moveaxis(shard.reshape(*before, peers, -1, *after), dim, 0)


def sent_and_summed(shard, axis, dim):
    peers = lax.axis_size(axis)
    blocks = lax.all_to_all(in_blocks(shard, dim, peers), axis, 0, 0, tiled=True)
    return jnp.sum(blocks.astype(jnp.float32), axis=0)


def local_grads(inputs, cotangent, w_gate, w_lin, w_out_t):
    gate_pre = jnp.dot(inputs, w_gate, preferred_element_type=jnp.float32)
    linear = jnp.dot(inputs, w_lin, preferred_element_type=jnp.float32)
    activated, pullback = jax.vjp(partial(jax.nn.gelu, approximate=True), gate_pre)
    hidden = (activated * linear).astype(jnp.bfloat16)
    hidden_grad = jnp.dot(cotangent, w_out_t, preferred_element_type=jnp.float32)
    d_gate = pullback(hidden_grad * linear)[0].astype(jnp.bfloat16)
    d_lin = (hidden_grad * activated).astype(jnp.bfloat16)
    return (jnp.concatenate([d_gate, d_lin], axis=1), hidden)


def shards(tokens, grad_out, w_gate, w_lin, w_out_t, code, decode, stragglers):
    device = lax.axis_index("blk")
    group_size = lax.axis_size("blk")
    slot_total = code.shape[1]
    part_rows = tokens.shape[0]
    is_alive = jnp.all(stragglers != device)
    own_decode = jnp.where(is_alive, decode[0], jnp.float32(0.0))
    token_pair = jnp.stack([tokens, grad_out])
    weighted_row = own_decode * code[0]
    total_weight = weighted_row[0]
    passed = weighted_row
    for slot in range(1, slot_total):
        passed = from_behind(passed, "blk", 1)
        total_weight = total_weight + passed[slot]
    coefficients = [total_weight]
    stacked = gathered_copies(token_pair, "mp", 2)[None]
    used_slots = len(coefficients)
    width = stacked.shape[-1]
    inputs_all = stacked[:, 0].reshape(used_slots * part_rows, width)
    cotangent_all = stacked[:, 1].reshape(used_slots * part_rows, width)
    right_side, hidden = local_grads(inputs_all, cotangent_all, w_gate, w_lin, w_out_t)
    local_width = hidden.shape[1]
    own_rows = width // group_size
    accumulated = jnp.zeros((width, 3 * local_width), jnp.float32)
    slot = 0
    lower = slot * part_rows
    product = jnp.concatenate(
        [
            jnp.dot(
                inputs_all.T,
                right_side[lower : lower + part_rows],
                preferred_element_type=jnp.float32,
            ),
            jnp.dot(
                cotangent_all.T,
                hidden[lower : lower + part_rows],
                preferred_element_type=jnp.float32,
            ),
        ],
        axis=1,
    )
    accumulated = accumulated + coefficients[slot] * product
    summed = sent_and_summed(accumulated.astype(jnp.bfloat16), "blk", 0)
    return summed.reshape(own_rows, 3, local_width)


def solution(mesh):
    in_specs = (
        P("blk", "mp"),
        P("blk", "mp"),
        P(None, "mp"),
        P(None, "mp"),
        P(None, "mp"),
        P("blk", None),
        P("blk"),
        P(),
    )
    out_specs = P("blk", None, "mp")
    return jax.shard_map(shards, mesh=mesh, in_specs=in_specs, out_specs=out_specs, check_vma=False)
```

profile of v0, /device:TPU:6, one launch (start us, length us, event | category | flops | bytes accessed | tf_op | source)
XLA Modules:
  0.0 237.2 jit_solution(6701647623635985856)
XLA Ops:
  0.0 1.1 pad_maximum_fusion
  1.1 0.2 copy.14
  1.3 1.2 broadcast_in_dim.3
  2.5 5.6 %all-to-all-start = ((bf16[4,2,128,512]{2,3,1,0:T(8,128)(2,1)}), bf16[4,2,128,512]{2,3,1,0:T(8,128)(2,1)}, u32[]{:S(2)}, u32[]{:S(2)}) async-start(bf16[4,2,128,512]{2,3,1,0:T(8,128)(2,1)} %broadcast_in_dim.3), calls=%async_computation | async-start | bytes 2097152 | tf_op jit(solution)/shard_map/all_to_all | solution.py:17
  8.7 1.3 compare_reduce_fusion
  10.7 0.7 fusion.34
  11.3 1.9 collective-permute-start
  13.3 0.7 broadcast_multiply_fusion
  13.9 6.7 %collective-permute-done = f32[5]{0:T(128)S(1)} collective-permute-done((f32[5]{0:T(128)S(1)}, f32[5]{0:T(128)S(1)}, u32[]{:S(2)}, u32[]{:S(2)}) %collective-permute-start) | collective-permute-done | bytes 52 | tf_op jit(solution)/shard_map/ppermute | solution.py:12
  20.7 0.6 slice.26
  21.9 0.1 collective-permute-start.1
  22.0 7.8 %collective-permute-done.1 = f32[5]{0:T(128)S(1)} collective-permute-done((f32[5]{0:T(128)S(1)}, f32[5]{0:T(128)S(1)}, u32[]{:S(2)}, u32[]{:S(2)}) %collective-permute-start.1) | collective-permute-done | bytes 52 | tf_op jit(solution)/shard_map/ppermute | solution.py:12
  29.8 0.6 slice.27
  31.0 0.1 collective-permute-start.2
  31.1 7.8 %collective-permute-done.2 = f32[5]{0:T(128)S(1)} collective-permute-done((f32[5]{0:T(128)S(1)}, f32[5]{0:T(128)S(1)}, u32[]{:S(2)}, u32[]{:S(2)}) %collective-permute-start.2) | collective-permute-done | bytes 52 | tf_op jit(solution)/shard_map/ppermute | solution.py:12
  38.9 0.6 slice.28
  40.1 0.1 collective-permute-start.3
  40.2 7.8 %collective-permute-done.3 = f32[5]{0:T(128)S(1)} collective-permute-done((f32[5]{0:T(128)S(1)}, f32[5]{0:T(128)S(1)}, u32[]{:S(2)}, u32[]{:S(2)}) %collective-permute-start.3) | collective-permute-done | bytes 52 | tf_op jit(solution)/shard_map/ppermute | solution.py:12
  48.0 0.6 slice.29
  49.2 0.0 all-to-all-done
  49.2 0.0 copy-start.1
  49.2 1.4 copy.15
  50.7 0.1 fusion.28
  50.8 2.3 fusion.3
  53.1 0.6 fusion.1
  53.8 0.8 fusion.13
  54.6 0.9 fusion.18
  55.5 1.5 fusion.14
  57.0 1.2 fusion
  58.2 177.1 %all_to_all.10 = bf16[64,32,1920]{2,1,0:T(8,128)(2,1)S(1)} all-to-all(bf16[64,32,1920]{2,1,0:T(8,128)(2,1)S(1)} %fusion), channel_id=1, replica_groups=mesh['blk'=64,'mp'=4] {'blk'}, dimensions={0} | all-to-all | bytes 15728640 | tf_op jit(solution)/shard_map/all_to_all | solution.py:38
  235.3 1.2 convert_reduce_fusion
  236.5 0.7 copy.19
  (3 shorter events, 0.0 us)
Async XLA Ops:
  0.0 53.8 %copy-start = (bf16[2048,640]{1,0:T(8,128)(2,1)S(1)}, bf16[2048,640]{1,0:T(8,128)(2,1)}, u32[]{:S(2)}) copy-start(bf16[2048,640]{1,0:T(8,128)(2,1)} %param.10) | copy-start | bytes 7864324
  2.5 46.8 %all-to-all-start = ((bf16[4,2,128,512]{2,3,1,0:T(8,128)(2,1)}), bf16[4,2,128,512]{2,3,1,0:T(8,128)(2,1)}, u32[]{:S(2)}, u32[]{:S(2)}) async-start(bf16[4,2,128,512]{2,3,1,0:T(8,128)(2,1)} %broadcast_in_dim.3), calls=%async_computation | async-start | bytes 2097152 | tf_op jit(solution)/shard_map/all_to_all | solution.py:17
  11.3 9.3 %collective-permute-start = (f32[5]{0:T(128)S(1)}, f32[5]{0:T(128)S(1)}, u32[]{:S(2)}, u32[]{:S(2)}) collective-permute-start(f32[5]{0:T(128)S(1)} %fusion.34), channel_id=1, source_target_pairs={{252,0},{0,4},{4,8},{8,12},{12,16},{16,20},{20,24},{24,28},{28,32}... | collective-permute-start | bytes 68 | tf_op jit(solution)/shard_map/ppermute | solution.py:12
  21.9 7.9 %collective-permute-start.1 = (f32[5]{0:T(128)S(1)}, f32[5]{0:T(128)S(1)}, u32[]{:S(2)}, u32[]{:S(2)}) collective-permute-start(f32[5]{0:T(128)S(1)} %collective-permute-done), channel_id=1, source_target_pairs={{252,0},{0,4},{4,8},{8,12},{12,16},{16,20},{20,24},{24,28},{28,32}... | collective-permute-start | bytes 68 | tf_op jit(solution)/shard_map/ppermute | solution.py:12
  31.0 7.9 %collective-permute-start.2 = (f32[5]{0:T(128)S(1)}, f32[5]{0:T(128)S(1)}, u32[]{:S(2)}, u32[]{:S(2)}) collective-permute-start(f32[5]{0:T(128)S(1)} %collective-permute-done.1), channel_id=1, source_target_pairs={{252,0},{0,4},{4,8},{8,12},{12,16},{16,20},{20,24},{24,28},{28,32}... | collective-permute-start | bytes 68 | tf_op jit(solution)/shard_map/ppermute | solution.py:12
  40.1 7.9 %collective-permute-start.3 = (f32[5]{0:T(128)S(1)}, f32[5]{0:T(128)S(1)}, u32[]{:S(2)}, u32[]{:S(2)}) collective-permute-start(f32[5]{0:T(128)S(1)} %collective-permute-done.2), channel_id=1, source_target_pairs={{252,0},{0,4},{4,8},{8,12},{12,16},{16,20},{20,24},{24,28},{28,32}... | collective-permute-start | bytes 68 | tf_op jit(solution)/shard_map/ppermute | solution.py:12
  49.2 3.9 %copy-start.1 = (bf16[2048,640]{1,0:T(8,128)(2,1)S(1)}, bf16[2048,640]{1,0:T(8,128)(2,1)}, u32[]{:S(2)}) copy-start(bf16[2048,640]{1,0:T(8,128)(2,1)} %param.12) | copy-start | bytes 7864324
where the time goes:
time: 238 us; the launch traced here: 237 us
  blocking collectives  177 us (74%)
  waiting for transfers between devices  30.1 us (13%)
  starting transfers between devices  7.77 us (3%)
  matrix products  6.18 us (3%)
  other arithmetic  6.13 us (3%)
  local copies, waits for them, and re-layouts  5.88 us (2%)
  between operations  4.07 us (2%)
    all_to_all x1, blocking collectives, sent_and_summed(): lax.all_to_all(in_blocks(shard, dim, peers), axis, 0, 0, tiled=True)  177 us
    ppermute x4, waiting for transfers between devices, from_behind(): return lax.ppermute(block, axis, route)  30.1 us
    all_to_all x1, starting transfers between devices, sent_to_all(): return lax.all_to_all(copies, axis, split_axis=0, concat_axis=0, tiled=True)  5.6 us
  transfers between devices with their start and end apart: 5, of which 4 were waited for; matrix products, arithmetic and copies ran while one was open for 2% of the time, Pallas kernels for 0%

commit v1 on v0

v1 whole, which is shorter than its diff:
```python
import jax
import jax.numpy as jnp
from jax import lax
from jax.experimental import pallas as pl
from jax.experimental.pallas import tpu as pltpu
from jax.sharding import Mesh, PartitionSpec as P


BF16 = jnp.bfloat16
F32 = jnp.float32
I32 = jnp.int32
ROOT_2_PI = 0.7978845608028654
CUBIC = 0.044715
BLK = ("xl", "y", "z")
PLANE = ("xl", "y", "xh", "c")
SMEM = pl.BlockSpec(memory_space=pltpu.SMEM)
VMEM = pl.BlockSpec(memory_space=pltpu.VMEM)
PARAMS = pltpu.CompilerParams(vmem_limit_bytes=16 * 1024 * 1024)


def place():
    return [lax.axis_index(a).astype(I32) for a in ("xl", "y", "z", "xh", "c")]


def across(block, flip, first):
    route = []
    for xl in range(2):
        for y in range(4):
            for xh in range(2):
                for c in range(2):
                    on_x = (c == 0) == first
                    to = (xl ^ (flip & 1), y, xh ^ (flip >> 1), c) if on_x else (xl, y ^ flip, xh, c)
                    number = lambda a: ((a[0] * 4 + a[1]) * 2 + a[2]) * 2 + a[3]
                    route.append((number((xl, y, xh, c)), number(to)))
    return lax.ppermute(block, PLANE, route)


def sibling(block):
    return lax.ppermute(block, "c", [(0, 1), (1, 0)])


def partner_of(z, c):
    return z ^ 1 if c == 0 else ((z + 1) % 8 if z % 2 else (z - 1) % 8)


def z_pair(block):
    return lax.ppermute(block, ("z", "c"), [(z * 2 + c, partner_of(z, c) * 2 + c) for z in range(8) for c in range(2)])


def z_step(block, step):
    return lax.ppermute(block, "z", [(z, (z + step) % 8) for z in range(8)])


def prepare_kernel(code, decode, stragglers, w_gate, w_lin, w_out_t, picked, w_in, w_out, sems):
    copies = [
        pltpu.make_async_copy(w_gate, w_in.at[:, :, pl.ds(0, 640)], sems.at[0]),
        pltpu.make_async_copy(w_lin, w_in.at[:, :, pl.ds(640, 640)], sems.at[1]),
        pltpu.make_async_copy(w_out_t, w_out, sems.at[2]),
    ]
    for copy in copies:
        copy.start()
    xl, y, z, _, _ = place()
    device = (xl * 4 + y) * 8 + z
    alive = stragglers[0] != device
    for i in range(1, 4):
        alive = alive & (stragglers[i] != device)
    scale = jnp.where(alive, decode[0], 0.0)
    slot = (lax.broadcasted_iota(I32, (64, 128), 0) - z) & 7
    value = jnp.zeros((64, 128), F32)
    for j in range(5):
        value = jnp.where(slot == j, scale * code[0, j], value)
    picked[...] = value
    for copy in copies:
        copy.wait()


def prepare(code, decode, stragglers, w_gate, w_lin, w_out_t):
    whole = pl.BlockSpec(memory_space=pltpu.HBM)
    return pl.pallas_call(
        prepare_kernel,
        out_shape=(
            jax.ShapeDtypeStruct((64, 128), F32),
            jax.ShapeDtypeStruct((4, 512, 1280), BF16),
            jax.ShapeDtypeStruct((4, 512, 640), BF16),
        ),
        in_specs=[SMEM] * 3 + [whole] * 3,
        out_specs=(VMEM, VMEM, VMEM),
        scratch_shapes=[pltpu.SemaphoreType.DMA((3,))],
        compiler_params=PARAMS,
        name="prepare",
    )(code, decode, stragglers, *[w.reshape(4, 512, 640) for w in (w_gate, w_lin, w_out_t)])


def first_kernel(own, other, w_in, w_out, acc, cols):
    acc[...] = jnp.zeros_like(acc)
    gather_kernel(0, own, other, w_in, w_out, acc, cols)


def middle_kernel(m, own, other, w_in, w_out, _, __, acc, cols):
    gather_kernel(m, own, other, w_in, w_out, acc, cols)


def final_kernel(m, own, other, w_in, w_out, _, __, values, acc, cols, *rest):
    gather_kernel(m, own, other, w_in, w_out, acc, cols)
    last_kernel(values, acc, cols, *rest)


def gather_kernel(m, own, other, w_in, w_out, acc, cols):
    xl, y, _, xh, c = place()
    for ec, block in ((0, own), (1, other)):
        x_first = (c ^ ec) == 0

        def step(j, _):
            eh = jnp.where(x_first, j, m >> 1)
            p0 = jnp.where(x_first, 2 * m, 4 * j + (m & 1))
            p1 = jnp.where(x_first, 2 * m + 1, 4 * j + 2 + (m & 1))
            shard = (xh ^ eh) * 2 + (c ^ ec)
            xs = block[pl.ds(2 * j, 2), 0].reshape(256, 512)
            ys = block[pl.ds(2 * j, 2), 1].reshape(256, 512)
            pre = jnp.dot(xs, w_in[shard], preferred_element_type=F32)
            acc[0, p0] += pre[:128, :640]
            acc[1, p0] += pre[:128, 640:]
            acc[0, p1] += pre[128:, :640]
            acc[1, p1] += pre[128:, 640:]
            dh = jnp.dot(ys, w_out[shard], preferred_element_type=F32)
            acc[2, p0] += dh[:128]
            acc[2, p1] += dh[128:]

            @pl.when((ec == ((y >> 1) ^ c)) & (eh == (xl ^ xh)))
            def _():
                low = (y & 1) == 0
                for n, v in ((0, xs), (1, ys)):
                    v = jnp.where(low, v[:, :256], v[:, 256:])
                    cols[n, p0] = v[:128]
                    cols[n, p1] = v[128:]

            return 0

        lax.fori_loop(0, 2, step, 0)


STATE = (jax.ShapeDtypeStruct((3, 8, 128, 640), F32), jax.ShapeDtypeStruct((2, 8, 128, 256), BF16))


def priced(giga):
    return pl.CostEstimate(flops=giga << 30, bytes_accessed=1 << 20, transcendentals=0)


def gathered(m, own, other, w_in, w_out, state):
    return pl.pallas_call(
        (lambda *refs: middle_kernel(m, *refs)) if state else first_kernel,
        out_shape=STATE,
        in_specs=[VMEM] * (4 + len(state)),
        out_specs=(VMEM, VMEM),
        input_output_aliases={4: 0, 5: 1} if state else {},
        compiler_params=PARAMS,
        cost_estimate=priced(2),
    )(own, other, w_in, w_out, *state)


def finished(m, own, other, w_in, w_out, state, values):
    return pl.pallas_call(
        lambda *refs: final_kernel(m, *refs),
        out_shape=STATE
        + (jax.ShapeDtypeStruct((4, 3, 32, 640), F32), jax.ShapeDtypeStruct((4, 3, 32, 640), BF16)),
        in_specs=[VMEM] * 7,
        out_specs=(VMEM,) * 4,
        input_output_aliases={4: 0, 5: 1},
        scratch_shapes=[
            pltpu.VMEM((8, 128, 1280), BF16),
            pltpu.VMEM((8, 128, 640), BF16),
            pltpu.VMEM((8, 3, 32, 640), F32),
        ],
        compiler_params=PARAMS,
        cost_estimate=priced(4),
        name="finish",
    )(own, other, w_in, w_out, *state, values)[2:]


def last_kernel(values, acc, cols, keep, send, gates, hidden, total):
    xl, y, z, _, c = place()
    workers = lax.broadcasted_iota(I32, (64, 128), 0)

    def part(p, _):
        dy, ex = p >> 1, p & 1
        number = ((xl ^ ex) * 4 + (y ^ dy)) * 8 + z
        mask = ((number - workers) & 63) < 5
        w = jnp.sum(jnp.where(mask, values[...], 0.0), axis=0, keepdims=True)[:, :1]
        for r in range(0, 128, 32):
            rows = pl.ds(r, 32)
            u = acc[0, p, rows]
            v = acc[1, p, rows]
            d = acc[2, p, rows] * w
            square = u * u
            t = jnp.tanh(ROOT_2_PI * (u + CUBIC * (square * u)))
            cdf = 0.5 * (1.0 + t)
            act = u * cdf
            slope = cdf + 0.5 * u * (1.0 - t * t) * (ROOT_2_PI * (1.0 + 3.0 * CUBIC * square))
            gates[p, rows, 0:640] = (d * v * slope).astype(BF16)
            gates[p, rows, 640:1280] = (d * act).astype(BF16)
            hidden[p, rows] = (act * v * w).astype(BF16)
        return 0

    lax.fori_loop(0, 8, part, 0)
    dims = (((0,), (0,)), ((), ()))
    both = lax.dot_general(
        cols[0].reshape(1024, 256), gates[...].reshape(1024, 1280), dims, preferred_element_type=F32
    )
    total[:, 0] = both[:, :640].reshape(8, 32, 640)
    total[:, 1] = both[:, 640:].reshape(8, 32, 640)
    total[:, 2] = lax.dot_general(
        cols[1].reshape(1024, 256), hidden[...].reshape(1024, 640), dims, preferred_element_type=F32
    ).reshape(8, 32, 640)
    odd = z & 1
    near = jnp.where(odd == 1, z + 1, z - 1) & 7
    near = jnp.where(c == 0, z ^ 1, near)
    for k in range(4):
        keep[k] = total[((z >> 1) + k & 3) * 2 + odd]
        send[k] = total[((near >> 1) + k & 3) * 2 + (1 - odd)].astype(BF16)


def all_steps(tokens, grad_out, w_gate, w_lin, w_out_t, code, decode, stragglers):
    own = jnp.stack([tokens, grad_out])
    row = [own] + [across(own, k, True) for k in (1, 2, 3)]
    picked, w_in, w_out = prepare(code, decode, stragglers, w_gate, w_lin, w_out_t)
    row, picked = lax.optimization_barrier((jnp.stack(row), picked))
    near = [row]
    for k in (1, 2, 3):
        near.append(across(row, k, False))
    values = lax.all_to_all(picked, BLK, 0, 0, tiled=True)
    swap = sibling(row)
    first, values = lax.optimization_barrier((row, values))
    state = gathered(0, first, swap, w_in, w_out, ())
    state, near[1], near[3] = lax.optimization_barrier((state, near[1], near[3]))
    other = {k: sibling(near[k]) for k in (1, 3)}
    for m in (1, 3):
        state = gathered(m, near[m], other[m], w_in, w_out, state)
    state, near[2] = lax.optimization_barrier((state, near[2]))
    keep, send = finished(2, near[2], sibling(near[2]), w_in, w_out, state, values)
    got = z_pair(send)
    mixed = keep + got.astype(F32)
    result = mixed[0]
    for k in (1, 3, 2):
        result = result + z_step(mixed[k].astype(BF16), 2 * k).astype(F32)
    return jnp.transpose(result, (1, 0, 2))


def solution(mesh):
    split = Mesh(mesh.devices.reshape(2, 4, 8, 2, 2), ("xl", "y", "z", "xh", "c"))
    mp = ("xh", "c")
    in_specs = (P(BLK, mp), P(BLK, mp), P(None, mp), P(None, mp), P(None, mp), P(BLK, None), P(BLK), P())
    return jax.shard_map(all_steps, mesh=split, in_specs=in_specs, out_specs=P(BLK, None, mp), check_vma=False)
```

time: 238 us -> 95.7 us (0.40)
  the two profiles are of different devices: /device:TPU:6 before, /device:TPU:32 now
where the time goes in v1:
time: 95.7 us; the launch traced here: 95.4 us
  waiting for transfers between devices  31.3 us (33%)
  blocking collectives  19 us (20%)
  Pallas kernels  18 us (19%)
  starting transfers between devices  17.7 us (18%)
  local copies, waits for them, and re-layouts  6.56 us (7%)
  other arithmetic  2.03 us (2%)
    all_to_all x1, blocking collectives, all_steps(): values = lax.all_to_all(picked, BLK, 0, 0, tiled=True)  19 us
    ppermute x3, waiting for transfers between devices, z_step(): return lax.ppermute(block, 'z', [(z, (z + step) % 8) for z in range(8)])  11.1 us
    ppermute x6, starting transfers between devices, across(): return lax.ppermute(block, PLANE, route)  9.73 us
    pallas_call x3, Pallas kernels, gathered(): pl.pallas_call((lambda *refs: middle_kernel(m, *refs)) if state else firs...  9.68 us
    ppermute x6, waiting for transfers between devices, across(): return lax.ppermute(block, PLANE, route)  9.05 us
    ppermute x1, waiting for transfers between devices, z_pair(): lax.ppermute(block, ('z', 'c'), [(z * 2 + c, partner_of(z, c) * 2 + c) fo...  7.42 us
    pallas_call x1, Pallas kernels, finished(): pl.pallas_call(lambda *refs: final_kernel(m, *refs), out_shape=STATE + (j...  7.11 us
    unnamed x10, local copies, waits for them, and re-layouts  6.52 us
  transfers between devices with their start and end apart: 14, of which 8 were waited for; matrix products, arithmetic and copies ran while one was open for 0% of the time, Pallas kernels for 11%

profile of v1, /device:TPU:32, one launch (start us, length us, event | category | flops | bytes accessed | tf_op | source)
XLA Modules:
  0.0 95.4 jit_solution(12462233205094496048)
XLA Ops:
  0.0 1.0 %fusion.4 = (bf16[1,2,128,512]{3,2,1,0:T(8,128)(2,1)S(1)}, bf16[2,128,512]{2,1,0:T(8,128)(2,1)S(1)}) fusion(bf16[1,128,512]{2,1,0:T(8,128)(2,1)} %bitcast.40, bf16[1,128,512]{2,1,0:T(8,128)(2,1)} %bitcast.41), kind=kLoop, calls=%fused_computation.11 | loop fusion | flops 131072 | bytes 786432 | tf_op jit(solution)/shard_map/stack | solution.py:226
  1.0 1.6 %collective-permute-start = (bf16[2,128,512]{2,1,0:T(8,128)(2,1)S(1)}, bf16[2,128,512]{2,1,0:T(8,128)(2,1)S(1)}, u32[]{:S(2)}, u32[]{:S(2)}) collective-permute-start(bf16[2,128,512]{2,1,0:T(8,128)(2,1)S(1)} %get-tuple-element.55), channel_id=1, source_target_pairs={{0,128},{1,33},{2,130},{3,35},{32,160},{33,1},{34,162},{35,3},{64,... | collective-permute-start | bytes 786440 | tf_op jit(solution)/shard_map/ppermute | solution.py:35
  2.6 2.7 %collective-permute-start.1 = (bf16[2,128,512]{2,1,0:T(8,128)(2,1)S(1)}, bf16[2,128,512]{2,1,0:T(8,128)(2,1)S(1)}, u32[]{:S(2)}, u32[]{:S(2)}) collective-permute-start(bf16[2,128,512]{2,1,0:T(8,128)(2,1)S(1)} %get-tuple-element.55), channel_id=1, source_target_pairs={{0,2},{1,65},{2,0},{3,67},{32,34},{33,97},{34,32},{35,99},{64,66},... | collective-permute-start | bytes 786440 | tf_op jit(solution)/shard_map/ppermute | solution.py:35
  5.3 0.5 collective-permute-start.2
  6.5 1.7 %copy-done = bf16[2048,640]{1,0:T(8,128)(2,1)S(1)} copy-done((bf16[2048,640]{1,0:T(8,128)(2,1)S(1)}, bf16[2048,640]{1,0:T(8,128)(2,1)}, u32[]{:S(2)}) %copy-start) | copy-done | bytes 2621464
  8.2 1.7 %copy-done.1 = bf16[2048,640]{1,0:T(8,128)(2,1)S(1)} copy-done((bf16[2048,640]{1,0:T(8,128)(2,1)S(1)}, bf16[2048,640]{1,0:T(8,128)(2,1)}, u32[]{:S(2)}) %copy-start.1) | copy-done | bytes 2621464
  9.9 1.7 %copy-done.2 = bf16[2048,640]{1,0:T(8,128)(2,1)S(1)} copy-done((bf16[2048,640]{1,0:T(8,128)(2,1)S(1)}, bf16[2048,640]{1,0:T(8,128)(2,1)}, u32[]{:S(2)}) %copy-start.2) | copy-done | bytes 2621464
  11.7 0.7 copy-done.3
  12.3 0.7 copy-done.4
  13.0 1.2 %prepare.1 = (f32[64,128]{1,0:T(8,128)S(1)}, bf16[4,512,1280]{2,1,0:T(8,128)(2,1)S(1)}, bf16[4,512,640]{2,1,0:T(8,128)(2,1)S(1)}) custom-call(f32[1,5]{1,0:T(1,128)S(1)} %copy-done.3, f32[1]{0:T(128)S(6)} %copy.22.decode, s32[4]{0:T(128)S(1)} %copy-done.4, bf16[4,512,640]{2,1,0:T(8,128)(2,1)S(1)} %bitcast.32, bf16[4,512,640]{2,1,0:T(8,128)(2,1)S(1)} %bitcast.33, ...), custom_call_target="tpu_custom_call" | custom-call | tf_op jit(solution)/shard_map/prepare/pallas_call | solution.py:79
  14.2 1.0 %collective-permute-done.2 = bf16[2,128,512]{2,1,0:T(8,128)(2,1)S(1)} collective-permute-done((bf16[2,128,512]{2,1,0:T(8,128)(2,1)S(1)}, bf16[2,128,512]{2,1,0:T(8,128)(2,1)S(1)}, u32[]{:S(2)}, u32[]{:S(2)}) %collective-permute-start.2) | collective-permute-done | bytes 262176 | tf_op jit(solution)/shard_map/ppermute | solution.py:35
  15.5 1.7 %collective-permute-start.4 = (bf16[4,2,128,512]{3,2,1,0:T(8,128)(2,1)S(1)}, bf16[4,2,128,512]{3,2,1,0:T(8,128)(2,1)S(1)}, u32[]{:S(2)}, u32[]{:S(2)}) collective-permute-start(bf16[4,2,128,512]{3,2,1,0:T(8,128)(2,1)S(1)} %pad_maximum_fusion.own), channel_id=1, source_target_pairs={{0,32},{1,129},{2,34},{3,131},{32,0},{33,161},{34,2},{35,163},{64,... | collective-permute-start | bytes 3145736 | tf_op jit(solution)/shard_map/ppermute | solution.py:35
  17.2 2.2 %collective-permute-start.5 = (bf16[4,2,128,512]{3,2,1,0:T(8,128)(2,1)S(1)}, bf16[4,2,128,512]{3,2,1,0:T(8,128)(2,1)S(1)}, u32[]{:S(2)}, u32[]{:S(2)}) collective-permute-start(bf16[4,2,128,512]{3,2,1,0:T(8,128)(2,1)S(1)} %pad_maximum_fusion.own), channel_id=1, source_target_pairs={{0,96},{1,131},{2,98},{3,129},{32,64},{33,163},{34,66},{35,161},{6... | collective-permute-start | bytes 3145736 | tf_op jit(solution)/shard_map/ppermute | solution.py:35
  19.4 19.0 %all_to_all.12 = f32[64,1,128]{2,1,0:T(1,128)S(1)} all-to-all(f32[64,1,128]{2,1,0:T(1,128)S(1)} %bitcast.36), channel_id=1, replica_groups=mesh['xl'=2,'y'=4,'z'=8,'xh'=2,'c'=2] {'xl','y','z'}, dimensions={0} | all-to-all | bytes 65536 | tf_op jit(solution)/shard_map/all_to_all | solution.py:230
  38.4 3.6 %shard_map.82 = (f32[3,8,128,640]{3,2,1,0:T(8,128)S(1)}, bf16[2,8,128,256]{3,2,1,0:T(8,128)(2,1)S(1)}) custom-call(bf16[4,2,128,512]{3,2,1,0:T(8,128)(2,1)S(1)} %pad_maximum_fusion.own, bf16[4,2,128,512]{3,2,1,0:T(8,128)(2,1)S(1)} %collective-permute-done.3.other, bf16[4,512,1280]{2,1,0:T(8,128)(2,1)S(1)} %get-tuple-element.31.w_in.refs_2_, ...), custom_call_target="tpu_custom_call" | custom-call | flops 2147483648 | bytes 1048576 | tf_op jit(solution)/shard_map/pallas_call | solution.py:150
  42.0 0.5 collective-permute-start.6
  42.5 1.1 %collective-permute-start.8 = (bf16[4,2,128,512]{3,2,1,0:T(8,128)(2,1)S(1)}, bf16[4,2,128,512]{3,2,1,0:T(8,128)(2,1)S(1)}, u32[]{:S(2)}, u32[]{:S(2)}) collective-permute-start(bf16[4,2,128,512]{3,2,1,0:T(8,128)(2,1)S(1)} %pad_maximum_fusion.own), channel_id=1, source_target_pairs={{0,64},{1,3},{2,66},{3,1},{32,96},{33,35},{34,98},{35,33},{64,0},{... | collective-permute-start | bytes 3145736 | tf_op jit(solution)/shard_map/ppermute | solution.py:35
  43.6 1.1 %collective-permute-done.7.refs_1_ = bf16[4,2,128,512]{3,2,1,0:T(8,128)(2,1)S(1)} collective-permute-done((bf16[4,2,128,512]{3,2,1,0:T(8,128)(2,1)S(1)}, bf16[4,2,128,512]{3,2,1,0:T(8,128)(2,1)S(1)}, u32[]{:S(2)}, u32[]{:S(2)}) %collective-permute-start.7) | collective-permute-done | bytes 1048608 | tf_op jit(solution)/shard_map/ppermute | solution.py:39
  44.7 3.0 %shard_map.83 = (f32[3,8,128,640]{3,2,1,0:T(8,128)S(1)}, bf16[2,8,128,256]{3,2,1,0:T(8,128)(2,1)S(1)}) custom-call(bf16[4,2,128,512]{3,2,1,0:T(8,128)(2,1)S(1)} %collective-permute-done.4.refs_0_, bf16[4,2,128,512]{3,2,1,0:T(8,128)(2,1)S(1)} %collective-permute-done.7.refs_1_, ...), custom_call_target="tpu_custom_call", output_to_operand_aliasing={{0}: (4, {}), {1}: (5, {})} | custom-call | flops 2147483648 | bytes 1048576 | tf_op jit(solution)/shard_map/pallas_call | solution.py:150
  47.8 3.1 %shard_map.84 = (f32[3,8,128,640]{3,2,1,0:T(8,128)S(1)}, bf16[2,8,128,256]{3,2,1,0:T(8,128)(2,1)S(1)}) custom-call(bf16[4,2,128,512]{3,2,1,0:T(8,128)(2,1)S(1)} %collective-permute-done.5.refs_0_, bf16[4,2,128,512]{3,2,1,0:T(8,128)(2,1)S(1)} %collective-permute-done.6.refs_1_, ...), custom_call_target="tpu_custom_call", output_to_operand_aliasing={{0}: (4, {}), {1}: (5, {})} | custom-call | flops 2147483648 | bytes 1048576 | tf_op jit(solution)/shard_map/pallas_call | solution.py:150
  50.8 8.0 %collective-permute-done.8.refs_0_ = bf16[4,2,128,512]{3,2,1,0:T(8,128)(2,1)S(1)} collective-permute-done((bf16[4,2,128,512]{3,2,1,0:T(8,128)(2,1)S(1)}, bf16[4,2,128,512]{3,2,1,0:T(8,128)(2,1)S(1)}, u32[]{:S(2)}, u32[]{:S(2)}) %collective-permute-start.8) | collective-permute-done | bytes 1048608 | tf_op jit(solution)/shard_map/ppermute | solution.py:35
  58.8 2.7 %collective-permute-done.9.refs_1_ = bf16[4,2,128,512]{3,2,1,0:T(8,128)(2,1)S(1)} collective-permute-done((bf16[4,2,128,512]{3,2,1,0:T(8,128)(2,1)S(1)}, bf16[4,2,128,512]{3,2,1,0:T(8,128)(2,1)S(1)}, u32[]{:S(2)}, u32[]{:S(2)}) %collective-permute-start.9) | collective-permute-done | bytes 1048608 | tf_op jit(solution)/shard_map/ppermute | solution.py:39
  61.5 7.1 %finish.1 = (f32[3,8,128,640]{3,2,1,0:T(8,128)S(1)}, bf16[2,8,128,256]{3,2,1,0:T(8,128)(2,1)S(1)}, f32[4,3,32,640]{3,2,1,0:T(8,128)S(1)}, bf16[4,3,32,640]{3,2,1,0:T(8,128)(2,1)S(1)}) custom-call(bf16[4,2,128,512]{3,2,1,0:T(8,128)(2,1)S(1)} %collective-permute-done.8.refs_0_, ...), custom_call_target="tpu_custom_call", output_to_operand_aliasing={{0}: (4, {}), {1}: (5, {})} | custom-call | flops 4294967296 | bytes 1048576 | tf_op jit(solution)/shard_map/finish/pallas_call | solution.py:162
  68.6 1.5 %collective-permute-start.10 = (bf16[4,3,32,640]{3,2,1,0:T(8,128)(2,1)S(1)}, bf16[4,3,32,640]{3,2,1,0:T(8,128)(2,1)S(1)}, u32[]{:S(2)}, u32[]{:S(2)}) collective-permute-start(bf16[4,3,32,640]{3,2,1,0:T(8,128)(2,1)S(1)} %get-tuple-element.48), channel_id=1, source_target_pairs={{0,4},{1,29},{4,0},{5,9},{8,12},{9,5},{12,8},{13,17},{16,20},{17,1... | collective-permute-start | bytes 1474568 | tf_op jit(solution)/shard_map/ppermute | solution.py:47
  70.1 7.4 %collective-permute-done.10 = bf16[4,3,32,640]{3,2,1,0:T(8,128)(2,1)S(1)} collective-permute-done((bf16[4,3,32,640]{3,2,1,0:T(8,128)(2,1)S(1)}, bf16[4,3,32,640]{3,2,1,0:T(8,128)(2,1)S(1)}, u32[]{:S(2)}, u32[]{:S(2)}) %collective-permute-start.10) | collective-permute-done | bytes 491552 | tf_op jit(solution)/shard_map/ppermute | solution.py:47
  77.7 0.7 collective-permute-start.11
  78.4 3.5 %collective-permute-start.12 = (bf16[3,32,640]{2,1,0:T(8,128)(2,1)S(1)}, bf16[3,32,640]{2,1,0:T(8,128)(2,1)S(1)}, u32[]{:S(2)}, u32[]{:S(2)}) collective-permute-start(bf16[3,32,640]{2,1,0:T(8,128)(2,1)S(1)} %get-tuple-element.53), channel_id=1, source_target_pairs={{0,24},{4,28},{8,0},{12,4},{16,8},{20,12},{24,16},{28,20},{1,25},{... | collective-permute-start | bytes 368648 | tf_op jit(solution)/shard_map/ppermute | solution.py:51
  81.9 1.6 %collective-permute-start.13 = (bf16[3,32,640]{2,1,0:T(8,128)(2,1)S(1)}, bf16[3,32,640]{2,1,0:T(8,128)(2,1)S(1)}, u32[]{:S(2)}, u32[]{:S(2)}) collective-permute-start(bf16[3,32,640]{2,1,0:T(8,128)(2,1)S(1)} %get-tuple-element.52), channel_id=1, source_target_pairs={{0,16},{4,20},{8,24},{12,28},{16,0},{20,4},{24,8},{28,12},{1,17},{... | collective-permute-start | bytes 368648 | tf_op jit(solution)/shard_map/ppermute | solution.py:51
  83.6 1.6 %collective-permute-done.11 = bf16[3,32,640]{2,1,0:T(8,128)(2,1)S(1)} collective-permute-done((bf16[3,32,640]{2,1,0:T(8,128)(2,1)S(1)}, bf16[3,32,640]{2,1,0:T(8,128)(2,1)S(1)}, u32[]{:S(2)}, u32[]{:S(2)}) %collective-permute-start.11) | collective-permute-done | bytes 122912 | tf_op jit(solution)/shard_map/ppermute | solution.py:51
  85.2 3.6 %collective-permute-done.12 = bf16[3,32,640]{2,1,0:T(8,128)(2,1)S(1)} collective-permute-done((bf16[3,32,640]{2,1,0:T(8,128)(2,1)S(1)}, bf16[3,32,640]{2,1,0:T(8,128)(2,1)S(1)}, u32[]{:S(2)}, u32[]{:S(2)}) %collective-permute-start.12) | collective-permute-done | bytes 122912 | tf_op jit(solution)/shard_map/ppermute | solution.py:51
  88.8 5.8 %collective-permute-done.13 = bf16[3,32,640]{2,1,0:T(8,128)(2,1)S(1)} collective-permute-done((bf16[3,32,640]{2,1,0:T(8,128)(2,1)S(1)}, bf16[3,32,640]{2,1,0:T(8,128)(2,1)S(1)}, u32[]{:S(2)}, u32[]{:S(2)}) %collective-permute-start.13) | collective-permute-done | bytes 122912 | tf_op jit(solution)/shard_map/ppermute | solution.py:51
  94.7 0.8 fusion.3
  (17 shorter events, 0.5 us)
Async XLA Ops:
  1.0 13.2 %collective-permute-start = (bf16[2,128,512]{2,1,0:T(8,128)(2,1)S(1)}, bf16[2,128,512]{2,1,0:T(8,128)(2,1)S(1)}, u32[]{:S(2)}, u32[]{:S(2)}) collective-permute-start(bf16[2,128,512]{2,1,0:T(8,128)(2,1)S(1)} %get-tuple-element.55), channel_id=1, source_target_pairs={{0,128},{1,33},{2,130},{3,35},{32,160},{33,1},{34,162},{35,3},{64,... | collective-permute-start | bytes 786440 | tf_op jit(solution)/shard_map/ppermute | solution.py:35
  2.6 11.7 %collective-permute-start.1 = (bf16[2,128,512]{2,1,0:T(8,128)(2,1)S(1)}, bf16[2,128,512]{2,1,0:T(8,128)(2,1)S(1)}, u32[]{:S(2)}, u32[]{:S(2)}) collective-permute-start(bf16[2,128,512]{2,1,0:T(8,128)(2,1)S(1)} %get-tuple-element.55), channel_id=1, source_target_pairs={{0,2},{1,65},{2,0},{3,67},{32,34},{33,97},{34,32},{35,99},{64,66},... | collective-permute-start | bytes 786440 | tf_op jit(solution)/shard_map/ppermute | solution.py:35
  5.3 10.0 %collective-permute-start.2 = (bf16[2,128,512]{2,1,0:T(8,128)(2,1)S(1)}, bf16[2,128,512]{2,1,0:T(8,128)(2,1)S(1)}, u32[]{:S(2)}, u32[]{:S(2)}) collective-permute-start(bf16[2,128,512]{2,1,0:T(8,128)(2,1)S(1)} %get-tuple-element.55), channel_id=1, source_target_pairs={{0,130},{1,97},{2,128},{3,99},{32,162},{33,65},{34,160},{35,67},{6... | collective-permute-start | bytes 786440 | tf_op jit(solution)/shard_map/ppermute | solution.py:35
  6.4 1.7 %copy-start = (bf16[2048,640]{1,0:T(8,128)(2,1)S(1)}, bf16[2048,640]{1,0:T(8,128)(2,1)}, u32[]{:S(2)}) copy-start(bf16[2048,640]{1,0:T(8,128)(2,1)} %param.10) | copy-start | bytes 7864324
  8.2 1.7 %copy-start.1 = (bf16[2048,640]{1,0:T(8,128)(2,1)S(1)}, bf16[2048,640]{1,0:T(8,128)(2,1)}, u32[]{:S(2)}) copy-start(bf16[2048,640]{1,0:T(8,128)(2,1)} %param.11) | copy-start | bytes 7864324
  9.9 1.7 %copy-start.2 = (bf16[2048,640]{1,0:T(8,128)(2,1)S(1)}, bf16[2048,640]{1,0:T(8,128)(2,1)}, u32[]{:S(2)}) copy-start(bf16[2048,640]{1,0:T(8,128)(2,1)} %param.12) | copy-start | bytes 7864324
  11.7 0.7 copy-start.3
  12.3 0.7 copy-start.4
  15.4 22.9 %collective-permute-start.3 = (bf16[4,2,128,512]{3,2,1,0:T(8,128)(2,1)S(1)}, bf16[4,2,128,512]{3,2,1,0:T(8,128)(2,1)S(1)}, u32[]{:S(2)}, u32[]{:S(2)}) collective-permute-start(bf16[4,2,128,512]{3,2,1,0:T(8,128)(2,1)S(1)} %pad_maximum_fusion.own), channel_id=1, source_target_pairs={{0,1},{1,0},{2,3},{3,2},{4,5},{5,4},{6,7},{7,6},{8,9},{9,8},{10,11... | collective-permute-start | bytes 3145736 | tf_op jit(solution)/shard_map/ppermute | solution.py:39
  15.5 26.4 %collective-permute-start.4 = (bf16[4,2,128,512]{3,2,1,0:T(8,128)(2,1)S(1)}, bf16[4,2,128,512]{3,2,1,0:T(8,128)(2,1)S(1)}, u32[]{:S(2)}, u32[]{:S(2)}) collective-permute-start(bf16[4,2,128,512]{3,2,1,0:T(8,128)(2,1)S(1)} %pad_maximum_fusion.own), channel_id=1, source_target_pairs={{0,32},{1,129},{2,34},{3,131},{32,0},{33,161},{34,2},{35,163},{64,... | collective-permute-start | bytes 3145736 | tf_op jit(solution)/shard_map/ppermute | solution.py:35
  17.2 24.8 %collective-permute-start.5 = (bf16[4,2,128,512]{3,2,1,0:T(8,128)(2,1)S(1)}, bf16[4,2,128,512]{3,2,1,0:T(8,128)(2,1)S(1)}, u32[]{:S(2)}, u32[]{:S(2)}) collective-permute-start(bf16[4,2,128,512]{3,2,1,0:T(8,128)(2,1)S(1)} %pad_maximum_fusion.own), channel_id=1, source_target_pairs={{0,96},{1,131},{2,98},{3,129},{32,64},{33,163},{34,66},{35,161},{6... | collective-permute-start | bytes 3145736 | tf_op jit(solution)/shard_map/ppermute | solution.py:35
  41.9 2.7 %collective-permute-start.7 = (bf16[4,2,128,512]{3,2,1,0:T(8,128)(2,1)S(1)}, bf16[4,2,128,512]{3,2,1,0:T(8,128)(2,1)S(1)}, u32[]{:S(2)}, u32[]{:S(2)}) collective-permute-start(bf16[4,2,128,512]{3,2,1,0:T(8,128)(2,1)S(1)} %collective-permute-done.4.refs_0_), channel_id=1, source_target_pairs={{0,1},{1,0},{2,3},{3,2},{4,5},{5,4},{6,7},{7,6},{8,9},{9,8},{10,11... | collective-permute-start | bytes 3145736 | tf_op jit(solution)/shard_map/ppermute | solution.py:39
  42.0 5.7 %collective-permute-start.6 = (bf16[4,2,128,512]{3,2,1,0:T(8,128)(2,1)S(1)}, bf16[4,2,128,512]{3,2,1,0:T(8,128)(2,1)S(1)}, u32[]{:S(2)}, u32[]{:S(2)}) collective-permute-start(bf16[4,2,128,512]{3,2,1,0:T(8,128)(2,1)S(1)} %collective-permute-done.5.refs_0_), channel_id=1, source_target_pairs={{0,1},{1,0},{2,3},{3,2},{4,5},{5,4},{6,7},{7,6},{8,9},{9,8},{10,11... | collective-permute-start | bytes 3145736 | tf_op jit(solution)/shard_map/ppermute | solution.py:39
  42.5 16.3 %collective-permute-start.8 = (bf16[4,2,128,512]{3,2,1,0:T(8,128)(2,1)S(1)}, bf16[4,2,128,512]{3,2,1,0:T(8,128)(2,1)S(1)}, u32[]{:S(2)}, u32[]{:S(2)}) collective-permute-start(bf16[4,2,128,512]{3,2,1,0:T(8,128)(2,1)S(1)} %pad_maximum_fusion.own), channel_id=1, source_target_pairs={{0,64},{1,3},{2,66},{3,1},{32,96},{33,35},{34,98},{35,33},{64,0},{... | collective-permute-start | bytes 3145736 | tf_op jit(solution)/shard_map/ppermute | solution.py:35
  58.8 2.7 %collective-permute-start.9 = (bf16[4,2,128,512]{3,2,1,0:T(8,128)(2,1)S(1)}, bf16[4,2,128,512]{3,2,1,0:T(8,128)(2,1)S(1)}, u32[]{:S(2)}, u32[]{:S(2)}) collective-permute-start(bf16[4,2,128,512]{3,2,1,0:T(8,128)(2,1)S(1)} %collective-permute-done.8.refs_0_), channel_id=1, source_target_pairs={{0,1},{1,0},{2,3},{3,2},{4,5},{5,4},{6,7},{7,6},{8,9},{9,8},{10,11... | collective-permute-start | bytes 3145736 | tf_op jit(solution)/shard_map/ppermute | solution.py:39
  68.6 8.9 %collective-permute-start.10 = (bf16[4,3,32,640]{3,2,1,0:T(8,128)(2,1)S(1)}, bf16[4,3,32,640]{3,2,1,0:T(8,128)(2,1)S(1)}, u32[]{:S(2)}, u32[]{:S(2)}) collective-permute-start(bf16[4,3,32,640]{3,2,1,0:T(8,128)(2,1)S(1)} %get-tuple-element.48), channel_id=1, source_target_pairs={{0,4},{1,29},{4,0},{5,9},{8,12},{9,5},{12,8},{13,17},{16,20},{17,1... | collective-permute-start | bytes 1474568 | tf_op jit(solution)/shard_map/ppermute | solution.py:47
  77.7 7.5 %collective-permute-start.11 = (bf16[3,32,640]{2,1,0:T(8,128)(2,1)S(1)}, bf16[3,32,640]{2,1,0:T(8,128)(2,1)S(1)}, u32[]{:S(2)}, u32[]{:S(2)}) collective-permute-start(bf16[3,32,640]{2,1,0:T(8,128)(2,1)S(1)} %get-tuple-element.51), channel_id=1, source_target_pairs={{0,8},{4,12},{8,16},{12,20},{16,24},{20,28},{24,0},{28,4},{1,9},{5... | collective-permute-start | bytes 368648 | tf_op jit(solution)/shard_map/ppermute | solution.py:51
  78.4 10.4 %collective-permute-start.12 = (bf16[3,32,640]{2,1,0:T(8,128)(2,1)S(1)}, bf16[3,32,640]{2,1,0:T(8,128)(2,1)S(1)}, u32[]{:S(2)}, u32[]{:S(2)}) collective-permute-start(bf16[3,32,640]{2,1,0:T(8,128)(2,1)S(1)} %get-tuple-element.53), channel_id=1, source_target_pairs={{0,24},{4,28},{8,0},{12,4},{16,8},{20,12},{24,16},{28,20},{1,25},{... | collective-permute-start | bytes 368648 | tf_op jit(solution)/shard_map/ppermute | solution.py:51
  81.9 12.7 %collective-permute-start.13 = (bf16[3,32,640]{2,1,0:T(8,128)(2,1)S(1)}, bf16[3,32,640]{2,1,0:T(8,128)(2,1)S(1)}, u32[]{:S(2)}, u32[]{:S(2)}) collective-permute-start(bf16[3,32,640]{2,1,0:T(8,128)(2,1)S(1)} %get-tuple-element.52), channel_id=1, source_target_pairs={{0,16},{4,20},{8,24},{12,28},{16,0},{20,4},{24,8},{28,12},{1,17},{... | collective-permute-start | bytes 368648 | tf_op jit(solution)/shard_map/ppermute | solution.py:51

commit v2 on v1

--- a/solution.py
+++ b/solution.py
@@ -51,7 +51,57 @@
     return lax.ppermute(block, "z", [(z, (z + step) % 8) for z in range(8)])
 
 
-def prepare_kernel(code, decode, stragglers, w_gate, w_lin, w_out_t, picked, w_in, w_out, sems):
+def hbm(array):
+    return pltpu.with_memory_space_constraint(array, pltpu.HBM)
+
+
+def message_kernel(decode, code_in, stragglers_in, tokens, grad_out, out, code, stragglers, sems):
+    pairs = (
+        (tokens, out.at[pl.ds(0, 128)]),
+        (grad_out, out.at[pl.ds(128, 128)]),
+        (code_in, code),
+        (stragglers_in, stragglers),
+    )
+    copies = [pltpu.make_async_copy(source, target, sems.at[i]) for i, (source, target) in enumerate(pairs)]
+    for copy in copies:
+        copy.start()
+    for copy in copies[2:]:
+        copy.wait()
+    xl, y, z, _, _ = place()
+    device = (xl * 4 + y) * 8 + z
+    alive = stragglers[0] != device
+    for i in range(1, 4):
+        alive = alive & (stragglers[i] != device)
+    scale = jnp.where(alive, decode[0], 0.0)
+    lane = lax.broadcasted_iota(I32, (8, 128), 1)
+    row = lax.broadcasted_iota(I32, (8, 128), 0)
+    value = jnp.zeros((8, 128), F32)
+    for j in range(5):
+        value = jnp.where(lane == j, scale * code[0, j], value)
+    high = value.astype(BF16).astype(F32)
+    rest = value - high
+    middle = rest.astype(BF16).astype(F32)
+    low = rest - middle
+    pieces = jnp.where(row == 0, high, jnp.where(row == 1, middle, jnp.where(row == 2, low, 0.0)))
+    out[256:264, :] = jnp.zeros((8, 512), BF16)
+    out[256:264, 0:128] = pieces.astype(BF16)
+    for copy in copies[:2]:
+        copy.wait()
+
+
+def message(code, decode, stragglers, tokens, grad_out):
+    return pl.pallas_call(
+        message_kernel,
+        out_shape=jax.ShapeDtypeStruct((264, 512), BF16),
+        in_specs=[SMEM] + [pl.BlockSpec(memory_space=pltpu.HBM)] * 4,
+        out_specs=VMEM,
+        scratch_shapes=[pltpu.SMEM((1, 5), F32), pltpu.SMEM((4,), I32), pltpu.SemaphoreType.DMA((4,))],
+        compiler_params=PARAMS,
+        name="message",
+    )(decode, *[hbm(a) for a in (code, stragglers, tokens, grad_out)])
+
+
+def weights_kernel(w_gate, w_lin, w_out_t, w_in, w_out, token, sems):
     copies = [
         pltpu.make_async_copy(w_gate, w_in.at[:, :, pl.ds(0, 640)], sems.at[0]),
         pltpu.make_async_copy(w_lin, w_in.at[:, :, pl.ds(640, 640)], sems.at[1]),
@@ -59,55 +109,62 @@
     ]
     for copy in copies:
         copy.start()
-    xl, y, z, _, _ = place()
-    device = (xl * 4 + y) * 8 + z
-    alive = stragglers[0] != device
-    for i in range(1, 4):
-        alive = alive & (stragglers[i] != device)
-    scale = jnp.where(alive, decode[0], 0.0)
-    slot = (lax.broadcasted_iota(I32, (64, 128), 0) - z) & 7
-    value = jnp.zeros((64, 128), F32)
-    for j in range(5):
-        value = jnp.where(slot == j, scale * code[0, j], value)
-    picked[...] = value
+    token[...] = jnp.zeros_like(token)
     for copy in copies:
         copy.wait()
 
 
-def prepare(code, decode, stragglers, w_gate, w_lin, w_out_t):
-    whole = pl.BlockSpec(memory_space=pltpu.HBM)
+def loaded_weights(w_gate, w_lin, w_out_t):
     return pl.pallas_call(
-        prepare_kernel,
+        weights_kernel,
         out_shape=(
-            jax.ShapeDtypeStruct((64, 128), F32),
             jax.ShapeDtypeStruct((4, 512, 1280), BF16),
             jax.ShapeDtypeStruct((4, 512, 640), BF16),
+            jax.ShapeDtypeStruct((8, 128), F32),
         ),
-        in_specs=[SMEM] * 3 + [whole] * 3,
+        in_specs=[pl.BlockSpec(memory_space=pltpu.HBM)] * 3,
         out_specs=(VMEM, VMEM, VMEM),
         scratch_shapes=[pltpu.SemaphoreType.DMA((3,))],
         compiler_params=PARAMS,
-        name="prepare",
-    )(code, decode, stragglers, *[w.reshape(4, 512, 640) for w in (w_gate, w_lin, w_out_t)])
-
-
-def first_kernel(own, other, w_in, w_out, acc, cols):
+        name="load",
+    )(*[hbm(w.reshape(4, 512, 640)) for w in (w_gate, w_lin, w_out_t)])
+
+
+def read_rows(ex, own, other, rows):
+    c = lax.axis_index("c").astype(I32)
+    for dy in range(4):
+        piece = [block[dy, 256:264, 0:128].astype(F32) for block in (own, other)]
+        piece = jnp.where(c == 1, piece[0], piece[1])
+        rows[2 * dy + ex : 2 * dy + ex + 1, :] = jnp.sum(piece, axis=0, keepdims=True)
+
+
+def first_kernel(own, other, w_in, w_out, acc, cols, rows):
     acc[...] = jnp.zeros_like(acc)
-    gather_kernel(0, own, other, w_in, w_out, acc, cols)
-
-
-def middle_kernel(m, own, other, w_in, w_out, _, __, acc, cols):
-    gather_kernel(m, own, other, w_in, w_out, acc, cols)
-
-
-def final_kernel(m, own, other, w_in, w_out, _, __, values, acc, cols, *rest):
-    gather_kernel(m, own, other, w_in, w_out, acc, cols)
-    last_kernel(values, acc, cols, *rest)
-
-
-def gather_kernel(m, own, other, w_in, w_out, acc, cols):
+    rows[...] = jnp.zeros_like(rows)
+    read_rows(0, own, other, rows)
+    gather_kernel(0, ((0, own), (1, other)), w_in, w_out, acc, cols)
+
+
+def second_kernel(own, other, w_in, w_out, _, __, ___, acc, cols, rows):
+    rows[...] = ___[...]
+    read_rows(1, own, other, rows)
+    gather_kernel(1, ((0, own), (1, other)), w_in, w_out, acc, cols)
+
+
+def middle_kernel(m, *refs):
+    *blocks, w_in, w_out, _, __, acc, cols = refs
+    gather_kernel(m, tuple(enumerate(blocks)), w_in, w_out, acc, cols)
+
+
+def final_kernel(m, other, w_in, w_out, _, __, *refs):
+    rows, (acc, cols, *rest) = refs[:5], refs[5:]
+    gather_kernel(m, ((1, other),), w_in, w_out, acc, cols)
+    last_kernel(rows, acc, cols, *rest)
+
+
+def gather_kernel(m, blocks, w_in, w_out, acc, cols):
     xl, y, _, xh, c = place()
-    for ec, block in ((0, own), (1, other)):
+    for ec, block in blocks:
         x_first = (c ^ ec) == 0
 
         def step(j, _):
@@ -115,8 +172,8 @@
             p0 = jnp.where(x_first, 2 * m, 4 * j + (m & 1))
             p1 = jnp.where(x_first, 2 * m + 1, 4 * j + 2 + (m & 1))
             shard = (xh ^ eh) * 2 + (c ^ ec)
-            xs = block[pl.ds(2 * j, 2), 0].reshape(256, 512)
-            ys = block[pl.ds(2 * j, 2), 1].reshape(256, 512)
+            xs = block[pl.ds(2 * j, 2), 0:128].reshape(256, 512)
+            ys = block[pl.ds(2 * j, 2), 128:256].reshape(256, 512)
             pre = jnp.dot(xs, w_in[shard], preferred_element_type=F32)
             acc[0, p0] += pre[:128, :640]
             acc[1, p0] += pre[:128, 640:]
@@ -146,26 +203,32 @@
     return pl.CostEstimate(flops=giga << 30, bytes_accessed=1 << 20, transcendentals=0)
 
 
-def gathered(m, own, other, w_in, w_out, state):
+ROWS = jax.ShapeDtypeStruct((8, 128), F32)
+
+
+def gathered(m, blocks, w_in, w_out, state):
+    n = len(blocks) + 2
+    with_rows = m in (0, 1)
+    kernels = {0: first_kernel, 1: second_kernel}
     return pl.pallas_call(
-        (lambda *refs: middle_kernel(m, *refs)) if state else first_kernel,
-        out_shape=STATE,
-        in_specs=[VMEM] * (4 + len(state)),
-        out_specs=(VMEM, VMEM),
-        input_output_aliases={4: 0, 5: 1} if state else {},
+        kernels.get(m, lambda *refs: middle_kernel(m, *refs)),
+        out_shape=STATE + ((ROWS,) if with_rows else ()),
+        in_specs=[VMEM] * (n + len(state)),
+        out_specs=(VMEM,) * (3 if with_rows else 2),
+        input_output_aliases={n: 0, n + 1: 1} if state else {},
         compiler_params=PARAMS,
-        cost_estimate=priced(2),
-    )(own, other, w_in, w_out, *state)
-
-
-def finished(m, own, other, w_in, w_out, state, values):
+        cost_estimate=priced(len(blocks)),
+    )(*blocks, w_in, w_out, *state)
+
+
+def finished(m, other, w_in, w_out, state, rows):
     return pl.pallas_call(
         lambda *refs: final_kernel(m, *refs),
         out_shape=STATE
         + (jax.ShapeDtypeStruct((4, 3, 32, 640), F32), jax.ShapeDtypeStruct((4, 3, 32, 640), BF16)),
-        in_specs=[VMEM] * 7,
+        in_specs=[VMEM] * 10,
         out_specs=(VMEM,) * 4,
-        input_output_aliases={4: 0, 5: 1},
+        input_output_aliases={3: 0, 4: 1},
         scratch_shapes=[
             pltpu.VMEM((8, 128, 1280), BF16),
             pltpu.VMEM((8, 128, 640), BF16),
@@ -174,18 +237,24 @@
         compiler_params=PARAMS,
         cost_estimate=priced(4),
         name="finish",
-    )(own, other, w_in, w_out, *state, values)[2:]
-
-
-def last_kernel(values, acc, cols, keep, send, gates, hidden, total):
+    )(other, w_in, w_out, *state, *rows)[2:]
+
+
+def last_kernel(rows, acc, cols, keep, send, gates, hidden, total):
     xl, y, z, _, c = place()
-    workers = lax.broadcasted_iota(I32, (64, 128), 0)
+    lane = lax.broadcasted_iota(I32, (8, 128), 1)
+    line = lax.broadcasted_iota(I32, (8, 128), 0)
+    line = (xl ^ (line & 1)) * 4 + (y ^ (line >> 1))
+    worker = line * 8 + ((z - lane) & 7)
+    terms = jnp.zeros((8, 128), F32)
+    for j in range(5):
+        terms = jnp.where(lane == j, rows[j][...], terms)
 
     def part(p, _):
         dy, ex = p >> 1, p & 1
         number = ((xl ^ ex) * 4 + (y ^ dy)) * 8 + z
-        mask = ((number - workers) & 63) < 5
-        w = jnp.sum(jnp.where(mask, values[...], 0.0), axis=0, keepdims=True)[:, :1]
+        mine = (((number - lane) & 63) == worker) & (lane < 5)
+        w = jnp.sum(jnp.where(mine, terms, 0.0))
         for r in range(0, 128, 32):
             rows = pl.ds(r, 32)
             u = acc[0, p, rows]
@@ -220,27 +289,28 @@
 
 
 def all_steps(tokens, grad_out, w_gate, w_lin, w_out_t, code, decode, stragglers):
-    own = jnp.stack([tokens, grad_out])
+    own = message(code, decode, stragglers, tokens, grad_out)
     row = [own] + [across(own, k, True) for k in (1, 2, 3)]
-    picked, w_in, w_out = prepare(code, decode, stragglers, w_gate, w_lin, w_out_t)
-    row, picked = lax.optimization_barrier((jnp.stack(row), picked))
+    w_in, w_out, token = loaded_weights(w_gate, w_lin, w_out_t)
+    row, _ = lax.optimization_barrier((jnp.stack(row), token))
     near = [row]
     for k in (1, 2, 3):
         near.append(across(row, k, False))
-    values = lax.all_to_all(picked, BLK, 0, 0, tiled=True)
     swap = sibling(row)
-    first, values = lax.optimization_barrier((row, values))
-    state = gathered(0, first, swap, w_in, w_out, ())
+    *state, rows = gathered(0, (row, swap), w_in, w_out, ())
     state, near[1], near[3] = lax.optimization_barrier((state, near[1], near[3]))
     other = {k: sibling(near[k]) for k in (1, 3)}
-    for m in (1, 3):
-        state = gathered(m, near[m], other[m], w_in, w_out, state)
+    *state, rows = gathered(1, (near[1], other[1]), w_in, w_out, (*state, rows))
+    planes = [rows] + [z_step(rows, j) for j in (1, 2, 3, 4)]
+    state = gathered(3, (near[3], other[3]), w_in, w_out, state)
     state, near[2] = lax.optimization_barrier((state, near[2]))
-    keep, send = finished(2, near[2], sibling(near[2]), w_in, w_out, state, values)
+    swap = sibling(near[2])
+    state = gathered(2, (near[2],), w_in, w_out, state)
+    keep, send = finished(2, swap, w_in, w_out, state, planes)
     got = z_pair(send)
     mixed = keep + got.astype(F32)
     result = mixed[0]
-    for k in (1, 3, 2):
+    for k in (2, 1, 3):
         result = result + z_step(mixed[k].astype(BF16), 2 * k).astype(F32)
     return jnp.transpose(result, (1, 0, 2))
 

time: 95.7 us -> 101 us (1.055)
  the two profiles are of different devices: /device:TPU:32 before, /device:TPU:1 now
where the time goes in v2:
time: 101 us; the launch traced here: 100 us
  waiting for transfers between devices  48.6 us (48%)
  starting transfers between devices  27.4 us (27%)
  Pallas kernels  22.5 us (22%)
  other arithmetic  1.05 us (1%)
    ppermute x6, waiting for transfers between devices, across(): return lax.ppermute(block, PLANE, route)  22.7 us
    ppermute x7, waiting for transfers between devices, z_step(): return lax.ppermute(block, 'z', [(z, (z + step) % 8) for z in range(8)])  16.6 us
    ppermute x7, starting transfers between devices, z_step(): return lax.ppermute(block, 'z', [(z, (z + step) % 8) for z in range(8)])  13.2 us
    pallas_call x4, Pallas kernels, gathered(): pl.pallas_call(kernels.get(m, lambda *refs: middle_kernel(m, *refs)), out...  11.7 us
    ppermute x1, waiting for transfers between devices, z_pair(): lax.ppermute(block, ('z', 'c'), [(z * 2 + c, partner_of(z, c) * 2 + c) fo...  6.95 us
    ppermute x6, starting transfers between devices, across(): return lax.ppermute(block, PLANE, route)  6.73 us
    pallas_call x1, Pallas kernels, finished(): pl.pallas_call(lambda *refs: final_kernel(m, *refs), out_shape=STATE + (j...  5.93 us
    ppermute x4, starting transfers between devices, sibling(): return lax.ppermute(block, 'c', [(0, 1), (1, 0)])  5.47 us
  transfers between devices with their start and end apart: 18, of which 12 were waited for; matrix products, arithmetic and copies ran while one was open for 0% of the time, Pallas kernels for 16%

profile of v2, /device:TPU:1, one launch (start us, length us, event | category | flops | bytes accessed | tf_op | source)
XLA Modules:
  0.0 100.4 jit_solution(7889321432265665340)
XLA Ops:
  0.7 1.0 message.1
  1.7 2.2 %collective-permute-start = (bf16[264,512]{1,0:T(8,128)(2,1)S(1)}, bf16[264,512]{1,0:T(8,128)(2,1)S(1)}, u32[]{:S(2)}, u32[]{:S(2)}) collective-permute-start(bf16[264,512]{1,0:T(8,128)(2,1)S(1)} %message.1), channel_id=1, source_target_pairs={{0,128},{1,33},{2,130},{3,35},{32,160},{33,1},{34,162},{35,3},{64,... | collective-permute-start | bytes 811016 | tf_op jit(solution)/shard_map/ppermute | solution.py:35
  3.9 2.6 %collective-permute-start.1 = (bf16[264,512]{1,0:T(8,128)(2,1)S(1)}, bf16[264,512]{1,0:T(8,128)(2,1)S(1)}, u32[]{:S(2)}, u32[]{:S(2)}) collective-permute-start(bf16[264,512]{1,0:T(8,128)(2,1)S(1)} %message.1), channel_id=1, source_target_pairs={{0,2},{1,65},{2,0},{3,67},{32,34},{33,97},{34,32},{35,99},{64,66},... | collective-permute-start | bytes 811016 | tf_op jit(solution)/shard_map/ppermute | solution.py:35
  6.5 1.2 %collective-permute-done = bf16[264,512]{1,0:T(8,128)(2,1)S(1)} collective-permute-done((bf16[264,512]{1,0:T(8,128)(2,1)S(1)}, bf16[264,512]{1,0:T(8,128)(2,1)S(1)}, u32[]{:S(2)}, u32[]{:S(2)}) %collective-permute-start) | collective-permute-done | bytes 270368 | tf_op jit(solution)/shard_map/ppermute | solution.py:35
  7.7 5.8 %collective-permute-done.1 = bf16[264,512]{1,0:T(8,128)(2,1)S(1)} collective-permute-done((bf16[264,512]{1,0:T(8,128)(2,1)S(1)}, bf16[264,512]{1,0:T(8,128)(2,1)S(1)}, u32[]{:S(2)}, u32[]{:S(2)}) %collective-permute-start.1) | collective-permute-done | bytes 270368 | tf_op jit(solution)/shard_map/ppermute | solution.py:35
  13.6 2.6 %collective-permute-done.2 = bf16[264,512]{1,0:T(8,128)(2,1)S(1)} collective-permute-done((bf16[264,512]{1,0:T(8,128)(2,1)S(1)}, bf16[264,512]{1,0:T(8,128)(2,1)S(1)}, u32[]{:S(2)}, u32[]{:S(2)}) %collective-permute-start.2) | collective-permute-done | bytes 270368 | tf_op jit(solution)/shard_map/ppermute | solution.py:35
  16.3 1.6 %collective-permute-start.3 = (bf16[4,264,512]{2,1,0:T(8,128)(2,1)S(1)}, bf16[4,264,512]{2,1,0:T(8,128)(2,1)S(1)}, u32[]{:S(2)}, u32[]{:S(2)}) collective-permute-start(bf16[4,264,512]{2,1,0:T(8,128)(2,1)S(1)} %pad_maximum_fusion.own), channel_id=1, source_target_pairs={{0,1},{1,0},{2,3},{3,2},{4,5},{5,4},{6,7},{7,6},{8,9},{9,8},{10,11... | collective-permute-start | bytes 3244040 | tf_op jit(solution)/shard_map/ppermute | solution.py:39
  17.9 1.9 %collective-permute-start.5 = (bf16[4,264,512]{2,1,0:T(8,128)(2,1)S(1)}, bf16[4,264,512]{2,1,0:T(8,128)(2,1)S(1)}, u32[]{:S(2)}, u32[]{:S(2)}) collective-permute-start(bf16[4,264,512]{2,1,0:T(8,128)(2,1)S(1)} %pad_maximum_fusion.own), channel_id=1, source_target_pairs={{0,96},{1,131},{2,98},{3,129},{32,64},{33,163},{34,66},{35,161},{6... | collective-permute-start | bytes 3244040 | tf_op jit(solution)/shard_map/ppermute | solution.py:35
  19.8 3.9 %load.1 = (bf16[4,512,1280]{2,1,0:T(8,128)(2,1)S(1)}, bf16[4,512,640]{2,1,0:T(8,128)(2,1)S(1)}, f32[8,128]{1,0:T(8,128)}) custom-call(bf16[4,512,640]{2,1,0:T(8,128)(2,1)} %bitcast.26, bf16[4,512,640]{2,1,0:T(8,128)(2,1)} %bitcast.27, bf16[4,512,640]{2,1,0:T(8,128)(2,1)} %bitcast.28), custom_call_target="tpu_custom_call" | custom-call | tf_op jit(solution)/shard_map/load/pallas_call | solution.py:118
  23.8 3.7 %shard_map.82 = (f32[3,8,128,640]{3,2,1,0:T(8,128)S(1)}, bf16[2,8,128,256]{3,2,1,0:T(8,128)(2,1)S(1)}, f32[8,128]{1,0:T(8,128)S(1)}) custom-call(bf16[4,264,512]{2,1,0:T(8,128)(2,1)S(1)} %pad_maximum_fusion.own, bf16[4,264,512]{2,1,0:T(8,128)(2,1)S(1)} %collective-permute-done.3.other, bf16[4,512,1280]{2,1,0:T(8,128)(2,1)S(1)} %get-tuple-element.26.w_in.refs_2_.refs_1_, ...), custom_call_target="tpu_custom_call" | custom-call | flops 2147483648 | bytes 1048576 | tf_op jit(solution)/shard_map/pallas_call | solution.py:213
  27.5 4.7 %collective-permute-done.4.own = bf16[4,264,512]{2,1,0:T(8,128)(2,1)S(1)} collective-permute-done((bf16[4,264,512]{2,1,0:T(8,128)(2,1)S(1)}, bf16[4,264,512]{2,1,0:T(8,128)(2,1)S(1)}, u32[]{:S(2)}, u32[]{:S(2)}) %collective-permute-start.4) | collective-permute-done | bytes 1081376 | tf_op jit(solution)/shard_map/ppermute | solution.py:35
  32.2 1.2 %collective-permute-done.5.refs_0_ = bf16[4,264,512]{2,1,0:T(8,128)(2,1)S(1)} collective-permute-done((bf16[4,264,512]{2,1,0:T(8,128)(2,1)S(1)}, bf16[4,264,512]{2,1,0:T(8,128)(2,1)S(1)}, u32[]{:S(2)}, u32[]{:S(2)}) %collective-permute-start.5) | collective-permute-done | bytes 1081376 | tf_op jit(solution)/shard_map/ppermute | solution.py:35
  33.4 2.5 %collective-permute-start.7 = (bf16[4,264,512]{2,1,0:T(8,128)(2,1)S(1)}, bf16[4,264,512]{2,1,0:T(8,128)(2,1)S(1)}, u32[]{:S(2)}, u32[]{:S(2)}) collective-permute-start(bf16[4,264,512]{2,1,0:T(8,128)(2,1)S(1)} %collective-permute-done.4.own), channel_id=1, source_target_pairs={{0,1},{1,0},{2,3},{3,2},{4,5},{5,4},{6,7},{7,6},{8,9},{9,8},{10,11... | collective-permute-start | bytes 3244040 | tf_op jit(solution)/shard_map/ppermute | solution.py:39
  36.0 2.3 %collective-permute-done.7.other = bf16[4,264,512]{2,1,0:T(8,128)(2,1)S(1)} collective-permute-done((bf16[4,264,512]{2,1,0:T(8,128)(2,1)S(1)}, bf16[4,264,512]{2,1,0:T(8,128)(2,1)S(1)}, u32[]{:S(2)}, u32[]{:S(2)}) %collective-permute-start.7) | collective-permute-done | bytes 1081376 | tf_op jit(solution)/shard_map/ppermute | solution.py:39
  38.3 3.2 %shard_map.83 = (f32[3,8,128,640]{3,2,1,0:T(8,128)S(1)}, bf16[2,8,128,256]{3,2,1,0:T(8,128)(2,1)S(1)}, f32[8,128]{1,0:T(8,128)S(1)}) custom-call(bf16[4,264,512]{2,1,0:T(8,128)(2,1)S(1)} %collective-permute-done.4.own, bf16[4,264,512]{2,1,0:T(8,128)(2,1)S(1)} %collective-permute-done.7.other, ...), custom_call_target="tpu_custom_call", output_to_operand_aliasing={{0}: (4, {}), {1}: (5, {})} | custom-call | flops 2147483648 | bytes 1048576 | tf_op jit(solution)/shard_map/pallas_call | solution.py:213
  41.5 3.2 %shard_map.84 = (f32[3,8,128,640]{3,2,1,0:T(8,128)S(1)}, bf16[2,8,128,256]{3,2,1,0:T(8,128)(2,1)S(1)}) custom-call(bf16[4,264,512]{2,1,0:T(8,128)(2,1)S(1)} %collective-permute-done.5.refs_0_, bf16[4,264,512]{2,1,0:T(8,128)(2,1)S(1)} %collective-permute-done.6.refs_1_, ...), custom_call_target="tpu_custom_call", output_to_operand_aliasing={{0}: (4, {}), {1}: (5, {})} | custom-call | flops 2147483648 | bytes 1048576 | tf_op jit(solution)/shard_map/pallas_call | solution.py:213
  44.7 7.0 %collective-permute-done.8.refs_0_ = bf16[4,264,512]{2,1,0:T(8,128)(2,1)S(1)} collective-permute-done((bf16[4,264,512]{2,1,0:T(8,128)(2,1)S(1)}, bf16[4,264,512]{2,1,0:T(8,128)(2,1)S(1)}, u32[]{:S(2)}, u32[]{:S(2)}) %collective-permute-start.8) | collective-permute-done | bytes 1081376 | tf_op jit(solution)/shard_map/ppermute | solution.py:35
  51.8 1.4 %collective-permute-start.9 = (bf16[4,264,512]{2,1,0:T(8,128)(2,1)S(1)}, bf16[4,264,512]{2,1,0:T(8,128)(2,1)S(1)}, u32[]{:S(2)}, u32[]{:S(2)}) collective-permute-start(bf16[4,264,512]{2,1,0:T(8,128)(2,1)S(1)} %collective-permute-done.8.refs_0_), channel_id=1, source_target_pairs={{0,1},{1,0},{2,3},{3,2},{4,5},{5,4},{6,7},{7,6},{8,9},{9,8},{10,11... | collective-permute-start | bytes 3244040 | tf_op jit(solution)/shard_map/ppermute | solution.py:39
  53.1 1.6 %collective-permute-start.10 = (f32[8,128]{1,0:T(8,128)S(1)}, f32[8,128]{1,0:T(8,128)S(1)}, u32[]{:S(2)}, u32[]{:S(2)}) collective-permute-start(f32[8,128]{1,0:T(8,128)S(1)} %get-tuple-element.44.refs_5_), channel_id=1, source_target_pairs={{0,4},{4,8},{8,12},{12,16},{16,20},{20,24},{24,28},{28,0},{1,5},{5... | collective-permute-start | bytes 12296 | tf_op jit(solution)/shard_map/ppermute | solution.py:51
  54.8 3.0 %collective-permute-start.11 = (f32[8,128]{1,0:T(8,128)S(1)}, f32[8,128]{1,0:T(8,128)S(1)}, u32[]{:S(2)}, u32[]{:S(2)}) collective-permute-start(f32[8,128]{1,0:T(8,128)S(1)} %get-tuple-element.44.refs_5_), channel_id=1, source_target_pairs={{0,8},{4,12},{8,16},{12,20},{16,24},{20,28},{24,0},{28,4},{1,9},{5... | collective-permute-start | bytes 12296 | tf_op jit(solution)/shard_map/ppermute | solution.py:51
  57.8 3.8 %collective-permute-start.12 = (f32[8,128]{1,0:T(8,128)S(1)}, f32[8,128]{1,0:T(8,128)S(1)}, u32[]{:S(2)}, u32[]{:S(2)}) collective-permute-start(f32[8,128]{1,0:T(8,128)S(1)} %get-tuple-element.44.refs_5_), channel_id=1, source_target_pairs={{0,12},{4,16},{8,20},{12,24},{16,28},{20,0},{24,4},{28,8},{1,13},{... | collective-permute-start | bytes 12296 | tf_op jit(solution)/shard_map/ppermute | solution.py:51
  62.0 1.6 %shard_map.85 = (f32[3,8,128,640]{3,2,1,0:T(8,128)S(1)}, bf16[2,8,128,256]{3,2,1,0:T(8,128)(2,1)S(1)}) custom-call(bf16[4,264,512]{2,1,0:T(8,128)(2,1)S(1)} %collective-permute-done.8.refs_0_, bf16[4,512,1280]{2,1,0:T(8,128)(2,1)S(1)} %get-tuple-element.26.w_in.refs_2_.refs_1_, ...), custom_call_target="tpu_custom_call", output_to_operand_aliasing={{0}: (3, {}), {1}: (4, {})} | custom-call | flops 1073741824 | bytes 1048576 | tf_op jit(solution)/shard_map/pallas_call | solution.py:213
  63.6 4.3 %collective-permute-done.13.refs_9_ = f32[8,128]{1,0:T(8,128)S(1)} collective-permute-done((f32[8,128]{1,0:T(8,128)S(1)}, f32[8,128]{1,0:T(8,128)S(1)}, u32[]{:S(2)}, u32[]{:S(2)}) %collective-permute-start.13) | collective-permute-done | bytes 4128 | tf_op jit(solution)/shard_map/ppermute | solution.py:51
  67.9 5.9 %finish.1 = (f32[3,8,128,640]{3,2,1,0:T(8,128)S(1)}, bf16[2,8,128,256]{3,2,1,0:T(8,128)(2,1)S(1)}, f32[4,3,32,640]{3,2,1,0:T(8,128)S(1)}, bf16[4,3,32,640]{3,2,1,0:T(8,128)(2,1)S(1)}) custom-call(bf16[4,264,512]{2,1,0:T(8,128)(2,1)S(1)} %collective-permute-done.9.refs_0_, ...), custom_call_target="tpu_custom_call", output_to_operand_aliasing={{0}: (3, {}), {1}: (4, {})} | custom-call | flops 4294967296 | bytes 1048576 | tf_op jit(solution)/shard_map/finish/pallas_call | solution.py:225
  73.8 2.0 %collective-permute-start.14 = (bf16[4,3,32,640]{3,2,1,0:T(8,128)(2,1)S(1)}, bf16[4,3,32,640]{3,2,1,0:T(8,128)(2,1)S(1)}, u32[]{:S(2)}, u32[]{:S(2)}) collective-permute-start(bf16[4,3,32,640]{3,2,1,0:T(8,128)(2,1)S(1)} %get-tuple-element.46), channel_id=1, source_target_pairs={{0,4},{1,29},{4,0},{5,9},{8,12},{9,5},{12,8},{13,17},{16,20},{17,1... | collective-permute-start | bytes 1474568 | tf_op jit(solution)/shard_map/ppermute | solution.py:47
  75.8 6.9 %collective-permute-done.14 = bf16[4,3,32,640]{3,2,1,0:T(8,128)(2,1)S(1)} collective-permute-done((bf16[4,3,32,640]{3,2,1,0:T(8,128)(2,1)S(1)}, bf16[4,3,32,640]{3,2,1,0:T(8,128)(2,1)S(1)}, u32[]{:S(2)}, u32[]{:S(2)}) %collective-permute-start.14) | collective-permute-done | bytes 491552 | tf_op jit(solution)/shard_map/ppermute | solution.py:47
  83.0 0.8 collective-permute-start.15
  83.8 2.9 %collective-permute-start.16 = (bf16[3,32,640]{2,1,0:T(8,128)(2,1)S(1)}, bf16[3,32,640]{2,1,0:T(8,128)(2,1)S(1)}, u32[]{:S(2)}, u32[]{:S(2)}) collective-permute-start(bf16[3,32,640]{2,1,0:T(8,128)(2,1)S(1)} %get-tuple-element.51), channel_id=1, source_target_pairs={{0,8},{4,12},{8,16},{12,20},{16,24},{20,28},{24,0},{28,4},{1,9},{5... | collective-permute-start | bytes 368648 | tf_op jit(solution)/shard_map/ppermute | solution.py:51
  87.3 3.6 %collective-permute-done.15 = bf16[3,32,640]{2,1,0:T(8,128)(2,1)S(1)} collective-permute-done((bf16[3,32,640]{2,1,0:T(8,128)(2,1)S(1)}, bf16[3,32,640]{2,1,0:T(8,128)(2,1)S(1)}, u32[]{:S(2)}, u32[]{:S(2)}) %collective-permute-start.15) | collective-permute-done | bytes 122912 | tf_op jit(solution)/shard_map/ppermute | solution.py:51
  90.9 1.3 %collective-permute-done.16 = bf16[3,32,640]{2,1,0:T(8,128)(2,1)S(1)} collective-permute-done((bf16[3,32,640]{2,1,0:T(8,128)(2,1)S(1)}, bf16[3,32,640]{2,1,0:T(8,128)(2,1)S(1)}, u32[]{:S(2)}, u32[]{:S(2)}) %collective-permute-start.16) | collective-permute-done | bytes 122912 | tf_op jit(solution)/shard_map/ppermute | solution.py:51
  92.3 7.4 %collective-permute-done.17 = bf16[3,32,640]{2,1,0:T(8,128)(2,1)S(1)} collective-permute-done((bf16[3,32,640]{2,1,0:T(8,128)(2,1)S(1)}, bf16[3,32,640]{2,1,0:T(8,128)(2,1)S(1)}, u32[]{:S(2)}, u32[]{:S(2)}) %collective-permute-start.17) | collective-permute-done | bytes 122912 | tf_op jit(solution)/shard_map/ppermute | solution.py:51
  99.7 0.8 fusion.3
  (15 shorter events, 1.5 us)
Async XLA Ops:
  1.7 6.1 %collective-permute-start = (bf16[264,512]{1,0:T(8,128)(2,1)S(1)}, bf16[264,512]{1,0:T(8,128)(2,1)S(1)}, u32[]{:S(2)}, u32[]{:S(2)}) collective-permute-start(bf16[264,512]{1,0:T(8,128)(2,1)S(1)} %message.1), channel_id=1, source_target_pairs={{0,128},{1,33},{2,130},{3,35},{32,160},{33,1},{34,162},{35,3},{64,... | collective-permute-start | bytes 811016 | tf_op jit(solution)/shard_map/ppermute | solution.py:35
  3.9 9.7 %collective-permute-start.1 = (bf16[264,512]{1,0:T(8,128)(2,1)S(1)}, bf16[264,512]{1,0:T(8,128)(2,1)S(1)}, u32[]{:S(2)}, u32[]{:S(2)}) collective-permute-start(bf16[264,512]{1,0:T(8,128)(2,1)S(1)} %message.1), channel_id=1, source_target_pairs={{0,2},{1,65},{2,0},{3,67},{32,34},{33,97},{34,32},{35,99},{64,66},... | collective-permute-start | bytes 811016 | tf_op jit(solution)/shard_map/ppermute | solution.py:35
  6.5 9.7 %collective-permute-start.2 = (bf16[264,512]{1,0:T(8,128)(2,1)S(1)}, bf16[264,512]{1,0:T(8,128)(2,1)S(1)}, u32[]{:S(2)}, u32[]{:S(2)}) collective-permute-start(bf16[264,512]{1,0:T(8,128)(2,1)S(1)} %message.1), channel_id=1, source_target_pairs={{0,130},{1,97},{2,128},{3,99},{32,162},{33,65},{34,160},{35,67},{6... | collective-permute-start | bytes 811016 | tf_op jit(solution)/shard_map/ppermute | solution.py:35
  16.3 7.4 %collective-permute-start.3 = (bf16[4,264,512]{2,1,0:T(8,128)(2,1)S(1)}, bf16[4,264,512]{2,1,0:T(8,128)(2,1)S(1)}, u32[]{:S(2)}, u32[]{:S(2)}) collective-permute-start(bf16[4,264,512]{2,1,0:T(8,128)(2,1)S(1)} %pad_maximum_fusion.own), channel_id=1, source_target_pairs={{0,1},{1,0},{2,3},{3,2},{4,5},{5,4},{6,7},{7,6},{8,9},{9,8},{10,11... | collective-permute-start | bytes 3244040 | tf_op jit(solution)/shard_map/ppermute | solution.py:39
  17.9 14.3 %collective-permute-start.4 = (bf16[4,264,512]{2,1,0:T(8,128)(2,1)S(1)}, bf16[4,264,512]{2,1,0:T(8,128)(2,1)S(1)}, u32[]{:S(2)}, u32[]{:S(2)}) collective-permute-start(bf16[4,264,512]{2,1,0:T(8,128)(2,1)S(1)} %pad_maximum_fusion.own), channel_id=1, source_target_pairs={{0,32},{1,129},{2,34},{3,131},{32,0},{33,161},{34,2},{35,163},{64,... | collective-permute-start | bytes 3244040 | tf_op jit(solution)/shard_map/ppermute | solution.py:35
  17.9 15.5 %collective-permute-start.5 = (bf16[4,264,512]{2,1,0:T(8,128)(2,1)S(1)}, bf16[4,264,512]{2,1,0:T(8,128)(2,1)S(1)}, u32[]{:S(2)}, u32[]{:S(2)}) collective-permute-start(bf16[4,264,512]{2,1,0:T(8,128)(2,1)S(1)} %pad_maximum_fusion.own), channel_id=1, source_target_pairs={{0,96},{1,131},{2,98},{3,129},{32,64},{33,163},{34,66},{35,161},{6... | collective-permute-start | bytes 3244040 | tf_op jit(solution)/shard_map/ppermute | solution.py:35
  33.4 4.9 %collective-permute-start.7 = (bf16[4,264,512]{2,1,0:T(8,128)(2,1)S(1)}, bf16[4,264,512]{2,1,0:T(8,128)(2,1)S(1)}, u32[]{:S(2)}, u32[]{:S(2)}) collective-permute-start(bf16[4,264,512]{2,1,0:T(8,128)(2,1)S(1)} %collective-permute-done.4.own), channel_id=1, source_target_pairs={{0,1},{1,0},{2,3},{3,2},{4,5},{5,4},{6,7},{7,6},{8,9},{9,8},{10,11... | collective-permute-start | bytes 3244040 | tf_op jit(solution)/shard_map/ppermute | solution.py:39
  36.0 5.5 %collective-permute-start.6 = (bf16[4,264,512]{2,1,0:T(8,128)(2,1)S(1)}, bf16[4,264,512]{2,1,0:T(8,128)(2,1)S(1)}, u32[]{:S(2)}, u32[]{:S(2)}) collective-permute-start(bf16[4,264,512]{2,1,0:T(8,128)(2,1)S(1)} %collective-permute-done.5.refs_0_), channel_id=1, source_target_pairs={{0,1},{1,0},{2,3},{3,2},{4,5},{5,4},{6,7},{7,6},{8,9},{9,8},{10,11... | collective-permute-start | bytes 3244040 | tf_op jit(solution)/shard_map/ppermute | solution.py:39
  36.0 15.8 %collective-permute-start.8 = (bf16[4,264,512]{2,1,0:T(8,128)(2,1)S(1)}, bf16[4,264,512]{2,1,0:T(8,128)(2,1)S(1)}, u32[]{:S(2)}, u32[]{:S(2)}) collective-permute-start(bf16[4,264,512]{2,1,0:T(8,128)(2,1)S(1)} %pad_maximum_fusion.own), channel_id=1, source_target_pairs={{0,64},{1,3},{2,66},{3,1},{32,96},{33,35},{34,98},{35,33},{64,0},{... | collective-permute-start | bytes 3244040 | tf_op jit(solution)/shard_map/ppermute | solution.py:35
  51.8 16.1 %collective-permute-start.9 = (bf16[4,264,512]{2,1,0:T(8,128)(2,1)S(1)}, bf16[4,264,512]{2,1,0:T(8,128)(2,1)S(1)}, u32[]{:S(2)}, u32[]{:S(2)}) collective-permute-start(bf16[4,264,512]{2,1,0:T(8,128)(2,1)S(1)} %collective-permute-done.8.refs_0_), channel_id=1, source_target_pairs={{0,1},{1,0},{2,3},{3,2},{4,5},{5,4},{6,7},{7,6},{8,9},{9,8},{10,11... | collective-permute-start | bytes 3244040 | tf_op jit(solution)/shard_map/ppermute | solution.py:39
  53.1 10.4 %collective-permute-start.10 = (f32[8,128]{1,0:T(8,128)S(1)}, f32[8,128]{1,0:T(8,128)S(1)}, u32[]{:S(2)}, u32[]{:S(2)}) collective-permute-start(f32[8,128]{1,0:T(8,128)S(1)} %get-tuple-element.44.refs_5_), channel_id=1, source_target_pairs={{0,4},{4,8},{8,12},{12,16},{16,20},{20,24},{24,28},{28,0},{1,5},{5... | collective-permute-start | bytes 12296 | tf_op jit(solution)/shard_map/ppermute | solution.py:51
  54.8 8.8 %collective-permute-start.11 = (f32[8,128]{1,0:T(8,128)S(1)}, f32[8,128]{1,0:T(8,128)S(1)}, u32[]{:S(2)}, u32[]{:S(2)}) collective-permute-start(f32[8,128]{1,0:T(8,128)S(1)} %get-tuple-element.44.refs_5_), channel_id=1, source_target_pairs={{0,8},{4,12},{8,16},{12,20},{16,24},{20,28},{24,0},{28,4},{1,9},{5... | collective-permute-start | bytes 12296 | tf_op jit(solution)/shard_map/ppermute | solution.py:51
  57.8 5.8 %collective-permute-start.12 = (f32[8,128]{1,0:T(8,128)S(1)}, f32[8,128]{1,0:T(8,128)S(1)}, u32[]{:S(2)}, u32[]{:S(2)}) collective-permute-start(f32[8,128]{1,0:T(8,128)S(1)} %get-tuple-element.44.refs_5_), channel_id=1, source_target_pairs={{0,12},{4,16},{8,20},{12,24},{16,28},{20,0},{24,4},{28,8},{1,13},{... | collective-permute-start | bytes 12296 | tf_op jit(solution)/shard_map/ppermute | solution.py:51
  61.5 6.4 %collective-permute-start.13 = (f32[8,128]{1,0:T(8,128)S(1)}, f32[8,128]{1,0:T(8,128)S(1)}, u32[]{:S(2)}, u32[]{:S(2)}) collective-permute-start(f32[8,128]{1,0:T(8,128)S(1)} %get-tuple-element.44.refs_5_), channel_id=1, source_target_pairs={{0,16},{4,20},{8,24},{12,28},{16,0},{20,4},{24,8},{28,12},{1,17},{... | collective-permute-start | bytes 12296 | tf_op jit(solution)/shard_map/ppermute | solution.py:51
  73.8 9.0 %collective-permute-start.14 = (bf16[4,3,32,640]{3,2,1,0:T(8,128)(2,1)S(1)}, bf16[4,3,32,640]{3,2,1,0:T(8,128)(2,1)S(1)}, u32[]{:S(2)}, u32[]{:S(2)}) collective-permute-start(bf16[4,3,32,640]{3,2,1,0:T(8,128)(2,1)S(1)} %get-tuple-element.46), channel_id=1, source_target_pairs={{0,4},{1,29},{4,0},{5,9},{8,12},{9,5},{12,8},{13,17},{16,20},{17,1... | collective-permute-start | bytes 1474568 | tf_op jit(solution)/shard_map/ppermute | solution.py:47
  83.0 7.9 %collective-permute-start.15 = (bf16[3,32,640]{2,1,0:T(8,128)(2,1)S(1)}, bf16[3,32,640]{2,1,0:T(8,128)(2,1)S(1)}, u32[]{:S(2)}, u32[]{:S(2)}) collective-permute-start(bf16[3,32,640]{2,1,0:T(8,128)(2,1)S(1)} %get-tuple-element.49), channel_id=1, source_target_pairs={{0,16},{4,20},{8,24},{12,28},{16,0},{20,4},{24,8},{28,12},{1,17},{... | collective-permute-start | bytes 368648 | tf_op jit(solution)/shard_map/ppermute | solution.py:51
  83.8 8.5 %collective-permute-start.16 = (bf16[3,32,640]{2,1,0:T(8,128)(2,1)S(1)}, bf16[3,32,640]{2,1,0:T(8,128)(2,1)S(1)}, u32[]{:S(2)}, u32[]{:S(2)}) collective-permute-start(bf16[3,32,640]{2,1,0:T(8,128)(2,1)S(1)} %get-tuple-element.51), channel_id=1, source_target_pairs={{0,8},{4,12},{8,16},{12,20},{16,24},{20,28},{24,0},{28,4},{1,9},{5... | collective-permute-start | bytes 368648 | tf_op jit(solution)/shard_map/ppermute | solution.py:51
  86.6 13.0 %collective-permute-start.17 = (bf16[3,32,640]{2,1,0:T(8,128)(2,1)S(1)}, bf16[3,32,640]{2,1,0:T(8,128)(2,1)S(1)}, u32[]{:S(2)}, u32[]{:S(2)}) collective-permute-start(bf16[3,32,640]{2,1,0:T(8,128)(2,1)S(1)} %get-tuple-element.50), channel_id=1, source_target_pairs={{0,24},{4,28},{8,0},{12,4},{16,8},{20,12},{24,16},{28,20},{1,25},{... | collective-permute-start | bytes 368648 | tf_op jit(solution)/shard_map/ppermute | solution.py:51

commit v3 on v2

--- a/solution.py
+++ b/solution.py
@@ -33,6 +33,10 @@
                     number = lambda a: ((a[0] * 4 + a[1]) * 2 + a[2]) * 2 + a[3]
                     route.append((number((xl, y, xh, c)), number(to)))
     return lax.ppermute(block, PLANE, route)
+
+
+def swapped(block, axis, size, flip):
+    return lax.ppermute(block, axis, [(i, i ^ flip) for i in range(size)])
 
 
 def sibling(block):
@@ -101,7 +105,7 @@
     )(decode, *[hbm(a) for a in (code, stragglers, tokens, grad_out)])
 
 
-def weights_kernel(w_gate, w_lin, w_out_t, w_in, w_out, token, sems):
+def weights_kernel(w_gate, w_lin, w_out_t, w_in, w_out, sems):
     copies = [
         pltpu.make_async_copy(w_gate, w_in.at[:, :, pl.ds(0, 640)], sems.at[0]),
         pltpu.make_async_copy(w_lin, w_in.at[:, :, pl.ds(640, 640)], sems.at[1]),
@@ -109,7 +113,6 @@
     ]
     for copy in copies:
         copy.start()
-    token[...] = jnp.zeros_like(token)
     for copy in copies:
         copy.wait()
 
@@ -120,35 +123,38 @@
         out_shape=(
             jax.ShapeDtypeStruct((4, 512, 1280), BF16),
             jax.ShapeDtypeStruct((4, 512, 640), BF16),
-            jax.ShapeDtypeStruct((8, 128), F32),
         ),
         in_specs=[pl.BlockSpec(memory_space=pltpu.HBM)] * 3,
-        out_specs=(VMEM, VMEM, VMEM),
+        out_specs=(VMEM, VMEM),
         scratch_shapes=[pltpu.SemaphoreType.DMA((3,))],
         compiler_params=PARAMS,
         name="load",
     )(*[hbm(w.reshape(4, 512, 640)) for w in (w_gate, w_lin, w_out_t)])
 
 
-def read_rows(ex, own, other, rows):
+def rows_kernel(own, other, rows):
     c = lax.axis_index("c").astype(I32)
+    rows[...] = jnp.zeros_like(rows)
     for dy in range(4):
         piece = [block[dy, 256:264, 0:128].astype(F32) for block in (own, other)]
         piece = jnp.where(c == 1, piece[0], piece[1])
-        rows[2 * dy + ex : 2 * dy + ex + 1, :] = jnp.sum(piece, axis=0, keepdims=True)
-
-
-def first_kernel(own, other, w_in, w_out, acc, cols, rows):
+        rows[dy : dy + 1, :] = jnp.sum(piece, axis=0, keepdims=True)
+
+
+def line_rows(own, other):
+    return pl.pallas_call(
+        rows_kernel,
+        out_shape=jax.ShapeDtypeStruct((8, 128), F32),
+        in_specs=[VMEM] * 2,
+        out_specs=VMEM,
+        compiler_params=PARAMS,
+        name="rows",
+    )(own, other)
+
+
+def first_kernel(own, other, w_in, w_out, acc, cols):
     acc[...] = jnp.zeros_like(acc)
-    rows[...] = jnp.zeros_like(rows)
-    read_rows(0, own, other, rows)
     gather_kernel(0, ((0, own), (1, other)), w_in, w_out, acc, cols)
-
-
-def second_kernel(own, other, w_in, w_out, _, __, ___, acc, cols, rows):
-    rows[...] = ___[...]
-    read_rows(1, own, other, rows)
-    gather_kernel(1, ((0, own), (1, other)), w_in, w_out, acc, cols)
 
 
 def middle_kernel(m, *refs):
@@ -156,10 +162,13 @@
     gather_kernel(m, tuple(enumerate(blocks)), w_in, w_out, acc, cols)
 
 
-def final_kernel(m, other, w_in, w_out, _, __, *refs):
-    rows, (acc, cols, *rest) = refs[:5], refs[5:]
-    gather_kernel(m, ((1, other),), w_in, w_out, acc, cols)
-    last_kernel(rows, acc, cols, *rest)
+def halves_kernel(low, high, w_in, w_out, _, __, acc, cols):
+    gather_kernel(2, ((0, (low, high)),), w_in, w_out, acc, cols)
+
+
+def final_kernel(low, high, w_in, w_out, _, __, own_terms, other_terms, acc, cols, *rest):
+    gather_kernel(2, ((1, (low, high)),), w_in, w_out, acc, cols)
+    last_kernel((own_terms, other_terms), acc, cols, *rest)
 
 
 def gather_kernel(m, blocks, w_in, w_out, acc, cols):
@@ -167,13 +176,13 @@
     for ec, block in blocks:
         x_first = (c ^ ec) == 0
 
-        def step(j, _):
+        def step(j, block, start):
             eh = jnp.where(x_first, j, m >> 1)
             p0 = jnp.where(x_first, 2 * m, 4 * j + (m & 1))
             p1 = jnp.where(x_first, 2 * m + 1, 4 * j + 2 + (m & 1))
             shard = (xh ^ eh) * 2 + (c ^ ec)
-            xs = block[pl.ds(2 * j, 2), 0:128].reshape(256, 512)
-            ys = block[pl.ds(2 * j, 2), 128:256].reshape(256, 512)
+            xs = block[pl.ds(start, 2), 0:128].reshape(256, 512)
+            ys = block[pl.ds(start, 2), 128:256].reshape(256, 512)
             pre = jnp.dot(xs, w_in[shard], preferred_element_type=F32)
             acc[0, p0] += pre[:128, :640]
             acc[1, p0] += pre[:128, 640:]
@@ -191,9 +200,16 @@
                     cols[n, p0] = v[:128]
                     cols[n, p1] = v[128:]
 
-            return 0
-
-        lax.fori_loop(0, 2, step, 0)
+        if isinstance(block, tuple):
+            for j in range(2):
+                step(j, block[j], 0)
+        else:
+
+            def body(j, carry):
+                step(j, block, 2 * j)
+                return carry
+
+            lax.fori_loop(0, 2, body, 0)
 
 
 STATE = (jax.ShapeDtypeStruct((3, 8, 128, 640), F32), jax.ShapeDtypeStruct((2, 8, 128, 256), BF16))
@@ -203,32 +219,28 @@
     return pl.CostEstimate(flops=giga << 30, bytes_accessed=1 << 20, transcendentals=0)
 
 
-ROWS = jax.ShapeDtypeStruct((8, 128), F32)
-
-
 def gathered(m, blocks, w_in, w_out, state):
     n = len(blocks) + 2
-    with_rows = m in (0, 1)
-    kernels = {0: first_kernel, 1: second_kernel}
+    kernels = {0: first_kernel, 2: halves_kernel}
     return pl.pallas_call(
         kernels.get(m, lambda *refs: middle_kernel(m, *refs)),
-        out_shape=STATE + ((ROWS,) if with_rows else ()),
+        out_shape=STATE,
         in_specs=[VMEM] * (n + len(state)),
-        out_specs=(VMEM,) * (3 if with_rows else 2),
+        out_specs=(VMEM, VMEM),
         input_output_aliases={n: 0, n + 1: 1} if state else {},
         compiler_params=PARAMS,
-        cost_estimate=priced(len(blocks)),
+        cost_estimate=priced(2 if m != 2 else 1),
     )(*blocks, w_in, w_out, *state)
 
 
-def finished(m, other, w_in, w_out, state, rows):
-    return pl.pallas_call(
-        lambda *refs: final_kernel(m, *refs),
+def finished(halves, w_in, w_out, state, terms):
+    return pl.pallas_call(
+        final_kernel,
         out_shape=STATE
         + (jax.ShapeDtypeStruct((4, 3, 32, 640), F32), jax.ShapeDtypeStruct((4, 3, 32, 640), BF16)),
-        in_specs=[VMEM] * 10,
+        in_specs=[VMEM] * 8,
         out_specs=(VMEM,) * 4,
-        input_output_aliases={3: 0, 4: 1},
+        input_output_aliases={4: 0, 5: 1},
         scratch_shapes=[
             pltpu.VMEM((8, 128, 1280), BF16),
             pltpu.VMEM((8, 128, 640), BF16),
@@ -237,24 +249,23 @@
         compiler_params=PARAMS,
         cost_estimate=priced(4),
         name="finish",
-    )(other, w_in, w_out, *state, *rows)[2:]
-
-
-def last_kernel(rows, acc, cols, keep, send, gates, hidden, total):
+    )(*halves, w_in, w_out, *state, *terms)[2:]
+
+
+def last_kernel(terms, acc, cols, keep, send, gates, hidden, total):
     xl, y, z, _, c = place()
     lane = lax.broadcasted_iota(I32, (8, 128), 1)
-    line = lax.broadcasted_iota(I32, (8, 128), 0)
-    line = (xl ^ (line & 1)) * 4 + (y ^ (line >> 1))
-    worker = line * 8 + ((z - lane) & 7)
-    terms = jnp.zeros((8, 128), F32)
-    for j in range(5):
-        terms = jnp.where(lane == j, rows[j][...], terms)
+    row = lax.broadcasted_iota(I32, (8, 128), 0)
+    known = (lane < 5) & (row < 4)
+    workers = [(((xl ^ ex) * 4 + (y ^ row)) & 7) * 8 + ((z - lane) & 7) for ex in range(2)]
 
     def part(p, _):
         dy, ex = p >> 1, p & 1
         number = ((xl ^ ex) * 4 + (y ^ dy)) * 8 + z
-        mine = (((number - lane) & 63) == worker) & (lane < 5)
-        w = jnp.sum(jnp.where(mine, terms, 0.0))
+        w = F32(0.0)
+        for worker, term in zip(workers, terms):
+            mine = known & (((number - lane) & 63) == worker)
+            w = w + jnp.sum(jnp.where(mine, term[...], 0.0))
         for r in range(0, 128, 32):
             rows = pl.ds(r, 32)
             u = acc[0, p, rows]
@@ -290,23 +301,33 @@
 
 def all_steps(tokens, grad_out, w_gate, w_lin, w_out_t, code, decode, stragglers):
     own = message(code, decode, stragglers, tokens, grad_out)
-    row = [own] + [across(own, k, True) for k in (1, 2, 3)]
-    w_in, w_out, token = loaded_weights(w_gate, w_lin, w_out_t)
-    row, _ = lax.optimization_barrier((jnp.stack(row), token))
-    near = [row]
+    row = [own]
     for k in (1, 2, 3):
-        near.append(across(row, k, False))
+        row.append(across(own, k, True))
+    w_in, w_out = loaded_weights(w_gate, w_lin, w_out_t)
+    row = jnp.stack(row)
+    near = {}
+    for k in (1, 3):
+        near[k] = across(row, k, False)
     swap = sibling(row)
-    *state, rows = gathered(0, (row, swap), w_in, w_out, ())
-    state, near[1], near[3] = lax.optimization_barrier((state, near[1], near[3]))
-    other = {k: sibling(near[k]) for k in (1, 3)}
-    *state, rows = gathered(1, (near[1], other[1]), w_in, w_out, (*state, rows))
-    planes = [rows] + [z_step(rows, j) for j in (1, 2, 3, 4)]
-    state = gathered(3, (near[3], other[3]), w_in, w_out, state)
-    state, near[2] = lax.optimization_barrier((state, near[2]))
-    swap = sibling(near[2])
-    state = gathered(2, (near[2],), w_in, w_out, state)
-    keep, send = finished(2, swap, w_in, w_out, state, planes)
+    planes = [line_rows(row, swap)]
+    for j in (1, 2, 3, 4):
+        planes.append(z_step(planes[0], j))
+    lane = lax.broadcasted_iota(I32, (8, 128), 1)
+    terms = sum(jnp.where(lane == j, plane, 0.0) for j, plane in enumerate(planes))
+    terms = (terms, swapped(terms, "xl", 2, 1))
+    low = across(near[1][:2], 3, False)
+    high = across(near[3][2:], 1, False)
+    other = {}
+    for k in (1, 3):
+        other[k] = sibling(near[k])
+    state = gathered(0, (row, swap), w_in, w_out, ())
+    for m in (1, 3):
+        state = gathered(m, (near[m], other[m]), w_in, w_out, state)
+    state, low, high = lax.optimization_barrier((state, low, high))
+    halves = [sibling(low), sibling(high)]
+    state = gathered(2, (low, high), w_in, w_out, state)
+    keep, send = finished(halves, w_in, w_out, state, terms)
     got = z_pair(send)
     mixed = keep + got.astype(F32)
     result = mixed[0]

time: 101 us -> 102 us (level)
  the two profiles are of different devices: /device:TPU:1 before, /device:TPU:6 now
where the time goes in v3:
time: 102 us; the launch traced here: 100 us
  waiting for transfers between devices  48.3 us (47%)
  starting transfers between devices  27.8 us (27%)
  Pallas kernels  22 us (22%)
  other arithmetic  1.06 us (1%)
    ppermute x7, waiting for transfers between devices, across(): return lax.ppermute(block, PLANE, route)  23.6 us
    ppermute x7, waiting for transfers between devices, z_step(): return lax.ppermute(block, 'z', [(z, (z + step) % 8) for z in range(8)])  16.6 us
    ppermute x7, starting transfers between devices, z_step(): return lax.ppermute(block, 'z', [(z, (z + step) % 8) for z in range(8)])  15 us
    pallas_call x4, Pallas kernels, gathered(): pl.pallas_call(kernels.get(m, lambda *refs: middle_kernel(m, *refs)), out...  11.7 us
    ppermute x7, starting transfers between devices, across(): return lax.ppermute(block, PLANE, route)  9.04 us
    ppermute x1, waiting for transfers between devices, z_pair(): lax.ppermute(block, ('z', 'c'), [(z * 2 + c, partner_of(z, c) * 2 + c) fo...  7.82 us
    pallas_call x1, Pallas kernels, finished(): pl.pallas_call(final_kernel, out_shape=STATE + (jax.ShapeDtypeStruct((4,...  5.94 us
    pallas_call x1, Pallas kernels, loaded_weights(): pl.pallas_call(weights_kernel, out_shape=(jax.ShapeDtypeStruct((4, 512, 1...  3.34 us
  transfers between devices with their start and end apart: 21, of which 11 were waited for; matrix products, arithmetic and copies ran while one was open for 0% of the time, Pallas kernels for 15%

profile of v3, /device:TPU:6, one launch (start us, length us, event | category | flops | bytes accessed | tf_op | source)
XLA Modules:
  0.0 100.2 jit_solution(3530843215347705112)
XLA Ops:
  0.7 1.0 %message.1 = bf16[264,512]{1,0:T(8,128)(2,1)S(1)} custom-call(f32[1]{0:T(128)S(6)} %copy.25.decode, f32[1,5]{1,0:T(1,128)} %code_in.1, s32[4]{0:T(128)} %stragglers_in.1, bf16[128,512]{1,0:T(8,128)(2,1)} %tokens.1, bf16[128,512]{1,0:T(8,128)(2,1)} %grad_out.1), custom_call_target="tpu_custom_call" | custom-call | tf_op jit(solution)/shard_map/message/pallas_call | solution.py:97
  1.7 0.9 collective-permute-start
  2.6 2.8 %collective-permute-start.1 = (bf16[264,512]{1,0:T(8,128)(2,1)S(1)}, bf16[264,512]{1,0:T(8,128)(2,1)S(1)}, u32[]{:S(2)}, u32[]{:S(2)}) collective-permute-start(bf16[264,512]{1,0:T(8,128)(2,1)S(1)} %message.1), channel_id=1, source_target_pairs={{0,2},{1,65},{2,0},{3,67},{32,34},{33,97},{34,32},{35,99},{64,66},... | collective-permute-start | bytes 811016 | tf_op jit(solution)/shard_map/ppermute | solution.py:35
  5.4 1.1 %collective-permute-start.2 = (bf16[264,512]{1,0:T(8,128)(2,1)S(1)}, bf16[264,512]{1,0:T(8,128)(2,1)S(1)}, u32[]{:S(2)}, u32[]{:S(2)}) collective-permute-start(bf16[264,512]{1,0:T(8,128)(2,1)S(1)} %message.1), channel_id=1, source_target_pairs={{0,130},{1,97},{2,128},{3,99},{32,162},{33,65},{34,160},{35,67},{6... | collective-permute-start | bytes 811016 | tf_op jit(solution)/shard_map/ppermute | solution.py:35
  6.5 1.8 %collective-permute-done = bf16[264,512]{1,0:T(8,128)(2,1)S(1)} collective-permute-done((bf16[264,512]{1,0:T(8,128)(2,1)S(1)}, bf16[264,512]{1,0:T(8,128)(2,1)S(1)}, u32[]{:S(2)}, u32[]{:S(2)}) %collective-permute-start) | collective-permute-done | bytes 270368 | tf_op jit(solution)/shard_map/ppermute | solution.py:35
  8.2 4.6 %collective-permute-done.1 = bf16[264,512]{1,0:T(8,128)(2,1)S(1)} collective-permute-done((bf16[264,512]{1,0:T(8,128)(2,1)S(1)}, bf16[264,512]{1,0:T(8,128)(2,1)S(1)}, u32[]{:S(2)}, u32[]{:S(2)}) %collective-permute-start.1) | collective-permute-done | bytes 270368 | tf_op jit(solution)/shard_map/ppermute | solution.py:35
  12.8 2.8 %collective-permute-done.2 = bf16[264,512]{1,0:T(8,128)(2,1)S(1)} collective-permute-done((bf16[264,512]{1,0:T(8,128)(2,1)S(1)}, bf16[264,512]{1,0:T(8,128)(2,1)S(1)}, u32[]{:S(2)}, u32[]{:S(2)}) %collective-permute-start.2) | collective-permute-done | bytes 270368 | tf_op jit(solution)/shard_map/ppermute | solution.py:35
  15.9 2.0 %collective-permute-start.3 = (bf16[4,264,512]{2,1,0:T(8,128)(2,1)S(1)}, bf16[4,264,512]{2,1,0:T(8,128)(2,1)S(1)}, u32[]{:S(2)}, u32[]{:S(2)}) collective-permute-start(bf16[4,264,512]{2,1,0:T(8,128)(2,1)S(1)} %pad_maximum_fusion.own), channel_id=1, source_target_pairs={{0,96},{1,131},{2,98},{3,129},{32,64},{33,163},{34,66},{35,161},{6... | collective-permute-start | bytes 3244040 | tf_op jit(solution)/shard_map/ppermute | solution.py:35
  17.9 13.1 %collective-permute-done.5.refs_0_ = bf16[4,264,512]{2,1,0:T(8,128)(2,1)S(1)} collective-permute-done((bf16[4,264,512]{2,1,0:T(8,128)(2,1)S(1)}, bf16[4,264,512]{2,1,0:T(8,128)(2,1)S(1)}, u32[]{:S(2)}, u32[]{:S(2)}) %collective-permute-start.5) | collective-permute-done | bytes 1081376 | tf_op jit(solution)/shard_map/ppermute | solution.py:35
  31.0 1.3 %collective-permute-done.3.refs_0_ = bf16[4,264,512]{2,1,0:T(8,128)(2,1)S(1)} collective-permute-done((bf16[4,264,512]{2,1,0:T(8,128)(2,1)S(1)}, bf16[4,264,512]{2,1,0:T(8,128)(2,1)S(1)}, u32[]{:S(2)}, u32[]{:S(2)}) %collective-permute-start.3) | collective-permute-done | bytes 1081376 | tf_op jit(solution)/shard_map/ppermute | solution.py:35
  32.3 3.3 %load.1 = (bf16[4,512,1280]{2,1,0:T(8,128)(2,1)S(1)}, bf16[4,512,640]{2,1,0:T(8,128)(2,1)S(1)}) custom-call(bf16[4,512,640]{2,1,0:T(8,128)(2,1)} %bitcast.26, bf16[4,512,640]{2,1,0:T(8,128)(2,1)} %bitcast.27, bf16[4,512,640]{2,1,0:T(8,128)(2,1)} %bitcast.28), custom_call_target="tpu_custom_call" | custom-call | tf_op jit(solution)/shard_map/load/pallas_call | solution.py:121
  35.7 2.0 %collective-permute-start.8 = (bf16[2,264,512]{2,1,0:T(8,128)(2,1)S(1)}, bf16[2,264,512]{2,1,0:T(8,128)(2,1)S(1)}, u32[]{:S(2)}, u32[]{:S(2)}) collective-permute-start(bf16[2,264,512]{2,1,0:T(8,128)(2,1)S(1)} %slice.27), channel_id=1, source_target_pairs={{0,96},{1,131},{2,98},{3,129},{32,64},{33,163},{34,66},{35,161},{6... | collective-permute-start | bytes 1622024 | tf_op jit(solution)/shard_map/ppermute | solution.py:35
  37.9 2.0 %collective-permute-start.12 = (f32[8,128]{1,0:T(8,128)S(1)}, f32[8,128]{1,0:T(8,128)S(1)}, u32[]{:S(2)}, u32[]{:S(2)}) collective-permute-start(f32[8,128]{1,0:T(8,128)S(1)} %rows.1), channel_id=1, source_target_pairs={{0,4},{4,8},{8,12},{12,16},{16,20},{20,24},{24,28},{28,0},{1,5},{5... | collective-permute-start | bytes 12296 | tf_op jit(solution)/shard_map/ppermute | solution.py:55
  39.9 3.7 %shard_map.82 = (f32[3,8,128,640]{3,2,1,0:T(8,128)S(1)}, bf16[2,8,128,256]{3,2,1,0:T(8,128)(2,1)S(1)}) custom-call(bf16[4,264,512]{2,1,0:T(8,128)(2,1)S(1)} %pad_maximum_fusion.own, bf16[4,264,512]{2,1,0:T(8,128)(2,1)S(1)} %collective-permute-done.7.other, bf16[4,512,1280]{2,1,0:T(8,128)(2,1)S(1)} %get-tuple-element.21.w_in.refs_2_, ...), custom_call_target="tpu_custom_call" | custom-call | flops 2147483648 | bytes 1048576 | tf_op jit(solution)/shard_map/pallas_call | solution.py:225
  43.7 3.2 %shard_map.83 = (f32[3,8,128,640]{3,2,1,0:T(8,128)S(1)}, bf16[2,8,128,256]{3,2,1,0:T(8,128)(2,1)S(1)}) custom-call(bf16[4,264,512]{2,1,0:T(8,128)(2,1)S(1)} %collective-permute-done.5.refs_0_, bf16[4,264,512]{2,1,0:T(8,128)(2,1)S(1)} %collective-permute-done.6.refs_1_, ...), custom_call_target="tpu_custom_call", output_to_operand_aliasing={{0}: (4, {}), {1}: (5, {})} | custom-call | flops 2147483648 | bytes 1048576 | tf_op jit(solution)/shard_map/pallas_call | solution.py:225
  46.9 3.2 %shard_map.84 = (f32[3,8,128,640]{3,2,1,0:T(8,128)S(1)}, bf16[2,8,128,256]{3,2,1,0:T(8,128)(2,1)S(1)}) custom-call(bf16[4,264,512]{2,1,0:T(8,128)(2,1)S(1)} %collective-permute-done.3.refs_0_, bf16[4,264,512]{2,1,0:T(8,128)(2,1)S(1)} %collective-permute-done.4.refs_1_, ...), custom_call_target="tpu_custom_call", output_to_operand_aliasing={{0}: (4, {}), {1}: (5, {})} | custom-call | flops 2147483648 | bytes 1048576 | tf_op jit(solution)/shard_map/pallas_call | solution.py:225
  50.2 0.6 collective-permute-start.10
  51.1 3.3 %collective-permute-start.13 = (f32[8,128]{1,0:T(8,128)S(1)}, f32[8,128]{1,0:T(8,128)S(1)}, u32[]{:S(2)}, u32[]{:S(2)}) collective-permute-start(f32[8,128]{1,0:T(8,128)S(1)} %rows.1), channel_id=1, source_target_pairs={{0,8},{4,12},{8,16},{12,20},{16,24},{20,28},{24,0},{28,4},{1,9},{5... | collective-permute-start | bytes 12296 | tf_op jit(solution)/shard_map/ppermute | solution.py:55
  54.3 4.0 %collective-permute-start.14 = (f32[8,128]{1,0:T(8,128)S(1)}, f32[8,128]{1,0:T(8,128)S(1)}, u32[]{:S(2)}, u32[]{:S(2)}) collective-permute-start(f32[8,128]{1,0:T(8,128)S(1)} %rows.1), channel_id=1, source_target_pairs={{0,12},{4,16},{8,20},{12,24},{16,28},{20,0},{24,4},{28,8},{1,13},{... | collective-permute-start | bytes 12296 | tf_op jit(solution)/shard_map/ppermute | solution.py:55
  58.4 0.6 collective-permute-start.15
  58.9 2.0 %collective-permute-done.14 = f32[8,128]{1,0:T(8,128)S(1)} collective-permute-done((f32[8,128]{1,0:T(8,128)S(1)}, f32[8,128]{1,0:T(8,128)S(1)}, u32[]{:S(2)}, u32[]{:S(2)}) %collective-permute-start.14) | collective-permute-done | bytes 4128 | tf_op jit(solution)/shard_map/ppermute | solution.py:55
  61.0 4.9 %collective-permute-done.15 = f32[8,128]{1,0:T(8,128)S(1)} collective-permute-done((f32[8,128]{1,0:T(8,128)S(1)}, f32[8,128]{1,0:T(8,128)S(1)}, u32[]{:S(2)}, u32[]{:S(2)}) %collective-permute-start.15) | collective-permute-done | bytes 4128 | tf_op jit(solution)/shard_map/ppermute | solution.py:55
  65.9 1.8 %collective-permute-start.16 = (f32[8,128]{1,0:T(8,128)S(1)}, f32[8,128]{1,0:T(8,128)S(1)}, u32[]{:S(2)}, u32[]{:S(2)}) collective-permute-start(f32[8,128]{1,0:T(8,128)S(1)} %select_add_fusion.own_terms), channel_id=1, source_target_pairs={{0,128},{128,0},{1,129},{129,1},{2,130},{130,2},{3,131},{131,3},{4... | collective-permute-start | bytes 12296 | tf_op jit(solution)/shard_map/ppermute | solution.py:39
  67.7 1.5 %shard_map.85 = (f32[3,8,128,640]{3,2,1,0:T(8,128)S(1)}, bf16[2,8,128,256]{3,2,1,0:T(8,128)(2,1)S(1)}) custom-call(bf16[2,264,512]{2,1,0:T(8,128)(2,1)S(1)} %collective-permute-done.8.low, bf16[2,264,512]{2,1,0:T(8,128)(2,1)S(1)} %collective-permute-done.9.high, ...), custom_call_target="tpu_custom_call", output_to_operand_aliasing={{0}: (4, {}), {1}: (5, {})} | custom-call | flops 1073741824 | bytes 1048576 | tf_op jit(solution)/shard_map/pallas_call | solution.py:225
  69.6 5.9 %finish.1 = (f32[3,8,128,640]{3,2,1,0:T(8,128)S(1)}, bf16[2,8,128,256]{3,2,1,0:T(8,128)(2,1)S(1)}, f32[4,3,32,640]{3,2,1,0:T(8,128)S(1)}, bf16[4,3,32,640]{3,2,1,0:T(8,128)(2,1)S(1)}) custom-call(bf16[2,264,512]{2,1,0:T(8,128)(2,1)S(1)} %collective-permute-done.10.low, ...), custom_call_target="tpu_custom_call", output_to_operand_aliasing={{0}: (4, {}), {1}: (5, {})} | custom-call | flops 4294967296 | bytes 1048576 | tf_op jit(solution)/shard_map/finish/pallas_call | solution.py:237
  75.6 1.1 %collective-permute-start.17 = (bf16[4,3,32,640]{3,2,1,0:T(8,128)(2,1)S(1)}, bf16[4,3,32,640]{3,2,1,0:T(8,128)(2,1)S(1)}, u32[]{:S(2)}, u32[]{:S(2)}) collective-permute-start(bf16[4,3,32,640]{3,2,1,0:T(8,128)(2,1)S(1)} %get-tuple-element.36), channel_id=1, source_target_pairs={{0,4},{1,29},{4,0},{5,9},{8,12},{9,5},{12,8},{13,17},{16,20},{17,1... | collective-permute-start | bytes 1474568 | tf_op jit(solution)/shard_map/ppermute | solution.py:51
  76.6 7.8 %collective-permute-done.17 = bf16[4,3,32,640]{3,2,1,0:T(8,128)(2,1)S(1)} collective-permute-done((bf16[4,3,32,640]{3,2,1,0:T(8,128)(2,1)S(1)}, bf16[4,3,32,640]{3,2,1,0:T(8,128)(2,1)S(1)}, u32[]{:S(2)}, u32[]{:S(2)}) %collective-permute-start.17) | collective-permute-done | bytes 491552 | tf_op jit(solution)/shard_map/ppermute | solution.py:51
  84.7 0.6 collective-permute-start.18
  85.3 4.5 %collective-permute-start.19 = (bf16[3,32,640]{2,1,0:T(8,128)(2,1)S(1)}, bf16[3,32,640]{2,1,0:T(8,128)(2,1)S(1)}, u32[]{:S(2)}, u32[]{:S(2)}) collective-permute-start(bf16[3,32,640]{2,1,0:T(8,128)(2,1)S(1)} %get-tuple-element.41), channel_id=1, source_target_pairs={{0,8},{4,12},{8,16},{12,20},{16,24},{20,28},{24,0},{28,4},{1,9},{5... | collective-permute-start | bytes 368648 | tf_op jit(solution)/shard_map/ppermute | solution.py:55
  89.8 6.2 %collective-permute-done.18 = bf16[3,32,640]{2,1,0:T(8,128)(2,1)S(1)} collective-permute-done((bf16[3,32,640]{2,1,0:T(8,128)(2,1)S(1)}, bf16[3,32,640]{2,1,0:T(8,128)(2,1)S(1)}, u32[]{:S(2)}, u32[]{:S(2)}) %collective-permute-start.18) | collective-permute-done | bytes 122912 | tf_op jit(solution)/shard_map/ppermute | solution.py:55
  96.0 3.4 %collective-permute-done.20 = bf16[3,32,640]{2,1,0:T(8,128)(2,1)S(1)} collective-permute-done((bf16[3,32,640]{2,1,0:T(8,128)(2,1)S(1)}, bf16[3,32,640]{2,1,0:T(8,128)(2,1)S(1)}, u32[]{:S(2)}, u32[]{:S(2)}) %collective-permute-start.20) | collective-permute-done | bytes 122912 | tf_op jit(solution)/shard_map/ppermute | solution.py:55
  99.4 0.8 fusion.3
  (28 shorter events, 1.3 us)
Async XLA Ops:
  1.7 6.5 %collective-permute-start = (bf16[264,512]{1,0:T(8,128)(2,1)S(1)}, bf16[264,512]{1,0:T(8,128)(2,1)S(1)}, u32[]{:S(2)}, u32[]{:S(2)}) collective-permute-start(bf16[264,512]{1,0:T(8,128)(2,1)S(1)} %message.1), channel_id=1, source_target_pairs={{0,128},{1,33},{2,130},{3,35},{32,160},{33,1},{34,162},{35,3},{64,... | collective-permute-start | bytes 811016 | tf_op jit(solution)/shard_map/ppermute | solution.py:35
  2.6 10.2 %collective-permute-start.1 = (bf16[264,512]{1,0:T(8,128)(2,1)S(1)}, bf16[264,512]{1,0:T(8,128)(2,1)S(1)}, u32[]{:S(2)}, u32[]{:S(2)}) collective-permute-start(bf16[264,512]{1,0:T(8,128)(2,1)S(1)} %message.1), channel_id=1, source_target_pairs={{0,2},{1,65},{2,0},{3,67},{32,34},{33,97},{34,32},{35,99},{64,66},... | collective-permute-start | bytes 811016 | tf_op jit(solution)/shard_map/ppermute | solution.py:35
  5.4 10.2 %collective-permute-start.2 = (bf16[264,512]{1,0:T(8,128)(2,1)S(1)}, bf16[264,512]{1,0:T(8,128)(2,1)S(1)}, u32[]{:S(2)}, u32[]{:S(2)}) collective-permute-start(bf16[264,512]{1,0:T(8,128)(2,1)S(1)} %message.1), channel_id=1, source_target_pairs={{0,130},{1,97},{2,128},{3,99},{32,162},{33,65},{34,160},{35,67},{6... | collective-permute-start | bytes 811016 | tf_op jit(solution)/shard_map/ppermute | solution.py:35
  15.8 15.2 %collective-permute-start.5 = (bf16[4,264,512]{2,1,0:T(8,128)(2,1)S(1)}, bf16[4,264,512]{2,1,0:T(8,128)(2,1)S(1)}, u32[]{:S(2)}, u32[]{:S(2)}) collective-permute-start(bf16[4,264,512]{2,1,0:T(8,128)(2,1)S(1)} %pad_maximum_fusion.own), channel_id=1, source_target_pairs={{0,32},{1,129},{2,34},{3,131},{32,0},{33,161},{34,2},{35,163},{64,... | collective-permute-start | bytes 3244040 | tf_op jit(solution)/shard_map/ppermute | solution.py:35
  15.9 16.4 %collective-permute-start.3 = (bf16[4,264,512]{2,1,0:T(8,128)(2,1)S(1)}, bf16[4,264,512]{2,1,0:T(8,128)(2,1)S(1)}, u32[]{:S(2)}, u32[]{:S(2)}) collective-permute-start(bf16[4,264,512]{2,1,0:T(8,128)(2,1)S(1)} %pad_maximum_fusion.own), channel_id=1, source_target_pairs={{0,96},{1,131},{2,98},{3,129},{32,64},{33,163},{34,66},{35,161},{6... | collective-permute-start | bytes 3244040 | tf_op jit(solution)/shard_map/ppermute | solution.py:35
  17.9 20.0 %collective-permute-start.7 = (bf16[4,264,512]{2,1,0:T(8,128)(2,1)S(1)}, bf16[4,264,512]{2,1,0:T(8,128)(2,1)S(1)}, u32[]{:S(2)}, u32[]{:S(2)}) collective-permute-start(bf16[4,264,512]{2,1,0:T(8,128)(2,1)S(1)} %pad_maximum_fusion.own), channel_id=1, source_target_pairs={{0,1},{1,0},{2,3},{3,2},{4,5},{5,4},{6,7},{7,6},{8,9},{9,8},{10,11... | collective-permute-start | bytes 3244040 | tf_op jit(solution)/shard_map/ppermute | solution.py:43
  31.0 12.7 %collective-permute-start.6 = (bf16[4,264,512]{2,1,0:T(8,128)(2,1)S(1)}, bf16[4,264,512]{2,1,0:T(8,128)(2,1)S(1)}, u32[]{:S(2)}, u32[]{:S(2)}) collective-permute-start(bf16[4,264,512]{2,1,0:T(8,128)(2,1)S(1)} %collective-permute-done.5.refs_0_), channel_id=1, source_target_pairs={{0,1},{1,0},{2,3},{3,2},{4,5},{5,4},{6,7},{7,6},{8,9},{9,8},{10,11... | collective-permute-start | bytes 3244040 | tf_op jit(solution)/shard_map/ppermute | solution.py:43
  32.3 14.6 %collective-permute-start.4 = (bf16[4,264,512]{2,1,0:T(8,128)(2,1)S(1)}, bf16[4,264,512]{2,1,0:T(8,128)(2,1)S(1)}, u32[]{:S(2)}, u32[]{:S(2)}) collective-permute-start(bf16[4,264,512]{2,1,0:T(8,128)(2,1)S(1)} %collective-permute-done.3.refs_0_), channel_id=1, source_target_pairs={{0,1},{1,0},{2,3},{3,2},{4,5},{5,4},{6,7},{7,6},{8,9},{9,8},{10,11... | collective-permute-start | bytes 3244040 | tf_op jit(solution)/shard_map/ppermute | solution.py:43
  35.7 14.4 %collective-permute-start.8 = (bf16[2,264,512]{2,1,0:T(8,128)(2,1)S(1)}, bf16[2,264,512]{2,1,0:T(8,128)(2,1)S(1)}, u32[]{:S(2)}, u32[]{:S(2)}) collective-permute-start(bf16[2,264,512]{2,1,0:T(8,128)(2,1)S(1)} %slice.27), channel_id=1, source_target_pairs={{0,96},{1,131},{2,98},{3,129},{32,64},{33,163},{34,66},{35,161},{6... | collective-permute-start | bytes 1622024 | tf_op jit(solution)/shard_map/ppermute | solution.py:35
  37.8 12.4 %collective-permute-start.9 = (bf16[2,264,512]{2,1,0:T(8,128)(2,1)S(1)}, bf16[2,264,512]{2,1,0:T(8,128)(2,1)S(1)}, u32[]{:S(2)}, u32[]{:S(2)}) collective-permute-start(bf16[2,264,512]{2,1,0:T(8,128)(2,1)S(1)} %slice.28), channel_id=1, source_target_pairs={{0,32},{1,129},{2,34},{3,131},{32,0},{33,161},{34,2},{35,163},{64,... | collective-permute-start | bytes 1622024 | tf_op jit(solution)/shard_map/ppermute | solution.py:35
  37.9 20.4 %collective-permute-start.12 = (f32[8,128]{1,0:T(8,128)S(1)}, f32[8,128]{1,0:T(8,128)S(1)}, u32[]{:S(2)}, u32[]{:S(2)}) collective-permute-start(f32[8,128]{1,0:T(8,128)S(1)} %rows.1), channel_id=1, source_target_pairs={{0,4},{4,8},{8,12},{12,16},{16,20},{20,24},{24,28},{28,0},{1,5},{5... | collective-permute-start | bytes 12296 | tf_op jit(solution)/shard_map/ppermute | solution.py:55
  50.2 19.4 %collective-permute-start.10 = (bf16[2,264,512]{2,1,0:T(8,128)(2,1)S(1)}, bf16[2,264,512]{2,1,0:T(8,128)(2,1)S(1)}, u32[]{:S(2)}, u32[]{:S(2)}) collective-permute-start(bf16[2,264,512]{2,1,0:T(8,128)(2,1)S(1)} %collective-permute-done.8.low), channel_id=1, source_target_pairs={{0,1},{1,0},{2,3},{3,2},{4,5},{5,4},{6,7},{7,6},{8,9},{9,8},{10,11... | collective-permute-start | bytes 1622024 | tf_op jit(solution)/shard_map/ppermute | solution.py:43
  50.8 18.8 %collective-permute-start.11 = (bf16[2,264,512]{2,1,0:T(8,128)(2,1)S(1)}, bf16[2,264,512]{2,1,0:T(8,128)(2,1)S(1)}, u32[]{:S(2)}, u32[]{:S(2)}) collective-permute-start(bf16[2,264,512]{2,1,0:T(8,128)(2,1)S(1)} %collective-permute-done.9.high), channel_id=1, source_target_pairs={{0,1},{1,0},{2,3},{3,2},{4,5},{5,4},{6,7},{7,6},{8,9},{9,8},{10,11... | collective-permute-start | bytes 1622024 | tf_op jit(solution)/shard_map/ppermute | solution.py:43
  51.1 7.9 %collective-permute-start.13 = (f32[8,128]{1,0:T(8,128)S(1)}, f32[8,128]{1,0:T(8,128)S(1)}, u32[]{:S(2)}, u32[]{:S(2)}) collective-permute-start(f32[8,128]{1,0:T(8,128)S(1)} %rows.1), channel_id=1, source_target_pairs={{0,8},{4,12},{8,16},{12,20},{16,24},{20,28},{24,0},{28,4},{1,9},{5... | collective-permute-start | bytes 12296 | tf_op jit(solution)/shard_map/ppermute | solution.py:55
  54.3 6.6 %collective-permute-start.14 = (f32[8,128]{1,0:T(8,128)S(1)}, f32[8,128]{1,0:T(8,128)S(1)}, u32[]{:S(2)}, u32[]{:S(2)}) collective-permute-start(f32[8,128]{1,0:T(8,128)S(1)} %rows.1), channel_id=1, source_target_pairs={{0,12},{4,16},{8,20},{12,24},{16,28},{20,0},{24,4},{28,8},{1,13},{... | collective-permute-start | bytes 12296 | tf_op jit(solution)/shard_map/ppermute | solution.py:55
  58.4 7.5 %collective-permute-start.15 = (f32[8,128]{1,0:T(8,128)S(1)}, f32[8,128]{1,0:T(8,128)S(1)}, u32[]{:S(2)}, u32[]{:S(2)}) collective-permute-start(f32[8,128]{1,0:T(8,128)S(1)} %rows.1), channel_id=1, source_target_pairs={{0,16},{4,20},{8,24},{12,28},{16,0},{20,4},{24,8},{28,12},{1,17},{... | collective-permute-start | bytes 12296 | tf_op jit(solution)/shard_map/ppermute | solution.py:55
  65.9 3.7 %collective-permute-start.16 = (f32[8,128]{1,0:T(8,128)S(1)}, f32[8,128]{1,0:T(8,128)S(1)}, u32[]{:S(2)}, u32[]{:S(2)}) collective-permute-start(f32[8,128]{1,0:T(8,128)S(1)} %select_add_fusion.own_terms), channel_id=1, source_target_pairs={{0,128},{128,0},{1,129},{129,1},{2,130},{130,2},{3,131},{131,3},{4... | collective-permute-start | bytes 12296 | tf_op jit(solution)/shard_map/ppermute | solution.py:39
  75.6 8.9 %collective-permute-start.17 = (bf16[4,3,32,640]{3,2,1,0:T(8,128)(2,1)S(1)}, bf16[4,3,32,640]{3,2,1,0:T(8,128)(2,1)S(1)}, u32[]{:S(2)}, u32[]{:S(2)}) collective-permute-start(bf16[4,3,32,640]{3,2,1,0:T(8,128)(2,1)S(1)} %get-tuple-element.36), channel_id=1, source_target_pairs={{0,4},{1,29},{4,0},{5,9},{8,12},{9,5},{12,8},{13,17},{16,20},{17,1... | collective-permute-start | bytes 1474568 | tf_op jit(solution)/shard_map/ppermute | solution.py:51
  84.7 11.3 %collective-permute-start.18 = (bf16[3,32,640]{2,1,0:T(8,128)(2,1)S(1)}, bf16[3,32,640]{2,1,0:T(8,128)(2,1)S(1)}, u32[]{:S(2)}, u32[]{:S(2)}) collective-permute-start(bf16[3,32,640]{2,1,0:T(8,128)(2,1)S(1)} %get-tuple-element.39), channel_id=1, source_target_pairs={{0,16},{4,20},{8,24},{12,28},{16,0},{20,4},{24,8},{28,12},{1,17},{... | collective-permute-start | bytes 368648 | tf_op jit(solution)/shard_map/ppermute | solution.py:55
  85.3 10.7 %collective-permute-start.19 = (bf16[3,32,640]{2,1,0:T(8,128)(2,1)S(1)}, bf16[3,32,640]{2,1,0:T(8,128)(2,1)S(1)}, u32[]{:S(2)}, u32[]{:S(2)}) collective-permute-start(bf16[3,32,640]{2,1,0:T(8,128)(2,1)S(1)} %get-tuple-element.41), channel_id=1, source_target_pairs={{0,8},{4,12},{8,16},{12,20},{16,24},{20,28},{24,0},{28,4},{1,9},{5... | collective-permute-start | bytes 368648 | tf_op jit(solution)/shard_map/ppermute | solution.py:55
  89.8 9.6 %collective-permute-start.20 = (bf16[3,32,640]{2,1,0:T(8,128)(2,1)S(1)}, bf16[3,32,640]{2,1,0:T(8,128)(2,1)S(1)}, u32[]{:S(2)}, u32[]{:S(2)}) collective-permute-start(bf16[3,32,640]{2,1,0:T(8,128)(2,1)S(1)} %get-tuple-element.40), channel_id=1, source_target_pairs={{0,24},{4,28},{8,0},{12,4},{16,8},{20,12},{24,16},{28,20},{1,25},{... | collective-permute-start | bytes 368648 | tf_op jit(solution)/shard_map/ppermute | solution.py:55

commit v4 on v3

--- a/solution.py
+++ b/solution.py
@@ -49,6 +49,12 @@
 
 def z_pair(block):
     return lax.ppermute(block, ("z", "c"), [(z * 2 + c, partner_of(z, c) * 2 + c) for z in range(8) for c in range(2)])
+
+
+def z_shift(block, step):
+    return lax.ppermute(
+        block, ("z", "c"), [(z * 2 + c, (z + step + c) % 8 * 2 + c) for z in range(8) for c in range(2)]
+    )
 
 
 def z_step(block, step):
@@ -132,84 +138,52 @@
     )(*[hbm(w.reshape(4, 512, 640)) for w in (w_gate, w_lin, w_out_t)])
 
 
-def rows_kernel(own, other, rows):
+def rows_kernel(own_low, own_high, other_low, other_high, rows):
     c = lax.axis_index("c").astype(I32)
     rows[...] = jnp.zeros_like(rows)
     for dy in range(4):
-        piece = [block[dy, 256:264, 0:128].astype(F32) for block in (own, other)]
+        pair = (own_low, other_low) if dy < 2 else (own_high, other_high)
+        piece = [block[dy % 2, 256:264, 0:128].astype(F32) for block in pair]
         piece = jnp.where(c == 1, piece[0], piece[1])
         rows[dy : dy + 1, :] = jnp.sum(piece, axis=0, keepdims=True)
 
 
-def line_rows(own, other):
+def line_rows(*blocks):
     return pl.pallas_call(
         rows_kernel,
         out_shape=jax.ShapeDtypeStruct((8, 128), F32),
-        in_specs=[VMEM] * 2,
+        in_specs=[VMEM] * 4,
         out_specs=VMEM,
         compiler_params=PARAMS,
         name="rows",
-    )(own, other)
-
-
-def first_kernel(own, other, w_in, w_out, acc, cols):
-    acc[...] = jnp.zeros_like(acc)
-    gather_kernel(0, ((0, own), (1, other)), w_in, w_out, acc, cols)
-
-
-def middle_kernel(m, *refs):
-    *blocks, w_in, w_out, _, __, acc, cols = refs
-    gather_kernel(m, tuple(enumerate(blocks)), w_in, w_out, acc, cols)
-
-
-def halves_kernel(low, high, w_in, w_out, _, __, acc, cols):
-    gather_kernel(2, ((0, (low, high)),), w_in, w_out, acc, cols)
-
-
-def final_kernel(low, high, w_in, w_out, _, __, own_terms, other_terms, acc, cols, *rest):
-    gather_kernel(2, ((1, (low, high)),), w_in, w_out, acc, cols)
-    last_kernel((own_terms, other_terms), acc, cols, *rest)
-
-
-def gather_kernel(m, blocks, w_in, w_out, acc, cols):
+    )(*blocks)
+
+
+def add_block(m, j, ec, block, w_in, w_out, acc, cols):
     xl, y, _, xh, c = place()
-    for ec, block in blocks:
-        x_first = (c ^ ec) == 0
-
-        def step(j, block, start):
-            eh = jnp.where(x_first, j, m >> 1)
-            p0 = jnp.where(x_first, 2 * m, 4 * j + (m & 1))
-            p1 = jnp.where(x_first, 2 * m + 1, 4 * j + 2 + (m & 1))
-            shard = (xh ^ eh) * 2 + (c ^ ec)
-            xs = block[pl.ds(start, 2), 0:128].reshape(256, 512)
-            ys = block[pl.ds(start, 2), 128:256].reshape(256, 512)
-            pre = jnp.dot(xs, w_in[shard], preferred_element_type=F32)
-            acc[0, p0] += pre[:128, :640]
-            acc[1, p0] += pre[:128, 640:]
-            acc[0, p1] += pre[128:, :640]
-            acc[1, p1] += pre[128:, 640:]
-            dh = jnp.dot(ys, w_out[shard], preferred_element_type=F32)
-            acc[2, p0] += dh[:128]
-            acc[2, p1] += dh[128:]
-
-            @pl.when((ec == ((y >> 1) ^ c)) & (eh == (xl ^ xh)))
-            def _():
-                low = (y & 1) == 0
-                for n, v in ((0, xs), (1, ys)):
-                    v = jnp.where(low, v[:, :256], v[:, 256:])
-                    cols[n, p0] = v[:128]
-                    cols[n, p1] = v[128:]
-
-        if isinstance(block, tuple):
-            for j in range(2):
-                step(j, block[j], 0)
-        else:
-
-            def body(j, carry):
-                step(j, block, 2 * j)
-                return carry
-
-            lax.fori_loop(0, 2, body, 0)
+    x_first = (c ^ ec) == 0
+    eh = jnp.where(x_first, j, m >> 1)
+    p0 = jnp.where(x_first, 2 * m, 4 * j + (m & 1))
+    p1 = jnp.where(x_first, 2 * m + 1, 4 * j + 2 + (m & 1))
+    shard = (xh ^ eh) * 2 + (c ^ ec)
+    xs = block[:, 0:128].reshape(256, 512)
+    ys = block[:, 128:256].reshape(256, 512)
+    pre = jnp.dot(xs, w_in[shard], preferred_element_type=F32)
+    acc[0, p0] += pre[:128, :640]
+    acc[1, p0] += pre[:128, 640:]
+    acc[0, p1] += pre[128:, :640]
+    acc[1, p1] += pre[128:, 640:]
+    dh = jnp.dot(ys, w_out[shard], preferred_element_type=F32)
+    acc[2, p0] += dh[:128]
+    acc[2, p1] += dh[128:]
+
+    @pl.when((ec == ((y >> 1) ^ c)) & (eh == (xl ^ xh)))
+    def _():
+        low = (y & 1) == 0
+        for n, v in ((0, xs), (1, ys)):
+            v = jnp.where(low, v[:, :256], v[:, 256:])
+            cols[n, p0] = v[:128]
+            cols[n, p1] = v[128:]
 
 
 STATE = (jax.ShapeDtypeStruct((3, 8, 128, 640), F32), jax.ShapeDtypeStruct((2, 8, 128, 256), BF16))
@@ -219,28 +193,44 @@
     return pl.CostEstimate(flops=giga << 30, bytes_accessed=1 << 20, transcendentals=0)
 
 
-def gathered(m, blocks, w_in, w_out, state):
-    n = len(blocks) + 2
-    kernels = {0: first_kernel, 2: halves_kernel}
-    return pl.pallas_call(
-        kernels.get(m, lambda *refs: middle_kernel(m, *refs)),
+def gathered(items, w_in, w_out, state):
+    n = len(items)
+
+    def kernel(*refs):
+        blocks, (w_in, w_out), (acc, cols) = refs[:n], refs[n : n + 2], refs[-2:]
+        if not state:
+            acc[...] = jnp.zeros_like(acc)
+        for (m, j, ec, _), block in zip(items, blocks):
+            add_block(m, j, ec, block, w_in, w_out, acc, cols)
+
+    return pl.pallas_call(
+        kernel,
         out_shape=STATE,
-        in_specs=[VMEM] * (n + len(state)),
+        in_specs=[VMEM] * (n + 2 + len(state)),
         out_specs=(VMEM, VMEM),
-        input_output_aliases={n: 0, n + 1: 1} if state else {},
-        compiler_params=PARAMS,
-        cost_estimate=priced(2 if m != 2 else 1),
-    )(*blocks, w_in, w_out, *state)
-
-
-def finished(halves, w_in, w_out, state, terms):
-    return pl.pallas_call(
-        final_kernel,
+        input_output_aliases={n + 2: 0, n + 3: 1} if state else {},
+        compiler_params=PARAMS,
+        cost_estimate=priced(n // 2),
+    )(*[item[3] for item in items], w_in, w_out, *state)
+
+
+def finished(items, w_in, w_out, state, terms):
+    n = len(items)
+
+    def kernel(*refs):
+        blocks, (w_in, w_out), terms = refs[:n], refs[n : n + 2], refs[n + 4 : n + 8]
+        acc, cols, *rest = refs[n + 8 :]
+        for (m, j, ec, _), block in zip(items, blocks):
+            add_block(m, j, ec, block, w_in, w_out, acc, cols)
+        last_kernel(terms, acc, cols, *rest)
+
+    return pl.pallas_call(
+        kernel,
         out_shape=STATE
         + (jax.ShapeDtypeStruct((4, 3, 32, 640), F32), jax.ShapeDtypeStruct((4, 3, 32, 640), BF16)),
-        in_specs=[VMEM] * 8,
+        in_specs=[VMEM] * (n + 8),
         out_specs=(VMEM,) * 4,
-        input_output_aliases={4: 0, 5: 1},
+        input_output_aliases={n + 2: 0, n + 3: 1},
         scratch_shapes=[
             pltpu.VMEM((8, 128, 1280), BF16),
             pltpu.VMEM((8, 128, 640), BF16),
@@ -249,7 +239,7 @@
         compiler_params=PARAMS,
         cost_estimate=priced(4),
         name="finish",
-    )(*halves, w_in, w_out, *state, *terms)[2:]
+    )(*[item[3] for item in items], w_in, w_out, *state, *terms)[2:]
 
 
 def last_kernel(terms, acc, cols, keep, send, gates, hidden, total):
@@ -263,9 +253,9 @@
         dy, ex = p >> 1, p & 1
         number = ((xl ^ ex) * 4 + (y ^ dy)) * 8 + z
         w = F32(0.0)
-        for worker, term in zip(workers, terms):
+        for i, worker in enumerate(workers):
             mine = known & (((number - lane) & 63) == worker)
-            w = w + jnp.sum(jnp.where(mine, term[...], 0.0))
+            w = w + jnp.sum(jnp.where(mine, terms[2 * i][...] + terms[2 * i + 1][...], 0.0))
         for r in range(0, 128, 32):
             rows = pl.ds(r, 32)
             u = acc[0, p, rows]
@@ -301,33 +291,44 @@
 
 def all_steps(tokens, grad_out, w_gate, w_lin, w_out_t, code, decode, stragglers):
     own = message(code, decode, stragglers, tokens, grad_out)
-    row = [own]
+    first = {}
     for k in (1, 2, 3):
-        row.append(across(own, k, True))
+        first[k] = across(own, k, True)
     w_in, w_out = loaded_weights(w_gate, w_lin, w_out_t)
-    row = jnp.stack(row)
-    near = {}
-    for k in (1, 3):
-        near[k] = across(row, k, False)
-    swap = sibling(row)
-    planes = [line_rows(row, swap)]
-    for j in (1, 2, 3, 4):
-        planes.append(z_step(planes[0], j))
+    low, high = jnp.stack([own, first[1]]), jnp.stack([first[2], first[3]])
+    blocks, others = {(0, 0): low, (0, 1): high}, {}
+    for j, half in enumerate((low, high)):
+        for k in (1, 3):
+            blocks[k, j] = across(half, k, False)
+        others[0, j] = sibling(half)
+    for j, came, flip in ((0, 1, 3), (1, 3, 1)):
+        blocks[2, j] = across(blocks[came, j], flip, False)
+    rows = line_rows(low, high, others[0, 0], others[0, 1])
+    c = lax.axis_index("c").astype(I32)
     lane = lax.broadcasted_iota(I32, (8, 128), 1)
-    terms = sum(jnp.where(lane == j, plane, 0.0) for j, plane in enumerate(planes))
-    terms = (terms, swapped(terms, "xl", 2, 1))
-    low = across(near[1][:2], 3, False)
-    high = across(near[3][2:], 1, False)
-    other = {}
-    for k in (1, 3):
-        other[k] = sibling(near[k])
-    state = gathered(0, (row, swap), w_in, w_out, ())
-    for m in (1, 3):
-        state = gathered(m, (near[m], other[m]), w_in, w_out, state)
-    state, low, high = lax.optimization_barrier((state, low, high))
-    halves = [sibling(low), sibling(high)]
-    state = gathered(2, (low, high), w_in, w_out, state)
-    keep, send = finished(halves, w_in, w_out, state, terms)
+    partial = jnp.where((lane == 0) & (c == 0), rows, 0.0)
+    for j in (1, 3):
+        partial = partial + jnp.where(lane == j + c, z_shift(rows, j), 0.0)
+    partials = [partial, swapped(partial, "xl", 2, 1)]
+    terms = []
+    for part in partials:
+        terms += [part, sibling(part)]
+    for j in range(2):
+        for k in (1, 3):
+            others[k, j] = sibling(blocks[k, j])
+
+    def items(keys, sides=(0, 1)):
+        return [(m, j, ec, (blocks, others)[ec][m, j]) for m, j in keys for ec in sides]
+
+    state = gathered(items([(0, 0), (0, 1)]), w_in, w_out, ())
+    for j in range(2):
+        state = gathered(items([(1, j), (3, j)]), w_in, w_out, state)
+    state, blocks[2, 0], blocks[2, 1] = lax.optimization_barrier((state, blocks[2, 0], blocks[2, 1]))
+    for j in range(2):
+        others[2, j] = sibling(blocks[2, j])
+    far = [(2, 0), (2, 1)]
+    state = gathered(items(far, (0,)), w_in, w_out, state)
+    keep, send = finished(items(far, (1,)), w_in, w_out, state, terms)
     got = z_pair(send)
     mixed = keep + got.astype(F32)
     result = mixed[0]

time: 102 us -> 99.3 us (0.974)
  waiting for transfers between devices: 48.3 us -> 41 us
  starting transfers between devices: 27.8 us -> 30.9 us
  Pallas kernels: 22 us -> 24.3 us
    ppermute x7 -> x3, waiting for transfers between devices: 16.6 us -> 7.62 us  [z_step(): return lax.ppermute(block, 'z', [(z, (z + step) % 8) for z in range(8)])]
    ppermute x0 -> x2, starting transfers between devices: none -> 7.83 us  [z_shift(): lax.ppermute(block, ('z', 'c'), [(z * 2 + c, (z + step + c) % 8 * 2 + c)...]
    ppermute x7 -> x3, starting transfers between devices: 15 us -> 9.68 us  [z_step(): return lax.ppermute(block, 'z', [(z, (z + step) % 8) for z in range(8)])]
    ppermute x7 -> x9, waiting for transfers between devices: 23.6 us -> 20.5 us  [across(): return lax.ppermute(block, PLANE, route)]
    ppermute x1, waiting for transfers between devices: 0.34 us -> 3.45 us  [swapped(): return lax.ppermute(block, axis, [(i, i ^ flip) for i in range(size)])]
    pallas_call x5, Pallas kernels: 17.7 us -> 19.9 us  [the longest x4 13.9 us: gathered(): pl.pallas_call(kernel, out_shape=STATE, in_specs=[VMEM] * (n + 2 + len(st...]
    ppermute x7 -> x9, starting transfers between devices: 9.04 us -> 10.9 us  [across(): return lax.ppermute(block, PLANE, route)]
    ppermute x1, starting transfers between devices: 1.8 us -> 0.01 us  [swapped(): return lax.ppermute(block, axis, [(i, i ^ flip) for i in range(size)])]
  transfers between devices with their start and end apart: 21 -> 26, of which waited for: 11 -> 10; matrix products, arithmetic and copies ran while one was open for 0% -> 0% of each run, Pallas kernels for 15% -> 18%
where the time goes in v4:
time: 99.3 us; the launch traced here: 98.1 us
  waiting for transfers between devices  41 us (41%)
  starting transfers between devices  30.9 us (31%)
  Pallas kernels  24.3 us (24%)
  other arithmetic  1.02 us (1%)
    ppermute x9, waiting for transfers between devices, across(): return lax.ppermute(block, PLANE, route)  20.5 us
    pallas_call x4, Pallas kernels, gathered(): pl.pallas_call(kernel, out_shape=STATE, in_specs=[VMEM] * (n + 2 + len(st...  13.9 us
    ppermute x9, starting transfers between devices, across(): return lax.ppermute(block, PLANE, route)  10.9 us
    ppermute x3, starting transfers between devices, z_step(): return lax.ppermute(block, 'z', [(z, (z + step) % 8) for z in range(8)])  9.68 us
    ppermute x2, starting transfers between devices, z_shift(): lax.ppermute(block, ('z', 'c'), [(z * 2 + c, (z + step + c) % 8 * 2 + c)...  7.83 us
    ppermute x1, waiting for transfers between devices, z_pair(): lax.ppermute(block, ('z', 'c'), [(z * 2 + c, partner_of(z, c) * 2 + c) fo...  7.77 us
    ppermute x3, waiting for transfers between devices, z_step(): return lax.ppermute(block, 'z', [(z, (z + step) % 8) for z in range(8)])  7.62 us
    pallas_call x1, Pallas kernels, finished(): pl.pallas_call(kernel, out_shape=STATE + (jax.ShapeDtypeStruct((4, 3, 32,...  6.04 us
  transfers between devices with their start and end apart: 26, of which 10 were waited for; matrix products, arithmetic and copies ran while one was open for 0% of the time, Pallas kernels for 18%

profile of v4, /device:TPU:6, one launch (start us, length us, event | category | flops | bytes accessed | tf_op | source)
XLA Modules:
  0.0 98.1 jit_solution(12468181118016640272)
XLA Ops:
  0.7 1.0 %message.1 = bf16[264,512]{1,0:T(8,128)(2,1)S(1)} custom-call(f32[1]{0:T(128)S(6)} %copy.25.decode, f32[1,5]{1,0:T(1,128)} %code_in.1, s32[4]{0:T(128)} %stragglers_in.1, bf16[128,512]{1,0:T(8,128)(2,1)} %tokens.1, bf16[128,512]{1,0:T(8,128)(2,1)} %grad_out.1), custom_call_target="tpu_custom_call" | custom-call | tf_op jit(solution)/shard_map/message/pallas_call | solution.py:103
  1.7 1.5 %collective-permute-start = (bf16[264,512]{1,0:T(8,128)(2,1)S(1)}, bf16[264,512]{1,0:T(8,128)(2,1)S(1)}, u32[]{:S(2)}, u32[]{:S(2)}) collective-permute-start(bf16[264,512]{1,0:T(8,128)(2,1)S(1)} %message.1), channel_id=1, source_target_pairs={{0,2},{1,65},{2,0},{3,67},{32,34},{33,97},{34,32},{35,99},{64,66},... | collective-permute-start | bytes 811016 | tf_op jit(solution)/shard_map/ppermute | solution.py:35
  3.2 2.1 %collective-permute-start.1 = (bf16[264,512]{1,0:T(8,128)(2,1)S(1)}, bf16[264,512]{1,0:T(8,128)(2,1)S(1)}, u32[]{:S(2)}, u32[]{:S(2)}) collective-permute-start(bf16[264,512]{1,0:T(8,128)(2,1)S(1)} %message.1), channel_id=1, source_target_pairs={{0,130},{1,97},{2,128},{3,99},{32,162},{33,65},{34,160},{35,67},{6... | collective-permute-start | bytes 811016 | tf_op jit(solution)/shard_map/ppermute | solution.py:35
  5.3 4.6 %collective-permute-done = bf16[264,512]{1,0:T(8,128)(2,1)S(1)} collective-permute-done((bf16[264,512]{1,0:T(8,128)(2,1)S(1)}, bf16[264,512]{1,0:T(8,128)(2,1)S(1)}, u32[]{:S(2)}, u32[]{:S(2)}) %collective-permute-start) | collective-permute-done | bytes 270368 | tf_op jit(solution)/shard_map/ppermute | solution.py:35
  9.8 2.8 %collective-permute-done.1 = bf16[264,512]{1,0:T(8,128)(2,1)S(1)} collective-permute-done((bf16[264,512]{1,0:T(8,128)(2,1)S(1)}, bf16[264,512]{1,0:T(8,128)(2,1)S(1)}, u32[]{:S(2)}, u32[]{:S(2)}) %collective-permute-start.1) | collective-permute-done | bytes 270368 | tf_op jit(solution)/shard_map/ppermute | solution.py:35
  12.8 1.7 %collective-permute-start.7 = (bf16[2,264,512]{2,1,0:T(8,128)(2,1)S(1)}, bf16[2,264,512]{2,1,0:T(8,128)(2,1)S(1)}, u32[]{:S(2)}, u32[]{:S(2)}) collective-permute-start(bf16[2,264,512]{2,1,0:T(8,128)(2,1)S(1)} %pad_maximum_fusion.1.refs_0_.own_low), channel_id=1, source_target_pairs={{0,32},{1,129},{2,34},{3,131},{32,0},{33,161},{34,2},{35,163},{64,... | collective-permute-start | bytes 1622024 | tf_op jit(solution)/shard_map/ppermute | solution.py:35
  14.5 2.2 %collective-permute-start.9 = (bf16[2,264,512]{2,1,0:T(8,128)(2,1)S(1)}, bf16[2,264,512]{2,1,0:T(8,128)(2,1)}, u32[]{:S(2)}, u32[]{:S(2)}) collective-permute-start(bf16[2,264,512]{2,1,0:T(8,128)(2,1)S(1)} %pad_maximum_fusion.1.refs_0_.own_low), channel_id=1, source_target_pairs={{0,96},{1,131},{2,98},{3,129},{32,64},{33,163},{34,66},{35,161},{6... | collective-permute-start | bytes 1622024 | tf_op jit(solution)/shard_map/ppermute | solution.py:35
  16.7 1.1 %collective-permute-start.4 = (bf16[2,264,512]{2,1,0:T(8,128)(2,1)S(1)}, bf16[2,264,512]{2,1,0:T(8,128)(2,1)S(1)}, u32[]{:S(2)}, u32[]{:S(2)}) collective-permute-start(bf16[2,264,512]{2,1,0:T(8,128)(2,1)S(1)} %pad_maximum_fusion.refs_2_.own_high), channel_id=1, source_target_pairs={{0,96},{1,131},{2,98},{3,129},{32,64},{33,163},{34,66},{35,161},{6... | collective-permute-start | bytes 1622024 | tf_op jit(solution)/shard_map/ppermute | solution.py:35
  17.8 4.5 %collective-permute-done.7.refs_0_ = bf16[2,264,512]{2,1,0:T(8,128)(2,1)S(1)} collective-permute-done((bf16[2,264,512]{2,1,0:T(8,128)(2,1)S(1)}, bf16[2,264,512]{2,1,0:T(8,128)(2,1)S(1)}, u32[]{:S(2)}, u32[]{:S(2)}) %collective-permute-start.7) | collective-permute-done | bytes 540704 | tf_op jit(solution)/shard_map/ppermute | solution.py:35
  22.3 2.9 %collective-permute-done.9.refs_2_ = bf16[2,264,512]{2,1,0:T(8,128)(2,1)} collective-permute-done((bf16[2,264,512]{2,1,0:T(8,128)(2,1)S(1)}, bf16[2,264,512]{2,1,0:T(8,128)(2,1)}, u32[]{:S(2)}, u32[]{:S(2)}) %collective-permute-start.9) | collective-permute-done | bytes 540704 | tf_op jit(solution)/shard_map/ppermute | solution.py:35
  25.2 5.7 %collective-permute-done.4.refs_2_ = bf16[2,264,512]{2,1,0:T(8,128)(2,1)S(1)} collective-permute-done((bf16[2,264,512]{2,1,0:T(8,128)(2,1)S(1)}, bf16[2,264,512]{2,1,0:T(8,128)(2,1)S(1)}, u32[]{:S(2)}, u32[]{:S(2)}) %collective-permute-start.4) | collective-permute-done | bytes 540704 | tf_op jit(solution)/shard_map/ppermute | solution.py:35
  30.9 0.5 collective-permute-start.3
  31.4 3.3 %load.1 = (bf16[4,512,1280]{2,1,0:T(8,128)(2,1)S(1)}, bf16[4,512,640]{2,1,0:T(8,128)(2,1)S(1)}) custom-call(bf16[4,512,640]{2,1,0:T(8,128)(2,1)} %bitcast.26, bf16[4,512,640]{2,1,0:T(8,128)(2,1)} %bitcast.27, bf16[4,512,640]{2,1,0:T(8,128)(2,1)} %bitcast.28), custom_call_target="tpu_custom_call" | custom-call | tf_op jit(solution)/shard_map/load/pallas_call | solution.py:127
  34.8 2.3 %collective-permute-start.13 = (bf16[2,264,512]{2,1,0:T(8,128)(2,1)S(1)}, bf16[2,264,512]{2,1,0:T(8,128)(2,1)S(1)}, u32[]{:S(2)}, u32[]{:S(2)}) collective-permute-start(bf16[2,264,512]{2,1,0:T(8,128)(2,1)S(1)} %collective-permute-done.7.refs_0_), channel_id=1, source_target_pairs={{0,96},{1,131},{2,98},{3,129},{32,64},{33,163},{34,66},{35,161},{6... | collective-permute-start | bytes 1622024 | tf_op jit(solution)/shard_map/ppermute | solution.py:35
  37.1 3.6 %shard_map.82 = (f32[3,8,128,640]{3,2,1,0:T(8,128)S(1)}, bf16[2,8,128,256]{3,2,1,0:T(8,128)(2,1)S(1)}) custom-call(bf16[2,264,512]{2,1,0:T(8,128)(2,1)S(1)} %pad_maximum_fusion.1.refs_0_.own_low, bf16[2,264,512]{2,1,0:T(8,128)(2,1)S(1)} %collective-permute-done.11.refs_1_.other_low, bf16[2,264,512]{2,1,0:T(8,128)(2,1)S(1)} %pad_maximum_fusion.refs_2_.own_high, ...), custom_call_target="tpu_custom_call" | custom-call | flops 2147483648 | bytes 1048576 | tf_op jit(solution)/shard_map/pallas_call | solution.py:206
  40.8 4.4 %shard_map.83 = (f32[3,8,128,640]{3,2,1,0:T(8,128)S(1)}, bf16[2,8,128,256]{3,2,1,0:T(8,128)(2,1)S(1)}) custom-call(bf16[2,264,512]{2,1,0:T(8,128)(2,1)S(1)} %collective-permute-done.7.refs_0_, bf16[2,264,512]{2,1,0:T(8,128)(2,1)} %collective-permute-done.8.refs_1_, ...), custom_call_target="tpu_custom_call", output_to_operand_aliasing={{0}: (6, {}), {1}: (7, {})} | custom-call | flops 2147483648 | bytes 1048576 | tf_op jit(solution)/shard_map/pallas_call | solution.py:206
  45.2 4.4 %shard_map.84 = (f32[3,8,128,640]{3,2,1,0:T(8,128)S(1)}, bf16[2,8,128,256]{3,2,1,0:T(8,128)(2,1)S(1)}) custom-call(bf16[2,264,512]{2,1,0:T(8,128)(2,1)} %collective-permute-done.2.refs_0_, bf16[2,264,512]{2,1,0:T(8,128)(2,1)} %collective-permute-done.3.refs_1_, ...), custom_call_target="tpu_custom_call", output_to_operand_aliasing={{0}: (6, {}), {1}: (7, {})} | custom-call | flops 2147483648 | bytes 1048576 | tf_op jit(solution)/shard_map/pallas_call | solution.py:206
  49.7 0.5 collective-permute-start.16
  50.2 2.0 %collective-permute-start.17 = (f32[8,128]{1,0:T(8,128)S(1)}, f32[8,128]{1,0:T(8,128)S(1)}, u32[]{:S(2)}, u32[]{:S(2)}) collective-permute-start(f32[8,128]{1,0:T(8,128)S(1)} %rows.1), channel_id=1, source_target_pairs={{0,4},{1,9},{4,8},{5,13},{8,12},{9,17},{12,16},{13,21},{16,20},{17... | collective-permute-start | bytes 12296 | tf_op jit(solution)/shard_map/ppermute | solution.py:55
  52.2 5.9 %collective-permute-start.18 = (f32[8,128]{1,0:T(8,128)S(1)}, f32[8,128]{1,0:T(8,128)S(1)}, u32[]{:S(2)}, u32[]{:S(2)}) collective-permute-start(f32[8,128]{1,0:T(8,128)S(1)} %rows.1), channel_id=1, source_target_pairs={{0,12},{1,17},{4,16},{5,21},{8,20},{9,25},{12,24},{13,29},{16,28},... | collective-permute-start | bytes 12296 | tf_op jit(solution)/shard_map/ppermute | solution.py:55
  58.0 1.6 %collective-permute-done.18 = f32[8,128]{1,0:T(8,128)S(1)} collective-permute-done((f32[8,128]{1,0:T(8,128)S(1)}, f32[8,128]{1,0:T(8,128)S(1)}, u32[]{:S(2)}, u32[]{:S(2)}) %collective-permute-start.18) | collective-permute-done | bytes 4128 | tf_op jit(solution)/shard_map/ppermute | solution.py:55
  59.8 3.4 %collective-permute-done.20.refs_8_ = f32[8,128]{1,0:T(8,128)S(1)} collective-permute-done((f32[8,128]{1,0:T(8,128)S(1)}, f32[8,128]{1,0:T(8,128)S(1)}, u32[]{:S(2)}, u32[]{:S(2)}) %collective-permute-start.20) | collective-permute-done | bytes 4128 | tf_op jit(solution)/shard_map/ppermute | solution.py:39
  63.3 1.5 %shard_map.85 = (f32[3,8,128,640]{3,2,1,0:T(8,128)S(1)}, bf16[2,8,128,256]{3,2,1,0:T(8,128)(2,1)S(1)}) custom-call(bf16[2,264,512]{2,1,0:T(8,128)(2,1)S(1)} %collective-permute-done.13.refs_0_, bf16[2,264,512]{2,1,0:T(8,128)(2,1)S(1)} %collective-permute-done.14.refs_1_, ...), custom_call_target="tpu_custom_call", output_to_operand_aliasing={{0}: (4, {}), {1}: (5, {})} | custom-call | flops 1073741824 | bytes 1048576 | tf_op jit(solution)/shard_map/pallas_call | solution.py:206
  64.9 6.0 %finish.1 = (f32[3,8,128,640]{3,2,1,0:T(8,128)S(1)}, bf16[2,8,128,256]{3,2,1,0:T(8,128)(2,1)S(1)}, f32[4,3,32,640]{3,2,1,0:T(8,128)S(1)}, bf16[4,3,32,640]{3,2,1,0:T(8,128)(2,1)S(1)}) custom-call(bf16[2,264,512]{2,1,0:T(8,128)(2,1)S(1)} %collective-permute-done.15.refs_0_, ...), custom_call_target="tpu_custom_call", output_to_operand_aliasing={{0}: (4, {}), {1}: (5, {})} | custom-call | flops 4294967296 | bytes 1048576 | tf_op jit(solution)/shard_map/finish/pallas_call | solution.py:227
  70.9 1.1 %collective-permute-start.22 = (bf16[4,3,32,640]{3,2,1,0:T(8,128)(2,1)S(1)}, bf16[4,3,32,640]{3,2,1,0:T(8,128)(2,1)S(1)}, u32[]{:S(2)}, u32[]{:S(2)}) collective-permute-start(bf16[4,3,32,640]{3,2,1,0:T(8,128)(2,1)S(1)} %get-tuple-element.36), channel_id=1, source_target_pairs={{0,4},{1,29},{4,0},{5,9},{8,12},{9,5},{12,8},{13,17},{16,20},{17,1... | collective-permute-start | bytes 1474568 | tf_op jit(solution)/shard_map/ppermute | solution.py:51
  72.1 7.8 %collective-permute-done.22 = bf16[4,3,32,640]{3,2,1,0:T(8,128)(2,1)S(1)} collective-permute-done((bf16[4,3,32,640]{3,2,1,0:T(8,128)(2,1)S(1)}, bf16[4,3,32,640]{3,2,1,0:T(8,128)(2,1)S(1)}, u32[]{:S(2)}, u32[]{:S(2)}) %collective-permute-start.22) | collective-permute-done | bytes 491552 | tf_op jit(solution)/shard_map/ppermute | solution.py:51
  80.0 5.5 %collective-permute-start.23 = (bf16[3,32,640]{2,1,0:T(8,128)(2,1)S(1)}, bf16[3,32,640]{2,1,0:T(8,128)(2,1)S(1)}, u32[]{:S(2)}, u32[]{:S(2)}) collective-permute-start(bf16[3,32,640]{2,1,0:T(8,128)(2,1)S(1)} %get-tuple-element.39), channel_id=1, source_target_pairs={{0,16},{4,20},{8,24},{12,28},{16,0},{20,4},{24,8},{28,12},{1,17},{... | collective-permute-start | bytes 368648 | tf_op jit(solution)/shard_map/ppermute | solution.py:61
  85.6 1.4 %collective-permute-start.24 = (bf16[3,32,640]{2,1,0:T(8,128)(2,1)S(1)}, bf16[3,32,640]{2,1,0:T(8,128)(2,1)S(1)}, u32[]{:S(2)}, u32[]{:S(2)}) collective-permute-start(bf16[3,32,640]{2,1,0:T(8,128)(2,1)S(1)} %get-tuple-element.41), channel_id=1, source_target_pairs={{0,8},{4,12},{8,16},{12,20},{16,24},{20,28},{24,0},{28,4},{1,9},{5... | collective-permute-start | bytes 368648 | tf_op jit(solution)/shard_map/ppermute | solution.py:61
  87.0 2.7 %collective-permute-start.25 = (bf16[3,32,640]{2,1,0:T(8,128)(2,1)S(1)}, bf16[3,32,640]{2,1,0:T(8,128)(2,1)S(1)}, u32[]{:S(2)}, u32[]{:S(2)}) collective-permute-start(bf16[3,32,640]{2,1,0:T(8,128)(2,1)S(1)} %get-tuple-element.40), channel_id=1, source_target_pairs={{0,24},{4,28},{8,0},{12,4},{16,8},{20,12},{24,16},{28,20},{1,25},{... | collective-permute-start | bytes 368648 | tf_op jit(solution)/shard_map/ppermute | solution.py:61
  89.7 3.2 %collective-permute-done.23 = bf16[3,32,640]{2,1,0:T(8,128)(2,1)S(1)} collective-permute-done((bf16[3,32,640]{2,1,0:T(8,128)(2,1)S(1)}, bf16[3,32,640]{2,1,0:T(8,128)(2,1)S(1)}, u32[]{:S(2)}, u32[]{:S(2)}) %collective-permute-start.23) | collective-permute-done | bytes 122912 | tf_op jit(solution)/shard_map/ppermute | solution.py:61
  92.9 4.4 %collective-permute-done.24 = bf16[3,32,640]{2,1,0:T(8,128)(2,1)S(1)} collective-permute-done((bf16[3,32,640]{2,1,0:T(8,128)(2,1)S(1)}, bf16[3,32,640]{2,1,0:T(8,128)(2,1)S(1)}, u32[]{:S(2)}, u32[]{:S(2)}) %collective-permute-start.24) | collective-permute-done | bytes 122912 | tf_op jit(solution)/shard_map/ppermute | solution.py:61
  97.3 0.8 fusion.3
  (36 shorter events, 0.8 us)
Async XLA Ops:
  1.7 8.2 %collective-permute-start = (bf16[264,512]{1,0:T(8,128)(2,1)S(1)}, bf16[264,512]{1,0:T(8,128)(2,1)S(1)}, u32[]{:S(2)}, u32[]{:S(2)}) collective-permute-start(bf16[264,512]{1,0:T(8,128)(2,1)S(1)} %message.1), channel_id=1, source_target_pairs={{0,2},{1,65},{2,0},{3,67},{32,34},{33,97},{34,32},{35,99},{64,66},... | collective-permute-start | bytes 811016 | tf_op jit(solution)/shard_map/ppermute | solution.py:35
  3.2 9.5 %collective-permute-start.1 = (bf16[264,512]{1,0:T(8,128)(2,1)S(1)}, bf16[264,512]{1,0:T(8,128)(2,1)S(1)}, u32[]{:S(2)}, u32[]{:S(2)}) collective-permute-start(bf16[264,512]{1,0:T(8,128)(2,1)S(1)} %message.1), channel_id=1, source_target_pairs={{0,130},{1,97},{2,128},{3,99},{32,162},{33,65},{34,160},{35,67},{6... | collective-permute-start | bytes 811016 | tf_op jit(solution)/shard_map/ppermute | solution.py:35
  5.3 7.5 %collective-permute-start.6 = (bf16[264,512]{1,0:T(8,128)(2,1)S(1)}, bf16[264,512]{1,0:T(8,128)(2,1)S(1)}, u32[]{:S(2)}, u32[]{:S(2)}) collective-permute-start(bf16[264,512]{1,0:T(8,128)(2,1)S(1)} %message.1), channel_id=1, source_target_pairs={{0,128},{1,33},{2,130},{3,35},{32,160},{33,1},{34,162},{35,3},{64,... | collective-permute-start | bytes 811016 | tf_op jit(solution)/shard_map/ppermute | solution.py:35
  12.7 5.1 %collective-permute-start.12 = (bf16[2,264,512]{2,1,0:T(8,128)(2,1)S(1)}, bf16[2,264,512]{2,1,0:T(8,128)(2,1)S(1)}, u32[]{:S(2)}, u32[]{:S(2)}) collective-permute-start(bf16[2,264,512]{2,1,0:T(8,128)(2,1)S(1)} %pad_maximum_fusion.refs_2_.own_high), channel_id=1, source_target_pairs={{0,1},{1,0},{2,3},{3,2},{4,5},{5,4},{6,7},{7,6},{8,9},{9,8},{10,11... | collective-permute-start | bytes 1622024 | tf_op jit(solution)/shard_map/ppermute | solution.py:43
  12.8 9.4 %collective-permute-start.7 = (bf16[2,264,512]{2,1,0:T(8,128)(2,1)S(1)}, bf16[2,264,512]{2,1,0:T(8,128)(2,1)S(1)}, u32[]{:S(2)}, u32[]{:S(2)}) collective-permute-start(bf16[2,264,512]{2,1,0:T(8,128)(2,1)S(1)} %pad_maximum_fusion.1.refs_0_.own_low), channel_id=1, source_target_pairs={{0,32},{1,129},{2,34},{3,131},{32,0},{33,161},{34,2},{35,163},{64,... | collective-permute-start | bytes 1622024 | tf_op jit(solution)/shard_map/ppermute | solution.py:35
  14.5 10.7 %collective-permute-start.9 = (bf16[2,264,512]{2,1,0:T(8,128)(2,1)S(1)}, bf16[2,264,512]{2,1,0:T(8,128)(2,1)}, u32[]{:S(2)}, u32[]{:S(2)}) collective-permute-start(bf16[2,264,512]{2,1,0:T(8,128)(2,1)S(1)} %pad_maximum_fusion.1.refs_0_.own_low), channel_id=1, source_target_pairs={{0,96},{1,131},{2,98},{3,129},{32,64},{33,163},{34,66},{35,161},{6... | collective-permute-start | bytes 1622024 | tf_op jit(solution)/shard_map/ppermute | solution.py:35
  16.7 14.2 %collective-permute-start.4 = (bf16[2,264,512]{2,1,0:T(8,128)(2,1)S(1)}, bf16[2,264,512]{2,1,0:T(8,128)(2,1)S(1)}, u32[]{:S(2)}, u32[]{:S(2)}) collective-permute-start(bf16[2,264,512]{2,1,0:T(8,128)(2,1)S(1)} %pad_maximum_fusion.refs_2_.own_high), channel_id=1, source_target_pairs={{0,96},{1,131},{2,98},{3,129},{32,64},{33,163},{34,66},{35,161},{6... | collective-permute-start | bytes 1622024 | tf_op jit(solution)/shard_map/ppermute | solution.py:35
  17.7 13.1 %collective-permute-start.2 = (bf16[2,264,512]{2,1,0:T(8,128)(2,1)S(1)}, bf16[2,264,512]{2,1,0:T(8,128)(2,1)}, u32[]{:S(2)}, u32[]{:S(2)}) collective-permute-start(bf16[2,264,512]{2,1,0:T(8,128)(2,1)S(1)} %pad_maximum_fusion.refs_2_.own_high), channel_id=1, source_target_pairs={{0,32},{1,129},{2,34},{3,131},{32,0},{33,161},{34,2},{35,163},{64,... | collective-permute-start | bytes 1622024 | tf_op jit(solution)/shard_map/ppermute | solution.py:35
  17.7 17.0 %collective-permute-start.11 = (bf16[2,264,512]{2,1,0:T(8,128)(2,1)S(1)}, bf16[2,264,512]{2,1,0:T(8,128)(2,1)S(1)}, u32[]{:S(2)}, u32[]{:S(2)}) collective-permute-start(bf16[2,264,512]{2,1,0:T(8,128)(2,1)S(1)} %pad_maximum_fusion.1.refs_0_.own_low), channel_id=1, source_target_pairs={{0,1},{1,0},{2,3},{3,2},{4,5},{5,4},{6,7},{7,6},{8,9},{9,8},{10,11... | collective-permute-start | bytes 1622024 | tf_op jit(solution)/shard_map/ppermute | solution.py:43
  22.3 12.6 %collective-permute-start.8 = (bf16[2,264,512]{2,1,0:T(8,128)(2,1)S(1)}, bf16[2,264,512]{2,1,0:T(8,128)(2,1)}, u32[]{:S(2)}, u32[]{:S(2)}) collective-permute-start(bf16[2,264,512]{2,1,0:T(8,128)(2,1)S(1)} %collective-permute-done.7.refs_0_), channel_id=1, source_target_pairs={{0,1},{1,0},{2,3},{3,2},{4,5},{5,4},{6,7},{7,6},{8,9},{9,8},{10,11... | collective-permute-start | bytes 1622024 | tf_op jit(solution)/shard_map/ppermute | solution.py:43
  25.2 15.6 %collective-permute-start.10 = (bf16[2,264,512]{2,1,0:T(8,128)(2,1)}, bf16[2,264,512]{2,1,0:T(8,128)(2,1)}, u32[]{:S(2)}, u32[]{:S(2)}) collective-permute-start(bf16[2,264,512]{2,1,0:T(8,128)(2,1)} %collective-permute-done.9.refs_2_), channel_id=1, source_target_pairs={{0,1},{1,0},{2,3},{3,2},{4,5},{5,4},{6,7},{7,6},{8,9},{9,8},{10,11... | collective-permute-start | bytes 1622024 | tf_op jit(solution)/shard_map/ppermute | solution.py:43
  30.9 14.3 %collective-permute-start.5 = (bf16[2,264,512]{2,1,0:T(8,128)(2,1)S(1)}, bf16[2,264,512]{2,1,0:T(8,128)(2,1)}, u32[]{:S(2)}, u32[]{:S(2)}) collective-permute-start(bf16[2,264,512]{2,1,0:T(8,128)(2,1)S(1)} %collective-permute-done.4.refs_2_), channel_id=1, source_target_pairs={{0,1},{1,0},{2,3},{3,2},{4,5},{5,4},{6,7},{7,6},{8,9},{9,8},{10,11... | collective-permute-start | bytes 1622024 | tf_op jit(solution)/shard_map/ppermute | solution.py:43
  30.9 14.3 %collective-permute-start.3 = (bf16[2,264,512]{2,1,0:T(8,128)(2,1)}, bf16[2,264,512]{2,1,0:T(8,128)(2,1)}, u32[]{:S(2)}, u32[]{:S(2)}) collective-permute-start(bf16[2,264,512]{2,1,0:T(8,128)(2,1)} %collective-permute-done.2.refs_0_), channel_id=1, source_target_pairs={{0,1},{1,0},{2,3},{3,2},{4,5},{5,4},{6,7},{7,6},{8,9},{9,8},{10,11... | collective-permute-start | bytes 1622024 | tf_op jit(solution)/shard_map/ppermute | solution.py:43
  34.7 14.8 %collective-permute-start.14 = (bf16[2,264,512]{2,1,0:T(8,128)(2,1)S(1)}, bf16[2,264,512]{2,1,0:T(8,128)(2,1)S(1)}, u32[]{:S(2)}, u32[]{:S(2)}) collective-permute-start(bf16[2,264,512]{2,1,0:T(8,128)(2,1)S(1)} %collective-permute-done.4.refs_2_), channel_id=1, source_target_pairs={{0,32},{1,129},{2,34},{3,131},{32,0},{33,161},{34,2},{35,163},{64,... | collective-permute-start | bytes 1622024 | tf_op jit(solution)/shard_map/ppermute | solution.py:35
  34.8 14.7 %collective-permute-start.13 = (bf16[2,264,512]{2,1,0:T(8,128)(2,1)S(1)}, bf16[2,264,512]{2,1,0:T(8,128)(2,1)S(1)}, u32[]{:S(2)}, u32[]{:S(2)}) collective-permute-start(bf16[2,264,512]{2,1,0:T(8,128)(2,1)S(1)} %collective-permute-done.7.refs_0_), channel_id=1, source_target_pairs={{0,96},{1,131},{2,98},{3,129},{32,64},{33,163},{34,66},{35,161},{6... | collective-permute-start | bytes 1622024 | tf_op jit(solution)/shard_map/ppermute | solution.py:35
  49.6 15.3 %collective-permute-start.15 = (bf16[2,264,512]{2,1,0:T(8,128)(2,1)S(1)}, bf16[2,264,512]{2,1,0:T(8,128)(2,1)S(1)}, u32[]{:S(2)}, u32[]{:S(2)}) collective-permute-start(bf16[2,264,512]{2,1,0:T(8,128)(2,1)S(1)} %collective-permute-done.13.refs_0_), channel_id=1, source_target_pairs={{0,1},{1,0},{2,3},{3,2},{4,5},{5,4},{6,7},{7,6},{8,9},{9,8},{10,11... | collective-permute-start | bytes 1622024 | tf_op jit(solution)/shard_map/ppermute | solution.py:43
  49.7 15.2 %collective-permute-start.16 = (bf16[2,264,512]{2,1,0:T(8,128)(2,1)S(1)}, bf16[2,264,512]{2,1,0:T(8,128)(2,1)S(1)}, u32[]{:S(2)}, u32[]{:S(2)}) collective-permute-start(bf16[2,264,512]{2,1,0:T(8,128)(2,1)S(1)} %collective-permute-done.14.refs_1_), channel_id=1, source_target_pairs={{0,1},{1,0},{2,3},{3,2},{4,5},{5,4},{6,7},{7,6},{8,9},{9,8},{10,11... | collective-permute-start | bytes 1622024 | tf_op jit(solution)/shard_map/ppermute | solution.py:43
  50.2 7.8 %collective-permute-start.17 = (f32[8,128]{1,0:T(8,128)S(1)}, f32[8,128]{1,0:T(8,128)S(1)}, u32[]{:S(2)}, u32[]{:S(2)}) collective-permute-start(f32[8,128]{1,0:T(8,128)S(1)} %rows.1), channel_id=1, source_target_pairs={{0,4},{1,9},{4,8},{5,13},{8,12},{9,17},{12,16},{13,21},{16,20},{17... | collective-permute-start | bytes 12296 | tf_op jit(solution)/shard_map/ppermute | solution.py:55
  52.2 7.5 %collective-permute-start.18 = (f32[8,128]{1,0:T(8,128)S(1)}, f32[8,128]{1,0:T(8,128)S(1)}, u32[]{:S(2)}, u32[]{:S(2)}) collective-permute-start(f32[8,128]{1,0:T(8,128)S(1)} %rows.1), channel_id=1, source_target_pairs={{0,12},{1,17},{4,16},{5,21},{8,20},{9,25},{12,24},{13,29},{16,28},... | collective-permute-start | bytes 12296 | tf_op jit(solution)/shard_map/ppermute | solution.py:55
  59.7 3.6 %collective-permute-start.20 = (f32[8,128]{1,0:T(8,128)S(1)}, f32[8,128]{1,0:T(8,128)S(1)}, u32[]{:S(2)}, u32[]{:S(2)}) collective-permute-start(f32[8,128]{1,0:T(8,128)S(1)} %select_add_fusion.refs_6_), channel_id=1, source_target_pairs={{0,128},{128,0},{1,129},{129,1},{2,130},{130,2},{3,131},{131,3},{4... | collective-permute-start | bytes 12296 | tf_op jit(solution)/shard_map/ppermute | solution.py:39
  59.7 5.1 %collective-permute-start.19 = (f32[8,128]{1,0:T(8,128)S(1)}, f32[8,128]{1,0:T(8,128)S(1)}, u32[]{:S(2)}, u32[]{:S(2)}) collective-permute-start(f32[8,128]{1,0:T(8,128)S(1)} %select_add_fusion.refs_6_), channel_id=1, source_target_pairs={{0,1},{1,0},{2,3},{3,2},{4,5},{5,4},{6,7},{7,6},{8,9},{9,8},{10,11... | collective-permute-start | bytes 12296 | tf_op jit(solution)/shard_map/ppermute | solution.py:43
  63.3 1.5 %collective-permute-start.21 = (f32[8,128]{1,0:T(8,128)S(1)}, f32[8,128]{1,0:T(8,128)S(1)}, u32[]{:S(2)}, u32[]{:S(2)}) collective-permute-start(f32[8,128]{1,0:T(8,128)S(1)} %collective-permute-done.20.refs_8_), channel_id=1, source_target_pairs={{0,1},{1,0},{2,3},{3,2},{4,5},{5,4},{6,7},{7,6},{8,9},{9,8},{10,11... | collective-permute-start | bytes 12296 | tf_op jit(solution)/shard_map/ppermute | solution.py:43
  70.9 8.9 %collective-permute-start.22 = (bf16[4,3,32,640]{3,2,1,0:T(8,128)(2,1)S(1)}, bf16[4,3,32,640]{3,2,1,0:T(8,128)(2,1)S(1)}, u32[]{:S(2)}, u32[]{:S(2)}) collective-permute-start(bf16[4,3,32,640]{3,2,1,0:T(8,128)(2,1)S(1)} %get-tuple-element.36), channel_id=1, source_target_pairs={{0,4},{1,29},{4,0},{5,9},{8,12},{9,5},{12,8},{13,17},{16,20},{17,1... | collective-permute-start | bytes 1474568 | tf_op jit(solution)/shard_map/ppermute | solution.py:51
  80.0 12.9 %collective-permute-start.23 = (bf16[3,32,640]{2,1,0:T(8,128)(2,1)S(1)}, bf16[3,32,640]{2,1,0:T(8,128)(2,1)S(1)}, u32[]{:S(2)}, u32[]{:S(2)}) collective-permute-start(bf16[3,32,640]{2,1,0:T(8,128)(2,1)S(1)} %get-tuple-element.39), channel_id=1, source_target_pairs={{0,16},{4,20},{8,24},{12,28},{16,0},{20,4},{24,8},{28,12},{1,17},{... | collective-permute-start | bytes 368648 | tf_op jit(solution)/shard_map/ppermute | solution.py:61
  85.6 11.8 %collective-permute-start.24 = (bf16[3,32,640]{2,1,0:T(8,128)(2,1)S(1)}, bf16[3,32,640]{2,1,0:T(8,128)(2,1)S(1)}, u32[]{:S(2)}, u32[]{:S(2)}) collective-permute-start(bf16[3,32,640]{2,1,0:T(8,128)(2,1)S(1)} %get-tuple-element.41), channel_id=1, source_target_pairs={{0,8},{4,12},{8,16},{12,20},{16,24},{20,28},{24,0},{28,4},{1,9},{5... | collective-permute-start | bytes 368648 | tf_op jit(solution)/shard_map/ppermute | solution.py:61
  87.0 10.3 %collective-permute-start.25 = (bf16[3,32,640]{2,1,0:T(8,128)(2,1)S(1)}, bf16[3,32,640]{2,1,0:T(8,128)(2,1)S(1)}, u32[]{:S(2)}, u32[]{:S(2)}) collective-permute-start(bf16[3,32,640]{2,1,0:T(8,128)(2,1)S(1)} %get-tuple-element.40), channel_id=1, source_target_pairs={{0,24},{4,28},{8,0},{12,4},{16,8},{20,12},{24,16},{28,20},{1,25},{... | collective-permute-start | bytes 368648 | tf_op jit(solution)/shard_map/ppermute | solution.py:61

commit v5 on v3

--- a/solution.py
+++ b/solution.py
@@ -49,6 +49,12 @@
 
 def z_pair(block):
     return lax.ppermute(block, ("z", "c"), [(z * 2 + c, partner_of(z, c) * 2 + c) for z in range(8) for c in range(2)])
+
+
+def z_shift(block, step):
+    return lax.ppermute(
+        block, ("z", "c"), [(z * 2 + c, (z + step + c) % 8 * 2 + c) for z in range(8) for c in range(2)]
+    )
 
 
 def z_step(block, step):
@@ -152,6 +158,25 @@
     )(own, other)
 
 
+def part_kernel(rows, near, far, out):
+    c = lax.axis_index("c").astype(I32)
+    lane = lax.broadcasted_iota(I32, (8, 128), 1)
+    total = jnp.where((lane == 0) & (c == 0), rows[...], 0.0)
+    total = jnp.where(lane == 1 + c, near[...], total)
+    out[...] = jnp.where(lane == 3 + c, far[...], total)
+
+
+def part_of_line(*rows):
+    return pl.pallas_call(
+        part_kernel,
+        out_shape=jax.ShapeDtypeStruct((8, 128), F32),
+        in_specs=[VMEM] * 3,
+        out_specs=VMEM,
+        compiler_params=PARAMS,
+        name="part",
+    )(*rows)
+
+
 def first_kernel(own, other, w_in, w_out, acc, cols):
     acc[...] = jnp.zeros_like(acc)
     gather_kernel(0, ((0, own), (1, other)), w_in, w_out, acc, cols)
@@ -166,9 +191,10 @@
     gather_kernel(2, ((0, (low, high)),), w_in, w_out, acc, cols)
 
 
-def final_kernel(low, high, w_in, w_out, _, __, own_terms, other_terms, acc, cols, *rest):
+def final_kernel(low, high, w_in, w_out, _, __, *refs):
+    terms, (acc, cols, *rest) = refs[:4], refs[4:]
     gather_kernel(2, ((1, (low, high)),), w_in, w_out, acc, cols)
-    last_kernel((own_terms, other_terms), acc, cols, *rest)
+    last_kernel(terms, acc, cols, *rest)
 
 
 def gather_kernel(m, blocks, w_in, w_out, acc, cols):
@@ -238,7 +264,7 @@
         final_kernel,
         out_shape=STATE
         + (jax.ShapeDtypeStruct((4, 3, 32, 640), F32), jax.ShapeDtypeStruct((4, 3, 32, 640), BF16)),
-        in_specs=[VMEM] * 8,
+        in_specs=[VMEM] * 10,
         out_specs=(VMEM,) * 4,
         input_output_aliases={4: 0, 5: 1},
         scratch_shapes=[
@@ -263,9 +289,9 @@
         dy, ex = p >> 1, p & 1
         number = ((xl ^ ex) * 4 + (y ^ dy)) * 8 + z
         w = F32(0.0)
-        for worker, term in zip(workers, terms):
+        for i, worker in enumerate(workers):
             mine = known & (((number - lane) & 63) == worker)
-            w = w + jnp.sum(jnp.where(mine, term[...], 0.0))
+            w = w + jnp.sum(jnp.where(mine, terms[2 * i][...] + terms[2 * i + 1][...], 0.0))
         for r in range(0, 128, 32):
             rows = pl.ds(r, 32)
             u = acc[0, p, rows]
@@ -310,12 +336,15 @@
     for k in (1, 3):
         near[k] = across(row, k, False)
     swap = sibling(row)
-    planes = [line_rows(row, swap)]
-    for j in (1, 2, 3, 4):
-        planes.append(z_step(planes[0], j))
-    lane = lax.broadcasted_iota(I32, (8, 128), 1)
-    terms = sum(jnp.where(lane == j, plane, 0.0) for j, plane in enumerate(planes))
-    terms = (terms, swapped(terms, "xl", 2, 1))
+    rows = line_rows(row, swap)
+    got = []
+    for j in (1, 3):
+        got.append(z_shift(rows, j))
+    partial = part_of_line(rows, *got)
+    partials = [partial, swapped(partial, "xl", 2, 1)]
+    terms = []
+    for part in partials:
+        terms += [part, sibling(part)]
     low = across(near[1][:2], 3, False)
     high = across(near[3][2:], 1, False)
     other = {}

time: 102 us -> 99.4 us (0.975)
  the two profiles are of different devices: /device:TPU:6 before, /device:TPU:1 now
where the time goes in v5:
time: 99.4 us; the launch traced here: 99.3 us
  starting transfers between devices  39 us (39%)
  waiting for transfers between devices  36.7 us (37%)
  Pallas kernels  21.6 us (22%)
  other arithmetic  1.03 us (1%)
    ppermute x7, waiting for transfers between devices, across(): return lax.ppermute(block, PLANE, route)  18.8 us
    ppermute x7, starting transfers between devices, sibling(): return lax.ppermute(block, 'c', [(0, 1), (1, 0)])  11.7 us
    pallas_call x4, Pallas kernels, gathered(): pl.pallas_call(kernels.get(m, lambda *refs: middle_kernel(m, *refs)), out...  11.3 us
    ppermute x3, starting transfers between devices, z_step(): return lax.ppermute(block, 'z', [(z, (z + step) % 8) for z in range(8)])  8.84 us
    ppermute x2, starting transfers between devices, z_shift(): lax.ppermute(block, ('z', 'c'), [(z * 2 + c, (z + step + c) % 8 * 2 + c)...  8.36 us
    ppermute x7, starting transfers between devices, across(): return lax.ppermute(block, PLANE, route)  8.25 us
    ppermute x3, waiting for transfers between devices, z_step(): return lax.ppermute(block, 'z', [(z, (z + step) % 8) for z in range(8)])  7.55 us
    ppermute x1, waiting for transfers between devices, z_pair(): lax.ppermute(block, ('z', 'c'), [(z * 2 + c, partner_of(z, c) * 2 + c) fo...  7.24 us
  transfers between devices with their start and end apart: 21, of which 9 were waited for; matrix products, arithmetic and copies ran while one was open for 0% of the time, Pallas kernels for 15%

profile of v5, /device:TPU:1, one launch (start us, length us, event | category | flops | bytes accessed | tf_op | source)
XLA Modules:
  0.0 99.3 jit_solution(8017117773451504524)
XLA Ops:
  0.7 1.0 %message.1 = bf16[264,512]{1,0:T(8,128)(2,1)S(1)} custom-call(f32[1]{0:T(128)S(6)} %copy.25.decode, f32[1,5]{1,0:T(1,128)} %code_in.1, s32[4]{0:T(128)} %stragglers_in.1, bf16[128,512]{1,0:T(8,128)(2,1)} %tokens.1, bf16[128,512]{1,0:T(8,128)(2,1)} %grad_out.1), custom_call_target="tpu_custom_call" | custom-call | tf_op jit(solution)/shard_map/message/pallas_call | solution.py:103
  1.7 2.2 %collective-permute-start = (bf16[264,512]{1,0:T(8,128)(2,1)S(1)}, bf16[264,512]{1,0:T(8,128)(2,1)S(1)}, u32[]{:S(2)}, u32[]{:S(2)}) collective-permute-start(bf16[264,512]{1,0:T(8,128)(2,1)S(1)} %message.1), channel_id=1, source_target_pairs={{0,128},{1,33},{2,130},{3,35},{32,160},{33,1},{34,162},{35,3},{64,... | collective-permute-start | bytes 811016 | tf_op jit(solution)/shard_map/ppermute | solution.py:35
  3.9 2.6 %collective-permute-start.1 = (bf16[264,512]{1,0:T(8,128)(2,1)S(1)}, bf16[264,512]{1,0:T(8,128)(2,1)S(1)}, u32[]{:S(2)}, u32[]{:S(2)}) collective-permute-start(bf16[264,512]{1,0:T(8,128)(2,1)S(1)} %message.1), channel_id=1, source_target_pairs={{0,2},{1,65},{2,0},{3,67},{32,34},{33,97},{34,32},{35,99},{64,66},... | collective-permute-start | bytes 811016 | tf_op jit(solution)/shard_map/ppermute | solution.py:35
  6.5 1.2 %collective-permute-done = bf16[264,512]{1,0:T(8,128)(2,1)S(1)} collective-permute-done((bf16[264,512]{1,0:T(8,128)(2,1)S(1)}, bf16[264,512]{1,0:T(8,128)(2,1)S(1)}, u32[]{:S(2)}, u32[]{:S(2)}) %collective-permute-start) | collective-permute-done | bytes 270368 | tf_op jit(solution)/shard_map/ppermute | solution.py:35
  7.7 5.8 %collective-permute-done.1 = bf16[264,512]{1,0:T(8,128)(2,1)S(1)} collective-permute-done((bf16[264,512]{1,0:T(8,128)(2,1)S(1)}, bf16[264,512]{1,0:T(8,128)(2,1)S(1)}, u32[]{:S(2)}, u32[]{:S(2)}) %collective-permute-start.1) | collective-permute-done | bytes 270368 | tf_op jit(solution)/shard_map/ppermute | solution.py:35
  13.6 2.6 %collective-permute-done.2 = bf16[264,512]{1,0:T(8,128)(2,1)S(1)} collective-permute-done((bf16[264,512]{1,0:T(8,128)(2,1)S(1)}, bf16[264,512]{1,0:T(8,128)(2,1)S(1)}, u32[]{:S(2)}, u32[]{:S(2)}) %collective-permute-start.2) | collective-permute-done | bytes 270368 | tf_op jit(solution)/shard_map/ppermute | solution.py:35
  16.3 1.0 %collective-permute-start.5 = (bf16[4,264,512]{2,1,0:T(8,128)(2,1)S(1)}, bf16[4,264,512]{2,1,0:T(8,128)(2,1)S(1)}, u32[]{:S(2)}, u32[]{:S(2)}) collective-permute-start(bf16[4,264,512]{2,1,0:T(8,128)(2,1)S(1)} %pad_maximum_fusion.own), channel_id=1, source_target_pairs={{0,32},{1,129},{2,34},{3,131},{32,0},{33,161},{34,2},{35,163},{64,... | collective-permute-start | bytes 3244040 | tf_op jit(solution)/shard_map/ppermute | solution.py:35
  17.3 1.8 %collective-permute-start.3 = (bf16[4,264,512]{2,1,0:T(8,128)(2,1)S(1)}, bf16[4,264,512]{2,1,0:T(8,128)(2,1)S(1)}, u32[]{:S(2)}, u32[]{:S(2)}) collective-permute-start(bf16[4,264,512]{2,1,0:T(8,128)(2,1)S(1)} %pad_maximum_fusion.own), channel_id=1, source_target_pairs={{0,96},{1,131},{2,98},{3,129},{32,64},{33,163},{34,66},{35,161},{6... | collective-permute-start | bytes 3244040 | tf_op jit(solution)/shard_map/ppermute | solution.py:35
  19.2 2.5 %collective-permute-start.7 = (bf16[4,264,512]{2,1,0:T(8,128)(2,1)S(1)}, bf16[4,264,512]{2,1,0:T(8,128)(2,1)S(1)}, u32[]{:S(2)}, u32[]{:S(2)}) collective-permute-start(bf16[4,264,512]{2,1,0:T(8,128)(2,1)S(1)} %pad_maximum_fusion.own), channel_id=1, source_target_pairs={{0,1},{1,0},{2,3},{3,2},{4,5},{5,4},{6,7},{7,6},{8,9},{9,8},{10,11... | collective-permute-start | bytes 3244040 | tf_op jit(solution)/shard_map/ppermute | solution.py:43
  21.7 9.0 %collective-permute-done.5.refs_0_ = bf16[4,264,512]{2,1,0:T(8,128)(2,1)S(1)} collective-permute-done((bf16[4,264,512]{2,1,0:T(8,128)(2,1)S(1)}, bf16[4,264,512]{2,1,0:T(8,128)(2,1)S(1)}, u32[]{:S(2)}, u32[]{:S(2)}) %collective-permute-start.5) | collective-permute-done | bytes 1081376 | tf_op jit(solution)/shard_map/ppermute | solution.py:35
  30.7 2.3 %collective-permute-start.6 = (bf16[4,264,512]{2,1,0:T(8,128)(2,1)S(1)}, bf16[4,264,512]{2,1,0:T(8,128)(2,1)S(1)}, u32[]{:S(2)}, u32[]{:S(2)}) collective-permute-start(bf16[4,264,512]{2,1,0:T(8,128)(2,1)S(1)} %collective-permute-done.5.refs_0_), channel_id=1, source_target_pairs={{0,1},{1,0},{2,3},{3,2},{4,5},{5,4},{6,7},{7,6},{8,9},{9,8},{10,11... | collective-permute-start | bytes 3244040 | tf_op jit(solution)/shard_map/ppermute | solution.py:43
  33.1 2.8 %collective-permute-start.4 = (bf16[4,264,512]{2,1,0:T(8,128)(2,1)S(1)}, bf16[4,264,512]{2,1,0:T(8,128)(2,1)S(1)}, u32[]{:S(2)}, u32[]{:S(2)}) collective-permute-start(bf16[4,264,512]{2,1,0:T(8,128)(2,1)S(1)} %collective-permute-done.3.refs_0_), channel_id=1, source_target_pairs={{0,1},{1,0},{2,3},{3,2},{4,5},{5,4},{6,7},{7,6},{8,9},{9,8},{10,11... | collective-permute-start | bytes 3244040 | tf_op jit(solution)/shard_map/ppermute | solution.py:43
  35.9 3.3 %load.1 = (bf16[4,512,1280]{2,1,0:T(8,128)(2,1)S(1)}, bf16[4,512,640]{2,1,0:T(8,128)(2,1)S(1)}) custom-call(bf16[4,512,640]{2,1,0:T(8,128)(2,1)} %bitcast.26, bf16[4,512,640]{2,1,0:T(8,128)(2,1)} %bitcast.27, bf16[4,512,640]{2,1,0:T(8,128)(2,1)} %bitcast.28), custom_call_target="tpu_custom_call" | custom-call | tf_op jit(solution)/shard_map/load/pallas_call | solution.py:127
  39.3 0.5 collective-permute-start.8
  39.9 3.6 %shard_map.82 = (f32[3,8,128,640]{3,2,1,0:T(8,128)S(1)}, bf16[2,8,128,256]{3,2,1,0:T(8,128)(2,1)S(1)}) custom-call(bf16[4,264,512]{2,1,0:T(8,128)(2,1)S(1)} %pad_maximum_fusion.own, bf16[4,264,512]{2,1,0:T(8,128)(2,1)S(1)} %collective-permute-done.7.other, bf16[4,512,1280]{2,1,0:T(8,128)(2,1)S(1)} %get-tuple-element.21.w_in.refs_2_, ...), custom_call_target="tpu_custom_call" | custom-call | flops 2147483648 | bytes 1048576 | tf_op jit(solution)/shard_map/pallas_call | solution.py:251
  43.5 3.1 %shard_map.83 = (f32[3,8,128,640]{3,2,1,0:T(8,128)S(1)}, bf16[2,8,128,256]{3,2,1,0:T(8,128)(2,1)S(1)}) custom-call(bf16[4,264,512]{2,1,0:T(8,128)(2,1)S(1)} %collective-permute-done.5.refs_0_, bf16[4,264,512]{2,1,0:T(8,128)(2,1)S(1)} %collective-permute-done.6.refs_1_, ...), custom_call_target="tpu_custom_call", output_to_operand_aliasing={{0}: (4, {}), {1}: (5, {})} | custom-call | flops 2147483648 | bytes 1048576 | tf_op jit(solution)/shard_map/pallas_call | solution.py:251
  46.7 3.1 %shard_map.84 = (f32[3,8,128,640]{3,2,1,0:T(8,128)S(1)}, bf16[2,8,128,256]{3,2,1,0:T(8,128)(2,1)S(1)}) custom-call(bf16[4,264,512]{2,1,0:T(8,128)(2,1)S(1)} %collective-permute-done.3.refs_0_, bf16[4,264,512]{2,1,0:T(8,128)(2,1)S(1)} %collective-permute-done.4.refs_1_, ...), custom_call_target="tpu_custom_call", output_to_operand_aliasing={{0}: (4, {}), {1}: (5, {})} | custom-call | flops 2147483648 | bytes 1048576 | tf_op jit(solution)/shard_map/pallas_call | solution.py:251
  49.8 1.8 %collective-permute-start.10 = (bf16[2,264,512]{2,1,0:T(8,128)(2,1)S(1)}, bf16[2,264,512]{2,1,0:T(8,128)(2,1)S(1)}, u32[]{:S(2)}, u32[]{:S(2)}) collective-permute-start(bf16[2,264,512]{2,1,0:T(8,128)(2,1)S(1)} %collective-permute-done.8.low), channel_id=1, source_target_pairs={{0,1},{1,0},{2,3},{3,2},{4,5},{5,4},{6,7},{7,6},{8,9},{9,8},{10,11... | collective-permute-start | bytes 1622024 | tf_op jit(solution)/shard_map/ppermute | solution.py:43
  51.8 3.3 %collective-permute-start.12 = (f32[8,128]{1,0:T(8,128)S(1)}, f32[8,128]{1,0:T(8,128)S(1)}, u32[]{:S(2)}, u32[]{:S(2)}) collective-permute-start(f32[8,128]{1,0:T(8,128)S(1)} %rows.1), channel_id=1, source_target_pairs={{0,4},{1,9},{4,8},{5,13},{8,12},{9,17},{12,16},{13,21},{16,20},{17... | collective-permute-start | bytes 12296 | tf_op jit(solution)/shard_map/ppermute | solution.py:55
  55.0 5.1 %collective-permute-start.13 = (f32[8,128]{1,0:T(8,128)S(1)}, f32[8,128]{1,0:T(8,128)S(1)}, u32[]{:S(2)}, u32[]{:S(2)}) collective-permute-start(f32[8,128]{1,0:T(8,128)S(1)} %rows.1), channel_id=1, source_target_pairs={{0,12},{1,17},{4,16},{5,21},{8,20},{9,25},{12,24},{13,29},{16,28},... | collective-permute-start | bytes 12296 | tf_op jit(solution)/shard_map/ppermute | solution.py:55
  60.2 1.3 %collective-permute-done.13.far = f32[8,128]{1,0:T(8,128)S(1)} collective-permute-done((f32[8,128]{1,0:T(8,128)S(1)}, f32[8,128]{1,0:T(8,128)S(1)}, u32[]{:S(2)}, u32[]{:S(2)}) %collective-permute-start.13) | collective-permute-done | bytes 4128 | tf_op jit(solution)/shard_map/ppermute | solution.py:55
  61.5 0.5 collective-permute-start.14
  62.0 1.9 %collective-permute-done.15.refs_2_ = f32[8,128]{1,0:T(8,128)S(1)} collective-permute-done((f32[8,128]{1,0:T(8,128)S(1)}, f32[8,128]{1,0:T(8,128)S(1)}, u32[]{:S(2)}, u32[]{:S(2)}) %collective-permute-start.15) | collective-permute-done | bytes 4128 | tf_op jit(solution)/shard_map/ppermute | solution.py:39
  64.0 1.6 %collective-permute-start.16 = (f32[8,128]{1,0:T(8,128)S(1)}, f32[8,128]{1,0:T(8,128)S(1)}, u32[]{:S(2)}, u32[]{:S(2)}) collective-permute-start(f32[8,128]{1,0:T(8,128)S(1)} %collective-permute-done.15.refs_2_), channel_id=1, source_target_pairs={{0,1},{1,0},{2,3},{3,2},{4,5},{5,4},{6,7},{7,6},{8,9},{9,8},{10,11... | collective-permute-start | bytes 12296 | tf_op jit(solution)/shard_map/ppermute | solution.py:43
  65.6 1.5 %shard_map.85 = (f32[3,8,128,640]{3,2,1,0:T(8,128)S(1)}, bf16[2,8,128,256]{3,2,1,0:T(8,128)(2,1)S(1)}) custom-call(bf16[2,264,512]{2,1,0:T(8,128)(2,1)S(1)} %collective-permute-done.8.low, bf16[2,264,512]{2,1,0:T(8,128)(2,1)S(1)} %collective-permute-done.9.high, ...), custom_call_target="tpu_custom_call", output_to_operand_aliasing={{0}: (4, {}), {1}: (5, {})} | custom-call | flops 1073741824 | bytes 1048576 | tf_op jit(solution)/shard_map/pallas_call | solution.py:251
  67.1 5.9 %finish.1 = (f32[3,8,128,640]{3,2,1,0:T(8,128)S(1)}, bf16[2,8,128,256]{3,2,1,0:T(8,128)(2,1)S(1)}, f32[4,3,32,640]{3,2,1,0:T(8,128)S(1)}, bf16[4,3,32,640]{3,2,1,0:T(8,128)(2,1)S(1)}) custom-call(bf16[2,264,512]{2,1,0:T(8,128)(2,1)S(1)} %collective-permute-done.10.low, ...), custom_call_target="tpu_custom_call", output_to_operand_aliasing={{0}: (4, {}), {1}: (5, {})} | custom-call | flops 4294967296 | bytes 1048576 | tf_op jit(solution)/shard_map/finish/pallas_call | solution.py:263
  73.0 1.7 %collective-permute-start.17 = (bf16[4,3,32,640]{3,2,1,0:T(8,128)(2,1)S(1)}, bf16[4,3,32,640]{3,2,1,0:T(8,128)(2,1)S(1)}, u32[]{:S(2)}, u32[]{:S(2)}) collective-permute-start(bf16[4,3,32,640]{3,2,1,0:T(8,128)(2,1)S(1)} %get-tuple-element.36), channel_id=1, source_target_pairs={{0,4},{1,29},{4,0},{5,9},{8,12},{9,5},{12,8},{13,17},{16,20},{17,1... | collective-permute-start | bytes 1474568 | tf_op jit(solution)/shard_map/ppermute | solution.py:51
  74.7 7.2 %collective-permute-done.17 = bf16[4,3,32,640]{3,2,1,0:T(8,128)(2,1)S(1)} collective-permute-done((bf16[4,3,32,640]{3,2,1,0:T(8,128)(2,1)S(1)}, bf16[4,3,32,640]{3,2,1,0:T(8,128)(2,1)S(1)}, u32[]{:S(2)}, u32[]{:S(2)}) %collective-permute-start.17) | collective-permute-done | bytes 491552 | tf_op jit(solution)/shard_map/ppermute | solution.py:51
  82.1 5.3 %collective-permute-start.18 = (bf16[3,32,640]{2,1,0:T(8,128)(2,1)S(1)}, bf16[3,32,640]{2,1,0:T(8,128)(2,1)S(1)}, u32[]{:S(2)}, u32[]{:S(2)}) collective-permute-start(bf16[3,32,640]{2,1,0:T(8,128)(2,1)S(1)} %get-tuple-element.39), channel_id=1, source_target_pairs={{0,16},{4,20},{8,24},{12,28},{16,0},{20,4},{24,8},{28,12},{1,17},{... | collective-permute-start | bytes 368648 | tf_op jit(solution)/shard_map/ppermute | solution.py:61
  87.6 3.3 %collective-permute-start.20 = (bf16[3,32,640]{2,1,0:T(8,128)(2,1)S(1)}, bf16[3,32,640]{2,1,0:T(8,128)(2,1)S(1)}, u32[]{:S(2)}, u32[]{:S(2)}) collective-permute-start(bf16[3,32,640]{2,1,0:T(8,128)(2,1)S(1)} %get-tuple-element.40), channel_id=1, source_target_pairs={{0,24},{4,28},{8,0},{12,4},{16,8},{20,12},{24,16},{28,20},{1,25},{... | collective-permute-start | bytes 368648 | tf_op jit(solution)/shard_map/ppermute | solution.py:61
  91.1 7.4 %collective-permute-done.19 = bf16[3,32,640]{2,1,0:T(8,128)(2,1)S(1)} collective-permute-done((bf16[3,32,640]{2,1,0:T(8,128)(2,1)S(1)}, bf16[3,32,640]{2,1,0:T(8,128)(2,1)S(1)}, u32[]{:S(2)}, u32[]{:S(2)}) %collective-permute-start.19) | collective-permute-done | bytes 122912 | tf_op jit(solution)/shard_map/ppermute | solution.py:61
  98.5 0.8 fusion.3
  (25 shorter events, 1.1 us)
Async XLA Ops:
  1.7 6.1 %collective-permute-start = (bf16[264,512]{1,0:T(8,128)(2,1)S(1)}, bf16[264,512]{1,0:T(8,128)(2,1)S(1)}, u32[]{:S(2)}, u32[]{:S(2)}) collective-permute-start(bf16[264,512]{1,0:T(8,128)(2,1)S(1)} %message.1), channel_id=1, source_target_pairs={{0,128},{1,33},{2,130},{3,35},{32,160},{33,1},{34,162},{35,3},{64,... | collective-permute-start | bytes 811016 | tf_op jit(solution)/shard_map/ppermute | solution.py:35
  3.9 9.7 %collective-permute-start.1 = (bf16[264,512]{1,0:T(8,128)(2,1)S(1)}, bf16[264,512]{1,0:T(8,128)(2,1)S(1)}, u32[]{:S(2)}, u32[]{:S(2)}) collective-permute-start(bf16[264,512]{1,0:T(8,128)(2,1)S(1)} %message.1), channel_id=1, source_target_pairs={{0,2},{1,65},{2,0},{3,67},{32,34},{33,97},{34,32},{35,99},{64,66},... | collective-permute-start | bytes 811016 | tf_op jit(solution)/shard_map/ppermute | solution.py:35
  6.5 9.7 %collective-permute-start.2 = (bf16[264,512]{1,0:T(8,128)(2,1)S(1)}, bf16[264,512]{1,0:T(8,128)(2,1)S(1)}, u32[]{:S(2)}, u32[]{:S(2)}) collective-permute-start(bf16[264,512]{1,0:T(8,128)(2,1)S(1)} %message.1), channel_id=1, source_target_pairs={{0,130},{1,97},{2,128},{3,99},{32,162},{33,65},{34,160},{35,67},{6... | collective-permute-start | bytes 811016 | tf_op jit(solution)/shard_map/ppermute | solution.py:35
  16.3 14.4 %collective-permute-start.5 = (bf16[4,264,512]{2,1,0:T(8,128)(2,1)S(1)}, bf16[4,264,512]{2,1,0:T(8,128)(2,1)S(1)}, u32[]{:S(2)}, u32[]{:S(2)}) collective-permute-start(bf16[4,264,512]{2,1,0:T(8,128)(2,1)S(1)} %pad_maximum_fusion.own), channel_id=1, source_target_pairs={{0,32},{1,129},{2,34},{3,131},{32,0},{33,161},{34,2},{35,163},{64,... | collective-permute-start | bytes 3244040 | tf_op jit(solution)/shard_map/ppermute | solution.py:35
  17.3 15.7 %collective-permute-start.3 = (bf16[4,264,512]{2,1,0:T(8,128)(2,1)S(1)}, bf16[4,264,512]{2,1,0:T(8,128)(2,1)S(1)}, u32[]{:S(2)}, u32[]{:S(2)}) collective-permute-start(bf16[4,264,512]{2,1,0:T(8,128)(2,1)S(1)} %pad_maximum_fusion.own), channel_id=1, source_target_pairs={{0,96},{1,131},{2,98},{3,129},{32,64},{33,163},{34,66},{35,161},{6... | collective-permute-start | bytes 3244040 | tf_op jit(solution)/shard_map/ppermute | solution.py:35
  19.2 20.7 %collective-permute-start.7 = (bf16[4,264,512]{2,1,0:T(8,128)(2,1)S(1)}, bf16[4,264,512]{2,1,0:T(8,128)(2,1)S(1)}, u32[]{:S(2)}, u32[]{:S(2)}) collective-permute-start(bf16[4,264,512]{2,1,0:T(8,128)(2,1)S(1)} %pad_maximum_fusion.own), channel_id=1, source_target_pairs={{0,1},{1,0},{2,3},{3,2},{4,5},{5,4},{6,7},{7,6},{8,9},{9,8},{10,11... | collective-permute-start | bytes 3244040 | tf_op jit(solution)/shard_map/ppermute | solution.py:43
  30.7 12.8 %collective-permute-start.6 = (bf16[4,264,512]{2,1,0:T(8,128)(2,1)S(1)}, bf16[4,264,512]{2,1,0:T(8,128)(2,1)S(1)}, u32[]{:S(2)}, u32[]{:S(2)}) collective-permute-start(bf16[4,264,512]{2,1,0:T(8,128)(2,1)S(1)} %collective-permute-done.5.refs_0_), channel_id=1, source_target_pairs={{0,1},{1,0},{2,3},{3,2},{4,5},{5,4},{6,7},{7,6},{8,9},{9,8},{10,11... | collective-permute-start | bytes 3244040 | tf_op jit(solution)/shard_map/ppermute | solution.py:43
  33.1 13.6 %collective-permute-start.4 = (bf16[4,264,512]{2,1,0:T(8,128)(2,1)S(1)}, bf16[4,264,512]{2,1,0:T(8,128)(2,1)S(1)}, u32[]{:S(2)}, u32[]{:S(2)}) collective-permute-start(bf16[4,264,512]{2,1,0:T(8,128)(2,1)S(1)} %collective-permute-done.3.refs_0_), channel_id=1, source_target_pairs={{0,1},{1,0},{2,3},{3,2},{4,5},{5,4},{6,7},{7,6},{8,9},{9,8},{10,11... | collective-permute-start | bytes 3244040 | tf_op jit(solution)/shard_map/ppermute | solution.py:43
  39.3 10.6 %collective-permute-start.8 = (bf16[2,264,512]{2,1,0:T(8,128)(2,1)S(1)}, bf16[2,264,512]{2,1,0:T(8,128)(2,1)S(1)}, u32[]{:S(2)}, u32[]{:S(2)}) collective-permute-start(bf16[2,264,512]{2,1,0:T(8,128)(2,1)S(1)} %slice.27), channel_id=1, source_target_pairs={{0,96},{1,131},{2,98},{3,129},{32,64},{33,163},{34,66},{35,161},{6... | collective-permute-start | bytes 1622024 | tf_op jit(solution)/shard_map/ppermute | solution.py:35
  39.8 10.0 %collective-permute-start.9 = (bf16[2,264,512]{2,1,0:T(8,128)(2,1)S(1)}, bf16[2,264,512]{2,1,0:T(8,128)(2,1)S(1)}, u32[]{:S(2)}, u32[]{:S(2)}) collective-permute-start(bf16[2,264,512]{2,1,0:T(8,128)(2,1)S(1)} %slice.28), channel_id=1, source_target_pairs={{0,32},{1,129},{2,34},{3,131},{32,0},{33,161},{34,2},{35,163},{64,... | collective-permute-start | bytes 1622024 | tf_op jit(solution)/shard_map/ppermute | solution.py:35
  49.8 17.2 %collective-permute-start.10 = (bf16[2,264,512]{2,1,0:T(8,128)(2,1)S(1)}, bf16[2,264,512]{2,1,0:T(8,128)(2,1)S(1)}, u32[]{:S(2)}, u32[]{:S(2)}) collective-permute-start(bf16[2,264,512]{2,1,0:T(8,128)(2,1)S(1)} %collective-permute-done.8.low), channel_id=1, source_target_pairs={{0,1},{1,0},{2,3},{3,2},{4,5},{5,4},{6,7},{7,6},{8,9},{9,8},{10,11... | collective-permute-start | bytes 1622024 | tf_op jit(solution)/shard_map/ppermute | solution.py:43
  51.7 15.4 %collective-permute-start.11 = (bf16[2,264,512]{2,1,0:T(8,128)(2,1)S(1)}, bf16[2,264,512]{2,1,0:T(8,128)(2,1)S(1)}, u32[]{:S(2)}, u32[]{:S(2)}) collective-permute-start(bf16[2,264,512]{2,1,0:T(8,128)(2,1)S(1)} %collective-permute-done.9.high), channel_id=1, source_target_pairs={{0,1},{1,0},{2,3},{3,2},{4,5},{5,4},{6,7},{7,6},{8,9},{9,8},{10,11... | collective-permute-start | bytes 1622024 | tf_op jit(solution)/shard_map/ppermute | solution.py:43
  51.8 8.4 %collective-permute-start.12 = (f32[8,128]{1,0:T(8,128)S(1)}, f32[8,128]{1,0:T(8,128)S(1)}, u32[]{:S(2)}, u32[]{:S(2)}) collective-permute-start(f32[8,128]{1,0:T(8,128)S(1)} %rows.1), channel_id=1, source_target_pairs={{0,4},{1,9},{4,8},{5,13},{8,12},{9,17},{12,16},{13,21},{16,20},{17... | collective-permute-start | bytes 12296 | tf_op jit(solution)/shard_map/ppermute | solution.py:55
  55.0 6.4 %collective-permute-start.13 = (f32[8,128]{1,0:T(8,128)S(1)}, f32[8,128]{1,0:T(8,128)S(1)}, u32[]{:S(2)}, u32[]{:S(2)}) collective-permute-start(f32[8,128]{1,0:T(8,128)S(1)} %rows.1), channel_id=1, source_target_pairs={{0,12},{1,17},{4,16},{5,21},{8,20},{9,25},{12,24},{13,29},{16,28},... | collective-permute-start | bytes 12296 | tf_op jit(solution)/shard_map/ppermute | solution.py:55
  61.4 2.5 %collective-permute-start.15 = (f32[8,128]{1,0:T(8,128)S(1)}, f32[8,128]{1,0:T(8,128)S(1)}, u32[]{:S(2)}, u32[]{:S(2)}) collective-permute-start(f32[8,128]{1,0:T(8,128)S(1)} %part.1.refs_0_), channel_id=1, source_target_pairs={{0,128},{128,0},{1,129},{129,1},{2,130},{130,2},{3,131},{131,3},{4... | collective-permute-start | bytes 12296 | tf_op jit(solution)/shard_map/ppermute | solution.py:39
  61.5 5.6 %collective-permute-start.14 = (f32[8,128]{1,0:T(8,128)S(1)}, f32[8,128]{1,0:T(8,128)S(1)}, u32[]{:S(2)}, u32[]{:S(2)}) collective-permute-start(f32[8,128]{1,0:T(8,128)S(1)} %part.1.refs_0_), channel_id=1, source_target_pairs={{0,1},{1,0},{2,3},{3,2},{4,5},{5,4},{6,7},{7,6},{8,9},{9,8},{10,11... | collective-permute-start | bytes 12296 | tf_op jit(solution)/shard_map/ppermute | solution.py:43
  64.0 3.1 %collective-permute-start.16 = (f32[8,128]{1,0:T(8,128)S(1)}, f32[8,128]{1,0:T(8,128)S(1)}, u32[]{:S(2)}, u32[]{:S(2)}) collective-permute-start(f32[8,128]{1,0:T(8,128)S(1)} %collective-permute-done.15.refs_2_), channel_id=1, source_target_pairs={{0,1},{1,0},{2,3},{3,2},{4,5},{5,4},{6,7},{7,6},{8,9},{9,8},{10,11... | collective-permute-start | bytes 12296 | tf_op jit(solution)/shard_map/ppermute | solution.py:43
  73.0 9.0 %collective-permute-start.17 = (bf16[4,3,32,640]{3,2,1,0:T(8,128)(2,1)S(1)}, bf16[4,3,32,640]{3,2,1,0:T(8,128)(2,1)S(1)}, u32[]{:S(2)}, u32[]{:S(2)}) collective-permute-start(bf16[4,3,32,640]{3,2,1,0:T(8,128)(2,1)S(1)} %get-tuple-element.36), channel_id=1, source_target_pairs={{0,4},{1,29},{4,0},{5,9},{8,12},{9,5},{12,8},{13,17},{16,20},{17,1... | collective-permute-start | bytes 1474568 | tf_op jit(solution)/shard_map/ppermute | solution.py:51
  82.1 8.9 %collective-permute-start.18 = (bf16[3,32,640]{2,1,0:T(8,128)(2,1)S(1)}, bf16[3,32,640]{2,1,0:T(8,128)(2,1)S(1)}, u32[]{:S(2)}, u32[]{:S(2)}) collective-permute-start(bf16[3,32,640]{2,1,0:T(8,128)(2,1)S(1)} %get-tuple-element.39), channel_id=1, source_target_pairs={{0,16},{4,20},{8,24},{12,28},{16,0},{20,4},{24,8},{28,12},{1,17},{... | collective-permute-start | bytes 368648 | tf_op jit(solution)/shard_map/ppermute | solution.py:61
  87.4 11.1 %collective-permute-start.19 = (bf16[3,32,640]{2,1,0:T(8,128)(2,1)S(1)}, bf16[3,32,640]{2,1,0:T(8,128)(2,1)S(1)}, u32[]{:S(2)}, u32[]{:S(2)}) collective-permute-start(bf16[3,32,640]{2,1,0:T(8,128)(2,1)S(1)} %get-tuple-element.41), channel_id=1, source_target_pairs={{0,8},{4,12},{8,16},{12,20},{16,24},{20,28},{24,0},{28,4},{1,9},{5... | collective-permute-start | bytes 368648 | tf_op jit(solution)/shard_map/ppermute | solution.py:61
  87.6 10.9 %collective-permute-start.20 = (bf16[3,32,640]{2,1,0:T(8,128)(2,1)S(1)}, bf16[3,32,640]{2,1,0:T(8,128)(2,1)S(1)}, u32[]{:S(2)}, u32[]{:S(2)}) collective-permute-start(bf16[3,32,640]{2,1,0:T(8,128)(2,1)S(1)} %get-tuple-element.40), channel_id=1, source_target_pairs={{0,24},{4,28},{8,0},{12,4},{16,8},{20,12},{24,16},{28,20},{1,25},{... | collective-permute-start | bytes 368648 | tf_op jit(solution)/shard_map/ppermute | solution.py:61

commit v6 on v5

--- a/solution.py
+++ b/solution.py
@@ -11,6 +11,7 @@
 I32 = jnp.int32
 ROOT_2_PI = 0.7978845608028654
 CUBIC = 0.044715
+CUTS = ((0, 384), (384, 640))
 BLK = ("xl", "y", "z")
 PLANE = ("xl", "y", "xh", "c")
 SMEM = pl.BlockSpec(memory_space=pltpu.SMEM)
@@ -112,11 +113,13 @@
 
 
 def weights_kernel(w_gate, w_lin, w_out_t, w_in, w_out, sems):
-    copies = [
-        pltpu.make_async_copy(w_gate, w_in.at[:, :, pl.ds(0, 640)], sems.at[0]),
-        pltpu.make_async_copy(w_lin, w_in.at[:, :, pl.ds(640, 640)], sems.at[1]),
-        pltpu.make_async_copy(w_out_t, w_out, sems.at[2]),
-    ]
+    pairs = [(w_out_t, w_out)]
+    for lower, upper in CUTS:
+        width = upper - lower
+        for n, w in enumerate((w_gate, w_lin)):
+            target = w_in.at[:, :, pl.ds(2 * lower + n * width, width)]
+            pairs.append((w.at[:, :, pl.ds(lower, width)], target))
+    copies = [pltpu.make_async_copy(*pair, sems.at[i]) for i, pair in enumerate(pairs)]
     for copy in copies:
         copy.start()
     for copy in copies:
@@ -132,7 +135,7 @@
         ),
         in_specs=[pl.BlockSpec(memory_space=pltpu.HBM)] * 3,
         out_specs=(VMEM, VMEM),
-        scratch_shapes=[pltpu.SemaphoreType.DMA((3,))],
+        scratch_shapes=[pltpu.SemaphoreType.DMA((5,))],
         compiler_params=PARAMS,
         name="load",
     )(*[hbm(w.reshape(4, 512, 640)) for w in (w_gate, w_lin, w_out_t)])
@@ -191,13 +194,13 @@
     gather_kernel(2, ((0, (low, high)),), w_in, w_out, acc, cols)
 
 
-def final_kernel(low, high, w_in, w_out, _, __, *refs):
+def final_kernel(cut, low, high, w_in, w_out, _, __, *refs):
     terms, (acc, cols, *rest) = refs[:4], refs[4:]
-    gather_kernel(2, ((1, (low, high)),), w_in, w_out, acc, cols)
-    last_kernel(terms, acc, cols, *rest)
-
-
-def gather_kernel(m, blocks, w_in, w_out, acc, cols):
+    gather_kernel(2, ((1, (low, high)),), w_in, w_out, acc, cols, (CUTS[cut],), cut == 0)
+    last_kernel(CUTS[cut], terms, acc, cols, *rest)
+
+
+def gather_kernel(m, blocks, w_in, w_out, acc, cols, cuts=CUTS, with_cols=True):
     xl, y, _, xh, c = place()
     for ec, block in blocks:
         x_first = (c ^ ec) == 0
@@ -209,14 +212,19 @@
             shard = (xh ^ eh) * 2 + (c ^ ec)
             xs = block[pl.ds(start, 2), 0:128].reshape(256, 512)
             ys = block[pl.ds(start, 2), 128:256].reshape(256, 512)
-            pre = jnp.dot(xs, w_in[shard], preferred_element_type=F32)
-            acc[0, p0] += pre[:128, :640]
-            acc[1, p0] += pre[:128, 640:]
-            acc[0, p1] += pre[128:, :640]
-            acc[1, p1] += pre[128:, 640:]
-            dh = jnp.dot(ys, w_out[shard], preferred_element_type=F32)
-            acc[2, p0] += dh[:128]
-            acc[2, p1] += dh[128:]
+            first, end = cuts[0][0], cuts[-1][1]
+            pre = jnp.dot(xs, w_in[shard, :, 2 * first : 2 * end], preferred_element_type=F32)
+            for lower, upper in cuts:
+                width = upper - lower
+                for n in range(2):
+                    at = 2 * (lower - first) + n * width
+                    acc[n, p0, :, lower:upper] += pre[:128, at : at + width]
+                    acc[n, p1, :, lower:upper] += pre[128:, at : at + width]
+            dh = jnp.dot(ys, w_out[shard, :, first:end], preferred_element_type=F32)
+            acc[2, p0, :, first:end] += dh[:128]
+            acc[2, p1, :, first:end] += dh[128:]
+            if not with_cols:
+                return
 
             @pl.when((ec == ((y >> 1) ^ c)) & (eh == (xl ^ xh)))
             def _():
@@ -259,28 +267,31 @@
     )(*blocks, w_in, w_out, *state)
 
 
-def finished(halves, w_in, w_out, state, terms):
-    return pl.pallas_call(
-        final_kernel,
+def finished(cut, halves, w_in, w_out, state, terms):
+    width = CUTS[cut][1] - CUTS[cut][0]
+    *state, keep, send = pl.pallas_call(
+        lambda *refs: final_kernel(cut, *refs),
         out_shape=STATE
-        + (jax.ShapeDtypeStruct((4, 3, 32, 640), F32), jax.ShapeDtypeStruct((4, 3, 32, 640), BF16)),
+        + (jax.ShapeDtypeStruct((4, 3, 32, width), F32), jax.ShapeDtypeStruct((4, 3, 32, width), BF16)),
         in_specs=[VMEM] * 10,
         out_specs=(VMEM,) * 4,
         input_output_aliases={4: 0, 5: 1},
         scratch_shapes=[
-            pltpu.VMEM((8, 128, 1280), BF16),
-            pltpu.VMEM((8, 128, 640), BF16),
-            pltpu.VMEM((8, 3, 32, 640), F32),
+            pltpu.VMEM((8, 128, 2 * width), BF16),
+            pltpu.VMEM((8, 128, width), BF16),
+            pltpu.VMEM((8, 3, 32, width), F32),
         ],
         compiler_params=PARAMS,
-        cost_estimate=priced(4),
-        name="finish",
-    )(*halves, w_in, w_out, *state, *terms)[2:]
-
-
-def last_kernel(terms, acc, cols, keep, send, gates, hidden, total):
+        cost_estimate=priced(2),
+    )(*halves, w_in, w_out, *state, *terms)
+    return state, keep, send
+
+
+def last_kernel(cut, terms, acc, cols, keep, send, gates, hidden, total):
     xl, y, z, _, c = place()
     lane = lax.broadcasted_iota(I32, (8, 128), 1)
+    lower, upper = cut
+    width = upper - lower
     row = lax.broadcasted_iota(I32, (8, 128), 0)
     known = (lane < 5) & (row < 4)
     workers = [(((xl ^ ex) * 4 + (y ^ row)) & 7) * 8 + ((z - lane) & 7) for ex in range(2)]
@@ -294,29 +305,29 @@
             w = w + jnp.sum(jnp.where(mine, terms[2 * i][...] + terms[2 * i + 1][...], 0.0))
         for r in range(0, 128, 32):
             rows = pl.ds(r, 32)
-            u = acc[0, p, rows]
-            v = acc[1, p, rows]
-            d = acc[2, p, rows] * w
+            u = acc[0, p, rows, lower:upper]
+            v = acc[1, p, rows, lower:upper]
+            d = acc[2, p, rows, lower:upper] * w
             square = u * u
             t = jnp.tanh(ROOT_2_PI * (u + CUBIC * (square * u)))
             cdf = 0.5 * (1.0 + t)
             act = u * cdf
             slope = cdf + 0.5 * u * (1.0 - t * t) * (ROOT_2_PI * (1.0 + 3.0 * CUBIC * square))
-            gates[p, rows, 0:640] = (d * v * slope).astype(BF16)
-            gates[p, rows, 640:1280] = (d * act).astype(BF16)
+            gates[p, rows, :width] = (d * v * slope).astype(BF16)
+            gates[p, rows, width:] = (d * act).astype(BF16)
             hidden[p, rows] = (act * v * w).astype(BF16)
         return 0
 
     lax.fori_loop(0, 8, part, 0)
     dims = (((0,), (0,)), ((), ()))
     both = lax.dot_general(
-        cols[0].reshape(1024, 256), gates[...].reshape(1024, 1280), dims, preferred_element_type=F32
+        cols[0].reshape(1024, 256), gates[...].reshape(1024, 2 * width), dims, preferred_element_type=F32
     )
-    total[:, 0] = both[:, :640].reshape(8, 32, 640)
-    total[:, 1] = both[:, 640:].reshape(8, 32, 640)
+    total[:, 0] = both[:, :width].reshape(8, 32, width)
+    total[:, 1] = both[:, width:].reshape(8, 32, width)
     total[:, 2] = lax.dot_general(
-        cols[1].reshape(1024, 256), hidden[...].reshape(1024, 640), dims, preferred_element_type=F32
-    ).reshape(8, 32, 640)
+        cols[1].reshape(1024, 256), hidden[...].reshape(1024, width), dims, preferred_element_type=F32
+    ).reshape(8, 32, width)
     odd = z & 1
     near = jnp.where(odd == 1, z + 1, z - 1) & 7
     near = jnp.where(c == 0, z ^ 1, near)
@@ -356,13 +367,22 @@
     state, low, high = lax.optimization_barrier((state, low, high))
     halves = [sibling(low), sibling(high)]
     state = gathered(2, (low, high), w_in, w_out, state)
-    keep, send = finished(halves, w_in, w_out, state, terms)
-    got = z_pair(send)
-    mixed = keep + got.astype(F32)
-    result = mixed[0]
-    for k in (2, 1, 3):
-        result = result + z_step(mixed[k].astype(BF16), 2 * k).astype(F32)
-    return jnp.transpose(result, (1, 0, 2))
+    keeps, got = [], []
+    for cut in range(2):
+        state, keep, send = finished(cut, halves, w_in, w_out, state, terms)
+        keeps.append(keep)
+        got.append(z_pair(send))
+    results = []
+    for cut in range(2):
+        mixed = keeps[cut] + got[cut].astype(F32)
+        sends = mixed.astype(BF16)
+        if cut == 0:
+            sends, keeps[1] = lax.optimization_barrier((sends, keeps[1]))
+        result = mixed[0]
+        for k in (2, 1, 3):
+            result = result + z_step(sends[k], 2 * k).astype(F32)
+        results.append(result)
+    return jnp.transpose(jnp.concatenate(results, axis=2), (1, 0, 2))
 
 
 def solution(mesh):

time: 99.4 us -> 101 us (1.016)
  starting transfers between devices: 39 us -> 44 us
  waiting for transfers between devices: 36.7 us -> 32.9 us
    ppermute x3 -> x6, starting transfers between devices: 8.84 us -> 12.7 us  [z_step(): return lax.ppermute(block, 'z', [(z, (z + step) % 8) for z in range(8)])]
    ppermute x1 -> x2, waiting for transfers between devices: 7.24 us -> 4.62 us  [z_pair(): lax.ppermute(block, ('z', 'c'), [(z * 2 + c, partner_of(z, c) * 2 + c) fo...]
    ppermute x3 -> x6, waiting for transfers between devices: 7.55 us -> 6.37 us  [z_step(): return lax.ppermute(block, 'z', [(z, (z + step) % 8) for z in range(8)])]
    ppermute x1 -> x2, starting transfers between devices: 1.73 us -> 2.85 us  [z_pair(): lax.ppermute(block, ('z', 'c'), [(z * 2 + c, partner_of(z, c) * 2 + c) fo...]
    pallas_call x1 -> x2, Pallas kernels: 5.85 us -> 6.78 us  [finished(): pl.pallas_call(lambda *refs: final_kernel(cut, *refs), out_shape=STATE +...]
  transfers between devices with their start and end apart: 21 -> 25, of which waited for: 9 -> 11; matrix products, arithmetic and copies ran while one was open for 0% -> 0% of each run, Pallas kernels for 15% -> 17%
where the time goes in v6:
time: 101 us
  starting transfers between devices  44 us (44%)
  waiting for transfers between devices  32.9 us (33%)
  Pallas kernels  22.2 us (22%)
  other arithmetic  1.07 us (1%)
    ppermute x7, waiting for transfers between devices, across(): return lax.ppermute(block, PLANE, route)  18.8 us
    ppermute x6, starting transfers between devices, z_step(): return lax.ppermute(block, 'z', [(z, (z + step) % 8) for z in range(8)])  12.7 us
    ppermute x7, starting transfers between devices, sibling(): return lax.ppermute(block, 'c', [(0, 1), (1, 0)])  11.7 us
    pallas_call x4, Pallas kernels, gathered(): pl.pallas_call(kernels.get(m, lambda *refs: middle_kernel(m, *refs)), out...  11.1 us
    ppermute x2, starting transfers between devices, z_shift(): lax.ppermute(block, ('z', 'c'), [(z * 2 + c, (z + step + c) % 8 * 2 + c)...  8.36 us
    ppermute x7, starting transfers between devices, across(): return lax.ppermute(block, PLANE, route)  8.25 us
    pallas_call x2, Pallas kernels, finished(): pl.pallas_call(lambda *refs: final_kernel(cut, *refs), out_shape=STATE +...  6.78 us
    ppermute x6, waiting for transfers between devices, z_step(): return lax.ppermute(block, 'z', [(z, (z + step) % 8) for z in range(8)])  6.37 us
  transfers between devices with their start and end apart: 25, of which 11 were waited for; matrix products, arithmetic and copies ran while one was open for 0% of the time, Pallas kernels for 17%

profile of v6, /device:TPU:1, one launch (start us, length us, event | category | flops | bytes accessed | tf_op | source)
XLA Modules:
  0.0 101.2 jit_solution(6477405963795926781)
XLA Ops:
  1.7 2.2 %collective-permute-start = (bf16[264,512]{1,0:T(8,128)(2,1)S(1)}, bf16[264,512]{1,0:T(8,128)(2,1)S(1)}, u32[]{:S(2)}, u32[]{:S(2)}) collective-permute-start(bf16[264,512]{1,0:T(8,128)(2,1)S(1)} %message.1), channel_id=1, source_target_pairs={{0,128},{1,33},{2,130},{3,35},{32,160},{33,1},{34,162},{35,3},{64,... | collective-permute-start | bytes 811016 | tf_op jit(solution)/shard_map/ppermute | solution.py:36
  3.9 2.6 %collective-permute-start.1 = (bf16[264,512]{1,0:T(8,128)(2,1)S(1)}, bf16[264,512]{1,0:T(8,128)(2,1)S(1)}, u32[]{:S(2)}, u32[]{:S(2)}) collective-permute-start(bf16[264,512]{1,0:T(8,128)(2,1)S(1)} %message.1), channel_id=1, source_target_pairs={{0,2},{1,65},{2,0},{3,67},{32,34},{33,97},{34,32},{35,99},{64,66},... | collective-permute-start | bytes 811016 | tf_op jit(solution)/shard_map/ppermute | solution.py:36
  6.5 1.2 %collective-permute-done = bf16[264,512]{1,0:T(8,128)(2,1)S(1)} collective-permute-done((bf16[264,512]{1,0:T(8,128)(2,1)S(1)}, bf16[264,512]{1,0:T(8,128)(2,1)S(1)}, u32[]{:S(2)}, u32[]{:S(2)}) %collective-permute-start) | collective-permute-done | bytes 270368 | tf_op jit(solution)/shard_map/ppermute | solution.py:36
  7.7 5.8 %collective-permute-done.1 = bf16[264,512]{1,0:T(8,128)(2,1)S(1)} collective-permute-done((bf16[264,512]{1,0:T(8,128)(2,1)S(1)}, bf16[264,512]{1,0:T(8,128)(2,1)S(1)}, u32[]{:S(2)}, u32[]{:S(2)}) %collective-permute-start.1) | collective-permute-done | bytes 270368 | tf_op jit(solution)/shard_map/ppermute | solution.py:36
  13.6 2.6 %collective-permute-done.2 = bf16[264,512]{1,0:T(8,128)(2,1)S(1)} collective-permute-done((bf16[264,512]{1,0:T(8,128)(2,1)S(1)}, bf16[264,512]{1,0:T(8,128)(2,1)S(1)}, u32[]{:S(2)}, u32[]{:S(2)}) %collective-permute-start.2) | collective-permute-done | bytes 270368 | tf_op jit(solution)/shard_map/ppermute | solution.py:36
  17.3 1.8 %collective-permute-start.3 = (bf16[4,264,512]{2,1,0:T(8,128)(2,1)S(1)}, bf16[4,264,512]{2,1,0:T(8,128)(2,1)S(1)}, u32[]{:S(2)}, u32[]{:S(2)}) collective-permute-start(bf16[4,264,512]{2,1,0:T(8,128)(2,1)S(1)} %pad_maximum_fusion.own), channel_id=1, source_target_pairs={{0,96},{1,131},{2,98},{3,129},{32,64},{33,163},{34,66},{35,161},{6... | collective-permute-start | bytes 3244040 | tf_op jit(solution)/shard_map/ppermute | solution.py:36
  19.2 2.5 %collective-permute-start.7 = (bf16[4,264,512]{2,1,0:T(8,128)(2,1)S(1)}, bf16[4,264,512]{2,1,0:T(8,128)(2,1)S(1)}, u32[]{:S(2)}, u32[]{:S(2)}) collective-permute-start(bf16[4,264,512]{2,1,0:T(8,128)(2,1)S(1)} %pad_maximum_fusion.own), channel_id=1, source_target_pairs={{0,1},{1,0},{2,3},{3,2},{4,5},{5,4},{6,7},{7,6},{8,9},{9,8},{10,11... | collective-permute-start | bytes 3244040 | tf_op jit(solution)/shard_map/ppermute | solution.py:44
  21.7 9.0 %collective-permute-done.5.refs_0_ = bf16[4,264,512]{2,1,0:T(8,128)(2,1)S(1)} collective-permute-done((bf16[4,264,512]{2,1,0:T(8,128)(2,1)S(1)}, bf16[4,264,512]{2,1,0:T(8,128)(2,1)S(1)}, u32[]{:S(2)}, u32[]{:S(2)}) %collective-permute-start.5) | collective-permute-done | bytes 1081376 | tf_op jit(solution)/shard_map/ppermute | solution.py:36
  30.7 2.3 %collective-permute-start.6 = (bf16[4,264,512]{2,1,0:T(8,128)(2,1)S(1)}, bf16[4,264,512]{2,1,0:T(8,128)(2,1)S(1)}, u32[]{:S(2)}, u32[]{:S(2)}) collective-permute-start(bf16[4,264,512]{2,1,0:T(8,128)(2,1)S(1)} %collective-permute-done.5.refs_0_), channel_id=1, source_target_pairs={{0,1},{1,0},{2,3},{3,2},{4,5},{5,4},{6,7},{7,6},{8,9},{9,8},{10,11... | collective-permute-start | bytes 3244040 | tf_op jit(solution)/shard_map/ppermute | solution.py:44
  33.1 2.8 %collective-permute-start.4 = (bf16[4,264,512]{2,1,0:T(8,128)(2,1)S(1)}, bf16[4,264,512]{2,1,0:T(8,128)(2,1)S(1)}, u32[]{:S(2)}, u32[]{:S(2)}) collective-permute-start(bf16[4,264,512]{2,1,0:T(8,128)(2,1)S(1)} %collective-permute-done.3.refs_0_), channel_id=1, source_target_pairs={{0,1},{1,0},{2,3},{3,2},{4,5},{5,4},{6,7},{7,6},{8,9},{9,8},{10,11... | collective-permute-start | bytes 3244040 | tf_op jit(solution)/shard_map/ppermute | solution.py:44
  35.9 3.3 %load.1 = (bf16[4,512,1280]{2,1,0:T(8,128)(2,1)S(1)}, bf16[4,512,640]{2,1,0:T(8,128)(2,1)S(1)}) custom-call(bf16[4,512,640]{2,1,0:T(8,128)(2,1)} %bitcast.38, bf16[4,512,640]{2,1,0:T(8,128)(2,1)} %bitcast.39, bf16[4,512,640]{2,1,0:T(8,128)(2,1)} %bitcast.40), custom_call_target="tpu_custom_call" | custom-call | tf_op jit(solution)/shard_map/load/pallas_call | solution.py:130
  39.9 3.5 %shard_map.82 = (f32[3,8,128,640]{3,2,1,0:T(8,128)S(1)}, bf16[2,8,128,256]{3,2,1,0:T(8,128)(2,1)S(1)}) custom-call(bf16[4,264,512]{2,1,0:T(8,128)(2,1)S(1)} %pad_maximum_fusion.own, bf16[4,264,512]{2,1,0:T(8,128)(2,1)S(1)} %collective-permute-done.7.other, bf16[4,512,1280]{2,1,0:T(8,128)(2,1)S(1)} %get-tuple-element.27.w_in.refs_2_, ...), custom_call_target="tpu_custom_call" | custom-call | flops 2147483648 | bytes 1048576 | tf_op jit(solution)/shard_map/pallas_call | solution.py:259
  43.4 3.1 %shard_map.83 = (f32[3,8,128,640]{3,2,1,0:T(8,128)S(1)}, bf16[2,8,128,256]{3,2,1,0:T(8,128)(2,1)S(1)}) custom-call(bf16[4,264,512]{2,1,0:T(8,128)(2,1)S(1)} %collective-permute-done.5.refs_0_, bf16[4,264,512]{2,1,0:T(8,128)(2,1)S(1)} %collective-permute-done.6.refs_1_, ...), custom_call_target="tpu_custom_call", output_to_operand_aliasing={{0}: (4, {}), {1}: (5, {})} | custom-call | flops 2147483648 | bytes 1048576 | tf_op jit(solution)/shard_map/pallas_call | solution.py:259
  46.5 3.0 %shard_map.84 = (f32[3,8,128,640]{3,2,1,0:T(8,128)S(1)}, bf16[2,8,128,256]{3,2,1,0:T(8,128)(2,1)S(1)}) custom-call(bf16[4,264,512]{2,1,0:T(8,128)(2,1)S(1)} %collective-permute-done.3.refs_0_, bf16[4,264,512]{2,1,0:T(8,128)(2,1)S(1)} %collective-permute-done.4.refs_1_, ...), custom_call_target="tpu_custom_call", output_to_operand_aliasing={{0}: (4, {}), {1}: (5, {})} | custom-call | flops 2147483648 | bytes 1048576 | tf_op jit(solution)/shard_map/pallas_call | solution.py:259
  49.6 1.8 %collective-permute-start.10 = (bf16[2,264,512]{2,1,0:T(8,128)(2,1)S(1)}, bf16[2,264,512]{2,1,0:T(8,128)(2,1)S(1)}, u32[]{:S(2)}, u32[]{:S(2)}) collective-permute-start(bf16[2,264,512]{2,1,0:T(8,128)(2,1)S(1)} %collective-permute-done.8.low), channel_id=1, source_target_pairs={{0,1},{1,0},{2,3},{3,2},{4,5},{5,4},{6,7},{7,6},{8,9},{9,8},{10,11... | collective-permute-start | bytes 1622024 | tf_op jit(solution)/shard_map/ppermute | solution.py:44
  51.5 3.2 %collective-permute-start.12 = (f32[8,128]{1,0:T(8,128)S(1)}, f32[8,128]{1,0:T(8,128)S(1)}, u32[]{:S(2)}, u32[]{:S(2)}) collective-permute-start(f32[8,128]{1,0:T(8,128)S(1)} %rows.1), channel_id=1, source_target_pairs={{0,4},{1,9},{4,8},{5,13},{8,12},{9,17},{12,16},{13,21},{16,20},{17... | collective-permute-start | bytes 12296 | tf_op jit(solution)/shard_map/ppermute | solution.py:56
  54.8 5.1 %collective-permute-start.13 = (f32[8,128]{1,0:T(8,128)S(1)}, f32[8,128]{1,0:T(8,128)S(1)}, u32[]{:S(2)}, u32[]{:S(2)}) collective-permute-start(f32[8,128]{1,0:T(8,128)S(1)} %rows.1), channel_id=1, source_target_pairs={{0,12},{1,17},{4,16},{5,21},{8,20},{9,25},{12,24},{13,29},{16,28},... | collective-permute-start | bytes 12296 | tf_op jit(solution)/shard_map/ppermute | solution.py:56
  59.9 1.3 %collective-permute-done.13.far = f32[8,128]{1,0:T(8,128)S(1)} collective-permute-done((f32[8,128]{1,0:T(8,128)S(1)}, f32[8,128]{1,0:T(8,128)S(1)}, u32[]{:S(2)}, u32[]{:S(2)}) %collective-permute-start.13) | collective-permute-done | bytes 4128 | tf_op jit(solution)/shard_map/ppermute | solution.py:56
  61.8 1.9 %collective-permute-done.15.refs_8_ = f32[8,128]{1,0:T(8,128)S(1)} collective-permute-done((f32[8,128]{1,0:T(8,128)S(1)}, f32[8,128]{1,0:T(8,128)S(1)}, u32[]{:S(2)}, u32[]{:S(2)}) %collective-permute-start.15) | collective-permute-done | bytes 4128 | tf_op jit(solution)/shard_map/ppermute | solution.py:40
  63.7 1.6 %collective-permute-start.16 = (f32[8,128]{1,0:T(8,128)S(1)}, f32[8,128]{1,0:T(8,128)S(1)}, u32[]{:S(2)}, u32[]{:S(2)}) collective-permute-start(f32[8,128]{1,0:T(8,128)S(1)} %collective-permute-done.15.refs_8_), channel_id=1, source_target_pairs={{0,1},{1,0},{2,3},{3,2},{4,5},{5,4},{6,7},{7,6},{8,9},{9,8},{10,11... | collective-permute-start | bytes 12296 | tf_op jit(solution)/shard_map/ppermute | solution.py:44
  65.3 1.5 %shard_map.85 = (f32[3,8,128,640]{3,2,1,0:T(8,128)S(1)}, bf16[2,8,128,256]{3,2,1,0:T(8,128)(2,1)S(1)}) custom-call(bf16[2,264,512]{2,1,0:T(8,128)(2,1)S(1)} %collective-permute-done.8.low, bf16[2,264,512]{2,1,0:T(8,128)(2,1)S(1)} %collective-permute-done.9.high, ...), custom_call_target="tpu_custom_call", output_to_operand_aliasing={{0}: (4, {}), {1}: (5, {})} | custom-call | flops 1073741824 | bytes 1048576 | tf_op jit(solution)/shard_map/pallas_call | solution.py:259
  66.8 3.9 %shard_map.86 = (f32[3,8,128,640]{3,2,1,0:T(8,128)S(1)}, bf16[2,8,128,256]{3,2,1,0:T(8,128)(2,1)S(1)}, f32[4,3,32,384]{3,2,1,0:T(8,128)S(1)}, bf16[4,3,32,384]{3,2,1,0:T(8,128)(2,1)S(1)}) custom-call(bf16[2,264,512]{2,1,0:T(8,128)(2,1)S(1)} %collective-permute-done.10.refs_0_, ...), custom_call_target="tpu_custom_call", output_to_operand_aliasing={{0}: (4, {}), {1}: (5, {})} | custom-call | flops 2147483648 | bytes 1048576 | tf_op jit(solution)/shard_map/pallas_call | solution.py:272
  70.7 1.8 %collective-permute-start.17 = (bf16[4,3,32,384]{3,2,1,0:T(8,128)(2,1)S(1)}, bf16[4,3,32,384]{3,2,1,0:T(8,128)(2,1)S(1)}, u32[]{:S(2)}, u32[]{:S(2)}) collective-permute-start(bf16[4,3,32,384]{3,2,1,0:T(8,128)(2,1)S(1)} %get-tuple-element.42), channel_id=1, source_target_pairs={{0,4},{1,29},{4,0},{5,9},{8,12},{9,5},{12,8},{13,17},{16,20},{17,1... | collective-permute-start | bytes 884744 | tf_op jit(solution)/shard_map/ppermute | solution.py:52
  72.5 2.9 %shard_map.87 = (f32[3,8,128,640]{3,2,1,0:T(8,128)S(1)}, bf16[2,8,128,256]{3,2,1,0:T(8,128)(2,1)S(1)}, f32[4,3,32,256]{3,2,1,0:T(8,128)S(1)}, bf16[4,3,32,256]{3,2,1,0:T(8,128)(2,1)S(1)}) custom-call(bf16[2,264,512]{2,1,0:T(8,128)(2,1)S(1)} %collective-permute-done.10.refs_0_, ...), custom_call_target="tpu_custom_call", output_to_operand_aliasing={{0}: (4, {}), {1}: (5, {})} | custom-call | flops 2147483648 | bytes 1048576 | tf_op jit(solution)/shard_map/pallas_call | solution.py:272
  76.5 1.1 %collective-permute-done.17 = bf16[4,3,32,384]{3,2,1,0:T(8,128)(2,1)S(1)} collective-permute-done((bf16[4,3,32,384]{3,2,1,0:T(8,128)(2,1)S(1)}, bf16[4,3,32,384]{3,2,1,0:T(8,128)(2,1)S(1)}, u32[]{:S(2)}, u32[]{:S(2)}) %collective-permute-start.17) | collective-permute-done | bytes 294944 | tf_op jit(solution)/shard_map/ppermute | solution.py:52
  77.7 3.5 %collective-permute-done.21 = bf16[4,3,32,256]{3,2,1,0:T(8,128)(2,1)S(1)} collective-permute-done((bf16[4,3,32,256]{3,2,1,0:T(8,128)(2,1)S(1)}, bf16[4,3,32,256]{3,2,1,0:T(8,128)(2,1)S(1)}, u32[]{:S(2)}, u32[]{:S(2)}) %collective-permute-start.21) | collective-permute-done | bytes 196640 | tf_op jit(solution)/shard_map/ppermute | solution.py:52
  81.3 4.3 %collective-permute-start.22 = (bf16[3,32,256]{2,1,0:T(8,128)(2,1)S(1)}, bf16[3,32,256]{2,1,0:T(8,128)(2,1)S(1)}, u32[]{:S(2)}, u32[]{:S(2)}) collective-permute-start(bf16[3,32,256]{2,1,0:T(8,128)(2,1)S(1)} %get-tuple-element.56), channel_id=1, source_target_pairs={{0,16},{4,20},{8,24},{12,28},{16,0},{20,4},{24,8},{28,12},{1,17},{... | collective-permute-start | bytes 147464 | tf_op jit(solution)/shard_map/ppermute | solution.py:62
  85.8 3.4 %collective-permute-start.24 = (bf16[3,32,256]{2,1,0:T(8,128)(2,1)S(1)}, bf16[3,32,256]{2,1,0:T(8,128)(2,1)S(1)}, u32[]{:S(2)}, u32[]{:S(2)}) collective-permute-start(bf16[3,32,256]{2,1,0:T(8,128)(2,1)S(1)} %get-tuple-element.57), channel_id=1, source_target_pairs={{0,24},{4,28},{8,0},{12,4},{16,8},{20,12},{24,16},{28,20},{1,25},{... | collective-permute-start | bytes 147464 | tf_op jit(solution)/shard_map/ppermute | solution.py:62
  89.2 1.3 %collective-permute-start.18 = (bf16[3,32,384]{2,1,0:T(8,128)(2,1)S(1)}, bf16[3,32,384]{2,1,0:T(8,128)(2,1)S(1)}, u32[]{:S(2)}, u32[]{:S(2)}) collective-permute-start(bf16[3,32,384]{2,1,0:T(8,128)(2,1)S(1)} %get-tuple-element.53), channel_id=1, source_target_pairs={{0,16},{4,20},{8,24},{12,28},{16,0},{20,4},{24,8},{28,12},{1,17},{... | collective-permute-start | bytes 221192 | tf_op jit(solution)/shard_map/ppermute | solution.py:62
  91.3 2.7 %collective-permute-start.20 = (bf16[3,32,384]{2,1,0:T(8,128)(2,1)S(1)}, bf16[3,32,384]{2,1,0:T(8,128)(2,1)S(1)}, u32[]{:S(2)}, u32[]{:S(2)}) collective-permute-start(bf16[3,32,384]{2,1,0:T(8,128)(2,1)S(1)} %get-tuple-element.54), channel_id=1, source_target_pairs={{0,24},{4,28},{8,0},{12,4},{16,8},{20,12},{24,16},{28,20},{1,25},{... | collective-permute-start | bytes 221192 | tf_op jit(solution)/shard_map/ppermute | solution.py:62
  94.1 2.9 %collective-permute-done.18 = bf16[3,32,384]{2,1,0:T(8,128)(2,1)S(1)} collective-permute-done((bf16[3,32,384]{2,1,0:T(8,128)(2,1)S(1)}, bf16[3,32,384]{2,1,0:T(8,128)(2,1)S(1)}, u32[]{:S(2)}, u32[]{:S(2)}) %collective-permute-start.18) | collective-permute-done | bytes 73760 | tf_op jit(solution)/shard_map/ppermute | solution.py:62
  98.1 2.3 %collective-permute-done.20 = bf16[3,32,384]{2,1,0:T(8,128)(2,1)S(1)} collective-permute-done((bf16[3,32,384]{2,1,0:T(8,128)(2,1)S(1)}, bf16[3,32,384]{2,1,0:T(8,128)(2,1)S(1)}, u32[]{:S(2)}, u32[]{:S(2)}) %collective-permute-start.20) | collective-permute-done | bytes 73760 | tf_op jit(solution)/shard_map/ppermute | solution.py:62
  (38 shorter events, 7.9 us)
Async XLA Ops:
  1.7 6.1 %collective-permute-start = (bf16[264,512]{1,0:T(8,128)(2,1)S(1)}, bf16[264,512]{1,0:T(8,128)(2,1)S(1)}, u32[]{:S(2)}, u32[]{:S(2)}) collective-permute-start(bf16[264,512]{1,0:T(8,128)(2,1)S(1)} %message.1), channel_id=1, source_target_pairs={{0,128},{1,33},{2,130},{3,35},{32,160},{33,1},{34,162},{35,3},{64,... | collective-permute-start | bytes 811016 | tf_op jit(solution)/shard_map/ppermute | solution.py:36
  3.9 9.7 %collective-permute-start.1 = (bf16[264,512]{1,0:T(8,128)(2,1)S(1)}, bf16[264,512]{1,0:T(8,128)(2,1)S(1)}, u32[]{:S(2)}, u32[]{:S(2)}) collective-permute-start(bf16[264,512]{1,0:T(8,128)(2,1)S(1)} %message.1), channel_id=1, source_target_pairs={{0,2},{1,65},{2,0},{3,67},{32,34},{33,97},{34,32},{35,99},{64,66},... | collective-permute-start | bytes 811016 | tf_op jit(solution)/shard_map/ppermute | solution.py:36
  6.5 9.7 %collective-permute-start.2 = (bf16[264,512]{1,0:T(8,128)(2,1)S(1)}, bf16[264,512]{1,0:T(8,128)(2,1)S(1)}, u32[]{:S(2)}, u32[]{:S(2)}) collective-permute-start(bf16[264,512]{1,0:T(8,128)(2,1)S(1)} %message.1), channel_id=1, source_target_pairs={{0,130},{1,97},{2,128},{3,99},{32,162},{33,65},{34,160},{35,67},{6... | collective-permute-start | bytes 811016 | tf_op jit(solution)/shard_map/ppermute | solution.py:36
  16.3 14.4 %collective-permute-start.5 = (bf16[4,264,512]{2,1,0:T(8,128)(2,1)S(1)}, bf16[4,264,512]{2,1,0:T(8,128)(2,1)S(1)}, u32[]{:S(2)}, u32[]{:S(2)}) collective-permute-start(bf16[4,264,512]{2,1,0:T(8,128)(2,1)S(1)} %pad_maximum_fusion.own), channel_id=1, source_target_pairs={{0,32},{1,129},{2,34},{3,131},{32,0},{33,161},{34,2},{35,163},{64,... | collective-permute-start | bytes 3244040 | tf_op jit(solution)/shard_map/ppermute | solution.py:36
  17.3 15.7 %collective-permute-start.3 = (bf16[4,264,512]{2,1,0:T(8,128)(2,1)S(1)}, bf16[4,264,512]{2,1,0:T(8,128)(2,1)S(1)}, u32[]{:S(2)}, u32[]{:S(2)}) collective-permute-start(bf16[4,264,512]{2,1,0:T(8,128)(2,1)S(1)} %pad_maximum_fusion.own), channel_id=1, source_target_pairs={{0,96},{1,131},{2,98},{3,129},{32,64},{33,163},{34,66},{35,161},{6... | collective-permute-start | bytes 3244040 | tf_op jit(solution)/shard_map/ppermute | solution.py:36
  19.2 20.7 %collective-permute-start.7 = (bf16[4,264,512]{2,1,0:T(8,128)(2,1)S(1)}, bf16[4,264,512]{2,1,0:T(8,128)(2,1)S(1)}, u32[]{:S(2)}, u32[]{:S(2)}) collective-permute-start(bf16[4,264,512]{2,1,0:T(8,128)(2,1)S(1)} %pad_maximum_fusion.own), channel_id=1, source_target_pairs={{0,1},{1,0},{2,3},{3,2},{4,5},{5,4},{6,7},{7,6},{8,9},{9,8},{10,11... | collective-permute-start | bytes 3244040 | tf_op jit(solution)/shard_map/ppermute | solution.py:44
  30.7 12.7 %collective-permute-start.6 = (bf16[4,264,512]{2,1,0:T(8,128)(2,1)S(1)}, bf16[4,264,512]{2,1,0:T(8,128)(2,1)S(1)}, u32[]{:S(2)}, u32[]{:S(2)}) collective-permute-start(bf16[4,264,512]{2,1,0:T(8,128)(2,1)S(1)} %collective-permute-done.5.refs_0_), channel_id=1, source_target_pairs={{0,1},{1,0},{2,3},{3,2},{4,5},{5,4},{6,7},{7,6},{8,9},{9,8},{10,11... | collective-permute-start | bytes 3244040 | tf_op jit(solution)/shard_map/ppermute | solution.py:44
  33.1 13.4 %collective-permute-start.4 = (bf16[4,264,512]{2,1,0:T(8,128)(2,1)S(1)}, bf16[4,264,512]{2,1,0:T(8,128)(2,1)S(1)}, u32[]{:S(2)}, u32[]{:S(2)}) collective-permute-start(bf16[4,264,512]{2,1,0:T(8,128)(2,1)S(1)} %collective-permute-done.3.refs_0_), channel_id=1, source_target_pairs={{0,1},{1,0},{2,3},{3,2},{4,5},{5,4},{6,7},{7,6},{8,9},{9,8},{10,11... | collective-permute-start | bytes 3244040 | tf_op jit(solution)/shard_map/ppermute | solution.py:44
  39.2 10.3 %collective-permute-start.8 = (bf16[2,264,512]{2,1,0:T(8,128)(2,1)S(1)}, bf16[2,264,512]{2,1,0:T(8,128)(2,1)S(1)}, u32[]{:S(2)}, u32[]{:S(2)}) collective-permute-start(bf16[2,264,512]{2,1,0:T(8,128)(2,1)S(1)} %slice.40), channel_id=1, source_target_pairs={{0,96},{1,131},{2,98},{3,129},{32,64},{33,163},{34,66},{35,161},{6... | collective-permute-start | bytes 1622024 | tf_op jit(solution)/shard_map/ppermute | solution.py:36
  39.8 9.8 %collective-permute-start.9 = (bf16[2,264,512]{2,1,0:T(8,128)(2,1)S(1)}, bf16[2,264,512]{2,1,0:T(8,128)(2,1)S(1)}, u32[]{:S(2)}, u32[]{:S(2)}) collective-permute-start(bf16[2,264,512]{2,1,0:T(8,128)(2,1)S(1)} %slice.41), channel_id=1, source_target_pairs={{0,32},{1,129},{2,34},{3,131},{32,0},{33,161},{34,2},{35,163},{64,... | collective-permute-start | bytes 1622024 | tf_op jit(solution)/shard_map/ppermute | solution.py:36
  49.6 17.2 %collective-permute-start.10 = (bf16[2,264,512]{2,1,0:T(8,128)(2,1)S(1)}, bf16[2,264,512]{2,1,0:T(8,128)(2,1)S(1)}, u32[]{:S(2)}, u32[]{:S(2)}) collective-permute-start(bf16[2,264,512]{2,1,0:T(8,128)(2,1)S(1)} %collective-permute-done.8.low), channel_id=1, source_target_pairs={{0,1},{1,0},{2,3},{3,2},{4,5},{5,4},{6,7},{7,6},{8,9},{9,8},{10,11... | collective-permute-start | bytes 1622024 | tf_op jit(solution)/shard_map/ppermute | solution.py:44
  51.4 15.4 %collective-permute-start.11 = (bf16[2,264,512]{2,1,0:T(8,128)(2,1)S(1)}, bf16[2,264,512]{2,1,0:T(8,128)(2,1)S(1)}, u32[]{:S(2)}, u32[]{:S(2)}) collective-permute-start(bf16[2,264,512]{2,1,0:T(8,128)(2,1)S(1)} %collective-permute-done.9.high), channel_id=1, source_target_pairs={{0,1},{1,0},{2,3},{3,2},{4,5},{5,4},{6,7},{7,6},{8,9},{9,8},{10,11... | collective-permute-start | bytes 1622024 | tf_op jit(solution)/shard_map/ppermute | solution.py:44
  51.5 8.4 %collective-permute-start.12 = (f32[8,128]{1,0:T(8,128)S(1)}, f32[8,128]{1,0:T(8,128)S(1)}, u32[]{:S(2)}, u32[]{:S(2)}) collective-permute-start(f32[8,128]{1,0:T(8,128)S(1)} %rows.1), channel_id=1, source_target_pairs={{0,4},{1,9},{4,8},{5,13},{8,12},{9,17},{12,16},{13,21},{16,20},{17... | collective-permute-start | bytes 12296 | tf_op jit(solution)/shard_map/ppermute | solution.py:56
  54.8 6.4 %collective-permute-start.13 = (f32[8,128]{1,0:T(8,128)S(1)}, f32[8,128]{1,0:T(8,128)S(1)}, u32[]{:S(2)}, u32[]{:S(2)}) collective-permute-start(f32[8,128]{1,0:T(8,128)S(1)} %rows.1), channel_id=1, source_target_pairs={{0,12},{1,17},{4,16},{5,21},{8,20},{9,25},{12,24},{13,29},{16,28},... | collective-permute-start | bytes 12296 | tf_op jit(solution)/shard_map/ppermute | solution.py:56
  61.1 2.5 %collective-permute-start.15 = (f32[8,128]{1,0:T(8,128)S(1)}, f32[8,128]{1,0:T(8,128)S(1)}, u32[]{:S(2)}, u32[]{:S(2)}) collective-permute-start(f32[8,128]{1,0:T(8,128)S(1)} %part.1.refs_6_), channel_id=1, source_target_pairs={{0,128},{128,0},{1,129},{129,1},{2,130},{130,2},{3,131},{131,3},{4... | collective-permute-start | bytes 12296 | tf_op jit(solution)/shard_map/ppermute | solution.py:40
  61.2 5.6 %collective-permute-start.14 = (f32[8,128]{1,0:T(8,128)S(1)}, f32[8,128]{1,0:T(8,128)S(1)}, u32[]{:S(2)}, u32[]{:S(2)}) collective-permute-start(f32[8,128]{1,0:T(8,128)S(1)} %part.1.refs_6_), channel_id=1, source_target_pairs={{0,1},{1,0},{2,3},{3,2},{4,5},{5,4},{6,7},{7,6},{8,9},{9,8},{10,11... | collective-permute-start | bytes 12296 | tf_op jit(solution)/shard_map/ppermute | solution.py:44
  63.7 3.1 %collective-permute-start.16 = (f32[8,128]{1,0:T(8,128)S(1)}, f32[8,128]{1,0:T(8,128)S(1)}, u32[]{:S(2)}, u32[]{:S(2)}) collective-permute-start(f32[8,128]{1,0:T(8,128)S(1)} %collective-permute-done.15.refs_8_), channel_id=1, source_target_pairs={{0,1},{1,0},{2,3},{3,2},{4,5},{5,4},{6,7},{7,6},{8,9},{9,8},{10,11... | collective-permute-start | bytes 12296 | tf_op jit(solution)/shard_map/ppermute | solution.py:44
  70.7 6.9 %collective-permute-start.17 = (bf16[4,3,32,384]{3,2,1,0:T(8,128)(2,1)S(1)}, bf16[4,3,32,384]{3,2,1,0:T(8,128)(2,1)S(1)}, u32[]{:S(2)}, u32[]{:S(2)}) collective-permute-start(bf16[4,3,32,384]{3,2,1,0:T(8,128)(2,1)S(1)} %get-tuple-element.42), channel_id=1, source_target_pairs={{0,4},{1,29},{4,0},{5,9},{8,12},{9,5},{12,8},{13,17},{16,20},{17,1... | collective-permute-start | bytes 884744 | tf_op jit(solution)/shard_map/ppermute | solution.py:52
  75.4 5.8 %collective-permute-start.21 = (bf16[4,3,32,256]{3,2,1,0:T(8,128)(2,1)S(1)}, bf16[4,3,32,256]{3,2,1,0:T(8,128)(2,1)S(1)}, u32[]{:S(2)}, u32[]{:S(2)}) collective-permute-start(bf16[4,3,32,256]{3,2,1,0:T(8,128)(2,1)S(1)} %get-tuple-element.48), channel_id=1, source_target_pairs={{0,4},{1,29},{4,0},{5,9},{8,12},{9,5},{12,8},{13,17},{16,20},{17,1... | collective-permute-start | bytes 589832 | tf_op jit(solution)/shard_map/ppermute | solution.py:52
  81.3 10.1 %collective-permute-start.22 = (bf16[3,32,256]{2,1,0:T(8,128)(2,1)S(1)}, bf16[3,32,256]{2,1,0:T(8,128)(2,1)S(1)}, u32[]{:S(2)}, u32[]{:S(2)}) collective-permute-start(bf16[3,32,256]{2,1,0:T(8,128)(2,1)S(1)} %get-tuple-element.56), channel_id=1, source_target_pairs={{0,16},{4,20},{8,24},{12,28},{16,0},{20,4},{24,8},{28,12},{1,17},{... | collective-permute-start | bytes 147464 | tf_op jit(solution)/shard_map/ppermute | solution.py:62
  85.6 8.5 %collective-permute-start.23 = (bf16[3,32,256]{2,1,0:T(8,128)(2,1)S(1)}, bf16[3,32,256]{2,1,0:T(8,128)(2,1)S(1)}, u32[]{:S(2)}, u32[]{:S(2)}) collective-permute-start(bf16[3,32,256]{2,1,0:T(8,128)(2,1)S(1)} %get-tuple-element.58), channel_id=1, source_target_pairs={{0,8},{4,12},{8,16},{12,20},{16,24},{20,28},{24,0},{28,4},{1,9},{5... | collective-permute-start | bytes 147464 | tf_op jit(solution)/shard_map/ppermute | solution.py:62
  85.8 8.3 %collective-permute-start.24 = (bf16[3,32,256]{2,1,0:T(8,128)(2,1)S(1)}, bf16[3,32,256]{2,1,0:T(8,128)(2,1)S(1)}, u32[]{:S(2)}, u32[]{:S(2)}) collective-permute-start(bf16[3,32,256]{2,1,0:T(8,128)(2,1)S(1)} %get-tuple-element.57), channel_id=1, source_target_pairs={{0,24},{4,28},{8,0},{12,4},{16,8},{20,12},{24,16},{28,20},{1,25},{... | collective-permute-start | bytes 147464 | tf_op jit(solution)/shard_map/ppermute | solution.py:62
  89.2 7.8 %collective-permute-start.18 = (bf16[3,32,384]{2,1,0:T(8,128)(2,1)S(1)}, bf16[3,32,384]{2,1,0:T(8,128)(2,1)S(1)}, u32[]{:S(2)}, u32[]{:S(2)}) collective-permute-start(bf16[3,32,384]{2,1,0:T(8,128)(2,1)S(1)} %get-tuple-element.53), channel_id=1, source_target_pairs={{0,16},{4,20},{8,24},{12,28},{16,0},{20,4},{24,8},{28,12},{1,17},{... | collective-permute-start | bytes 221192 | tf_op jit(solution)/shard_map/ppermute | solution.py:62
  90.4 7.6 %collective-permute-start.19 = (bf16[3,32,384]{2,1,0:T(8,128)(2,1)S(1)}, bf16[3,32,384]{2,1,0:T(8,128)(2,1)S(1)}, u32[]{:S(2)}, u32[]{:S(2)}) collective-permute-start(bf16[3,32,384]{2,1,0:T(8,128)(2,1)S(1)} %get-tuple-element.55), channel_id=1, source_target_pairs={{0,8},{4,12},{8,16},{12,20},{16,24},{20,28},{24,0},{28,4},{1,9},{5... | collective-permute-start | bytes 221192 | tf_op jit(solution)/shard_map/ppermute | solution.py:62
  91.3 9.1 %collective-permute-start.20 = (bf16[3,32,384]{2,1,0:T(8,128)(2,1)S(1)}, bf16[3,32,384]{2,1,0:T(8,128)(2,1)S(1)}, u32[]{:S(2)}, u32[]{:S(2)}) collective-permute-start(bf16[3,32,384]{2,1,0:T(8,128)(2,1)S(1)} %get-tuple-element.54), channel_id=1, source_target_pairs={{0,24},{4,28},{8,0},{12,4},{16,8},{20,12},{24,16},{28,20},{1,25},{... | collective-permute-start | bytes 221192 | tf_op jit(solution)/shard_map/ppermute | solution.py:62

commit v7 on v6

--- a/solution.py
+++ b/solution.py
@@ -11,7 +11,8 @@
 I32 = jnp.int32
 ROOT_2_PI = 0.7978845608028654
 CUBIC = 0.044715
-CUTS = ((0, 384), (384, 640))
+CUTS = ((0, 256), (256, 640))
+OWN, EARLY, LATE, FAR = ((0, 0), (0, 1)), ((1, 0), (3, 1)), ((1, 1), (3, 0)), ((2, 0), (2, 1))
 BLK = ("xl", "y", "z")
 PLANE = ("xl", "y", "xh", "c")
 SMEM = pl.BlockSpec(memory_space=pltpu.SMEM)
@@ -141,24 +142,25 @@
     )(*[hbm(w.reshape(4, 512, 640)) for w in (w_gate, w_lin, w_out_t)])
 
 
-def rows_kernel(own, other, rows):
+def rows_kernel(own_low, own_high, other_low, other_high, rows):
     c = lax.axis_index("c").astype(I32)
     rows[...] = jnp.zeros_like(rows)
     for dy in range(4):
-        piece = [block[dy, 256:264, 0:128].astype(F32) for block in (own, other)]
+        pair = (own_low, other_low) if dy < 2 else (own_high, other_high)
+        piece = [block[dy % 2, 256:264, 0:128].astype(F32) for block in pair]
         piece = jnp.where(c == 1, piece[0], piece[1])
         rows[dy : dy + 1, :] = jnp.sum(piece, axis=0, keepdims=True)
 
 
-def line_rows(own, other):
+def line_rows(*blocks):
     return pl.pallas_call(
         rows_kernel,
         out_shape=jax.ShapeDtypeStruct((8, 128), F32),
-        in_specs=[VMEM] * 2,
+        in_specs=[VMEM] * 4,
         out_specs=VMEM,
         compiler_params=PARAMS,
         name="rows",
-    )(own, other)
+    )(*blocks)
 
 
 def part_kernel(rows, near, far, out):
@@ -180,70 +182,36 @@
     )(*rows)
 
 
-def first_kernel(own, other, w_in, w_out, acc, cols):
-    acc[...] = jnp.zeros_like(acc)
-    gather_kernel(0, ((0, own), (1, other)), w_in, w_out, acc, cols)
-
-
-def middle_kernel(m, *refs):
-    *blocks, w_in, w_out, _, __, acc, cols = refs
-    gather_kernel(m, tuple(enumerate(blocks)), w_in, w_out, acc, cols)
-
-
-def halves_kernel(low, high, w_in, w_out, _, __, acc, cols):
-    gather_kernel(2, ((0, (low, high)),), w_in, w_out, acc, cols)
-
-
-def final_kernel(cut, low, high, w_in, w_out, _, __, *refs):
-    terms, (acc, cols, *rest) = refs[:4], refs[4:]
-    gather_kernel(2, ((1, (low, high)),), w_in, w_out, acc, cols, (CUTS[cut],), cut == 0)
-    last_kernel(CUTS[cut], terms, acc, cols, *rest)
-
-
-def gather_kernel(m, blocks, w_in, w_out, acc, cols, cuts=CUTS, with_cols=True):
+def add_block(m, j, ec, block, w_in, w_out, acc, cols, cuts=CUTS, with_cols=True):
     xl, y, _, xh, c = place()
-    for ec, block in blocks:
-        x_first = (c ^ ec) == 0
-
-        def step(j, block, start):
-            eh = jnp.where(x_first, j, m >> 1)
-            p0 = jnp.where(x_first, 2 * m, 4 * j + (m & 1))
-            p1 = jnp.where(x_first, 2 * m + 1, 4 * j + 2 + (m & 1))
-            shard = (xh ^ eh) * 2 + (c ^ ec)
-            xs = block[pl.ds(start, 2), 0:128].reshape(256, 512)
-            ys = block[pl.ds(start, 2), 128:256].reshape(256, 512)
-            first, end = cuts[0][0], cuts[-1][1]
-            pre = jnp.dot(xs, w_in[shard, :, 2 * first : 2 * end], preferred_element_type=F32)
-            for lower, upper in cuts:
-                width = upper - lower
-                for n in range(2):
-                    at = 2 * (lower - first) + n * width
-                    acc[n, p0, :, lower:upper] += pre[:128, at : at + width]
-                    acc[n, p1, :, lower:upper] += pre[128:, at : at + width]
-            dh = jnp.dot(ys, w_out[shard, :, first:end], preferred_element_type=F32)
-            acc[2, p0, :, first:end] += dh[:128]
-            acc[2, p1, :, first:end] += dh[128:]
-            if not with_cols:
-                return
-
-            @pl.when((ec == ((y >> 1) ^ c)) & (eh == (xl ^ xh)))
-            def _():
-                low = (y & 1) == 0
-                for n, v in ((0, xs), (1, ys)):
-                    v = jnp.where(low, v[:, :256], v[:, 256:])
-                    cols[n, p0] = v[:128]
-                    cols[n, p1] = v[128:]
-
-        if isinstance(block, tuple):
-            for j in range(2):
-                step(j, block[j], 0)
-        else:
-
-            def body(j, carry):
-                step(j, block, 2 * j)
-                return carry
-
-            lax.fori_loop(0, 2, body, 0)
+    x_first = (c ^ ec) == 0
+    eh = jnp.where(x_first, j, m >> 1)
+    p0 = jnp.where(x_first, 2 * m, 4 * j + (m & 1))
+    p1 = jnp.where(x_first, 2 * m + 1, 4 * j + 2 + (m & 1))
+    shard = (xh ^ eh) * 2 + (c ^ ec)
+    xs = block[:, 0:128].reshape(256, 512)
+    ys = block[:, 128:256].reshape(256, 512)
+    first, end = cuts[0][0], cuts[-1][1]
+    pre = jnp.dot(xs, w_in[shard, :, 2 * first : 2 * end], preferred_element_type=F32)
+    for lower, upper in cuts:
+        width = upper - lower
+        for n in range(2):
+            at = 2 * (lower - first) + n * width
+            acc[n, p0, :, lower:upper] += pre[:128, at : at + width]
+            acc[n, p1, :, lower:upper] += pre[128:, at : at + width]
+    dh = jnp.dot(ys, w_out[shard, :, first:end], preferred_element_type=F32)
+    acc[2, p0, :, first:end] += dh[:128]
+    acc[2, p1, :, first:end] += dh[128:]
+    if not with_cols:
+        return
+
+    @pl.when((ec == ((y >> 1) ^ c)) & (eh == (xl ^ xh)))
+    def _():
+        low = (y & 1) == 0
+        for n, v in ((0, xs), (1, ys)):
+            v = jnp.where(low, v[:, :256], v[:, 256:])
+            cols[n, p0] = v[:128]
+            cols[n, p1] = v[128:]
 
 
 STATE = (jax.ShapeDtypeStruct((3, 8, 128, 640), F32), jax.ShapeDtypeStruct((2, 8, 128, 256), BF16))
@@ -253,24 +221,39 @@
     return pl.CostEstimate(flops=giga << 30, bytes_accessed=1 << 20, transcendentals=0)
 
 
-def gathered(m, blocks, w_in, w_out, state):
-    n = len(blocks) + 2
-    kernels = {0: first_kernel, 2: halves_kernel}
-    return pl.pallas_call(
-        kernels.get(m, lambda *refs: middle_kernel(m, *refs)),
+def gathered(items, w_in, w_out, state):
+    n = len(items)
+
+    def kernel(*refs):
+        blocks, (w_in, w_out), (acc, cols) = refs[:n], refs[n : n + 2], refs[-2:]
+        if not state:
+            acc[...] = jnp.zeros_like(acc)
+        for (m, j, ec, _), block in zip(items, blocks):
+            add_block(m, j, ec, block, w_in, w_out, acc, cols)
+
+    return pl.pallas_call(
+        kernel,
         out_shape=STATE,
-        in_specs=[VMEM] * (n + len(state)),
+        in_specs=[VMEM] * (n + 2 + len(state)),
         out_specs=(VMEM, VMEM),
-        input_output_aliases={n: 0, n + 1: 1} if state else {},
-        compiler_params=PARAMS,
-        cost_estimate=priced(2 if m != 2 else 1),
-    )(*blocks, w_in, w_out, *state)
-
-
-def finished(cut, halves, w_in, w_out, state, terms):
+        input_output_aliases={n + 2: 0, n + 3: 1} if state else {},
+        compiler_params=PARAMS,
+        cost_estimate=priced(n // 2),
+    )(*[item[3] for item in items], w_in, w_out, *state)
+
+
+def finished(cut, items, w_in, w_out, state, terms):
     width = CUTS[cut][1] - CUTS[cut][0]
+
+    def kernel(*refs):
+        blocks, (w_in, w_out), terms = refs[:2], refs[2:4], refs[6:10]
+        acc, cols, *rest = refs[10:]
+        for (m, j, ec, _), block in zip(items, blocks):
+            add_block(m, j, ec, block, w_in, w_out, acc, cols, (CUTS[cut],), cut == 0)
+        last_kernel(CUTS[cut], terms, acc, cols, *rest)
+
     *state, keep, send = pl.pallas_call(
-        lambda *refs: final_kernel(cut, *refs),
+        kernel,
         out_shape=STATE
         + (jax.ShapeDtypeStruct((4, 3, 32, width), F32), jax.ShapeDtypeStruct((4, 3, 32, width), BF16)),
         in_specs=[VMEM] * 10,
@@ -283,7 +266,7 @@
         ],
         compiler_params=PARAMS,
         cost_estimate=priced(2),
-    )(*halves, w_in, w_out, *state, *terms)
+    )(*[item[3] for item in items], w_in, w_out, *state, *terms)
     return state, keep, send
 
 
@@ -338,16 +321,19 @@
 
 def all_steps(tokens, grad_out, w_gate, w_lin, w_out_t, code, decode, stragglers):
     own = message(code, decode, stragglers, tokens, grad_out)
-    row = [own]
+    first = {}
     for k in (1, 2, 3):
-        row.append(across(own, k, True))
+        first[k] = across(own, k, True)
     w_in, w_out = loaded_weights(w_gate, w_lin, w_out_t)
-    row = jnp.stack(row)
-    near = {}
-    for k in (1, 3):
-        near[k] = across(row, k, False)
-    swap = sibling(row)
-    rows = line_rows(row, swap)
+    blocks = {(0, 0): jnp.stack([own, first[1]]), (0, 1): jnp.stack([first[2], first[3]])}
+    others = {}
+    for k, j in EARLY + LATE:
+        blocks[k, j] = across(blocks[0, j], k, False)
+    for j, came in ((0, 1), (1, 3)):
+        blocks[2, j] = across(blocks[came, j], came ^ 2, False)
+    for k, j in OWN + EARLY + LATE:
+        others[k, j] = sibling(blocks[k, j])
+    rows = line_rows(blocks[0, 0], blocks[0, 1], others[0, 0], others[0, 1])
     got = []
     for j in (1, 3):
         got.append(z_shift(rows, j))
@@ -356,17 +342,18 @@
     terms = []
     for part in partials:
         terms += [part, sibling(part)]
-    low = across(near[1][:2], 3, False)
-    high = across(near[3][2:], 1, False)
-    other = {}
-    for k in (1, 3):
-        other[k] = sibling(near[k])
-    state = gathered(0, (row, swap), w_in, w_out, ())
-    for m in (1, 3):
-        state = gathered(m, (near[m], other[m]), w_in, w_out, state)
-    state, low, high = lax.optimization_barrier((state, low, high))
-    halves = [sibling(low), sibling(high)]
-    state = gathered(2, (low, high), w_in, w_out, state)
+
+    def items(keys, sides=(0, 1)):
+        return [(m, j, ec, (blocks, others)[ec][m, j]) for m, j in keys for ec in sides]
+
+    state = ()
+    for keys in (OWN, EARLY, LATE):
+        state = gathered(items(keys), w_in, w_out, state)
+    state, blocks[2, 0], blocks[2, 1] = lax.optimization_barrier((state, blocks[2, 0], blocks[2, 1]))
+    for k, j in FAR:
+        others[k, j] = sibling(blocks[k, j])
+    state = gathered(items(FAR, (0,)), w_in, w_out, state)
+    halves = items(FAR, (1,))
     keeps, got = [], []
     for cut in range(2):
         state, keep, send = finished(cut, halves, w_in, w_out, state, terms)

time: 101 us -> 94.8 us (0.939)
  waiting for transfers between devices: 32.9 us -> 23.1 us
  starting transfers between devices: 44 us -> 47.2 us
    ppermute x2, waiting for transfers between devices: 4.62 us -> 0.01 us  [z_pair(): lax.ppermute(block, ('z', 'c'), [(z * 2 + c, partner_of(z, c) * 2 + c) fo...]
    ppermute x7 -> x9, waiting for transfers between devices: 18.8 us -> 14.8 us  [across(): return lax.ppermute(block, PLANE, route)]
    ppermute x7 -> x9, starting transfers between devices: 8.25 us -> 11.5 us  [across(): return lax.ppermute(block, PLANE, route)]
    ppermute x7 -> x10, starting transfers between devices: 11.7 us -> 9.56 us  [sibling(): return lax.ppermute(block, 'c', [(0, 1), (1, 0)])]
    ppermute x6, starting transfers between devices: 12.7 us -> 14.2 us  [z_step(): return lax.ppermute(block, 'z', [(z, (z + step) % 8) for z in range(8)])]
  transfers between devices with their start and end apart: 25 -> 30, of which waited for: 11 -> 8; matrix products, arithmetic and copies ran while one was open for 0% -> 0% of each run, Pallas kernels for 17% -> 19%
where the time goes in v7:
time: 94.8 us; the launch traced here: 94.7 us
  starting transfers between devices  47.2 us (50%)
  waiting for transfers between devices  23.1 us (24%)
  Pallas kernels  22.5 us (24%)
  other arithmetic  1.03 us (1%)
    ppermute x9, waiting for transfers between devices, across(): return lax.ppermute(block, PLANE, route)  14.8 us
    ppermute x6, starting transfers between devices, z_step(): return lax.ppermute(block, 'z', [(z, (z + step) % 8) for z in range(8)])  14.2 us
    ppermute x9, starting transfers between devices, across(): return lax.ppermute(block, PLANE, route)  11.5 us
    pallas_call x4, Pallas kernels, gathered(): pl.pallas_call(kernel, out_shape=STATE, in_specs=[VMEM] * (n + 2 + len(st...  11.2 us
    ppermute x10, starting transfers between devices, sibling(): return lax.ppermute(block, 'c', [(0, 1), (1, 0)])  9.56 us
    ppermute x2, starting transfers between devices, z_shift(): lax.ppermute(block, ('z', 'c'), [(z * 2 + c, (z + step + c) % 8 * 2 + c)...  8.2 us
    pallas_call x2, Pallas kernels, finished(): pl.pallas_call(kernel, out_shape=STATE + (jax.ShapeDtypeStruct((4, 3, 32,...  6.94 us
    ppermute x6, waiting for transfers between devices, z_step(): return lax.ppermute(block, 'z', [(z, (z + step) % 8) for z in range(8)])  5.76 us
  transfers between devices with their start and end apart: 30, of which 8 were waited for; matrix products, arithmetic and copies ran while one was open for 0% of the time, Pallas kernels for 19%

profile of v7, /device:TPU:1, one launch (start us, length us, event | category | flops | bytes accessed | tf_op | source)
XLA Modules:
  0.0 94.7 jit_solution(16649614040692212962)
XLA Ops:
  1.7 3.8 %collective-permute-start = (bf16[264,512]{1,0:T(8,128)(2,1)S(1)}, bf16[264,512]{1,0:T(8,128)(2,1)S(1)}, u32[]{:S(2)}, u32[]{:S(2)}) collective-permute-start(bf16[264,512]{1,0:T(8,128)(2,1)S(1)} %message.1), channel_id=1, source_target_pairs={{0,2},{1,65},{2,0},{3,67},{32,34},{33,97},{34,32},{35,99},{64,66},... | collective-permute-start | bytes 811016 | tf_op jit(solution)/shard_map/ppermute | solution.py:37
  6.3 3.4 %collective-permute-done = bf16[264,512]{1,0:T(8,128)(2,1)S(1)} collective-permute-done((bf16[264,512]{1,0:T(8,128)(2,1)S(1)}, bf16[264,512]{1,0:T(8,128)(2,1)S(1)}, u32[]{:S(2)}, u32[]{:S(2)}) %collective-permute-start) | collective-permute-done | bytes 270368 | tf_op jit(solution)/shard_map/ppermute | solution.py:37
  9.6 2.9 %collective-permute-done.1 = bf16[264,512]{1,0:T(8,128)(2,1)S(1)} collective-permute-done((bf16[264,512]{1,0:T(8,128)(2,1)S(1)}, bf16[264,512]{1,0:T(8,128)(2,1)S(1)}, u32[]{:S(2)}, u32[]{:S(2)}) %collective-permute-start.1) | collective-permute-done | bytes 270368 | tf_op jit(solution)/shard_map/ppermute | solution.py:37
  12.6 3.4 %collective-permute-start.12 = (bf16[2,264,512]{2,1,0:T(8,128)(2,1)S(1)}, bf16[2,264,512]{2,1,0:T(8,128)(2,1)S(1)}, u32[]{:S(2)}, u32[]{:S(2)}) collective-permute-start(bf16[2,264,512]{2,1,0:T(8,128)(2,1)S(1)} %pad_maximum_fusion.refs_2_.own_high), channel_id=1, source_target_pairs={{0,1},{1,0},{2,3},{3,2},{4,5},{5,4},{6,7},{7,6},{8,9},{9,8},{10,11... | collective-permute-start | bytes 1622024 | tf_op jit(solution)/shard_map/ppermute | solution.py:45
  16.9 1.5 %collective-permute-start.2 = (bf16[2,264,512]{2,1,0:T(8,128)(2,1)S(1)}, bf16[2,264,512]{2,1,0:T(8,128)(2,1)S(1)}, u32[]{:S(2)}, u32[]{:S(2)}) collective-permute-start(bf16[2,264,512]{2,1,0:T(8,128)(2,1)S(1)} %pad_maximum_fusion.refs_2_.own_high), channel_id=1, source_target_pairs={{0,32},{1,129},{2,34},{3,131},{32,0},{33,161},{34,2},{35,163},{64,... | collective-permute-start | bytes 1622024 | tf_op jit(solution)/shard_map/ppermute | solution.py:37
  18.3 1.9 %collective-permute-start.5 = (bf16[2,264,512]{2,1,0:T(8,128)(2,1)S(1)}, bf16[2,264,512]{2,1,0:T(8,128)(2,1)S(1)}, u32[]{:S(2)}, u32[]{:S(2)}) collective-permute-start(bf16[2,264,512]{2,1,0:T(8,128)(2,1)S(1)} %pad_maximum_fusion.1.refs_0_.own_low), channel_id=1, source_target_pairs={{0,96},{1,131},{2,98},{3,129},{32,64},{33,163},{34,66},{35,161},{6... | collective-permute-start | bytes 1622024 | tf_op jit(solution)/shard_map/ppermute | solution.py:37
  20.2 1.2 %collective-permute-start.11 = (bf16[2,264,512]{2,1,0:T(8,128)(2,1)S(1)}, bf16[2,264,512]{2,1,0:T(8,128)(2,1)S(1)}, u32[]{:S(2)}, u32[]{:S(2)}) collective-permute-start(bf16[2,264,512]{2,1,0:T(8,128)(2,1)S(1)} %pad_maximum_fusion.1.refs_0_.own_low), channel_id=1, source_target_pairs={{0,1},{1,0},{2,3},{3,2},{4,5},{5,4},{6,7},{7,6},{8,9},{9,8},{10,11... | collective-permute-start | bytes 1622024 | tf_op jit(solution)/shard_map/ppermute | solution.py:45
  21.5 4.2 %collective-permute-done.9.refs_2_ = bf16[2,264,512]{2,1,0:T(8,128)(2,1)S(1)} collective-permute-done((bf16[2,264,512]{2,1,0:T(8,128)(2,1)S(1)}, bf16[2,264,512]{2,1,0:T(8,128)(2,1)S(1)}, u32[]{:S(2)}, u32[]{:S(2)}) %collective-permute-start.9) | collective-permute-done | bytes 540704 | tf_op jit(solution)/shard_map/ppermute | solution.py:37
  26.9 4.3 %collective-permute-done.2.refs_0_ = bf16[2,264,512]{2,1,0:T(8,128)(2,1)S(1)} collective-permute-done((bf16[2,264,512]{2,1,0:T(8,128)(2,1)S(1)}, bf16[2,264,512]{2,1,0:T(8,128)(2,1)S(1)}, u32[]{:S(2)}, u32[]{:S(2)}) %collective-permute-start.2) | collective-permute-done | bytes 540704 | tf_op jit(solution)/shard_map/ppermute | solution.py:37
  31.2 1.5 %collective-permute-start.3 = (bf16[2,264,512]{2,1,0:T(8,128)(2,1)S(1)}, bf16[2,264,512]{2,1,0:T(8,128)(2,1)S(1)}, u32[]{:S(2)}, u32[]{:S(2)}) collective-permute-start(bf16[2,264,512]{2,1,0:T(8,128)(2,1)S(1)} %collective-permute-done.2.refs_0_), channel_id=1, source_target_pairs={{0,1},{1,0},{2,3},{3,2},{4,5},{5,4},{6,7},{7,6},{8,9},{9,8},{10,11... | collective-permute-start | bytes 1622024 | tf_op jit(solution)/shard_map/ppermute | solution.py:45
  32.7 3.4 %load.1 = (bf16[4,512,1280]{2,1,0:T(8,128)(2,1)S(1)}, bf16[4,512,640]{2,1,0:T(8,128)(2,1)S(1)}) custom-call(bf16[4,512,640]{2,1,0:T(8,128)(2,1)} %bitcast.38, bf16[4,512,640]{2,1,0:T(8,128)(2,1)} %bitcast.39, bf16[4,512,640]{2,1,0:T(8,128)(2,1)} %bitcast.40), custom_call_target="tpu_custom_call" | custom-call | tf_op jit(solution)/shard_map/load/pallas_call | solution.py:131
  36.0 1.3 %collective-permute-start.14 = (bf16[2,264,512]{2,1,0:T(8,128)(2,1)S(1)}, bf16[2,264,512]{2,1,0:T(8,128)(2,1)S(1)}, u32[]{:S(2)}, u32[]{:S(2)}) collective-permute-start(bf16[2,264,512]{2,1,0:T(8,128)(2,1)S(1)} %collective-permute-done.9.refs_2_), channel_id=1, source_target_pairs={{0,32},{1,129},{2,34},{3,131},{32,0},{33,161},{34,2},{35,163},{64,... | collective-permute-start | bytes 1622024 | tf_op jit(solution)/shard_map/ppermute | solution.py:37
  37.3 1.4 %collective-permute-start.13 = (bf16[2,264,512]{2,1,0:T(8,128)(2,1)S(1)}, bf16[2,264,512]{2,1,0:T(8,128)(2,1)S(1)}, u32[]{:S(2)}, u32[]{:S(2)}) collective-permute-start(bf16[2,264,512]{2,1,0:T(8,128)(2,1)S(1)} %collective-permute-done.7.refs_0_), channel_id=1, source_target_pairs={{0,96},{1,131},{2,98},{3,129},{32,64},{33,163},{34,66},{35,161},{6... | collective-permute-start | bytes 1622024 | tf_op jit(solution)/shard_map/ppermute | solution.py:37
  38.7 3.6 %shard_map.82 = (f32[3,8,128,640]{3,2,1,0:T(8,128)S(1)}, bf16[2,8,128,256]{3,2,1,0:T(8,128)(2,1)S(1)}) custom-call(bf16[2,264,512]{2,1,0:T(8,128)(2,1)S(1)} %pad_maximum_fusion.1.refs_0_.own_low, bf16[2,264,512]{2,1,0:T(8,128)(2,1)S(1)} %collective-permute-done.11.refs_1_.other_low, bf16[2,264,512]{2,1,0:T(8,128)(2,1)S(1)} %pad_maximum_fusion.refs_2_.own_high, ...), custom_call_target="tpu_custom_call" | custom-call | flops 2147483648 | bytes 1048576 | tf_op jit(solution)/shard_map/pallas_call | solution.py:234
  42.4 3.0 %shard_map.83 = (f32[3,8,128,640]{3,2,1,0:T(8,128)S(1)}, bf16[2,8,128,256]{3,2,1,0:T(8,128)(2,1)S(1)}) custom-call(bf16[2,264,512]{2,1,0:T(8,128)(2,1)S(1)} %collective-permute-done.7.refs_0_, bf16[2,264,512]{2,1,0:T(8,128)(2,1)S(1)} %collective-permute-done.8.refs_1_, ...), custom_call_target="tpu_custom_call", output_to_operand_aliasing={{0}: (6, {}), {1}: (7, {})} | custom-call | flops 2147483648 | bytes 1048576 | tf_op jit(solution)/shard_map/pallas_call | solution.py:234
  45.4 3.0 %shard_map.84 = (f32[3,8,128,640]{3,2,1,0:T(8,128)S(1)}, bf16[2,8,128,256]{3,2,1,0:T(8,128)(2,1)S(1)}) custom-call(bf16[2,264,512]{2,1,0:T(8,128)(2,1)S(1)} %collective-permute-done.2.refs_0_, bf16[2,264,512]{2,1,0:T(8,128)(2,1)S(1)} %collective-permute-done.3.refs_1_, ...), custom_call_target="tpu_custom_call", output_to_operand_aliasing={{0}: (6, {}), {1}: (7, {})} | custom-call | flops 2147483648 | bytes 1048576 | tf_op jit(solution)/shard_map/pallas_call | solution.py:234
  49.1 3.1 %collective-permute-start.17 = (f32[8,128]{1,0:T(8,128)S(1)}, f32[8,128]{1,0:T(8,128)S(1)}, u32[]{:S(2)}, u32[]{:S(2)}) collective-permute-start(f32[8,128]{1,0:T(8,128)S(1)} %rows.1), channel_id=1, source_target_pairs={{0,4},{1,9},{4,8},{5,13},{8,12},{9,17},{12,16},{13,21},{16,20},{17... | collective-permute-start | bytes 12296 | tf_op jit(solution)/shard_map/ppermute | solution.py:57
  52.2 5.1 %collective-permute-start.18 = (f32[8,128]{1,0:T(8,128)S(1)}, f32[8,128]{1,0:T(8,128)S(1)}, u32[]{:S(2)}, u32[]{:S(2)}) collective-permute-start(f32[8,128]{1,0:T(8,128)S(1)} %rows.1), channel_id=1, source_target_pairs={{0,12},{1,17},{4,16},{5,21},{8,20},{9,25},{12,24},{13,29},{16,28},... | collective-permute-start | bytes 12296 | tf_op jit(solution)/shard_map/ppermute | solution.py:57
  57.3 1.3 %collective-permute-done.18.far = f32[8,128]{1,0:T(8,128)S(1)} collective-permute-done((f32[8,128]{1,0:T(8,128)S(1)}, f32[8,128]{1,0:T(8,128)S(1)}, u32[]{:S(2)}, u32[]{:S(2)}) %collective-permute-start.18) | collective-permute-done | bytes 4128 | tf_op jit(solution)/shard_map/ppermute | solution.py:57
  59.8 1.3 %collective-permute-done.20.refs_8_ = f32[8,128]{1,0:T(8,128)S(1)} collective-permute-done((f32[8,128]{1,0:T(8,128)S(1)}, f32[8,128]{1,0:T(8,128)S(1)}, u32[]{:S(2)}, u32[]{:S(2)}) %collective-permute-start.20) | collective-permute-done | bytes 4128 | tf_op jit(solution)/shard_map/ppermute | solution.py:41
  61.1 1.3 %collective-permute-start.21 = (f32[8,128]{1,0:T(8,128)S(1)}, f32[8,128]{1,0:T(8,128)S(1)}, u32[]{:S(2)}, u32[]{:S(2)}) collective-permute-start(f32[8,128]{1,0:T(8,128)S(1)} %collective-permute-done.20.refs_8_), channel_id=1, source_target_pairs={{0,1},{1,0},{2,3},{3,2},{4,5},{5,4},{6,7},{7,6},{8,9},{9,8},{10,11... | collective-permute-start | bytes 12296 | tf_op jit(solution)/shard_map/ppermute | solution.py:45
  62.4 1.5 %shard_map.85 = (f32[3,8,128,640]{3,2,1,0:T(8,128)S(1)}, bf16[2,8,128,256]{3,2,1,0:T(8,128)(2,1)S(1)}) custom-call(bf16[2,264,512]{2,1,0:T(8,128)(2,1)S(1)} %collective-permute-done.13.refs_0_, bf16[2,264,512]{2,1,0:T(8,128)(2,1)S(1)} %collective-permute-done.14.refs_1_, ...), custom_call_target="tpu_custom_call", output_to_operand_aliasing={{0}: (4, {}), {1}: (5, {})} | custom-call | flops 1073741824 | bytes 1048576 | tf_op jit(solution)/shard_map/pallas_call | solution.py:234
  63.9 3.3 %shard_map.86 = (f32[3,8,128,640]{3,2,1,0:T(8,128)S(1)}, bf16[2,8,128,256]{3,2,1,0:T(8,128)(2,1)S(1)}, f32[4,3,32,256]{3,2,1,0:T(8,128)S(1)}, bf16[4,3,32,256]{3,2,1,0:T(8,128)(2,1)S(1)}) custom-call(bf16[2,264,512]{2,1,0:T(8,128)(2,1)S(1)} %collective-permute-done.15.refs_0_, ...), custom_call_target="tpu_custom_call", output_to_operand_aliasing={{0}: (4, {}), {1}: (5, {})} | custom-call | flops 2147483648 | bytes 1048576 | tf_op jit(solution)/shard_map/pallas_call | solution.py:255
  67.2 1.8 %collective-permute-start.22 = (bf16[4,3,32,256]{3,2,1,0:T(8,128)(2,1)S(1)}, bf16[4,3,32,256]{3,2,1,0:T(8,128)(2,1)S(1)}, u32[]{:S(2)}, u32[]{:S(2)}) collective-permute-start(bf16[4,3,32,256]{3,2,1,0:T(8,128)(2,1)S(1)} %get-tuple-element.42), channel_id=1, source_target_pairs={{0,4},{1,29},{4,0},{5,9},{8,12},{9,5},{12,8},{13,17},{16,20},{17,1... | collective-permute-start | bytes 589832 | tf_op jit(solution)/shard_map/ppermute | solution.py:53
  69.0 3.7 %shard_map.87 = (f32[3,8,128,640]{3,2,1,0:T(8,128)S(1)}, bf16[2,8,128,256]{3,2,1,0:T(8,128)(2,1)S(1)}, f32[4,3,32,384]{3,2,1,0:T(8,128)S(1)}, bf16[4,3,32,384]{3,2,1,0:T(8,128)(2,1)S(1)}) custom-call(bf16[2,264,512]{2,1,0:T(8,128)(2,1)S(1)} %collective-permute-done.15.refs_0_, ...), custom_call_target="tpu_custom_call", output_to_operand_aliasing={{0}: (4, {}), {1}: (5, {})} | custom-call | flops 2147483648 | bytes 1048576 | tf_op jit(solution)/shard_map/pallas_call | solution.py:255
  72.7 1.1 %collective-permute-start.26 = (bf16[4,3,32,384]{3,2,1,0:T(8,128)(2,1)S(1)}, bf16[4,3,32,384]{3,2,1,0:T(8,128)(2,1)S(1)}, u32[]{:S(2)}, u32[]{:S(2)}) collective-permute-start(bf16[4,3,32,384]{3,2,1,0:T(8,128)(2,1)S(1)} %get-tuple-element.48), channel_id=1, source_target_pairs={{0,4},{1,29},{4,0},{5,9},{8,12},{9,5},{12,8},{13,17},{16,20},{17,1... | collective-permute-start | bytes 884744 | tf_op jit(solution)/shard_map/ppermute | solution.py:53
  73.8 5.2 %collective-permute-start.23 = (bf16[3,32,256]{2,1,0:T(8,128)(2,1)S(1)}, bf16[3,32,256]{2,1,0:T(8,128)(2,1)S(1)}, u32[]{:S(2)}, u32[]{:S(2)}) collective-permute-start(bf16[3,32,256]{2,1,0:T(8,128)(2,1)S(1)} %get-tuple-element.56), channel_id=1, source_target_pairs={{0,16},{4,20},{8,24},{12,28},{16,0},{20,4},{24,8},{28,12},{1,17},{... | collective-permute-start | bytes 147464 | tf_op jit(solution)/shard_map/ppermute | solution.py:63
  79.1 3.6 %collective-permute-start.25 = (bf16[3,32,256]{2,1,0:T(8,128)(2,1)S(1)}, bf16[3,32,256]{2,1,0:T(8,128)(2,1)S(1)}, u32[]{:S(2)}, u32[]{:S(2)}) collective-permute-start(bf16[3,32,256]{2,1,0:T(8,128)(2,1)S(1)} %get-tuple-element.57), channel_id=1, source_target_pairs={{0,24},{4,28},{8,0},{12,4},{16,8},{20,12},{24,16},{28,20},{1,25},{... | collective-permute-start | bytes 147464 | tf_op jit(solution)/shard_map/ppermute | solution.py:63
  82.8 1.8 %collective-permute-start.27 = (bf16[3,32,384]{2,1,0:T(8,128)(2,1)S(1)}, bf16[3,32,384]{2,1,0:T(8,128)(2,1)S(1)}, u32[]{:S(2)}, u32[]{:S(2)}) collective-permute-start(bf16[3,32,384]{2,1,0:T(8,128)(2,1)S(1)} %get-tuple-element.53), channel_id=1, source_target_pairs={{0,16},{4,20},{8,24},{12,28},{16,0},{20,4},{24,8},{28,12},{1,17},{... | collective-permute-start | bytes 221192 | tf_op jit(solution)/shard_map/ppermute | solution.py:63
  85.0 3.2 %collective-permute-start.29 = (bf16[3,32,384]{2,1,0:T(8,128)(2,1)S(1)}, bf16[3,32,384]{2,1,0:T(8,128)(2,1)S(1)}, u32[]{:S(2)}, u32[]{:S(2)}) collective-permute-start(bf16[3,32,384]{2,1,0:T(8,128)(2,1)S(1)} %get-tuple-element.54), channel_id=1, source_target_pairs={{0,24},{4,28},{8,0},{12,4},{16,8},{20,12},{24,16},{28,20},{1,25},{... | collective-permute-start | bytes 221192 | tf_op jit(solution)/shard_map/ppermute | solution.py:63
  88.2 4.6 %collective-permute-done.27 = bf16[3,32,384]{2,1,0:T(8,128)(2,1)S(1)} collective-permute-done((bf16[3,32,384]{2,1,0:T(8,128)(2,1)S(1)}, bf16[3,32,384]{2,1,0:T(8,128)(2,1)S(1)}, u32[]{:S(2)}, u32[]{:S(2)}) %collective-permute-start.27) | collective-permute-done | bytes 73760 | tf_op jit(solution)/shard_map/ppermute | solution.py:63
  92.9 1.1 %collective-permute-done.29 = bf16[3,32,384]{2,1,0:T(8,128)(2,1)S(1)} collective-permute-done((bf16[3,32,384]{2,1,0:T(8,128)(2,1)S(1)}, bf16[3,32,384]{2,1,0:T(8,128)(2,1)S(1)}, u32[]{:S(2)}, u32[]{:S(2)}) %collective-permute-start.29) | collective-permute-done | bytes 73760 | tf_op jit(solution)/shard_map/ppermute | solution.py:63
  (47 shorter events, 7.2 us)
Async XLA Ops:
  1.7 8.0 %collective-permute-start = (bf16[264,512]{1,0:T(8,128)(2,1)S(1)}, bf16[264,512]{1,0:T(8,128)(2,1)S(1)}, u32[]{:S(2)}, u32[]{:S(2)}) collective-permute-start(bf16[264,512]{1,0:T(8,128)(2,1)S(1)} %message.1), channel_id=1, source_target_pairs={{0,2},{1,65},{2,0},{3,67},{32,34},{33,97},{34,32},{35,99},{64,66},... | collective-permute-start | bytes 811016 | tf_op jit(solution)/shard_map/ppermute | solution.py:37
  5.5 7.0 %collective-permute-start.1 = (bf16[264,512]{1,0:T(8,128)(2,1)S(1)}, bf16[264,512]{1,0:T(8,128)(2,1)S(1)}, u32[]{:S(2)}, u32[]{:S(2)}) collective-permute-start(bf16[264,512]{1,0:T(8,128)(2,1)S(1)} %message.1), channel_id=1, source_target_pairs={{0,130},{1,97},{2,128},{3,99},{32,162},{33,65},{34,160},{35,67},{6... | collective-permute-start | bytes 811016 | tf_op jit(solution)/shard_map/ppermute | solution.py:37
  6.3 10.5 %collective-permute-start.4 = (bf16[264,512]{1,0:T(8,128)(2,1)S(1)}, bf16[264,512]{1,0:T(8,128)(2,1)S(1)}, u32[]{:S(2)}, u32[]{:S(2)}) collective-permute-start(bf16[264,512]{1,0:T(8,128)(2,1)S(1)} %message.1), channel_id=1, source_target_pairs={{0,128},{1,33},{2,130},{3,35},{32,160},{33,1},{34,162},{35,3},{64,... | collective-permute-start | bytes 811016 | tf_op jit(solution)/shard_map/ppermute | solution.py:37
  12.6 7.7 %collective-permute-start.12 = (bf16[2,264,512]{2,1,0:T(8,128)(2,1)S(1)}, bf16[2,264,512]{2,1,0:T(8,128)(2,1)S(1)}, u32[]{:S(2)}, u32[]{:S(2)}) collective-permute-start(bf16[2,264,512]{2,1,0:T(8,128)(2,1)S(1)} %pad_maximum_fusion.refs_2_.own_high), channel_id=1, source_target_pairs={{0,1},{1,0},{2,3},{3,2},{4,5},{5,4},{6,7},{7,6},{8,9},{9,8},{10,11... | collective-permute-start | bytes 1622024 | tf_op jit(solution)/shard_map/ppermute | solution.py:45
  16.0 9.7 %collective-permute-start.9 = (bf16[2,264,512]{2,1,0:T(8,128)(2,1)S(1)}, bf16[2,264,512]{2,1,0:T(8,128)(2,1)S(1)}, u32[]{:S(2)}, u32[]{:S(2)}) collective-permute-start(bf16[2,264,512]{2,1,0:T(8,128)(2,1)S(1)} %pad_maximum_fusion.refs_2_.own_high), channel_id=1, source_target_pairs={{0,96},{1,131},{2,98},{3,129},{32,64},{33,163},{34,66},{35,161},{6... | collective-permute-start | bytes 1622024 | tf_op jit(solution)/shard_map/ppermute | solution.py:37
  16.8 9.8 %collective-permute-start.7 = (bf16[2,264,512]{2,1,0:T(8,128)(2,1)S(1)}, bf16[2,264,512]{2,1,0:T(8,128)(2,1)S(1)}, u32[]{:S(2)}, u32[]{:S(2)}) collective-permute-start(bf16[2,264,512]{2,1,0:T(8,128)(2,1)S(1)} %pad_maximum_fusion.1.refs_0_.own_low), channel_id=1, source_target_pairs={{0,32},{1,129},{2,34},{3,131},{32,0},{33,161},{34,2},{35,163},{64,... | collective-permute-start | bytes 1622024 | tf_op jit(solution)/shard_map/ppermute | solution.py:37
  16.9 14.3 %collective-permute-start.2 = (bf16[2,264,512]{2,1,0:T(8,128)(2,1)S(1)}, bf16[2,264,512]{2,1,0:T(8,128)(2,1)S(1)}, u32[]{:S(2)}, u32[]{:S(2)}) collective-permute-start(bf16[2,264,512]{2,1,0:T(8,128)(2,1)S(1)} %pad_maximum_fusion.refs_2_.own_high), channel_id=1, source_target_pairs={{0,32},{1,129},{2,34},{3,131},{32,0},{33,161},{34,2},{35,163},{64,... | collective-permute-start | bytes 1622024 | tf_op jit(solution)/shard_map/ppermute | solution.py:37
  18.3 14.3 %collective-permute-start.5 = (bf16[2,264,512]{2,1,0:T(8,128)(2,1)S(1)}, bf16[2,264,512]{2,1,0:T(8,128)(2,1)S(1)}, u32[]{:S(2)}, u32[]{:S(2)}) collective-permute-start(bf16[2,264,512]{2,1,0:T(8,128)(2,1)S(1)} %pad_maximum_fusion.1.refs_0_.own_low), channel_id=1, source_target_pairs={{0,96},{1,131},{2,98},{3,129},{32,64},{33,163},{34,66},{35,161},{6... | collective-permute-start | bytes 1622024 | tf_op jit(solution)/shard_map/ppermute | solution.py:37
  20.2 15.8 %collective-permute-start.11 = (bf16[2,264,512]{2,1,0:T(8,128)(2,1)S(1)}, bf16[2,264,512]{2,1,0:T(8,128)(2,1)S(1)}, u32[]{:S(2)}, u32[]{:S(2)}) collective-permute-start(bf16[2,264,512]{2,1,0:T(8,128)(2,1)S(1)} %pad_maximum_fusion.1.refs_0_.own_low), channel_id=1, source_target_pairs={{0,1},{1,0},{2,3},{3,2},{4,5},{5,4},{6,7},{7,6},{8,9},{9,8},{10,11... | collective-permute-start | bytes 1622024 | tf_op jit(solution)/shard_map/ppermute | solution.py:45
  25.7 11.7 %collective-permute-start.10 = (bf16[2,264,512]{2,1,0:T(8,128)(2,1)S(1)}, bf16[2,264,512]{2,1,0:T(8,128)(2,1)S(1)}, u32[]{:S(2)}, u32[]{:S(2)}) collective-permute-start(bf16[2,264,512]{2,1,0:T(8,128)(2,1)S(1)} %collective-permute-done.9.refs_2_), channel_id=1, source_target_pairs={{0,1},{1,0},{2,3},{3,2},{4,5},{5,4},{6,7},{7,6},{8,9},{9,8},{10,11... | collective-permute-start | bytes 1622024 | tf_op jit(solution)/shard_map/ppermute | solution.py:45
  26.6 15.7 %collective-permute-start.8 = (bf16[2,264,512]{2,1,0:T(8,128)(2,1)S(1)}, bf16[2,264,512]{2,1,0:T(8,128)(2,1)S(1)}, u32[]{:S(2)}, u32[]{:S(2)}) collective-permute-start(bf16[2,264,512]{2,1,0:T(8,128)(2,1)S(1)} %collective-permute-done.7.refs_0_), channel_id=1, source_target_pairs={{0,1},{1,0},{2,3},{3,2},{4,5},{5,4},{6,7},{7,6},{8,9},{9,8},{10,11... | collective-permute-start | bytes 1622024 | tf_op jit(solution)/shard_map/ppermute | solution.py:45
  31.2 14.2 %collective-permute-start.3 = (bf16[2,264,512]{2,1,0:T(8,128)(2,1)S(1)}, bf16[2,264,512]{2,1,0:T(8,128)(2,1)S(1)}, u32[]{:S(2)}, u32[]{:S(2)}) collective-permute-start(bf16[2,264,512]{2,1,0:T(8,128)(2,1)S(1)} %collective-permute-done.2.refs_0_), channel_id=1, source_target_pairs={{0,1},{1,0},{2,3},{3,2},{4,5},{5,4},{6,7},{7,6},{8,9},{9,8},{10,11... | collective-permute-start | bytes 1622024 | tf_op jit(solution)/shard_map/ppermute | solution.py:45
  32.7 12.7 %collective-permute-start.6 = (bf16[2,264,512]{2,1,0:T(8,128)(2,1)S(1)}, bf16[2,264,512]{2,1,0:T(8,128)(2,1)S(1)}, u32[]{:S(2)}, u32[]{:S(2)}) collective-permute-start(bf16[2,264,512]{2,1,0:T(8,128)(2,1)S(1)} %collective-permute-done.5.refs_2_), channel_id=1, source_target_pairs={{0,1},{1,0},{2,3},{3,2},{4,5},{5,4},{6,7},{7,6},{8,9},{9,8},{10,11... | collective-permute-start | bytes 1622024 | tf_op jit(solution)/shard_map/ppermute | solution.py:45
  36.0 12.4 %collective-permute-start.14 = (bf16[2,264,512]{2,1,0:T(8,128)(2,1)S(1)}, bf16[2,264,512]{2,1,0:T(8,128)(2,1)S(1)}, u32[]{:S(2)}, u32[]{:S(2)}) collective-permute-start(bf16[2,264,512]{2,1,0:T(8,128)(2,1)S(1)} %collective-permute-done.9.refs_2_), channel_id=1, source_target_pairs={{0,32},{1,129},{2,34},{3,131},{32,0},{33,161},{34,2},{35,163},{64,... | collective-permute-start | bytes 1622024 | tf_op jit(solution)/shard_map/ppermute | solution.py:37
  37.3 11.1 %collective-permute-start.13 = (bf16[2,264,512]{2,1,0:T(8,128)(2,1)S(1)}, bf16[2,264,512]{2,1,0:T(8,128)(2,1)S(1)}, u32[]{:S(2)}, u32[]{:S(2)}) collective-permute-start(bf16[2,264,512]{2,1,0:T(8,128)(2,1)S(1)} %collective-permute-done.7.refs_0_), channel_id=1, source_target_pairs={{0,96},{1,131},{2,98},{3,129},{32,64},{33,163},{34,66},{35,161},{6... | collective-permute-start | bytes 1622024 | tf_op jit(solution)/shard_map/ppermute | solution.py:37
  48.5 15.4 %collective-permute-start.15 = (bf16[2,264,512]{2,1,0:T(8,128)(2,1)S(1)}, bf16[2,264,512]{2,1,0:T(8,128)(2,1)S(1)}, u32[]{:S(2)}, u32[]{:S(2)}) collective-permute-start(bf16[2,264,512]{2,1,0:T(8,128)(2,1)S(1)} %collective-permute-done.13.refs_0_), channel_id=1, source_target_pairs={{0,1},{1,0},{2,3},{3,2},{4,5},{5,4},{6,7},{7,6},{8,9},{9,8},{10,11... | collective-permute-start | bytes 1622024 | tf_op jit(solution)/shard_map/ppermute | solution.py:45
  48.6 15.3 %collective-permute-start.16 = (bf16[2,264,512]{2,1,0:T(8,128)(2,1)S(1)}, bf16[2,264,512]{2,1,0:T(8,128)(2,1)S(1)}, u32[]{:S(2)}, u32[]{:S(2)}) collective-permute-start(bf16[2,264,512]{2,1,0:T(8,128)(2,1)S(1)} %collective-permute-done.14.refs_1_), channel_id=1, source_target_pairs={{0,1},{1,0},{2,3},{3,2},{4,5},{5,4},{6,7},{7,6},{8,9},{9,8},{10,11... | collective-permute-start | bytes 1622024 | tf_op jit(solution)/shard_map/ppermute | solution.py:45
  49.1 8.2 %collective-permute-start.17 = (f32[8,128]{1,0:T(8,128)S(1)}, f32[8,128]{1,0:T(8,128)S(1)}, u32[]{:S(2)}, u32[]{:S(2)}) collective-permute-start(f32[8,128]{1,0:T(8,128)S(1)} %rows.1), channel_id=1, source_target_pairs={{0,4},{1,9},{4,8},{5,13},{8,12},{9,17},{12,16},{13,21},{16,20},{17... | collective-permute-start | bytes 12296 | tf_op jit(solution)/shard_map/ppermute | solution.py:57
  52.2 6.4 %collective-permute-start.18 = (f32[8,128]{1,0:T(8,128)S(1)}, f32[8,128]{1,0:T(8,128)S(1)}, u32[]{:S(2)}, u32[]{:S(2)}) collective-permute-start(f32[8,128]{1,0:T(8,128)S(1)} %rows.1), channel_id=1, source_target_pairs={{0,12},{1,17},{4,16},{5,21},{8,20},{9,25},{12,24},{13,29},{16,28},... | collective-permute-start | bytes 12296 | tf_op jit(solution)/shard_map/ppermute | solution.py:57
  58.6 2.5 %collective-permute-start.20 = (f32[8,128]{1,0:T(8,128)S(1)}, f32[8,128]{1,0:T(8,128)S(1)}, u32[]{:S(2)}, u32[]{:S(2)}) collective-permute-start(f32[8,128]{1,0:T(8,128)S(1)} %part.1.refs_6_), channel_id=1, source_target_pairs={{0,128},{128,0},{1,129},{129,1},{2,130},{130,2},{3,131},{131,3},{4... | collective-permute-start | bytes 12296 | tf_op jit(solution)/shard_map/ppermute | solution.py:41
  59.4 4.5 %collective-permute-start.19 = (f32[8,128]{1,0:T(8,128)S(1)}, f32[8,128]{1,0:T(8,128)S(1)}, u32[]{:S(2)}, u32[]{:S(2)}) collective-permute-start(f32[8,128]{1,0:T(8,128)S(1)} %part.1.refs_6_), channel_id=1, source_target_pairs={{0,1},{1,0},{2,3},{3,2},{4,5},{5,4},{6,7},{7,6},{8,9},{9,8},{10,11... | collective-permute-start | bytes 12296 | tf_op jit(solution)/shard_map/ppermute | solution.py:45
  61.1 2.8 %collective-permute-start.21 = (f32[8,128]{1,0:T(8,128)S(1)}, f32[8,128]{1,0:T(8,128)S(1)}, u32[]{:S(2)}, u32[]{:S(2)}) collective-permute-start(f32[8,128]{1,0:T(8,128)S(1)} %collective-permute-done.20.refs_8_), channel_id=1, source_target_pairs={{0,1},{1,0},{2,3},{3,2},{4,5},{5,4},{6,7},{7,6},{8,9},{9,8},{10,11... | collective-permute-start | bytes 12296 | tf_op jit(solution)/shard_map/ppermute | solution.py:45
  67.2 6.5 %collective-permute-start.22 = (bf16[4,3,32,256]{3,2,1,0:T(8,128)(2,1)S(1)}, bf16[4,3,32,256]{3,2,1,0:T(8,128)(2,1)S(1)}, u32[]{:S(2)}, u32[]{:S(2)}) collective-permute-start(bf16[4,3,32,256]{3,2,1,0:T(8,128)(2,1)S(1)} %get-tuple-element.42), channel_id=1, source_target_pairs={{0,4},{1,29},{4,0},{5,9},{8,12},{9,5},{12,8},{13,17},{16,20},{17,1... | collective-permute-start | bytes 589832 | tf_op jit(solution)/shard_map/ppermute | solution.py:53
  72.7 10.0 %collective-permute-start.26 = (bf16[4,3,32,384]{3,2,1,0:T(8,128)(2,1)S(1)}, bf16[4,3,32,384]{3,2,1,0:T(8,128)(2,1)S(1)}, u32[]{:S(2)}, u32[]{:S(2)}) collective-permute-start(bf16[4,3,32,384]{3,2,1,0:T(8,128)(2,1)S(1)} %get-tuple-element.48), channel_id=1, source_target_pairs={{0,4},{1,29},{4,0},{5,9},{8,12},{9,5},{12,8},{13,17},{16,20},{17,1... | collective-permute-start | bytes 884744 | tf_op jit(solution)/shard_map/ppermute | solution.py:53
  73.8 11.1 %collective-permute-start.23 = (bf16[3,32,256]{2,1,0:T(8,128)(2,1)S(1)}, bf16[3,32,256]{2,1,0:T(8,128)(2,1)S(1)}, u32[]{:S(2)}, u32[]{:S(2)}) collective-permute-start(bf16[3,32,256]{2,1,0:T(8,128)(2,1)S(1)} %get-tuple-element.56), channel_id=1, source_target_pairs={{0,16},{4,20},{8,24},{12,28},{16,0},{20,4},{24,8},{28,12},{1,17},{... | collective-permute-start | bytes 147464 | tf_op jit(solution)/shard_map/ppermute | solution.py:63
  79.1 9.1 %collective-permute-start.24 = (bf16[3,32,256]{2,1,0:T(8,128)(2,1)S(1)}, bf16[3,32,256]{2,1,0:T(8,128)(2,1)S(1)}, u32[]{:S(2)}, u32[]{:S(2)}) collective-permute-start(bf16[3,32,256]{2,1,0:T(8,128)(2,1)S(1)} %get-tuple-element.58), channel_id=1, source_target_pairs={{0,8},{4,12},{8,16},{12,20},{16,24},{20,28},{24,0},{28,4},{1,9},{5... | collective-permute-start | bytes 147464 | tf_op jit(solution)/shard_map/ppermute | solution.py:63
  79.1 9.1 %collective-permute-start.25 = (bf16[3,32,256]{2,1,0:T(8,128)(2,1)S(1)}, bf16[3,32,256]{2,1,0:T(8,128)(2,1)S(1)}, u32[]{:S(2)}, u32[]{:S(2)}) collective-permute-start(bf16[3,32,256]{2,1,0:T(8,128)(2,1)S(1)} %get-tuple-element.57), channel_id=1, source_target_pairs={{0,24},{4,28},{8,0},{12,4},{16,8},{20,12},{24,16},{28,20},{1,25},{... | collective-permute-start | bytes 147464 | tf_op jit(solution)/shard_map/ppermute | solution.py:63
  82.8 10.1 %collective-permute-start.27 = (bf16[3,32,384]{2,1,0:T(8,128)(2,1)S(1)}, bf16[3,32,384]{2,1,0:T(8,128)(2,1)S(1)}, u32[]{:S(2)}, u32[]{:S(2)}) collective-permute-start(bf16[3,32,384]{2,1,0:T(8,128)(2,1)S(1)} %get-tuple-element.53), channel_id=1, source_target_pairs={{0,16},{4,20},{8,24},{12,28},{16,0},{20,4},{24,8},{28,12},{1,17},{... | collective-permute-start | bytes 221192 | tf_op jit(solution)/shard_map/ppermute | solution.py:63
  84.6 8.3 %collective-permute-start.28 = (bf16[3,32,384]{2,1,0:T(8,128)(2,1)S(1)}, bf16[3,32,384]{2,1,0:T(8,128)(2,1)S(1)}, u32[]{:S(2)}, u32[]{:S(2)}) collective-permute-start(bf16[3,32,384]{2,1,0:T(8,128)(2,1)S(1)} %get-tuple-element.55), channel_id=1, source_target_pairs={{0,8},{4,12},{8,16},{12,20},{16,24},{20,28},{24,0},{28,4},{1,9},{5... | collective-permute-start | bytes 221192 | tf_op jit(solution)/shard_map/ppermute | solution.py:63
  85.0 9.0 %collective-permute-start.29 = (bf16[3,32,384]{2,1,0:T(8,128)(2,1)S(1)}, bf16[3,32,384]{2,1,0:T(8,128)(2,1)S(1)}, u32[]{:S(2)}, u32[]{:S(2)}) collective-permute-start(bf16[3,32,384]{2,1,0:T(8,128)(2,1)S(1)} %get-tuple-element.54), channel_id=1, source_target_pairs={{0,24},{4,28},{8,0},{12,4},{16,8},{20,12},{24,16},{28,20},{1,25},{... | collective-permute-start | bytes 221192 | tf_op jit(solution)/shard_map/ppermute | solution.py:63

commit v8 on v7

--- a/solution.py
+++ b/solution.py
@@ -346,12 +346,12 @@
     def items(keys, sides=(0, 1)):
         return [(m, j, ec, (blocks, others)[ec][m, j]) for m, j in keys for ec in sides]
 
-    state = ()
-    for keys in (OWN, EARLY, LATE):
-        state = gathered(items(keys), w_in, w_out, state)
+    state = gathered(items(OWN), w_in, w_out, ())
+    state = gathered(items(EARLY), w_in, w_out, state)
     state, blocks[2, 0], blocks[2, 1] = lax.optimization_barrier((state, blocks[2, 0], blocks[2, 1]))
     for k, j in FAR:
         others[k, j] = sibling(blocks[k, j])
+    state = gathered(items(LATE), w_in, w_out, state)
     state = gathered(items(FAR, (0,)), w_in, w_out, state)
     halves = items(FAR, (1,))
     keeps, got = [], []
@@ -359,17 +359,19 @@
         state, keep, send = finished(cut, halves, w_in, w_out, state, terms)
         keeps.append(keep)
         got.append(z_pair(send))
-    results = []
+    results, across_ring = [], []
     for cut in range(2):
         mixed = keeps[cut] + got[cut].astype(F32)
         sends = mixed.astype(BF16)
         if cut == 0:
             sends, keeps[1] = lax.optimization_barrier((sends, keeps[1]))
+        across_ring.append(sends[2])
         result = mixed[0]
-        for k in (2, 1, 3):
+        for k in (1, 3):
             result = result + z_step(sends[k], 2 * k).astype(F32)
         results.append(result)
-    return jnp.transpose(jnp.concatenate(results, axis=2), (1, 0, 2))
+    opposite = z_step(jnp.concatenate(across_ring, axis=2), 4)
+    return jnp.transpose(jnp.concatenate(results, axis=2) + opposite.astype(F32), (1, 0, 2))
 
 
 def solution(mesh):

time: 94.8 us -> 100 us (1.055)
  the two profiles are of different devices: /device:TPU:1 before, /device:TPU:6 now
where the time goes in v8:
time: 100 us; the launch traced here: 99.8 us
  waiting for transfers between devices  47.5 us (48%)
  starting transfers between devices  27.8 us (28%)
  Pallas kernels  22.5 us (22%)
  other arithmetic  1.02 us (1%)
    ppermute x9, waiting for transfers between devices, across(): return lax.ppermute(block, PLANE, route)  20.1 us
    ppermute x5, waiting for transfers between devices, z_step(): return lax.ppermute(block, 'z', [(z, (z + step) % 8) for z in range(8)])  13.3 us
    pallas_call x4, Pallas kernels, gathered(): pl.pallas_call(kernel, out_shape=STATE, in_specs=[VMEM] * (n + 2 + len(st...  11.2 us
    ppermute x5, starting transfers between devices, z_step(): return lax.ppermute(block, 'z', [(z, (z + step) % 8) for z in range(8)])  10.7 us
    ppermute x2, waiting for transfers between devices, z_shift(): lax.ppermute(block, ('z', 'c'), [(z * 2 + c, (z + step + c) % 8 * 2 + c)...  10.5 us
    ppermute x9, starting transfers between devices, across(): return lax.ppermute(block, PLANE, route)  9.39 us
    pallas_call x2, Pallas kernels, finished(): pl.pallas_call(kernel, out_shape=STATE + (jax.ShapeDtypeStruct((4, 3, 32,...  6.94 us
    ppermute x2, starting transfers between devices, z_shift(): lax.ppermute(block, ('z', 'c'), [(z * 2 + c, (z + step + c) % 8 * 2 + c)...  3.64 us
  transfers between devices with their start and end apart: 29, of which 11 were waited for; matrix products, arithmetic and copies ran while one was open for 0% of the time, Pallas kernels for 18%

profile of v8, /device:TPU:6, one launch (start us, length us, event | category | flops | bytes accessed | tf_op | source)
XLA Modules:
  0.0 99.8 jit_solution(16630990582910422697)
XLA Ops:
  0.7 1.0 %message.1 = bf16[264,512]{1,0:T(8,128)(2,1)S(1)} custom-call(f32[1]{0:T(128)S(6)} %copy.29.decode, f32[1,5]{1,0:T(1,128)} %code_in.1, s32[4]{0:T(128)} %stragglers_in.1, bf16[128,512]{1,0:T(8,128)(2,1)} %tokens.1, bf16[128,512]{1,0:T(8,128)(2,1)} %grad_out.1), custom_call_target="tpu_custom_call" | custom-call | tf_op jit(solution)/shard_map/message/pallas_call | solution.py:105
  1.7 1.5 %collective-permute-start.3 = (bf16[264,512]{1,0:T(8,128)(2,1)S(1)}, bf16[264,512]{1,0:T(8,128)(2,1)S(1)}, u32[]{:S(2)}, u32[]{:S(2)}) collective-permute-start(bf16[264,512]{1,0:T(8,128)(2,1)S(1)} %message.1), channel_id=1, source_target_pairs={{0,2},{1,65},{2,0},{3,67},{32,34},{33,97},{34,32},{35,99},{64,66},... | collective-permute-start | bytes 811016 | tf_op jit(solution)/shard_map/ppermute | solution.py:37
  3.2 2.1 %collective-permute-start.4 = (bf16[264,512]{1,0:T(8,128)(2,1)S(1)}, bf16[264,512]{1,0:T(8,128)(2,1)S(1)}, u32[]{:S(2)}, u32[]{:S(2)}) collective-permute-start(bf16[264,512]{1,0:T(8,128)(2,1)S(1)} %message.1), channel_id=1, source_target_pairs={{0,130},{1,97},{2,128},{3,99},{32,162},{33,65},{34,160},{35,67},{6... | collective-permute-start | bytes 811016 | tf_op jit(solution)/shard_map/ppermute | solution.py:37
  5.3 4.6 %collective-permute-done.3 = bf16[264,512]{1,0:T(8,128)(2,1)S(1)} collective-permute-done((bf16[264,512]{1,0:T(8,128)(2,1)S(1)}, bf16[264,512]{1,0:T(8,128)(2,1)S(1)}, u32[]{:S(2)}, u32[]{:S(2)}) %collective-permute-start.3) | collective-permute-done | bytes 270368 | tf_op jit(solution)/shard_map/ppermute | solution.py:37
  9.8 2.8 %collective-permute-done.4 = bf16[264,512]{1,0:T(8,128)(2,1)S(1)} collective-permute-done((bf16[264,512]{1,0:T(8,128)(2,1)S(1)}, bf16[264,512]{1,0:T(8,128)(2,1)S(1)}, u32[]{:S(2)}, u32[]{:S(2)}) %collective-permute-start.4) | collective-permute-done | bytes 270368 | tf_op jit(solution)/shard_map/ppermute | solution.py:37
  12.8 3.1 %collective-permute-start.5 = (bf16[2,264,512]{2,1,0:T(8,128)(2,1)S(1)}, bf16[2,264,512]{2,1,0:T(8,128)(2,1)S(1)}, u32[]{:S(2)}, u32[]{:S(2)}) collective-permute-start(bf16[2,264,512]{2,1,0:T(8,128)(2,1)S(1)} %pad_maximum_fusion.1.refs_2_.own_high), channel_id=1, source_target_pairs={{0,96},{1,131},{2,98},{3,129},{32,64},{33,163},{34,66},{35,161},{6... | collective-permute-start | bytes 1622024 | tf_op jit(solution)/shard_map/ppermute | solution.py:37
  16.2 1.9 %collective-permute-start.13 = (bf16[2,264,512]{2,1,0:T(8,128)(2,1)S(1)}, bf16[2,264,512]{2,1,0:T(8,128)(2,1)S(1)}, u32[]{:S(2)}, u32[]{:S(2)}) collective-permute-start(bf16[2,264,512]{2,1,0:T(8,128)(2,1)S(1)} %pad_maximum_fusion.1.refs_2_.own_high), channel_id=1, source_target_pairs={{0,32},{1,129},{2,34},{3,131},{32,0},{33,161},{34,2},{35,163},{64,... | collective-permute-start | bytes 1622024 | tf_op jit(solution)/shard_map/ppermute | solution.py:37
  18.3 5.2 %collective-permute-done.5.refs_2_ = bf16[2,264,512]{2,1,0:T(8,128)(2,1)S(1)} collective-permute-done((bf16[2,264,512]{2,1,0:T(8,128)(2,1)S(1)}, bf16[2,264,512]{2,1,0:T(8,128)(2,1)S(1)}, u32[]{:S(2)}, u32[]{:S(2)}) %collective-permute-start.5) | collective-permute-done | bytes 540704 | tf_op jit(solution)/shard_map/ppermute | solution.py:37
  23.4 1.9 %collective-permute-done.1.refs_0_ = bf16[2,264,512]{2,1,0:T(8,128)(2,1)S(1)} collective-permute-done((bf16[2,264,512]{2,1,0:T(8,128)(2,1)S(1)}, bf16[2,264,512]{2,1,0:T(8,128)(2,1)S(1)}, u32[]{:S(2)}, u32[]{:S(2)}) %collective-permute-start.1) | collective-permute-done | bytes 540704 | tf_op jit(solution)/shard_map/ppermute | solution.py:37
  25.5 5.6 %collective-permute-done.13.refs_0_ = bf16[2,264,512]{2,1,0:T(8,128)(2,1)S(1)} collective-permute-done((bf16[2,264,512]{2,1,0:T(8,128)(2,1)S(1)}, bf16[2,264,512]{2,1,0:T(8,128)(2,1)S(1)}, u32[]{:S(2)}, u32[]{:S(2)}) %collective-permute-start.13) | collective-permute-done | bytes 540704 | tf_op jit(solution)/shard_map/ppermute | solution.py:37
  31.4 3.4 %load.1 = (bf16[4,512,1280]{2,1,0:T(8,128)(2,1)S(1)}, bf16[4,512,640]{2,1,0:T(8,128)(2,1)S(1)}) custom-call(bf16[4,512,640]{2,1,0:T(8,128)(2,1)} %bitcast.34, bf16[4,512,640]{2,1,0:T(8,128)(2,1)} %bitcast.35, bf16[4,512,640]{2,1,0:T(8,128)(2,1)} %bitcast.36), custom_call_target="tpu_custom_call" | custom-call | tf_op jit(solution)/shard_map/load/pallas_call | solution.py:131
  35.4 3.6 %shard_map.82 = (f32[3,8,128,640]{3,2,1,0:T(8,128)S(1)}, bf16[2,8,128,256]{3,2,1,0:T(8,128)(2,1)S(1)}) custom-call(bf16[2,264,512]{2,1,0:T(8,128)(2,1)S(1)} %pad_maximum_fusion.refs_0_.own_low, bf16[2,264,512]{2,1,0:T(8,128)(2,1)S(1)} %collective-permute-done.7.refs_1_.other_low, bf16[2,264,512]{2,1,0:T(8,128)(2,1)S(1)} %pad_maximum_fusion.1.refs_2_.own_high, ...), custom_call_target="tpu_custom_call" | custom-call | flops 2147483648 | bytes 1048576 | tf_op jit(solution)/shard_map/pallas_call | solution.py:234
  39.0 3.0 %shard_map.83 = (f32[3,8,128,640]{3,2,1,0:T(8,128)S(1)}, bf16[2,8,128,256]{3,2,1,0:T(8,128)(2,1)S(1)}) custom-call(bf16[2,264,512]{2,1,0:T(8,128)(2,1)S(1)} %collective-permute-done.1.refs_0_, bf16[2,264,512]{2,1,0:T(8,128)(2,1)S(1)} %collective-permute-done.2.refs_1_, ...), custom_call_target="tpu_custom_call", output_to_operand_aliasing={{0}: (6, {}), {1}: (7, {})} | custom-call | flops 2147483648 | bytes 1048576 | tf_op jit(solution)/shard_map/pallas_call | solution.py:234
  42.7 2.0 %collective-permute-start.17 = (f32[8,128]{1,0:T(8,128)S(1)}, f32[8,128]{1,0:T(8,128)S(1)}, u32[]{:S(2)}, u32[]{:S(2)}) collective-permute-start(f32[8,128]{1,0:T(8,128)S(1)} %rows.1), channel_id=1, source_target_pairs={{0,4},{1,9},{4,8},{5,13},{8,12},{9,17},{12,16},{13,21},{16,20},{17... | collective-permute-start | bytes 12296 | tf_op jit(solution)/shard_map/ppermute | solution.py:57
  44.7 5.5 %collective-permute-done.17.near = f32[8,128]{1,0:T(8,128)S(1)} collective-permute-done((f32[8,128]{1,0:T(8,128)S(1)}, f32[8,128]{1,0:T(8,128)S(1)}, u32[]{:S(2)}, u32[]{:S(2)}) %collective-permute-start.17) | collective-permute-done | bytes 4128 | tf_op jit(solution)/shard_map/ppermute | solution.py:57
  50.2 1.7 %collective-permute-start.18 = (f32[8,128]{1,0:T(8,128)S(1)}, f32[8,128]{1,0:T(8,128)S(1)}, u32[]{:S(2)}, u32[]{:S(2)}) collective-permute-start(f32[8,128]{1,0:T(8,128)S(1)} %rows.1), channel_id=1, source_target_pairs={{0,12},{1,17},{4,16},{5,21},{8,20},{9,25},{12,24},{13,29},{16,28},... | collective-permute-start | bytes 12296 | tf_op jit(solution)/shard_map/ppermute | solution.py:57
  51.9 5.0 %collective-permute-done.18.far = f32[8,128]{1,0:T(8,128)S(1)} collective-permute-done((f32[8,128]{1,0:T(8,128)S(1)}, f32[8,128]{1,0:T(8,128)S(1)}, u32[]{:S(2)}, u32[]{:S(2)}) %collective-permute-start.18) | collective-permute-done | bytes 4128 | tf_op jit(solution)/shard_map/ppermute | solution.py:57
  56.9 3.6 %collective-permute-done.20.refs_8_ = f32[8,128]{1,0:T(8,128)S(1)} collective-permute-done((f32[8,128]{1,0:T(8,128)S(1)}, f32[8,128]{1,0:T(8,128)S(1)}, u32[]{:S(2)}, u32[]{:S(2)}) %collective-permute-start.20) | collective-permute-done | bytes 4128 | tf_op jit(solution)/shard_map/ppermute | solution.py:41
  60.5 0.5 collective-permute-start.21
  61.0 3.0 %shard_map.84 = (f32[3,8,128,640]{3,2,1,0:T(8,128)S(1)}, bf16[2,8,128,256]{3,2,1,0:T(8,128)(2,1)S(1)}) custom-call(bf16[2,264,512]{2,1,0:T(8,128)(2,1)S(1)} %collective-permute-done.13.refs_0_, bf16[2,264,512]{2,1,0:T(8,128)(2,1)S(1)} %collective-permute-done.14.refs_1_, ...), custom_call_target="tpu_custom_call", output_to_operand_aliasing={{0}: (6, {}), {1}: (7, {})} | custom-call | flops 2147483648 | bytes 1048576 | tf_op jit(solution)/shard_map/pallas_call | solution.py:234
  64.1 1.5 %shard_map.85 = (f32[3,8,128,640]{3,2,1,0:T(8,128)S(1)}, bf16[2,8,128,256]{3,2,1,0:T(8,128)(2,1)S(1)}) custom-call(bf16[2,264,512]{2,1,0:T(8,128)(2,1)S(1)} %collective-permute-done.9.refs_0_, bf16[2,264,512]{2,1,0:T(8,128)(2,1)S(1)} %collective-permute-done.10.refs_1_, ...), custom_call_target="tpu_custom_call", output_to_operand_aliasing={{0}: (4, {}), {1}: (5, {})} | custom-call | flops 1073741824 | bytes 1048576 | tf_op jit(solution)/shard_map/pallas_call | solution.py:234
  65.6 3.3 %shard_map.86 = (f32[3,8,128,640]{3,2,1,0:T(8,128)S(1)}, bf16[2,8,128,256]{3,2,1,0:T(8,128)(2,1)S(1)}, f32[4,3,32,256]{3,2,1,0:T(8,128)S(1)}, bf16[4,3,32,256]{3,2,1,0:T(8,128)(2,1)S(1)}) custom-call(bf16[2,264,512]{2,1,0:T(8,128)(2,1)S(1)} %collective-permute-done.11.refs_0_, ...), custom_call_target="tpu_custom_call", output_to_operand_aliasing={{0}: (4, {}), {1}: (5, {})} | custom-call | flops 2147483648 | bytes 1048576 | tf_op jit(solution)/shard_map/pallas_call | solution.py:255
  69.0 3.7 %shard_map.87 = (f32[3,8,128,640]{3,2,1,0:T(8,128)S(1)}, bf16[2,8,128,256]{3,2,1,0:T(8,128)(2,1)S(1)}, f32[4,3,32,384]{3,2,1,0:T(8,128)S(1)}, bf16[4,3,32,384]{3,2,1,0:T(8,128)(2,1)S(1)}) custom-call(bf16[2,264,512]{2,1,0:T(8,128)(2,1)S(1)} %collective-permute-done.11.refs_0_, ...), custom_call_target="tpu_custom_call", output_to_operand_aliasing={{0}: (4, {}), {1}: (5, {})} | custom-call | flops 2147483648 | bytes 1048576 | tf_op jit(solution)/shard_map/pallas_call | solution.py:255
  72.7 2.1 %collective-permute-start.25 = (bf16[4,3,32,384]{3,2,1,0:T(8,128)(2,1)S(1)}, bf16[4,3,32,384]{3,2,1,0:T(8,128)(2,1)S(1)}, u32[]{:S(2)}, u32[]{:S(2)}) collective-permute-start(bf16[4,3,32,384]{3,2,1,0:T(8,128)(2,1)S(1)} %get-tuple-element.48), channel_id=1, source_target_pairs={{0,4},{1,29},{4,0},{5,9},{8,12},{9,5},{12,8},{13,17},{16,20},{17,1... | collective-permute-start | bytes 884744 | tf_op jit(solution)/shard_map/ppermute | solution.py:53
  75.0 4.1 %collective-permute-start.24 = (bf16[3,32,256]{2,1,0:T(8,128)(2,1)S(1)}, bf16[3,32,256]{2,1,0:T(8,128)(2,1)S(1)}, u32[]{:S(2)}, u32[]{:S(2)}) collective-permute-start(bf16[3,32,256]{2,1,0:T(8,128)(2,1)S(1)} %get-tuple-element.57), channel_id=1, source_target_pairs={{0,24},{4,28},{8,0},{12,4},{16,8},{20,12},{24,16},{28,20},{1,25},{... | collective-permute-start | bytes 147464 | tf_op jit(solution)/shard_map/ppermute | solution.py:63
  79.1 5.0 %collective-permute-done.23 = bf16[3,32,256]{2,1,0:T(8,128)(2,1)S(1)} collective-permute-done((bf16[3,32,256]{2,1,0:T(8,128)(2,1)S(1)}, bf16[3,32,256]{2,1,0:T(8,128)(2,1)S(1)}, u32[]{:S(2)}, u32[]{:S(2)}) %collective-permute-start.23) | collective-permute-done | bytes 49184 | tf_op jit(solution)/shard_map/ppermute | solution.py:63
  84.2 2.8 %collective-permute-start.26 = (bf16[3,32,384]{2,1,0:T(8,128)(2,1)S(1)}, bf16[3,32,384]{2,1,0:T(8,128)(2,1)S(1)}, u32[]{:S(2)}, u32[]{:S(2)}) collective-permute-start(bf16[3,32,384]{2,1,0:T(8,128)(2,1)S(1)} %get-tuple-element.55), channel_id=1, source_target_pairs={{0,8},{4,12},{8,16},{12,20},{16,24},{20,28},{24,0},{28,4},{1,9},{5... | collective-permute-start | bytes 221192 | tf_op jit(solution)/shard_map/ppermute | solution.py:63
  87.0 1.4 %collective-permute-start.27 = (bf16[3,32,384]{2,1,0:T(8,128)(2,1)S(1)}, bf16[3,32,384]{2,1,0:T(8,128)(2,1)S(1)}, u32[]{:S(2)}, u32[]{:S(2)}) collective-permute-start(bf16[3,32,384]{2,1,0:T(8,128)(2,1)S(1)} %get-tuple-element.54), channel_id=1, source_target_pairs={{0,24},{4,28},{8,0},{12,4},{16,8},{20,12},{24,16},{28,20},{1,25},{... | collective-permute-start | bytes 221192 | tf_op jit(solution)/shard_map/ppermute | solution.py:63
  88.5 2.3 %collective-permute-start.28 = (bf16[3,32,640]{2,1,0:T(8,128)(2,1)S(1)}, bf16[3,32,640]{2,1,0:T(8,128)(2,1)S(1)}, u32[]{:S(2)}, u32[]{:S(2)}) collective-permute-start(bf16[3,32,640]{2,1,0:T(8,128)(2,1)S(1)} %pad_maximum_fusion.2), channel_id=1, source_target_pairs={{0,16},{4,20},{8,24},{12,28},{16,0},{20,4},{24,8},{28,12},{1,17},{... | collective-permute-start | bytes 368648 | tf_op jit(solution)/shard_map/ppermute | solution.py:63
  90.8 2.6 %collective-permute-done.27 = bf16[3,32,384]{2,1,0:T(8,128)(2,1)S(1)} collective-permute-done((bf16[3,32,384]{2,1,0:T(8,128)(2,1)S(1)}, bf16[3,32,384]{2,1,0:T(8,128)(2,1)S(1)}, u32[]{:S(2)}, u32[]{:S(2)}) %collective-permute-start.27) | collective-permute-done | bytes 73760 | tf_op jit(solution)/shard_map/ppermute | solution.py:63
  93.4 5.7 %collective-permute-done.28 = bf16[3,32,640]{2,1,0:T(8,128)(2,1)S(1)} collective-permute-done((bf16[3,32,640]{2,1,0:T(8,128)(2,1)S(1)}, bf16[3,32,640]{2,1,0:T(8,128)(2,1)S(1)}, u32[]{:S(2)}, u32[]{:S(2)}) %collective-permute-start.28) | collective-permute-done | bytes 122912 | tf_op jit(solution)/shard_map/ppermute | solution.py:63
  99.1 0.7 fusion
  (46 shorter events, 2.8 us)
Async XLA Ops:
  1.7 8.2 %collective-permute-start.3 = (bf16[264,512]{1,0:T(8,128)(2,1)S(1)}, bf16[264,512]{1,0:T(8,128)(2,1)S(1)}, u32[]{:S(2)}, u32[]{:S(2)}) collective-permute-start(bf16[264,512]{1,0:T(8,128)(2,1)S(1)} %message.1), channel_id=1, source_target_pairs={{0,2},{1,65},{2,0},{3,67},{32,34},{33,97},{34,32},{35,99},{64,66},... | collective-permute-start | bytes 811016 | tf_op jit(solution)/shard_map/ppermute | solution.py:37
  3.2 9.5 %collective-permute-start.4 = (bf16[264,512]{1,0:T(8,128)(2,1)S(1)}, bf16[264,512]{1,0:T(8,128)(2,1)S(1)}, u32[]{:S(2)}, u32[]{:S(2)}) collective-permute-start(bf16[264,512]{1,0:T(8,128)(2,1)S(1)} %message.1), channel_id=1, source_target_pairs={{0,130},{1,97},{2,128},{3,99},{32,162},{33,65},{34,160},{35,67},{6... | collective-permute-start | bytes 811016 | tf_op jit(solution)/shard_map/ppermute | solution.py:37
  5.3 10.6 %collective-permute-start = (bf16[264,512]{1,0:T(8,128)(2,1)S(1)}, bf16[264,512]{1,0:T(8,128)(2,1)S(1)}, u32[]{:S(2)}, u32[]{:S(2)}) collective-permute-start(bf16[264,512]{1,0:T(8,128)(2,1)S(1)} %message.1), channel_id=1, source_target_pairs={{0,128},{1,33},{2,130},{3,35},{32,160},{33,1},{34,162},{35,3},{64,... | collective-permute-start | bytes 811016 | tf_op jit(solution)/shard_map/ppermute | solution.py:37
  12.7 5.4 %collective-permute-start.8 = (bf16[2,264,512]{2,1,0:T(8,128)(2,1)S(1)}, bf16[2,264,512]{2,1,0:T(8,128)(2,1)S(1)}, u32[]{:S(2)}, u32[]{:S(2)}) collective-permute-start(bf16[2,264,512]{2,1,0:T(8,128)(2,1)S(1)} %pad_maximum_fusion.1.refs_2_.own_high), channel_id=1, source_target_pairs={{0,1},{1,0},{2,3},{3,2},{4,5},{5,4},{6,7},{7,6},{8,9},{9,8},{10,11... | collective-permute-start | bytes 1622024 | tf_op jit(solution)/shard_map/ppermute | solution.py:45
  12.8 10.7 %collective-permute-start.5 = (bf16[2,264,512]{2,1,0:T(8,128)(2,1)S(1)}, bf16[2,264,512]{2,1,0:T(8,128)(2,1)S(1)}, u32[]{:S(2)}, u32[]{:S(2)}) collective-permute-start(bf16[2,264,512]{2,1,0:T(8,128)(2,1)S(1)} %pad_maximum_fusion.1.refs_2_.own_high), channel_id=1, source_target_pairs={{0,96},{1,131},{2,98},{3,129},{32,64},{33,163},{34,66},{35,161},{6... | collective-permute-start | bytes 1622024 | tf_op jit(solution)/shard_map/ppermute | solution.py:37
  15.9 9.4 %collective-permute-start.1 = (bf16[2,264,512]{2,1,0:T(8,128)(2,1)S(1)}, bf16[2,264,512]{2,1,0:T(8,128)(2,1)S(1)}, u32[]{:S(2)}, u32[]{:S(2)}) collective-permute-start(bf16[2,264,512]{2,1,0:T(8,128)(2,1)S(1)} %pad_maximum_fusion.refs_0_.own_low), channel_id=1, source_target_pairs={{0,32},{1,129},{2,34},{3,131},{32,0},{33,161},{34,2},{35,163},{64,... | collective-permute-start | bytes 1622024 | tf_op jit(solution)/shard_map/ppermute | solution.py:37
  16.2 9.2 %collective-permute-start.7 = (bf16[2,264,512]{2,1,0:T(8,128)(2,1)S(1)}, bf16[2,264,512]{2,1,0:T(8,128)(2,1)S(1)}, u32[]{:S(2)}, u32[]{:S(2)}) collective-permute-start(bf16[2,264,512]{2,1,0:T(8,128)(2,1)S(1)} %pad_maximum_fusion.refs_0_.own_low), channel_id=1, source_target_pairs={{0,1},{1,0},{2,3},{3,2},{4,5},{5,4},{6,7},{7,6},{8,9},{9,8},{10,11... | collective-permute-start | bytes 1622024 | tf_op jit(solution)/shard_map/ppermute | solution.py:45
  16.2 15.0 %collective-permute-start.13 = (bf16[2,264,512]{2,1,0:T(8,128)(2,1)S(1)}, bf16[2,264,512]{2,1,0:T(8,128)(2,1)S(1)}, u32[]{:S(2)}, u32[]{:S(2)}) collective-permute-start(bf16[2,264,512]{2,1,0:T(8,128)(2,1)S(1)} %pad_maximum_fusion.1.refs_2_.own_high), channel_id=1, source_target_pairs={{0,32},{1,129},{2,34},{3,131},{32,0},{33,161},{34,2},{35,163},{64,... | collective-permute-start | bytes 1622024 | tf_op jit(solution)/shard_map/ppermute | solution.py:37
  18.0 16.7 %collective-permute-start.15 = (bf16[2,264,512]{2,1,0:T(8,128)(2,1)S(1)}, bf16[2,264,512]{2,1,0:T(8,128)(2,1)S(1)}, u32[]{:S(2)}, u32[]{:S(2)}) collective-permute-start(bf16[2,264,512]{2,1,0:T(8,128)(2,1)S(1)} %pad_maximum_fusion.refs_0_.own_low), channel_id=1, source_target_pairs={{0,96},{1,131},{2,98},{3,129},{32,64},{33,163},{34,66},{35,161},{6... | collective-permute-start | bytes 1622024 | tf_op jit(solution)/shard_map/ppermute | solution.py:37
  23.4 11.4 %collective-permute-start.6 = (bf16[2,264,512]{2,1,0:T(8,128)(2,1)S(1)}, bf16[2,264,512]{2,1,0:T(8,128)(2,1)S(1)}, u32[]{:S(2)}, u32[]{:S(2)}) collective-permute-start(bf16[2,264,512]{2,1,0:T(8,128)(2,1)S(1)} %collective-permute-done.5.refs_2_), channel_id=1, source_target_pairs={{0,1},{1,0},{2,3},{3,2},{4,5},{5,4},{6,7},{7,6},{8,9},{9,8},{10,11... | collective-permute-start | bytes 1622024 | tf_op jit(solution)/shard_map/ppermute | solution.py:45
  25.4 13.6 %collective-permute-start.2 = (bf16[2,264,512]{2,1,0:T(8,128)(2,1)S(1)}, bf16[2,264,512]{2,1,0:T(8,128)(2,1)S(1)}, u32[]{:S(2)}, u32[]{:S(2)}) collective-permute-start(bf16[2,264,512]{2,1,0:T(8,128)(2,1)S(1)} %collective-permute-done.1.refs_0_), channel_id=1, source_target_pairs={{0,1},{1,0},{2,3},{3,2},{4,5},{5,4},{6,7},{7,6},{8,9},{9,8},{10,11... | collective-permute-start | bytes 1622024 | tf_op jit(solution)/shard_map/ppermute | solution.py:45
  25.4 16.7 %collective-permute-start.10 = (bf16[2,264,512]{2,1,0:T(8,128)(2,1)S(1)}, bf16[2,264,512]{2,1,0:T(8,128)(2,1)S(1)}, u32[]{:S(2)}, u32[]{:S(2)}) collective-permute-start(bf16[2,264,512]{2,1,0:T(8,128)(2,1)S(1)} %collective-permute-done.5.refs_2_), channel_id=1, source_target_pairs={{0,32},{1,129},{2,34},{3,131},{32,0},{33,161},{34,2},{35,163},{64,... | collective-permute-start | bytes 1622024 | tf_op jit(solution)/shard_map/ppermute | solution.py:37
  31.2 10.9 %collective-permute-start.9 = (bf16[2,264,512]{2,1,0:T(8,128)(2,1)S(1)}, bf16[2,264,512]{2,1,0:T(8,128)(2,1)S(1)}, u32[]{:S(2)}, u32[]{:S(2)}) collective-permute-start(bf16[2,264,512]{2,1,0:T(8,128)(2,1)S(1)} %collective-permute-done.1.refs_0_), channel_id=1, source_target_pairs={{0,96},{1,131},{2,98},{3,129},{32,64},{33,163},{34,66},{35,161},{6... | collective-permute-start | bytes 1622024 | tf_op jit(solution)/shard_map/ppermute | solution.py:37
  34.8 25.8 %collective-permute-start.14 = (bf16[2,264,512]{2,1,0:T(8,128)(2,1)S(1)}, bf16[2,264,512]{2,1,0:T(8,128)(2,1)S(1)}, u32[]{:S(2)}, u32[]{:S(2)}) collective-permute-start(bf16[2,264,512]{2,1,0:T(8,128)(2,1)S(1)} %collective-permute-done.13.refs_0_), channel_id=1, source_target_pairs={{0,1},{1,0},{2,3},{3,2},{4,5},{5,4},{6,7},{7,6},{8,9},{9,8},{10,11... | collective-permute-start | bytes 1622024 | tf_op jit(solution)/shard_map/ppermute | solution.py:45
  34.9 26.2 %collective-permute-start.16 = (bf16[2,264,512]{2,1,0:T(8,128)(2,1)S(1)}, bf16[2,264,512]{2,1,0:T(8,128)(2,1)S(1)}, u32[]{:S(2)}, u32[]{:S(2)}) collective-permute-start(bf16[2,264,512]{2,1,0:T(8,128)(2,1)S(1)} %collective-permute-done.15.refs_2_), channel_id=1, source_target_pairs={{0,1},{1,0},{2,3},{3,2},{4,5},{5,4},{6,7},{7,6},{8,9},{9,8},{10,11... | collective-permute-start | bytes 1622024 | tf_op jit(solution)/shard_map/ppermute | solution.py:45
  42.1 23.5 %collective-permute-start.11 = (bf16[2,264,512]{2,1,0:T(8,128)(2,1)S(1)}, bf16[2,264,512]{2,1,0:T(8,128)(2,1)S(1)}, u32[]{:S(2)}, u32[]{:S(2)}) collective-permute-start(bf16[2,264,512]{2,1,0:T(8,128)(2,1)S(1)} %collective-permute-done.9.refs_0_), channel_id=1, source_target_pairs={{0,1},{1,0},{2,3},{3,2},{4,5},{5,4},{6,7},{7,6},{8,9},{9,8},{10,11... | collective-permute-start | bytes 1622024 | tf_op jit(solution)/shard_map/ppermute | solution.py:45
  42.3 23.4 %collective-permute-start.12 = (bf16[2,264,512]{2,1,0:T(8,128)(2,1)S(1)}, bf16[2,264,512]{2,1,0:T(8,128)(2,1)S(1)}, u32[]{:S(2)}, u32[]{:S(2)}) collective-permute-start(bf16[2,264,512]{2,1,0:T(8,128)(2,1)S(1)} %collective-permute-done.10.refs_1_), channel_id=1, source_target_pairs={{0,1},{1,0},{2,3},{3,2},{4,5},{5,4},{6,7},{7,6},{8,9},{9,8},{10,11... | collective-permute-start | bytes 1622024 | tf_op jit(solution)/shard_map/ppermute | solution.py:45
  42.7 7.5 %collective-permute-start.17 = (f32[8,128]{1,0:T(8,128)S(1)}, f32[8,128]{1,0:T(8,128)S(1)}, u32[]{:S(2)}, u32[]{:S(2)}) collective-permute-start(f32[8,128]{1,0:T(8,128)S(1)} %rows.1), channel_id=1, source_target_pairs={{0,4},{1,9},{4,8},{5,13},{8,12},{9,17},{12,16},{13,21},{16,20},{17... | collective-permute-start | bytes 12296 | tf_op jit(solution)/shard_map/ppermute | solution.py:57
  50.2 6.6 %collective-permute-start.18 = (f32[8,128]{1,0:T(8,128)S(1)}, f32[8,128]{1,0:T(8,128)S(1)}, u32[]{:S(2)}, u32[]{:S(2)}) collective-permute-start(f32[8,128]{1,0:T(8,128)S(1)} %rows.1), channel_id=1, source_target_pairs={{0,12},{1,17},{4,16},{5,21},{8,20},{9,25},{12,24},{13,29},{16,28},... | collective-permute-start | bytes 12296 | tf_op jit(solution)/shard_map/ppermute | solution.py:57
  56.8 3.7 %collective-permute-start.20 = (f32[8,128]{1,0:T(8,128)S(1)}, f32[8,128]{1,0:T(8,128)S(1)}, u32[]{:S(2)}, u32[]{:S(2)}) collective-permute-start(f32[8,128]{1,0:T(8,128)S(1)} %part.1.refs_6_), channel_id=1, source_target_pairs={{0,128},{128,0},{1,129},{129,1},{2,130},{130,2},{3,131},{131,3},{4... | collective-permute-start | bytes 12296 | tf_op jit(solution)/shard_map/ppermute | solution.py:41
  60.5 5.1 %collective-permute-start.19 = (f32[8,128]{1,0:T(8,128)S(1)}, f32[8,128]{1,0:T(8,128)S(1)}, u32[]{:S(2)}, u32[]{:S(2)}) collective-permute-start(f32[8,128]{1,0:T(8,128)S(1)} %part.1.refs_6_), channel_id=1, source_target_pairs={{0,1},{1,0},{2,3},{3,2},{4,5},{5,4},{6,7},{7,6},{8,9},{9,8},{10,11... | collective-permute-start | bytes 12296 | tf_op jit(solution)/shard_map/ppermute | solution.py:45
  60.5 5.1 %collective-permute-start.21 = (f32[8,128]{1,0:T(8,128)S(1)}, f32[8,128]{1,0:T(8,128)S(1)}, u32[]{:S(2)}, u32[]{:S(2)}) collective-permute-start(f32[8,128]{1,0:T(8,128)S(1)} %collective-permute-done.20.refs_8_), channel_id=1, source_target_pairs={{0,1},{1,0},{2,3},{3,2},{4,5},{5,4},{6,7},{7,6},{8,9},{9,8},{10,11... | collective-permute-start | bytes 12296 | tf_op jit(solution)/shard_map/ppermute | solution.py:45
  68.9 5.9 %collective-permute-start.22 = (bf16[4,3,32,256]{3,2,1,0:T(8,128)(2,1)S(1)}, bf16[4,3,32,256]{3,2,1,0:T(8,128)(2,1)S(1)}, u32[]{:S(2)}, u32[]{:S(2)}) collective-permute-start(bf16[4,3,32,256]{3,2,1,0:T(8,128)(2,1)S(1)} %get-tuple-element.42), channel_id=1, source_target_pairs={{0,4},{1,29},{4,0},{5,9},{8,12},{9,5},{12,8},{13,17},{16,20},{17,1... | collective-permute-start | bytes 589832 | tf_op jit(solution)/shard_map/ppermute | solution.py:53
  72.7 11.4 %collective-permute-start.25 = (bf16[4,3,32,384]{3,2,1,0:T(8,128)(2,1)S(1)}, bf16[4,3,32,384]{3,2,1,0:T(8,128)(2,1)S(1)}, u32[]{:S(2)}, u32[]{:S(2)}) collective-permute-start(bf16[4,3,32,384]{3,2,1,0:T(8,128)(2,1)S(1)} %get-tuple-element.48), channel_id=1, source_target_pairs={{0,4},{1,29},{4,0},{5,9},{8,12},{9,5},{12,8},{13,17},{16,20},{17,1... | collective-permute-start | bytes 884744 | tf_op jit(solution)/shard_map/ppermute | solution.py:53
  74.9 9.2 %collective-permute-start.23 = (bf16[3,32,256]{2,1,0:T(8,128)(2,1)S(1)}, bf16[3,32,256]{2,1,0:T(8,128)(2,1)S(1)}, u32[]{:S(2)}, u32[]{:S(2)}) collective-permute-start(bf16[3,32,256]{2,1,0:T(8,128)(2,1)S(1)} %get-tuple-element.58), channel_id=1, source_target_pairs={{0,8},{4,12},{8,16},{12,20},{16,24},{20,28},{24,0},{28,4},{1,9},{5... | collective-permute-start | bytes 147464 | tf_op jit(solution)/shard_map/ppermute | solution.py:63
  75.0 9.1 %collective-permute-start.24 = (bf16[3,32,256]{2,1,0:T(8,128)(2,1)S(1)}, bf16[3,32,256]{2,1,0:T(8,128)(2,1)S(1)}, u32[]{:S(2)}, u32[]{:S(2)}) collective-permute-start(bf16[3,32,256]{2,1,0:T(8,128)(2,1)S(1)} %get-tuple-element.57), channel_id=1, source_target_pairs={{0,24},{4,28},{8,0},{12,4},{16,8},{20,12},{24,16},{28,20},{1,25},{... | collective-permute-start | bytes 147464 | tf_op jit(solution)/shard_map/ppermute | solution.py:63
  84.2 6.6 %collective-permute-start.26 = (bf16[3,32,384]{2,1,0:T(8,128)(2,1)S(1)}, bf16[3,32,384]{2,1,0:T(8,128)(2,1)S(1)}, u32[]{:S(2)}, u32[]{:S(2)}) collective-permute-start(bf16[3,32,384]{2,1,0:T(8,128)(2,1)S(1)} %get-tuple-element.55), channel_id=1, source_target_pairs={{0,8},{4,12},{8,16},{12,20},{16,24},{20,28},{24,0},{28,4},{1,9},{5... | collective-permute-start | bytes 221192 | tf_op jit(solution)/shard_map/ppermute | solution.py:63
  87.0 6.4 %collective-permute-start.27 = (bf16[3,32,384]{2,1,0:T(8,128)(2,1)S(1)}, bf16[3,32,384]{2,1,0:T(8,128)(2,1)S(1)}, u32[]{:S(2)}, u32[]{:S(2)}) collective-permute-start(bf16[3,32,384]{2,1,0:T(8,128)(2,1)S(1)} %get-tuple-element.54), channel_id=1, source_target_pairs={{0,24},{4,28},{8,0},{12,4},{16,8},{20,12},{24,16},{28,20},{1,25},{... | collective-permute-start | bytes 221192 | tf_op jit(solution)/shard_map/ppermute | solution.py:63
  88.5 10.6 %collective-permute-start.28 = (bf16[3,32,640]{2,1,0:T(8,128)(2,1)S(1)}, bf16[3,32,640]{2,1,0:T(8,128)(2,1)S(1)}, u32[]{:S(2)}, u32[]{:S(2)}) collective-permute-start(bf16[3,32,640]{2,1,0:T(8,128)(2,1)S(1)} %pad_maximum_fusion.2), channel_id=1, source_target_pairs={{0,16},{4,20},{8,24},{12,28},{16,0},{20,4},{24,8},{28,12},{1,17},{... | collective-permute-start | bytes 368648 | tf_op jit(solution)/shard_map/ppermute | solution.py:63

commit v9 on v8

--- a/solution.py
+++ b/solution.py
@@ -1,3 +1,5 @@
+from functools import partial as partial_call
+
 import jax
 import jax.numpy as jnp
 from jax import lax
@@ -11,7 +13,7 @@
 I32 = jnp.int32
 ROOT_2_PI = 0.7978845608028654
 CUBIC = 0.044715
-CUTS = ((0, 256), (256, 640))
+CUTS = ((0, 384), (384, 640))
 OWN, EARLY, LATE, FAR = ((0, 0), (0, 1)), ((1, 0), (3, 1)), ((1, 1), (3, 0)), ((2, 0), (2, 1))
 BLK = ("xl", "y", "z")
 PLANE = ("xl", "y", "xh", "c")
@@ -114,13 +116,18 @@
 
 
 def weights_kernel(w_gate, w_lin, w_out_t, w_in, w_out, sems):
-    pairs = [(w_out_t, w_out)]
-    for lower, upper in CUTS:
-        width = upper - lower
-        for n, w in enumerate((w_gate, w_lin)):
-            target = w_in.at[:, :, pl.ds(2 * lower + n * width, width)]
-            pairs.append((w.at[:, :, pl.ds(lower, width)], target))
-    copies = [pltpu.make_async_copy(*pair, sems.at[i]) for i, pair in enumerate(pairs)]
+    xh = lax.axis_index("xh").astype(I32)
+    copies = []
+    for side in range(2):
+        for eh in range(2):
+            source, target = 2 * (xh ^ eh) + side, pl.ds(512 * (2 * side + eh), 512)
+            copies.append((w_out_t.at[source], w_out.at[target]))
+            for lower, upper in CUTS:
+                width = upper - lower
+                for n, w in enumerate((w_gate, w_lin)):
+                    columns = pl.ds(2 * lower + n * width, width)
+                    copies.append((w.at[source, :, pl.ds(lower, width)], w_in.at[target, columns]))
+    copies = [pltpu.make_async_copy(*pair, sems.at[i]) for i, pair in enumerate(copies)]
     for copy in copies:
         copy.start()
     for copy in copies:
@@ -131,12 +138,12 @@
     return pl.pallas_call(
         weights_kernel,
         out_shape=(
-            jax.ShapeDtypeStruct((4, 512, 1280), BF16),
-            jax.ShapeDtypeStruct((4, 512, 640), BF16),
+            jax.ShapeDtypeStruct((2048, 1280), BF16),
+            jax.ShapeDtypeStruct((2048, 640), BF16),
         ),
         in_specs=[pl.BlockSpec(memory_space=pltpu.HBM)] * 3,
         out_specs=(VMEM, VMEM),
-        scratch_shapes=[pltpu.SemaphoreType.DMA((5,))],
+        scratch_shapes=[pltpu.SemaphoreType.DMA((20,))],
         compiler_params=PARAMS,
         name="load",
     )(*[hbm(w.reshape(4, 512, 640)) for w in (w_gate, w_lin, w_out_t)])
@@ -182,36 +189,71 @@
     )(*rows)
 
 
-def add_block(m, j, ec, block, w_in, w_out, acc, cols, cuts=CUTS, with_cols=True):
-    xl, y, _, xh, c = place()
-    x_first = (c ^ ec) == 0
-    eh = jnp.where(x_first, j, m >> 1)
-    p0 = jnp.where(x_first, 2 * m, 4 * j + (m & 1))
-    p1 = jnp.where(x_first, 2 * m + 1, 4 * j + 2 + (m & 1))
-    shard = (xh ^ eh) * 2 + (c ^ ec)
-    xs = block[:, 0:128].reshape(256, 512)
-    ys = block[:, 128:256].reshape(256, 512)
-    first, end = cuts[0][0], cuts[-1][1]
-    pre = jnp.dot(xs, w_in[shard, :, 2 * first : 2 * end], preferred_element_type=F32)
-    for lower, upper in cuts:
-        width = upper - lower
-        for n in range(2):
-            at = 2 * (lower - first) + n * width
-            acc[n, p0, :, lower:upper] += pre[:128, at : at + width]
-            acc[n, p1, :, lower:upper] += pre[128:, at : at + width]
-    dh = jnp.dot(ys, w_out[shard, :, first:end], preferred_element_type=F32)
-    acc[2, p0, :, first:end] += dh[:128]
-    acc[2, p1, :, first:end] += dh[128:]
-    if not with_cols:
+def sides(own, other):
+    c = lax.axis_index("c").astype(I32)
+    pairs = [(mine[...], theirs[...]) for mine, theirs in zip(own, other)]
+    x_first = [jnp.where(c == 0, mine, theirs) for mine, theirs in pairs]
+    y_first = [jnp.where(c == 0, theirs, mine) for mine, theirs in pairs]
+    return x_first, y_first
+
+
+def add_rows(side, ehs, rows, blocks, w_in, w_out, acc, cols, stored=(), cuts=CUTS):
+    xl, y, _, xh, _ = place()
+    low, end = 1024 * side + 512 * ehs[0], 1024 * side + 512 * (ehs[-1] + 1)
+    parts = []
+    for n in range(2):
+        pieces = [[b[:, 128 * n : 128 * n + 128].reshape(256, 512) for b in row] for row in blocks]
+        parts.append(jnp.concatenate([jnp.concatenate(p, axis=1) for p in pieces], axis=0))
+    first, last = cuts[0][0], cuts[-1][1]
+    pre = jnp.dot(parts[0], w_in[low:end, 2 * first : 2 * last], preferred_element_type=F32)
+    dh = jnp.dot(parts[1], w_out[low:end, first:last], preferred_element_type=F32)
+    for i, p in enumerate(rows):
+        at_rows = slice(128 * i, 128 * i + 128)
+        values = [(2, first, last, dh[at_rows])]
+        for lower, upper in cuts:
+            for n in range(2):
+                at = 2 * (lower - first) + n * (upper - lower)
+                values.append((n, lower, upper, pre[at_rows, at : at + upper - lower]))
+        for n, lower, upper, value in values:
+            if p in stored:
+                acc[n, p, :, lower:upper] = value
+            else:
+                acc[n, p, :, lower:upper] += value
+    if cols is None:
         return
-
-    @pl.when((ec == ((y >> 1) ^ c)) & (eh == (xl ^ xh)))
-    def _():
-        low = (y & 1) == 0
-        for n, v in ((0, xs), (1, ys)):
-            v = jnp.where(low, v[:, :256], v[:, 256:])
-            cols[n, p0] = v[:128]
-            cols[n, p1] = v[128:]
+    for k, eh in enumerate(ehs):
+
+        @pl.when(((y >> 1) == side) & ((xl ^ xh) == eh))
+        def _():
+            for n in range(2):
+                v = parts[n][:, 512 * k : 512 * k + 512]
+                v = jnp.where((y & 1) == 0, v[:, :256], v[:, 256:])
+                for i, p in enumerate(rows):
+                    cols[n, p] = v[128 * i : 128 * i + 128]
+
+
+def first_kernel(own0, own1, other0, other1, w_in, w_out, acc, cols):
+    (a0, a1), (b0, b1) = sides((own0, own1), (other0, other1))
+    for p in (3, 5, 7):
+        acc[:, p] = jnp.zeros((3, 128, 640), F32)
+    add_rows(1, (0,), (0, 2, 4, 6), [[b0], [b1]], w_in, w_out, acc, cols, stored=(0, 2, 4, 6))
+    add_rows(0, (0, 1), (0, 1), [[a0, a1]], w_in, w_out, acc, cols, stored=(1,))
+
+
+def near_kernel(side, *refs):
+    own, other, (w_in, w_out), (acc, cols) = refs[0:4], refs[4:8], refs[8:10], refs[-2:]
+    b10, b11, b30, b31 = sides(own, other)[side]
+    if side == 0:
+        rows, blocks = (2, 3, 6, 7), [[b10, b11], [b30, b31]]
+    else:
+        rows, blocks = (1, 3, 5, 7), [[b10, b30], [b11, b31]]
+    add_rows(side, (0, 1), rows, blocks, w_in, w_out, acc, cols)
+
+
+def far_rows(cut, own, other, w_in, w_out, acc, cols):
+    (a0, a1), (b0, b1) = sides(own, other)
+    add_rows(0, (0, 1), (4, 5), [[a0, a1]], w_in, w_out, acc, cols, cuts=(CUTS[cut],))
+    add_rows(1, (1,), (0, 2, 4, 6), [[b0], [b1]], w_in, w_out, acc, cols, cuts=(CUTS[cut],))
 
 
 STATE = (jax.ShapeDtypeStruct((3, 8, 128, 640), F32), jax.ShapeDtypeStruct((2, 8, 128, 256), BF16))
@@ -221,16 +263,8 @@
     return pl.CostEstimate(flops=giga << 30, bytes_accessed=1 << 20, transcendentals=0)
 
 
-def gathered(items, w_in, w_out, state):
-    n = len(items)
-
-    def kernel(*refs):
-        blocks, (w_in, w_out), (acc, cols) = refs[:n], refs[n : n + 2], refs[-2:]
-        if not state:
-            acc[...] = jnp.zeros_like(acc)
-        for (m, j, ec, _), block in zip(items, blocks):
-            add_block(m, j, ec, block, w_in, w_out, acc, cols)
-
+def gathered(kernel, blocks, w_in, w_out, state):
+    n = len(blocks)
     return pl.pallas_call(
         kernel,
         out_shape=STATE,
@@ -239,26 +273,25 @@
         input_output_aliases={n + 2: 0, n + 3: 1} if state else {},
         compiler_params=PARAMS,
         cost_estimate=priced(n // 2),
-    )(*[item[3] for item in items], w_in, w_out, *state)
-
-
-def finished(cut, items, w_in, w_out, state, terms):
+    )(*blocks, w_in, w_out, *state)
+
+
+def finished(cut, blocks, w_in, w_out, state, terms):
     width = CUTS[cut][1] - CUTS[cut][0]
 
     def kernel(*refs):
-        blocks, (w_in, w_out), terms = refs[:2], refs[2:4], refs[6:10]
-        acc, cols, *rest = refs[10:]
-        for (m, j, ec, _), block in zip(items, blocks):
-            add_block(m, j, ec, block, w_in, w_out, acc, cols, (CUTS[cut],), cut == 0)
+        own, other, weights, terms = refs[:2], refs[2:4], refs[4:6], refs[8:12]
+        acc, cols, *rest = refs[12:]
+        far_rows(cut, own, other, *weights, acc, None if cut else cols)
         last_kernel(CUTS[cut], terms, acc, cols, *rest)
 
     *state, keep, send = pl.pallas_call(
         kernel,
         out_shape=STATE
         + (jax.ShapeDtypeStruct((4, 3, 32, width), F32), jax.ShapeDtypeStruct((4, 3, 32, width), BF16)),
-        in_specs=[VMEM] * 10,
+        in_specs=[VMEM] * 12,
         out_specs=(VMEM,) * 4,
-        input_output_aliases={4: 0, 5: 1},
+        input_output_aliases={6: 0, 7: 1},
         scratch_shapes=[
             pltpu.VMEM((8, 128, 2 * width), BF16),
             pltpu.VMEM((8, 128, width), BF16),
@@ -266,7 +299,7 @@
         ],
         compiler_params=PARAMS,
         cost_estimate=priced(2),
-    )(*[item[3] for item in items], w_in, w_out, *state, *terms)
+    )(*blocks, w_in, w_out, *state, *terms)
     return state, keep, send
 
 
@@ -343,17 +376,17 @@
     for part in partials:
         terms += [part, sibling(part)]
 
-    def items(keys, sides=(0, 1)):
-        return [(m, j, ec, (blocks, others)[ec][m, j]) for m, j in keys for ec in sides]
-
-    state = gathered(items(OWN), w_in, w_out, ())
-    state = gathered(items(EARLY), w_in, w_out, state)
+    def both(keys):
+        return [blocks[key] for key in keys] + [others[key] for key in keys]
+
+    state = gathered(first_kernel, both(OWN), w_in, w_out, ())
+    pairs = both(sorted(EARLY + LATE))
+    state = gathered(partial_call(near_kernel, 0), pairs, w_in, w_out, state)
     state, blocks[2, 0], blocks[2, 1] = lax.optimization_barrier((state, blocks[2, 0], blocks[2, 1]))
     for k, j in FAR:
         others[k, j] = sibling(blocks[k, j])
-    state = gathered(items(LATE), w_in, w_out, state)
-    state = gathered(items(FAR, (0,)), w_in, w_out, state)
-    halves = items(FAR, (1,))
+    state = gathered(partial_call(near_kernel, 1), pairs, w_in, w_out, state)
+    halves = both(FAR)
     keeps, got = [], []
     for cut in range(2):
         state, keep, send = finished(cut, halves, w_in, w_out, state, terms)

time: 100 us -> 88.5 us (0.89)
  waiting for transfers between devices: 47.5 us -> 29.2 us
  starting transfers between devices: 27.8 us -> 36.6 us
  Pallas kernels: 22.5 us -> 20 us
    ppermute x2, waiting for transfers between devices: 10.5 us -> 1.68 us  [z_shift(): lax.ppermute(block, ('z', 'c'), [(z * 2 + c, (z + step + c) % 8 * 2 + c)...]
    ppermute x5, waiting for transfers between devices: 13.3 us -> 7.05 us  [z_step(): return lax.ppermute(block, 'z', [(z, (z + step) % 8) for z in range(8)])]
    ppermute x2, starting transfers between devices: 3.64 us -> 7.83 us  [z_shift(): lax.ppermute(block, ('z', 'c'), [(z * 2 + c, (z + step + c) % 8 * 2 + c)...]
    pallas_call x4 -> x3, Pallas kernels: 11.2 us -> 7.75 us  [gathered(): pl.pallas_call(kernel, out_shape=STATE, in_specs=[VMEM] * (n + 2 + len(st...]
    ppermute x9, starting transfers between devices: 9.39 us -> 12.6 us  [across(): return lax.ppermute(block, PLANE, route)]
    ppermute x1, waiting for transfers between devices: 3.59 us -> 1.02 us  [swapped(): return lax.ppermute(block, axis, [(i, i ^ flip) for i in range(size)])]
    ppermute x9, waiting for transfers between devices: 20.1 us -> 17.8 us  [across(): return lax.ppermute(block, PLANE, route)]
    ppermute x2, waiting for transfers between devices: 0.01 us -> 1.66 us  [z_pair(): lax.ppermute(block, ('z', 'c'), [(z * 2 + c, partner_of(z, c) * 2 + c) fo...]
  transfers between devices with their start and end apart: 29 -> 29, of which waited for: 11 -> 15; matrix products, arithmetic and copies ran while one was open for 0% -> 0% of each run, Pallas kernels for 18% -> 16%
where the time goes in v9:
time: 88.5 us; the launch traced here: 87.7 us
  starting transfers between devices  36.6 us (41%)
  waiting for transfers between devices  29.2 us (33%)
  Pallas kernels  20 us (23%)
  other arithmetic  1.02 us (1%)
    ppermute x9, waiting for transfers between devices, across(): return lax.ppermute(block, PLANE, route)  17.8 us
    ppermute x9, starting transfers between devices, across(): return lax.ppermute(block, PLANE, route)  12.6 us
    ppermute x5, starting transfers between devices, z_step(): return lax.ppermute(block, 'z', [(z, (z + step) % 8) for z in range(8)])  9.44 us
    pallas_call x2, Pallas kernels, finished(): pl.pallas_call(kernel, out_shape=STATE + (jax.ShapeDtypeStruct((4, 3, 32,...  7.84 us
    ppermute x2, starting transfers between devices, z_shift(): lax.ppermute(block, ('z', 'c'), [(z * 2 + c, (z + step + c) % 8 * 2 + c)...  7.83 us
    pallas_call x3, Pallas kernels, gathered(): pl.pallas_call(kernel, out_shape=STATE, in_specs=[VMEM] * (n + 2 + len(st...  7.75 us
    ppermute x5, waiting for transfers between devices, z_step(): return lax.ppermute(block, 'z', [(z, (z + step) % 8) for z in range(8)])  7.05 us
    pallas_call x1, Pallas kernels, loaded_weights(): pl.pallas_call(weights_kernel, out_shape=(jax.ShapeDtypeStruct((2048, 128...  3.4 us
  transfers between devices with their start and end apart: 29, of which 15 were waited for; matrix products, arithmetic and copies ran while one was open for 0% of the time, Pallas kernels for 16%

profile of v9, /device:TPU:6, one launch (start us, length us, event | category | flops | bytes accessed | tf_op | source)
XLA Modules:
  0.0 87.7 jit_solution(2555958985116398003)
XLA Ops:
  0.7 1.0 %message.1 = bf16[264,512]{1,0:T(8,128)(2,1)S(1)} custom-call(f32[1]{0:T(128)S(6)} %copy.25.decode, f32[1,5]{1,0:T(1,128)} %code_in.1, s32[4]{0:T(128)} %stragglers_in.1, bf16[128,512]{1,0:T(8,128)(2,1)} %tokens.1, bf16[128,512]{1,0:T(8,128)(2,1)} %grad_out.1), custom_call_target="tpu_custom_call" | custom-call | tf_op jit(solution)/shard_map/message/pallas_call | solution.py:107
  2.6 1.5 %collective-permute-start.3 = (bf16[264,512]{1,0:T(8,128)(2,1)S(1)}, bf16[264,512]{1,0:T(8,128)(2,1)S(1)}, u32[]{:S(2)}, u32[]{:S(2)}) collective-permute-start(bf16[264,512]{1,0:T(8,128)(2,1)S(1)} %message.1), channel_id=1, source_target_pairs={{0,130},{1,97},{2,128},{3,99},{32,162},{33,65},{34,160},{35,67},{6... | collective-permute-start | bytes 811016 | tf_op jit(solution)/shard_map/ppermute | solution.py:39
  4.0 1.8 %collective-permute-start.2 = (bf16[264,512]{1,0:T(8,128)(2,1)S(1)}, bf16[264,512]{1,0:T(8,128)(2,1)S(1)}, u32[]{:S(2)}, u32[]{:S(2)}) collective-permute-start(bf16[264,512]{1,0:T(8,128)(2,1)S(1)} %message.1), channel_id=1, source_target_pairs={{0,2},{1,65},{2,0},{3,67},{32,34},{33,97},{34,32},{35,99},{64,66},... | collective-permute-start | bytes 811016 | tf_op jit(solution)/shard_map/ppermute | solution.py:39
  5.8 2.4 %collective-permute-done = bf16[264,512]{1,0:T(8,128)(2,1)S(1)} collective-permute-done((bf16[264,512]{1,0:T(8,128)(2,1)S(1)}, bf16[264,512]{1,0:T(8,128)(2,1)S(1)}, u32[]{:S(2)}, u32[]{:S(2)}) %collective-permute-start) | collective-permute-done | bytes 270368 | tf_op jit(solution)/shard_map/ppermute | solution.py:39
  8.4 3.1 %collective-permute-start.5 = (bf16[2,264,512]{2,1,0:T(8,128)(2,1)S(1)}, bf16[2,264,512]{2,1,0:T(8,128)(2,1)S(1)}, u32[]{:S(2)}, u32[]{:S(2)}) collective-permute-start(bf16[2,264,512]{2,1,0:T(8,128)(2,1)S(1)} %pad_maximum_fusion.own0.own_low), channel_id=1, source_target_pairs={{0,96},{1,131},{2,98},{3,129},{32,64},{33,163},{34,66},{35,161},{6... | collective-permute-start | bytes 1622024 | tf_op jit(solution)/shard_map/ppermute | solution.py:39
  11.6 1.9 %collective-permute-done.3 = bf16[264,512]{1,0:T(8,128)(2,1)S(1)} collective-permute-done((bf16[264,512]{1,0:T(8,128)(2,1)S(1)}, bf16[264,512]{1,0:T(8,128)(2,1)S(1)}, u32[]{:S(2)}, u32[]{:S(2)}) %collective-permute-start.3) | collective-permute-done | bytes 270368 | tf_op jit(solution)/shard_map/ppermute | solution.py:39
  13.5 3.3 %collective-permute-start.6 = (bf16[2,264,512]{2,1,0:T(8,128)(2,1)S(1)}, bf16[2,264,512]{2,1,0:T(8,128)(2,1)S(1)}, u32[]{:S(2)}, u32[]{:S(2)}) collective-permute-start(bf16[2,264,512]{2,1,0:T(8,128)(2,1)S(1)} %pad_maximum_fusion.1.own1.own_high), channel_id=1, source_target_pairs={{0,96},{1,131},{2,98},{3,129},{32,64},{33,163},{34,66},{35,161},{6... | collective-permute-start | bytes 1622024 | tf_op jit(solution)/shard_map/ppermute | solution.py:39
  16.9 2.1 %collective-permute-done.5.refs_2_ = bf16[2,264,512]{2,1,0:T(8,128)(2,1)S(1)} collective-permute-done((bf16[2,264,512]{2,1,0:T(8,128)(2,1)S(1)}, bf16[2,264,512]{2,1,0:T(8,128)(2,1)S(1)}, u32[]{:S(2)}, u32[]{:S(2)}) %collective-permute-start.5) | collective-permute-done | bytes 540704 | tf_op jit(solution)/shard_map/ppermute | solution.py:39
  19.1 1.8 %collective-permute-done.1.refs_0_ = bf16[2,264,512]{2,1,0:T(8,128)(2,1)S(1)} collective-permute-done((bf16[2,264,512]{2,1,0:T(8,128)(2,1)S(1)}, bf16[2,264,512]{2,1,0:T(8,128)(2,1)S(1)}, u32[]{:S(2)}, u32[]{:S(2)}) %collective-permute-start.1) | collective-permute-done | bytes 540704 | tf_op jit(solution)/shard_map/ppermute | solution.py:39
  20.8 4.0 %collective-permute-done.6.refs_3_ = bf16[2,264,512]{2,1,0:T(8,128)(2,1)S(1)} collective-permute-done((bf16[2,264,512]{2,1,0:T(8,128)(2,1)S(1)}, bf16[2,264,512]{2,1,0:T(8,128)(2,1)S(1)}, u32[]{:S(2)}, u32[]{:S(2)}) %collective-permute-start.6) | collective-permute-done | bytes 540704 | tf_op jit(solution)/shard_map/ppermute | solution.py:39
  24.8 1.8 %collective-permute-done.4.refs_1_ = bf16[2,264,512]{2,1,0:T(8,128)(2,1)S(1)} collective-permute-done((bf16[2,264,512]{2,1,0:T(8,128)(2,1)S(1)}, bf16[2,264,512]{2,1,0:T(8,128)(2,1)S(1)}, u32[]{:S(2)}, u32[]{:S(2)}) %collective-permute-start.4) | collective-permute-done | bytes 540704 | tf_op jit(solution)/shard_map/ppermute | solution.py:39
  26.6 3.4 %load.1 = (bf16[2048,1280]{1,0:T(8,128)(2,1)S(1)}, bf16[2048,640]{1,0:T(8,128)(2,1)S(1)}) custom-call(bf16[4,512,640]{2,1,0:T(8,128)(2,1)} %bitcast.34, bf16[4,512,640]{2,1,0:T(8,128)(2,1)} %bitcast.35, bf16[4,512,640]{2,1,0:T(8,128)(2,1)} %bitcast.36), custom_call_target="tpu_custom_call" | custom-call | tf_op jit(solution)/shard_map/load/pallas_call | solution.py:138
  30.0 1.8 %collective-permute-start.13 = (bf16[2,264,512]{2,1,0:T(8,128)(2,1)S(1)}, bf16[2,264,512]{2,1,0:T(8,128)(2,1)S(1)}, u32[]{:S(2)}, u32[]{:S(2)}) collective-permute-start(bf16[2,264,512]{2,1,0:T(8,128)(2,1)S(1)} %collective-permute-done.1.refs_0_), channel_id=1, source_target_pairs={{0,96},{1,131},{2,98},{3,129},{32,64},{33,163},{34,66},{35,161},{6... | collective-permute-start | bytes 1622024 | tf_op jit(solution)/shard_map/ppermute | solution.py:39
  31.9 2.9 %shard_map.82 = (f32[3,8,128,640]{3,2,1,0:T(8,128)S(1)}, bf16[2,8,128,256]{3,2,1,0:T(8,128)(2,1)S(1)}) custom-call(bf16[2,264,512]{2,1,0:T(8,128)(2,1)S(1)} %pad_maximum_fusion.own0.own_low, bf16[2,264,512]{2,1,0:T(8,128)(2,1)S(1)} %pad_maximum_fusion.1.own1.own_high, bf16[2,264,512]{2,1,0:T(8,128)(2,1)S(1)} %collective-permute-done.11.other0.other_low, ...), custom_call_target="tpu_custom_call" | custom-call | flops 2147483648 | bytes 1048576 | tf_op jit(solution)/shard_map/pallas_call | solution.py:268
  34.8 2.4 %shard_map.83 = (f32[3,8,128,640]{3,2,1,0:T(8,128)S(1)}, bf16[2,8,128,256]{3,2,1,0:T(8,128)(2,1)S(1)}) custom-call(bf16[2,264,512]{2,1,0:T(8,128)(2,1)S(1)} %collective-permute-done.1.refs_0_, bf16[2,264,512]{2,1,0:T(8,128)(2,1)S(1)} %collective-permute-done.4.refs_1_, ...), custom_call_target="tpu_custom_call", output_to_operand_aliasing={{0}: (10, {}), {1}: (11, {})} | custom-call | flops 4294967296 | bytes 1048576 | tf_op jit(solution)/shard_map/pallas_call | solution.py:268
  37.3 3.4 %collective-permute-done.13.refs_0_ = bf16[2,264,512]{2,1,0:T(8,128)(2,1)S(1)} collective-permute-done((bf16[2,264,512]{2,1,0:T(8,128)(2,1)S(1)}, bf16[2,264,512]{2,1,0:T(8,128)(2,1)S(1)}, u32[]{:S(2)}, u32[]{:S(2)}) %collective-permute-start.13) | collective-permute-done | bytes 540704 | tf_op jit(solution)/shard_map/ppermute | solution.py:39
  41.7 4.7 %collective-permute-start.18 = (f32[8,128]{1,0:T(8,128)S(1)}, f32[8,128]{1,0:T(8,128)S(1)}, u32[]{:S(2)}, u32[]{:S(2)}) collective-permute-start(f32[8,128]{1,0:T(8,128)S(1)} %rows.1), channel_id=1, source_target_pairs={{0,12},{1,17},{4,16},{5,21},{8,20},{9,25},{12,24},{13,29},{16,28},... | collective-permute-start | bytes 12296 | tf_op jit(solution)/shard_map/ppermute | solution.py:59
  46.4 3.1 %collective-permute-start.17 = (f32[8,128]{1,0:T(8,128)S(1)}, f32[8,128]{1,0:T(8,128)S(1)}, u32[]{:S(2)}, u32[]{:S(2)}) collective-permute-start(f32[8,128]{1,0:T(8,128)S(1)} %rows.1), channel_id=1, source_target_pairs={{0,4},{1,9},{4,8},{5,13},{8,12},{9,17},{12,16},{13,21},{16,20},{17... | collective-permute-start | bytes 12296 | tf_op jit(solution)/shard_map/ppermute | solution.py:59
  50.1 1.1 %collective-permute-done.17.near = f32[8,128]{1,0:T(8,128)S(1)} collective-permute-done((f32[8,128]{1,0:T(8,128)S(1)}, f32[8,128]{1,0:T(8,128)S(1)}, u32[]{:S(2)}, u32[]{:S(2)}) %collective-permute-start.17) | collective-permute-done | bytes 4128 | tf_op jit(solution)/shard_map/ppermute | solution.py:59
  52.2 1.8 %collective-permute-start.19 = (f32[8,128]{1,0:T(8,128)S(1)}, f32[8,128]{1,0:T(8,128)S(1)}, u32[]{:S(2)}, u32[]{:S(2)}) collective-permute-start(f32[8,128]{1,0:T(8,128)S(1)} %part.1.refs_8_), channel_id=1, source_target_pairs={{0,1},{1,0},{2,3},{3,2},{4,5},{5,4},{6,7},{7,6},{8,9},{9,8},{10,11... | collective-permute-start | bytes 12296 | tf_op jit(solution)/shard_map/ppermute | solution.py:47
  53.9 1.0 %collective-permute-done.20.refs_10_ = f32[8,128]{1,0:T(8,128)S(1)} collective-permute-done((f32[8,128]{1,0:T(8,128)S(1)}, f32[8,128]{1,0:T(8,128)S(1)}, u32[]{:S(2)}, u32[]{:S(2)}) %collective-permute-start.20) | collective-permute-done | bytes 4128 | tf_op jit(solution)/shard_map/ppermute | solution.py:43
  55.8 2.4 %shard_map.84 = (f32[3,8,128,640]{3,2,1,0:T(8,128)S(1)}, bf16[2,8,128,256]{3,2,1,0:T(8,128)(2,1)S(1)}) custom-call(bf16[2,264,512]{2,1,0:T(8,128)(2,1)S(1)} %collective-permute-done.1.refs_0_, bf16[2,264,512]{2,1,0:T(8,128)(2,1)S(1)} %collective-permute-done.4.refs_1_, ...), custom_call_target="tpu_custom_call", output_to_operand_aliasing={{0}: (10, {}), {1}: (11, {})} | custom-call | flops 4294967296 | bytes 1048576 | tf_op jit(solution)/shard_map/pallas_call | solution.py:268
  58.3 4.6 %shard_map.85 = (f32[3,8,128,640]{3,2,1,0:T(8,128)S(1)}, bf16[2,8,128,256]{3,2,1,0:T(8,128)(2,1)S(1)}, f32[4,3,32,384]{3,2,1,0:T(8,128)S(1)}, bf16[4,3,32,384]{3,2,1,0:T(8,128)(2,1)S(1)}) custom-call(bf16[2,264,512]{2,1,0:T(8,128)(2,1)S(1)} %collective-permute-done.13.refs_0_, ...), custom_call_target="tpu_custom_call", output_to_operand_aliasing={{0}: (6, {}), {1}: (7, {})} | custom-call | flops 2147483648 | bytes 1048576 | tf_op jit(solution)/shard_map/pallas_call | solution.py:288
  62.9 1.5 %collective-permute-start.22 = (bf16[4,3,32,384]{3,2,1,0:T(8,128)(2,1)S(1)}, bf16[4,3,32,384]{3,2,1,0:T(8,128)(2,1)S(1)}, u32[]{:S(2)}, u32[]{:S(2)}) collective-permute-start(bf16[4,3,32,384]{3,2,1,0:T(8,128)(2,1)S(1)} %get-tuple-element.38), channel_id=1, source_target_pairs={{0,4},{1,29},{4,0},{5,9},{8,12},{9,5},{12,8},{13,17},{16,20},{17,1... | collective-permute-start | bytes 884744 | tf_op jit(solution)/shard_map/ppermute | solution.py:55
  64.3 3.2 %shard_map.86 = (f32[3,8,128,640]{3,2,1,0:T(8,128)S(1)}, bf16[2,8,128,256]{3,2,1,0:T(8,128)(2,1)S(1)}, f32[4,3,32,256]{3,2,1,0:T(8,128)S(1)}, bf16[4,3,32,256]{3,2,1,0:T(8,128)(2,1)S(1)}) custom-call(bf16[2,264,512]{2,1,0:T(8,128)(2,1)S(1)} %collective-permute-done.13.refs_0_, ...), custom_call_target="tpu_custom_call", output_to_operand_aliasing={{0}: (6, {}), {1}: (7, {})} | custom-call | flops 2147483648 | bytes 1048576 | tf_op jit(solution)/shard_map/pallas_call | solution.py:288
  67.6 1.0 %collective-permute-start.25 = (bf16[4,3,32,256]{3,2,1,0:T(8,128)(2,1)S(1)}, bf16[4,3,32,256]{3,2,1,0:T(8,128)(2,1)S(1)}, u32[]{:S(2)}, u32[]{:S(2)}) collective-permute-start(bf16[4,3,32,256]{3,2,1,0:T(8,128)(2,1)S(1)} %get-tuple-element.44), channel_id=1, source_target_pairs={{0,4},{1,29},{4,0},{5,9},{8,12},{9,5},{12,8},{13,17},{16,20},{17,1... | collective-permute-start | bytes 589832 | tf_op jit(solution)/shard_map/ppermute | solution.py:55
  68.6 1.4 %collective-permute-done.22 = bf16[4,3,32,384]{3,2,1,0:T(8,128)(2,1)S(1)} collective-permute-done((bf16[4,3,32,384]{3,2,1,0:T(8,128)(2,1)S(1)}, bf16[4,3,32,384]{3,2,1,0:T(8,128)(2,1)S(1)}, u32[]{:S(2)}, u32[]{:S(2)}) %collective-permute-start.22) | collective-permute-done | bytes 294944 | tf_op jit(solution)/shard_map/ppermute | solution.py:55
  70.0 2.7 %collective-permute-start.24 = (bf16[3,32,384]{2,1,0:T(8,128)(2,1)S(1)}, bf16[3,32,384]{2,1,0:T(8,128)(2,1)S(1)}, u32[]{:S(2)}, u32[]{:S(2)}) collective-permute-start(bf16[3,32,384]{2,1,0:T(8,128)(2,1)S(1)} %get-tuple-element.50), channel_id=1, source_target_pairs={{0,24},{4,28},{8,0},{12,4},{16,8},{20,12},{24,16},{28,20},{1,25},{... | collective-permute-start | bytes 221192 | tf_op jit(solution)/shard_map/ppermute | solution.py:65
  73.4 3.6 %collective-permute-start.27 = (bf16[3,32,256]{2,1,0:T(8,128)(2,1)S(1)}, bf16[3,32,256]{2,1,0:T(8,128)(2,1)S(1)}, u32[]{:S(2)}, u32[]{:S(2)}) collective-permute-start(bf16[3,32,256]{2,1,0:T(8,128)(2,1)S(1)} %get-tuple-element.53), channel_id=1, source_target_pairs={{0,24},{4,28},{8,0},{12,4},{16,8},{20,12},{24,16},{28,20},{1,25},{... | collective-permute-start | bytes 147464 | tf_op jit(solution)/shard_map/ppermute | solution.py:65
  77.1 2.8 %collective-permute-start.28 = (bf16[3,32,640]{2,1,0:T(8,128)(2,1)S(1)}, bf16[3,32,640]{2,1,0:T(8,128)(2,1)S(1)}, u32[]{:S(2)}, u32[]{:S(2)}) collective-permute-start(bf16[3,32,640]{2,1,0:T(8,128)(2,1)S(1)} %pad_maximum_fusion.2), channel_id=1, source_target_pairs={{0,16},{4,20},{8,24},{12,28},{16,0},{20,4},{24,8},{28,12},{1,17},{... | collective-permute-start | bytes 368648 | tf_op jit(solution)/shard_map/ppermute | solution.py:65
  79.9 4.8 %collective-permute-done.26 = bf16[3,32,256]{2,1,0:T(8,128)(2,1)S(1)} collective-permute-done((bf16[3,32,256]{2,1,0:T(8,128)(2,1)S(1)}, bf16[3,32,256]{2,1,0:T(8,128)(2,1)S(1)}, u32[]{:S(2)}, u32[]{:S(2)}) %collective-permute-start.26) | collective-permute-done | bytes 49184 | tf_op jit(solution)/shard_map/ppermute | solution.py:65
  84.8 2.3 %collective-permute-done.28 = bf16[3,32,640]{2,1,0:T(8,128)(2,1)S(1)} collective-permute-done((bf16[3,32,640]{2,1,0:T(8,128)(2,1)S(1)}, bf16[3,32,640]{2,1,0:T(8,128)(2,1)S(1)}, u32[]{:S(2)}, u32[]{:S(2)}) %collective-permute-start.28) | collective-permute-done | bytes 122912 | tf_op jit(solution)/shard_map/ppermute | solution.py:65
  (45 shorter events, 6.5 us)
Async XLA Ops:
  1.7 6.5 %collective-permute-start = (bf16[264,512]{1,0:T(8,128)(2,1)S(1)}, bf16[264,512]{1,0:T(8,128)(2,1)S(1)}, u32[]{:S(2)}, u32[]{:S(2)}) collective-permute-start(bf16[264,512]{1,0:T(8,128)(2,1)S(1)} %message.1), channel_id=1, source_target_pairs={{0,128},{1,33},{2,130},{3,35},{32,160},{33,1},{34,162},{35,3},{64,... | collective-permute-start | bytes 811016 | tf_op jit(solution)/shard_map/ppermute | solution.py:39
  2.6 10.9 %collective-permute-start.3 = (bf16[264,512]{1,0:T(8,128)(2,1)S(1)}, bf16[264,512]{1,0:T(8,128)(2,1)S(1)}, u32[]{:S(2)}, u32[]{:S(2)}) collective-permute-start(bf16[264,512]{1,0:T(8,128)(2,1)S(1)} %message.1), channel_id=1, source_target_pairs={{0,130},{1,97},{2,128},{3,99},{32,162},{33,65},{34,160},{35,67},{6... | collective-permute-start | bytes 811016 | tf_op jit(solution)/shard_map/ppermute | solution.py:39
  4.0 9.4 %collective-permute-start.2 = (bf16[264,512]{1,0:T(8,128)(2,1)S(1)}, bf16[264,512]{1,0:T(8,128)(2,1)S(1)}, u32[]{:S(2)}, u32[]{:S(2)}) collective-permute-start(bf16[264,512]{1,0:T(8,128)(2,1)S(1)} %message.1), channel_id=1, source_target_pairs={{0,2},{1,65},{2,0},{3,67},{32,34},{33,97},{34,32},{35,99},{64,66},... | collective-permute-start | bytes 811016 | tf_op jit(solution)/shard_map/ppermute | solution.py:39
  8.3 8.7 %collective-permute-start.11 = (bf16[2,264,512]{2,1,0:T(8,128)(2,1)S(1)}, bf16[2,264,512]{2,1,0:T(8,128)(2,1)S(1)}, u32[]{:S(2)}, u32[]{:S(2)}) collective-permute-start(bf16[2,264,512]{2,1,0:T(8,128)(2,1)S(1)} %pad_maximum_fusion.own0.own_low), channel_id=1, source_target_pairs={{0,1},{1,0},{2,3},{3,2},{4,5},{5,4},{6,7},{7,6},{8,9},{9,8},{10,11... | collective-permute-start | bytes 1622024 | tf_op jit(solution)/shard_map/ppermute | solution.py:47
  8.4 10.7 %collective-permute-start.5 = (bf16[2,264,512]{2,1,0:T(8,128)(2,1)S(1)}, bf16[2,264,512]{2,1,0:T(8,128)(2,1)S(1)}, u32[]{:S(2)}, u32[]{:S(2)}) collective-permute-start(bf16[2,264,512]{2,1,0:T(8,128)(2,1)S(1)} %pad_maximum_fusion.own0.own_low), channel_id=1, source_target_pairs={{0,96},{1,131},{2,98},{3,129},{32,64},{33,163},{34,66},{35,161},{6... | collective-permute-start | bytes 1622024 | tf_op jit(solution)/shard_map/ppermute | solution.py:39
  11.5 9.4 %collective-permute-start.1 = (bf16[2,264,512]{2,1,0:T(8,128)(2,1)S(1)}, bf16[2,264,512]{2,1,0:T(8,128)(2,1)S(1)}, u32[]{:S(2)}, u32[]{:S(2)}) collective-permute-start(bf16[2,264,512]{2,1,0:T(8,128)(2,1)S(1)} %pad_maximum_fusion.own0.own_low), channel_id=1, source_target_pairs={{0,32},{1,129},{2,34},{3,131},{32,0},{33,161},{34,2},{35,163},{64,... | collective-permute-start | bytes 1622024 | tf_op jit(solution)/shard_map/ppermute | solution.py:39
  13.5 11.3 %collective-permute-start.6 = (bf16[2,264,512]{2,1,0:T(8,128)(2,1)S(1)}, bf16[2,264,512]{2,1,0:T(8,128)(2,1)S(1)}, u32[]{:S(2)}, u32[]{:S(2)}) collective-permute-start(bf16[2,264,512]{2,1,0:T(8,128)(2,1)S(1)} %pad_maximum_fusion.1.own1.own_high), channel_id=1, source_target_pairs={{0,96},{1,131},{2,98},{3,129},{32,64},{33,163},{34,66},{35,161},{6... | collective-permute-start | bytes 1622024 | tf_op jit(solution)/shard_map/ppermute | solution.py:39
  16.8 9.8 %collective-permute-start.4 = (bf16[2,264,512]{2,1,0:T(8,128)(2,1)S(1)}, bf16[2,264,512]{2,1,0:T(8,128)(2,1)S(1)}, u32[]{:S(2)}, u32[]{:S(2)}) collective-permute-start(bf16[2,264,512]{2,1,0:T(8,128)(2,1)S(1)} %pad_maximum_fusion.1.own1.own_high), channel_id=1, source_target_pairs={{0,32},{1,129},{2,34},{3,131},{32,0},{33,161},{34,2},{35,163},{64,... | collective-permute-start | bytes 1622024 | tf_op jit(solution)/shard_map/ppermute | solution.py:39
  16.9 13.1 %collective-permute-start.12 = (bf16[2,264,512]{2,1,0:T(8,128)(2,1)S(1)}, bf16[2,264,512]{2,1,0:T(8,128)(2,1)S(1)}, u32[]{:S(2)}, u32[]{:S(2)}) collective-permute-start(bf16[2,264,512]{2,1,0:T(8,128)(2,1)S(1)} %pad_maximum_fusion.1.own1.own_high), channel_id=1, source_target_pairs={{0,1},{1,0},{2,3},{3,2},{4,5},{5,4},{6,7},{7,6},{8,9},{9,8},{10,11... | collective-permute-start | bytes 1622024 | tf_op jit(solution)/shard_map/ppermute | solution.py:47
  19.0 12.8 %collective-permute-start.9 = (bf16[2,264,512]{2,1,0:T(8,128)(2,1)S(1)}, bf16[2,264,512]{2,1,0:T(8,128)(2,1)S(1)}, u32[]{:S(2)}, u32[]{:S(2)}) collective-permute-start(bf16[2,264,512]{2,1,0:T(8,128)(2,1)S(1)} %collective-permute-done.5.refs_2_), channel_id=1, source_target_pairs={{0,1},{1,0},{2,3},{3,2},{4,5},{5,4},{6,7},{7,6},{8,9},{9,8},{10,11... | collective-permute-start | bytes 1622024 | tf_op jit(solution)/shard_map/ppermute | solution.py:47
  20.8 14.0 %collective-permute-start.7 = (bf16[2,264,512]{2,1,0:T(8,128)(2,1)S(1)}, bf16[2,264,512]{2,1,0:T(8,128)(2,1)S(1)}, u32[]{:S(2)}, u32[]{:S(2)}) collective-permute-start(bf16[2,264,512]{2,1,0:T(8,128)(2,1)S(1)} %collective-permute-done.1.refs_0_), channel_id=1, source_target_pairs={{0,1},{1,0},{2,3},{3,2},{4,5},{5,4},{6,7},{7,6},{8,9},{9,8},{10,11... | collective-permute-start | bytes 1622024 | tf_op jit(solution)/shard_map/ppermute | solution.py:47
  24.8 10.0 %collective-permute-start.10 = (bf16[2,264,512]{2,1,0:T(8,128)(2,1)S(1)}, bf16[2,264,512]{2,1,0:T(8,128)(2,1)S(1)}, u32[]{:S(2)}, u32[]{:S(2)}) collective-permute-start(bf16[2,264,512]{2,1,0:T(8,128)(2,1)S(1)} %collective-permute-done.6.refs_3_), channel_id=1, source_target_pairs={{0,1},{1,0},{2,3},{3,2},{4,5},{5,4},{6,7},{7,6},{8,9},{9,8},{10,11... | collective-permute-start | bytes 1622024 | tf_op jit(solution)/shard_map/ppermute | solution.py:47
  26.6 8.2 %collective-permute-start.8 = (bf16[2,264,512]{2,1,0:T(8,128)(2,1)S(1)}, bf16[2,264,512]{2,1,0:T(8,128)(2,1)S(1)}, u32[]{:S(2)}, u32[]{:S(2)}) collective-permute-start(bf16[2,264,512]{2,1,0:T(8,128)(2,1)S(1)} %collective-permute-done.4.refs_1_), channel_id=1, source_target_pairs={{0,1},{1,0},{2,3},{3,2},{4,5},{5,4},{6,7},{7,6},{8,9},{9,8},{10,11... | collective-permute-start | bytes 1622024 | tf_op jit(solution)/shard_map/ppermute | solution.py:47
  30.0 10.7 %collective-permute-start.13 = (bf16[2,264,512]{2,1,0:T(8,128)(2,1)S(1)}, bf16[2,264,512]{2,1,0:T(8,128)(2,1)S(1)}, u32[]{:S(2)}, u32[]{:S(2)}) collective-permute-start(bf16[2,264,512]{2,1,0:T(8,128)(2,1)S(1)} %collective-permute-done.1.refs_0_), channel_id=1, source_target_pairs={{0,96},{1,131},{2,98},{3,129},{32,64},{33,163},{34,66},{35,161},{6... | collective-permute-start | bytes 1622024 | tf_op jit(solution)/shard_map/ppermute | solution.py:39
  31.9 9.4 %collective-permute-start.14 = (bf16[2,264,512]{2,1,0:T(8,128)(2,1)S(1)}, bf16[2,264,512]{2,1,0:T(8,128)(2,1)S(1)}, u32[]{:S(2)}, u32[]{:S(2)}) collective-permute-start(bf16[2,264,512]{2,1,0:T(8,128)(2,1)S(1)} %collective-permute-done.6.refs_3_), channel_id=1, source_target_pairs={{0,32},{1,129},{2,34},{3,131},{32,0},{33,161},{34,2},{35,163},{64,... | collective-permute-start | bytes 1622024 | tf_op jit(solution)/shard_map/ppermute | solution.py:39
  41.2 17.0 %collective-permute-start.15 = (bf16[2,264,512]{2,1,0:T(8,128)(2,1)S(1)}, bf16[2,264,512]{2,1,0:T(8,128)(2,1)S(1)}, u32[]{:S(2)}, u32[]{:S(2)}) collective-permute-start(bf16[2,264,512]{2,1,0:T(8,128)(2,1)S(1)} %collective-permute-done.13.refs_0_), channel_id=1, source_target_pairs={{0,1},{1,0},{2,3},{3,2},{4,5},{5,4},{6,7},{7,6},{8,9},{9,8},{10,11... | collective-permute-start | bytes 1622024 | tf_op jit(solution)/shard_map/ppermute | solution.py:47
  41.2 17.0 %collective-permute-start.16 = (bf16[2,264,512]{2,1,0:T(8,128)(2,1)S(1)}, bf16[2,264,512]{2,1,0:T(8,128)(2,1)S(1)}, u32[]{:S(2)}, u32[]{:S(2)}) collective-permute-start(bf16[2,264,512]{2,1,0:T(8,128)(2,1)S(1)} %collective-permute-done.14.refs_1_), channel_id=1, source_target_pairs={{0,1},{1,0},{2,3},{3,2},{4,5},{5,4},{6,7},{7,6},{8,9},{9,8},{10,11... | collective-permute-start | bytes 1622024 | tf_op jit(solution)/shard_map/ppermute | solution.py:47
  41.7 8.4 %collective-permute-start.18 = (f32[8,128]{1,0:T(8,128)S(1)}, f32[8,128]{1,0:T(8,128)S(1)}, u32[]{:S(2)}, u32[]{:S(2)}) collective-permute-start(f32[8,128]{1,0:T(8,128)S(1)} %rows.1), channel_id=1, source_target_pairs={{0,12},{1,17},{4,16},{5,21},{8,20},{9,25},{12,24},{13,29},{16,28},... | collective-permute-start | bytes 12296 | tf_op jit(solution)/shard_map/ppermute | solution.py:59
  46.4 4.8 %collective-permute-start.17 = (f32[8,128]{1,0:T(8,128)S(1)}, f32[8,128]{1,0:T(8,128)S(1)}, u32[]{:S(2)}, u32[]{:S(2)}) collective-permute-start(f32[8,128]{1,0:T(8,128)S(1)} %rows.1), channel_id=1, source_target_pairs={{0,4},{1,9},{4,8},{5,13},{8,12},{9,17},{12,16},{13,21},{16,20},{17... | collective-permute-start | bytes 12296 | tf_op jit(solution)/shard_map/ppermute | solution.py:59
  51.3 3.7 %collective-permute-start.20 = (f32[8,128]{1,0:T(8,128)S(1)}, f32[8,128]{1,0:T(8,128)S(1)}, u32[]{:S(2)}, u32[]{:S(2)}) collective-permute-start(f32[8,128]{1,0:T(8,128)S(1)} %part.1.refs_8_), channel_id=1, source_target_pairs={{0,128},{128,0},{1,129},{129,1},{2,130},{130,2},{3,131},{131,3},{4... | collective-permute-start | bytes 12296 | tf_op jit(solution)/shard_map/ppermute | solution.py:43
  52.2 6.1 %collective-permute-start.19 = (f32[8,128]{1,0:T(8,128)S(1)}, f32[8,128]{1,0:T(8,128)S(1)}, u32[]{:S(2)}, u32[]{:S(2)}) collective-permute-start(f32[8,128]{1,0:T(8,128)S(1)} %part.1.refs_8_), channel_id=1, source_target_pairs={{0,1},{1,0},{2,3},{3,2},{4,5},{5,4},{6,7},{7,6},{8,9},{9,8},{10,11... | collective-permute-start | bytes 12296 | tf_op jit(solution)/shard_map/ppermute | solution.py:47
  55.0 3.3 %collective-permute-start.21 = (f32[8,128]{1,0:T(8,128)S(1)}, f32[8,128]{1,0:T(8,128)S(1)}, u32[]{:S(2)}, u32[]{:S(2)}) collective-permute-start(f32[8,128]{1,0:T(8,128)S(1)} %collective-permute-done.20.refs_10_), channel_id=1, source_target_pairs={{0,1},{1,0},{2,3},{3,2},{4,5},{5,4},{6,7},{7,6},{8,9},{9,8},{10,11... | collective-permute-start | bytes 12296 | tf_op jit(solution)/shard_map/ppermute | solution.py:47
  62.9 7.0 %collective-permute-start.22 = (bf16[4,3,32,384]{3,2,1,0:T(8,128)(2,1)S(1)}, bf16[4,3,32,384]{3,2,1,0:T(8,128)(2,1)S(1)}, u32[]{:S(2)}, u32[]{:S(2)}) collective-permute-start(bf16[4,3,32,384]{3,2,1,0:T(8,128)(2,1)S(1)} %get-tuple-element.38), channel_id=1, source_target_pairs={{0,4},{1,29},{4,0},{5,9},{8,12},{9,5},{12,8},{13,17},{16,20},{17,1... | collective-permute-start | bytes 884744 | tf_op jit(solution)/shard_map/ppermute | solution.py:55
  67.6 5.8 %collective-permute-start.25 = (bf16[4,3,32,256]{3,2,1,0:T(8,128)(2,1)S(1)}, bf16[4,3,32,256]{3,2,1,0:T(8,128)(2,1)S(1)}, u32[]{:S(2)}, u32[]{:S(2)}) collective-permute-start(bf16[4,3,32,256]{3,2,1,0:T(8,128)(2,1)S(1)} %get-tuple-element.44), channel_id=1, source_target_pairs={{0,4},{1,29},{4,0},{5,9},{8,12},{9,5},{12,8},{13,17},{16,20},{17,1... | collective-permute-start | bytes 589832 | tf_op jit(solution)/shard_map/ppermute | solution.py:55
  70.0 14.7 %collective-permute-start.24 = (bf16[3,32,384]{2,1,0:T(8,128)(2,1)S(1)}, bf16[3,32,384]{2,1,0:T(8,128)(2,1)S(1)}, u32[]{:S(2)}, u32[]{:S(2)}) collective-permute-start(bf16[3,32,384]{2,1,0:T(8,128)(2,1)S(1)} %get-tuple-element.50), channel_id=1, source_target_pairs={{0,24},{4,28},{8,0},{12,4},{16,8},{20,12},{24,16},{28,20},{1,25},{... | collective-permute-start | bytes 221192 | tf_op jit(solution)/shard_map/ppermute | solution.py:65
  72.7 12.0 %collective-permute-start.23 = (bf16[3,32,384]{2,1,0:T(8,128)(2,1)S(1)}, bf16[3,32,384]{2,1,0:T(8,128)(2,1)S(1)}, u32[]{:S(2)}, u32[]{:S(2)}) collective-permute-start(bf16[3,32,384]{2,1,0:T(8,128)(2,1)S(1)} %get-tuple-element.51), channel_id=1, source_target_pairs={{0,8},{4,12},{8,16},{12,20},{16,24},{20,28},{24,0},{28,4},{1,9},{5... | collective-permute-start | bytes 221192 | tf_op jit(solution)/shard_map/ppermute | solution.py:65
  73.4 6.5 %collective-permute-start.27 = (bf16[3,32,256]{2,1,0:T(8,128)(2,1)S(1)}, bf16[3,32,256]{2,1,0:T(8,128)(2,1)S(1)}, u32[]{:S(2)}, u32[]{:S(2)}) collective-permute-start(bf16[3,32,256]{2,1,0:T(8,128)(2,1)S(1)} %get-tuple-element.53), channel_id=1, source_target_pairs={{0,24},{4,28},{8,0},{12,4},{16,8},{20,12},{24,16},{28,20},{1,25},{... | collective-permute-start | bytes 147464 | tf_op jit(solution)/shard_map/ppermute | solution.py:65
  77.0 7.6 %collective-permute-start.26 = (bf16[3,32,256]{2,1,0:T(8,128)(2,1)S(1)}, bf16[3,32,256]{2,1,0:T(8,128)(2,1)S(1)}, u32[]{:S(2)}, u32[]{:S(2)}) collective-permute-start(bf16[3,32,256]{2,1,0:T(8,128)(2,1)S(1)} %get-tuple-element.54), channel_id=1, source_target_pairs={{0,8},{4,12},{8,16},{12,20},{16,24},{20,28},{24,0},{28,4},{1,9},{5... | collective-permute-start | bytes 147464 | tf_op jit(solution)/shard_map/ppermute | solution.py:65
  77.1 9.9 %collective-permute-start.28 = (bf16[3,32,640]{2,1,0:T(8,128)(2,1)S(1)}, bf16[3,32,640]{2,1,0:T(8,128)(2,1)S(1)}, u32[]{:S(2)}, u32[]{:S(2)}) collective-permute-start(bf16[3,32,640]{2,1,0:T(8,128)(2,1)S(1)} %pad_maximum_fusion.2), channel_id=1, source_target_pairs={{0,16},{4,20},{8,24},{12,28},{16,0},{20,4},{24,8},{28,12},{1,17},{... | collective-permute-start | bytes 368648 | tf_op jit(solution)/shard_map/ppermute | solution.py:65

commit v10 on v9

--- a/solution.py
+++ b/solution.py
@@ -352,6 +352,38 @@
         send[k] = total[((near >> 1) + k & 3) * 2 + (1 - odd)].astype(BF16)
 
 
+def mix_kernel(keep, got, *refs):
+    mixed = [keep[k] + got[k].astype(F32) for k in range(4)]
+    width = keep.shape[-1]
+    if len(refs) == 5:
+        before, own, plus, minus, opposite = refs
+        opposite[:, :, : 640 - width] = before[...]
+        opposite[:, :, 640 - width :] = mixed[2].astype(BF16)
+    else:
+        own, plus, minus, opposite = refs
+        opposite[...] = mixed[2].astype(BF16)
+    own[...] = mixed[0]
+    plus[...] = mixed[1].astype(BF16)
+    minus[...] = mixed[3].astype(BF16)
+
+
+def mixed(keep, got, *before):
+    width = keep.shape[-1]
+    shape = (3, 32, width)
+    return pl.pallas_call(
+        mix_kernel,
+        out_shape=(
+            jax.ShapeDtypeStruct(shape, F32),
+            jax.ShapeDtypeStruct(shape, BF16),
+            jax.ShapeDtypeStruct(shape, BF16),
+            jax.ShapeDtypeStruct((3, 32, 640) if before else shape, BF16),
+        ),
+        in_specs=[VMEM] * (2 + len(before)),
+        out_specs=(VMEM,) * 4,
+        compiler_params=PARAMS,
+    )(keep, got, *before)
+
+
 def all_steps(tokens, grad_out, w_gate, w_lin, w_out_t, code, decode, stragglers):
     own = message(code, decode, stragglers, tokens, grad_out)
     first = {}
@@ -392,18 +424,14 @@
         state, keep, send = finished(cut, halves, w_in, w_out, state, terms)
         keeps.append(keep)
         got.append(z_pair(send))
-    results, across_ring = [], []
+    results, opposite = [], []
     for cut in range(2):
-        mixed = keeps[cut] + got[cut].astype(F32)
-        sends = mixed.astype(BF16)
-        if cut == 0:
-            sends, keeps[1] = lax.optimization_barrier((sends, keeps[1]))
-        across_ring.append(sends[2])
-        result = mixed[0]
-        for k in (1, 3):
-            result = result + z_step(sends[k], 2 * k).astype(F32)
+        own, plus, minus, opposite = mixed(keeps[cut], got[cut], *([opposite] if cut else []))
+        result = own
+        for k, block in ((1, plus), (3, minus)):
+            result = result + z_step(block, 2 * k).astype(F32)
         results.append(result)
-    opposite = z_step(jnp.concatenate(across_ring, axis=2), 4)
+    opposite = z_step(opposite, 4)
     return jnp.transpose(jnp.concatenate(results, axis=2) + opposite.astype(F32), (1, 0, 2))
 
 

time: 88.5 us -> 93.7 us (1.059)
  waiting for transfers between devices: 29.2 us -> 32.6 us
  starting transfers between devices: 36.6 us -> 38.8 us
    ppermute x2, waiting for transfers between devices: 1.66 us -> 4.72 us  [z_pair(): lax.ppermute(block, ('z', 'c'), [(z * 2 + c, partner_of(z, c) * 2 + c) fo...]
    ppermute x5, starting transfers between devices: 9.44 us -> 11.7 us  [z_step(): return lax.ppermute(block, 'z', [(z, (z + step) % 8) for z in range(8)])]
where the time goes in v10:
time: 93.7 us; the launch traced here: 93.2 us
  starting transfers between devices  38.8 us (41%)
  waiting for transfers between devices  32.6 us (35%)
  Pallas kernels  20.1 us (21%)
    ppermute x9, waiting for transfers between devices, across(): return lax.ppermute(block, PLANE, route)  17.8 us
    ppermute x9, starting transfers between devices, across(): return lax.ppermute(block, PLANE, route)  12.6 us
    ppermute x5, starting transfers between devices, z_step(): return lax.ppermute(block, 'z', [(z, (z + step) % 8) for z in range(8)])  11.7 us
    pallas_call x2, Pallas kernels, finished(): pl.pallas_call(kernel, out_shape=STATE + (jax.ShapeDtypeStruct((4, 3, 32,...  7.84 us
    ppermute x2, starting transfers between devices, z_shift(): lax.ppermute(block, ('z', 'c'), [(z * 2 + c, (z + step + c) % 8 * 2 + c)...  7.83 us
    pallas_call x3, Pallas kernels, gathered(): pl.pallas_call(kernel, out_shape=STATE, in_specs=[VMEM] * (n + 2 + len(st...  7.75 us
    ppermute x5, waiting for transfers between devices, z_step(): return lax.ppermute(block, 'z', [(z, (z + step) % 8) for z in range(8)])  7.34 us
    ppermute x2, waiting for transfers between devices, z_pair(): lax.ppermute(block, ('z', 'c'), [(z * 2 + c, partner_of(z, c) * 2 + c) fo...  4.72 us
  transfers between devices with their start and end apart: 29, of which 15 were waited for; matrix products, arithmetic and copies ran while one was open for 0% of the time, Pallas kernels for 16%

profile of v10, /device:TPU:6, one launch (start us, length us, event | category | flops | bytes accessed | tf_op | source)
XLA Modules:
  0.0 93.2 jit_solution(3416742611503958482)
XLA Ops:
  2.6 1.5 %collective-permute-start.3 = (bf16[264,512]{1,0:T(8,128)(2,1)S(1)}, bf16[264,512]{1,0:T(8,128)(2,1)S(1)}, u32[]{:S(2)}, u32[]{:S(2)}) collective-permute-start(bf16[264,512]{1,0:T(8,128)(2,1)S(1)} %message.1), channel_id=1, source_target_pairs={{0,130},{1,97},{2,128},{3,99},{32,162},{33,65},{34,160},{35,67},{6... | collective-permute-start | bytes 811016 | tf_op jit(solution)/shard_map/ppermute | solution.py:39
  4.0 1.8 %collective-permute-start.2 = (bf16[264,512]{1,0:T(8,128)(2,1)S(1)}, bf16[264,512]{1,0:T(8,128)(2,1)S(1)}, u32[]{:S(2)}, u32[]{:S(2)}) collective-permute-start(bf16[264,512]{1,0:T(8,128)(2,1)S(1)} %message.1), channel_id=1, source_target_pairs={{0,2},{1,65},{2,0},{3,67},{32,34},{33,97},{34,32},{35,99},{64,66},... | collective-permute-start | bytes 811016 | tf_op jit(solution)/shard_map/ppermute | solution.py:39
  5.8 2.4 %collective-permute-done = bf16[264,512]{1,0:T(8,128)(2,1)S(1)} collective-permute-done((bf16[264,512]{1,0:T(8,128)(2,1)S(1)}, bf16[264,512]{1,0:T(8,128)(2,1)S(1)}, u32[]{:S(2)}, u32[]{:S(2)}) %collective-permute-start) | collective-permute-done | bytes 270368 | tf_op jit(solution)/shard_map/ppermute | solution.py:39
  8.4 3.1 %collective-permute-start.5 = (bf16[2,264,512]{2,1,0:T(8,128)(2,1)S(1)}, bf16[2,264,512]{2,1,0:T(8,128)(2,1)S(1)}, u32[]{:S(2)}, u32[]{:S(2)}) collective-permute-start(bf16[2,264,512]{2,1,0:T(8,128)(2,1)S(1)} %pad_maximum_fusion.own0.own_low), channel_id=1, source_target_pairs={{0,96},{1,131},{2,98},{3,129},{32,64},{33,163},{34,66},{35,161},{6... | collective-permute-start | bytes 1622024 | tf_op jit(solution)/shard_map/ppermute | solution.py:39
  11.6 1.9 %collective-permute-done.3 = bf16[264,512]{1,0:T(8,128)(2,1)S(1)} collective-permute-done((bf16[264,512]{1,0:T(8,128)(2,1)S(1)}, bf16[264,512]{1,0:T(8,128)(2,1)S(1)}, u32[]{:S(2)}, u32[]{:S(2)}) %collective-permute-start.3) | collective-permute-done | bytes 270368 | tf_op jit(solution)/shard_map/ppermute | solution.py:39
  13.5 3.3 %collective-permute-start.6 = (bf16[2,264,512]{2,1,0:T(8,128)(2,1)S(1)}, bf16[2,264,512]{2,1,0:T(8,128)(2,1)S(1)}, u32[]{:S(2)}, u32[]{:S(2)}) collective-permute-start(bf16[2,264,512]{2,1,0:T(8,128)(2,1)S(1)} %pad_maximum_fusion.1.own1.own_high), channel_id=1, source_target_pairs={{0,96},{1,131},{2,98},{3,129},{32,64},{33,163},{34,66},{35,161},{6... | collective-permute-start | bytes 1622024 | tf_op jit(solution)/shard_map/ppermute | solution.py:39
  16.9 2.1 %collective-permute-done.5.refs_2_ = bf16[2,264,512]{2,1,0:T(8,128)(2,1)S(1)} collective-permute-done((bf16[2,264,512]{2,1,0:T(8,128)(2,1)S(1)}, bf16[2,264,512]{2,1,0:T(8,128)(2,1)S(1)}, u32[]{:S(2)}, u32[]{:S(2)}) %collective-permute-start.5) | collective-permute-done | bytes 540704 | tf_op jit(solution)/shard_map/ppermute | solution.py:39
  19.1 1.8 %collective-permute-done.1.refs_0_ = bf16[2,264,512]{2,1,0:T(8,128)(2,1)S(1)} collective-permute-done((bf16[2,264,512]{2,1,0:T(8,128)(2,1)S(1)}, bf16[2,264,512]{2,1,0:T(8,128)(2,1)S(1)}, u32[]{:S(2)}, u32[]{:S(2)}) %collective-permute-start.1) | collective-permute-done | bytes 540704 | tf_op jit(solution)/shard_map/ppermute | solution.py:39
  20.8 4.0 %collective-permute-done.6.refs_3_ = bf16[2,264,512]{2,1,0:T(8,128)(2,1)S(1)} collective-permute-done((bf16[2,264,512]{2,1,0:T(8,128)(2,1)S(1)}, bf16[2,264,512]{2,1,0:T(8,128)(2,1)S(1)}, u32[]{:S(2)}, u32[]{:S(2)}) %collective-permute-start.6) | collective-permute-done | bytes 540704 | tf_op jit(solution)/shard_map/ppermute | solution.py:39
  24.8 1.8 %collective-permute-done.4.refs_1_ = bf16[2,264,512]{2,1,0:T(8,128)(2,1)S(1)} collective-permute-done((bf16[2,264,512]{2,1,0:T(8,128)(2,1)S(1)}, bf16[2,264,512]{2,1,0:T(8,128)(2,1)S(1)}, u32[]{:S(2)}, u32[]{:S(2)}) %collective-permute-start.4) | collective-permute-done | bytes 540704 | tf_op jit(solution)/shard_map/ppermute | solution.py:39
  26.6 3.4 %load.1 = (bf16[2048,1280]{1,0:T(8,128)(2,1)S(1)}, bf16[2048,640]{1,0:T(8,128)(2,1)S(1)}) custom-call(bf16[4,512,640]{2,1,0:T(8,128)(2,1)} %bitcast.10, bf16[4,512,640]{2,1,0:T(8,128)(2,1)} %bitcast.11, bf16[4,512,640]{2,1,0:T(8,128)(2,1)} %bitcast.12), custom_call_target="tpu_custom_call" | custom-call | tf_op jit(solution)/shard_map/load/pallas_call | solution.py:138
  30.0 1.8 %collective-permute-start.13 = (bf16[2,264,512]{2,1,0:T(8,128)(2,1)S(1)}, bf16[2,264,512]{2,1,0:T(8,128)(2,1)S(1)}, u32[]{:S(2)}, u32[]{:S(2)}) collective-permute-start(bf16[2,264,512]{2,1,0:T(8,128)(2,1)S(1)} %collective-permute-done.1.refs_0_), channel_id=1, source_target_pairs={{0,96},{1,131},{2,98},{3,129},{32,64},{33,163},{34,66},{35,161},{6... | collective-permute-start | bytes 1622024 | tf_op jit(solution)/shard_map/ppermute | solution.py:39
  31.9 2.9 %shard_map.82 = (f32[3,8,128,640]{3,2,1,0:T(8,128)S(1)}, bf16[2,8,128,256]{3,2,1,0:T(8,128)(2,1)S(1)}) custom-call(bf16[2,264,512]{2,1,0:T(8,128)(2,1)S(1)} %pad_maximum_fusion.own0.own_low, bf16[2,264,512]{2,1,0:T(8,128)(2,1)S(1)} %pad_maximum_fusion.1.own1.own_high, bf16[2,264,512]{2,1,0:T(8,128)(2,1)S(1)} %collective-permute-done.11.other0.other_low, ...), custom_call_target="tpu_custom_call" | custom-call | flops 2147483648 | bytes 1048576 | tf_op jit(solution)/shard_map/pallas_call | solution.py:268
  34.8 2.4 %shard_map.83 = (f32[3,8,128,640]{3,2,1,0:T(8,128)S(1)}, bf16[2,8,128,256]{3,2,1,0:T(8,128)(2,1)S(1)}) custom-call(bf16[2,264,512]{2,1,0:T(8,128)(2,1)S(1)} %collective-permute-done.1.refs_0_, bf16[2,264,512]{2,1,0:T(8,128)(2,1)S(1)} %collective-permute-done.4.refs_1_, ...), custom_call_target="tpu_custom_call", output_to_operand_aliasing={{0}: (10, {}), {1}: (11, {})} | custom-call | flops 4294967296 | bytes 1048576 | tf_op jit(solution)/shard_map/pallas_call | solution.py:268
  37.3 3.4 %collective-permute-done.13.refs_0_ = bf16[2,264,512]{2,1,0:T(8,128)(2,1)S(1)} collective-permute-done((bf16[2,264,512]{2,1,0:T(8,128)(2,1)S(1)}, bf16[2,264,512]{2,1,0:T(8,128)(2,1)S(1)}, u32[]{:S(2)}, u32[]{:S(2)}) %collective-permute-start.13) | collective-permute-done | bytes 540704 | tf_op jit(solution)/shard_map/ppermute | solution.py:39
  41.7 4.7 %collective-permute-start.18 = (f32[8,128]{1,0:T(8,128)S(1)}, f32[8,128]{1,0:T(8,128)S(1)}, u32[]{:S(2)}, u32[]{:S(2)}) collective-permute-start(f32[8,128]{1,0:T(8,128)S(1)} %rows.1), channel_id=1, source_target_pairs={{0,12},{1,17},{4,16},{5,21},{8,20},{9,25},{12,24},{13,29},{16,28},... | collective-permute-start | bytes 12296 | tf_op jit(solution)/shard_map/ppermute | solution.py:59
  46.4 3.1 %collective-permute-start.17 = (f32[8,128]{1,0:T(8,128)S(1)}, f32[8,128]{1,0:T(8,128)S(1)}, u32[]{:S(2)}, u32[]{:S(2)}) collective-permute-start(f32[8,128]{1,0:T(8,128)S(1)} %rows.1), channel_id=1, source_target_pairs={{0,4},{1,9},{4,8},{5,13},{8,12},{9,17},{12,16},{13,21},{16,20},{17... | collective-permute-start | bytes 12296 | tf_op jit(solution)/shard_map/ppermute | solution.py:59
  50.1 1.1 %collective-permute-done.17.near = f32[8,128]{1,0:T(8,128)S(1)} collective-permute-done((f32[8,128]{1,0:T(8,128)S(1)}, f32[8,128]{1,0:T(8,128)S(1)}, u32[]{:S(2)}, u32[]{:S(2)}) %collective-permute-start.17) | collective-permute-done | bytes 4128 | tf_op jit(solution)/shard_map/ppermute | solution.py:59
  52.2 1.8 %collective-permute-start.19 = (f32[8,128]{1,0:T(8,128)S(1)}, f32[8,128]{1,0:T(8,128)S(1)}, u32[]{:S(2)}, u32[]{:S(2)}) collective-permute-start(f32[8,128]{1,0:T(8,128)S(1)} %part.1.refs_8_), channel_id=1, source_target_pairs={{0,1},{1,0},{2,3},{3,2},{4,5},{5,4},{6,7},{7,6},{8,9},{9,8},{10,11... | collective-permute-start | bytes 12296 | tf_op jit(solution)/shard_map/ppermute | solution.py:47
  53.9 1.0 %collective-permute-done.20.refs_10_ = f32[8,128]{1,0:T(8,128)S(1)} collective-permute-done((f32[8,128]{1,0:T(8,128)S(1)}, f32[8,128]{1,0:T(8,128)S(1)}, u32[]{:S(2)}, u32[]{:S(2)}) %collective-permute-start.20) | collective-permute-done | bytes 4128 | tf_op jit(solution)/shard_map/ppermute | solution.py:43
  55.8 2.4 %shard_map.84 = (f32[3,8,128,640]{3,2,1,0:T(8,128)S(1)}, bf16[2,8,128,256]{3,2,1,0:T(8,128)(2,1)S(1)}) custom-call(bf16[2,264,512]{2,1,0:T(8,128)(2,1)S(1)} %collective-permute-done.1.refs_0_, bf16[2,264,512]{2,1,0:T(8,128)(2,1)S(1)} %collective-permute-done.4.refs_1_, ...), custom_call_target="tpu_custom_call", output_to_operand_aliasing={{0}: (10, {}), {1}: (11, {})} | custom-call | flops 4294967296 | bytes 1048576 | tf_op jit(solution)/shard_map/pallas_call | solution.py:268
  58.3 4.6 %shard_map.85 = (f32[3,8,128,640]{3,2,1,0:T(8,128)S(1)}, bf16[2,8,128,256]{3,2,1,0:T(8,128)(2,1)S(1)}, f32[4,3,32,384]{3,2,1,0:T(8,128)S(1)}, bf16[4,3,32,384]{3,2,1,0:T(8,128)(2,1)S(1)}) custom-call(bf16[2,264,512]{2,1,0:T(8,128)(2,1)S(1)} %collective-permute-done.13.refs_0_, ...), custom_call_target="tpu_custom_call", output_to_operand_aliasing={{0}: (6, {}), {1}: (7, {})} | custom-call | flops 2147483648 | bytes 1048576 | tf_op jit(solution)/shard_map/pallas_call | solution.py:288
  62.9 1.5 %collective-permute-start.22 = (bf16[4,3,32,384]{3,2,1,0:T(8,128)(2,1)S(1)}, bf16[4,3,32,384]{3,2,1,0:T(8,128)(2,1)S(1)}, u32[]{:S(2)}, u32[]{:S(2)}) collective-permute-start(bf16[4,3,32,384]{3,2,1,0:T(8,128)(2,1)S(1)} %get-tuple-element.44), channel_id=1, source_target_pairs={{0,4},{1,29},{4,0},{5,9},{8,12},{9,5},{12,8},{13,17},{16,20},{17,1... | collective-permute-start | bytes 884744 | tf_op jit(solution)/shard_map/ppermute | solution.py:55
  64.3 3.2 %shard_map.87 = (f32[3,8,128,640]{3,2,1,0:T(8,128)S(1)}, bf16[2,8,128,256]{3,2,1,0:T(8,128)(2,1)S(1)}, f32[4,3,32,256]{3,2,1,0:T(8,128)S(1)}, bf16[4,3,32,256]{3,2,1,0:T(8,128)(2,1)S(1)}) custom-call(bf16[2,264,512]{2,1,0:T(8,128)(2,1)S(1)} %collective-permute-done.13.refs_0_, ...), custom_call_target="tpu_custom_call", output_to_operand_aliasing={{0}: (6, {}), {1}: (7, {})} | custom-call | flops 2147483648 | bytes 1048576 | tf_op jit(solution)/shard_map/pallas_call | solution.py:288
  68.6 1.4 %collective-permute-done.22.got = bf16[4,3,32,384]{3,2,1,0:T(8,128)(2,1)S(1)} collective-permute-done((bf16[4,3,32,384]{3,2,1,0:T(8,128)(2,1)S(1)}, bf16[4,3,32,384]{3,2,1,0:T(8,128)(2,1)S(1)}, u32[]{:S(2)}, u32[]{:S(2)}) %collective-permute-start.22) | collective-permute-done | bytes 294944 | tf_op jit(solution)/shard_map/ppermute | solution.py:55
  70.0 3.4 %collective-permute-done.25.got = bf16[4,3,32,256]{3,2,1,0:T(8,128)(2,1)S(1)} collective-permute-done((bf16[4,3,32,256]{3,2,1,0:T(8,128)(2,1)S(1)}, bf16[4,3,32,256]{3,2,1,0:T(8,128)(2,1)S(1)}, u32[]{:S(2)}, u32[]{:S(2)}) %collective-permute-start.25) | collective-permute-done | bytes 196640 | tf_op jit(solution)/shard_map/ppermute | solution.py:55
  73.4 1.4 %collective-permute-start.26 = (bf16[3,32,256]{2,1,0:T(8,128)(2,1)S(1)}, bf16[3,32,256]{2,1,0:T(8,128)(2,1)S(1)}, u32[]{:S(2)}, u32[]{:S(2)}) collective-permute-start(bf16[3,32,256]{2,1,0:T(8,128)(2,1)S(1)} %get-tuple-element.54), channel_id=1, source_target_pairs={{0,8},{4,12},{8,16},{12,20},{16,24},{20,28},{24,0},{28,4},{1,9},{5... | collective-permute-start | bytes 147464 | tf_op jit(solution)/shard_map/ppermute | solution.py:65
  74.8 2.8 %collective-permute-start.27 = (bf16[3,32,256]{2,1,0:T(8,128)(2,1)S(1)}, bf16[3,32,256]{2,1,0:T(8,128)(2,1)S(1)}, u32[]{:S(2)}, u32[]{:S(2)}) collective-permute-start(bf16[3,32,256]{2,1,0:T(8,128)(2,1)S(1)} %get-tuple-element.55), channel_id=1, source_target_pairs={{0,24},{4,28},{8,0},{12,4},{16,8},{20,12},{24,16},{28,20},{1,25},{... | collective-permute-start | bytes 147464 | tf_op jit(solution)/shard_map/ppermute | solution.py:65
  77.8 4.0 %collective-permute-start.24 = (bf16[3,32,384]{2,1,0:T(8,128)(2,1)S(1)}, bf16[3,32,384]{2,1,0:T(8,128)(2,1)S(1)}, u32[]{:S(2)}, u32[]{:S(2)}) collective-permute-start(bf16[3,32,384]{2,1,0:T(8,128)(2,1)S(1)} %get-tuple-element.47), channel_id=1, source_target_pairs={{0,24},{4,28},{8,0},{12,4},{16,8},{20,12},{24,16},{28,20},{1,25},{... | collective-permute-start | bytes 221192 | tf_op jit(solution)/shard_map/ppermute | solution.py:65
  81.8 3.4 %collective-permute-start.28 = (bf16[3,32,640]{2,1,0:T(8,128)(2,1)S(1)}, bf16[3,32,640]{2,1,0:T(8,128)(2,1)S(1)}, u32[]{:S(2)}, u32[]{:S(2)}) collective-permute-start(bf16[3,32,640]{2,1,0:T(8,128)(2,1)S(1)} %get-tuple-element.56), channel_id=1, source_target_pairs={{0,16},{4,20},{8,24},{12,28},{16,0},{20,4},{24,8},{28,12},{1,17},{... | collective-permute-start | bytes 368648 | tf_op jit(solution)/shard_map/ppermute | solution.py:65
  85.1 1.6 %collective-permute-done.24 = bf16[3,32,384]{2,1,0:T(8,128)(2,1)S(1)} collective-permute-done((bf16[3,32,384]{2,1,0:T(8,128)(2,1)S(1)}, bf16[3,32,384]{2,1,0:T(8,128)(2,1)S(1)}, u32[]{:S(2)}, u32[]{:S(2)}) %collective-permute-start.24) | collective-permute-done | bytes 73760 | tf_op jit(solution)/shard_map/ppermute | solution.py:65
  86.8 5.7 %collective-permute-done.28 = bf16[3,32,640]{2,1,0:T(8,128)(2,1)S(1)} collective-permute-done((bf16[3,32,640]{2,1,0:T(8,128)(2,1)S(1)}, bf16[3,32,640]{2,1,0:T(8,128)(2,1)S(1)}, u32[]{:S(2)}, u32[]{:S(2)}) %collective-permute-start.28) | collective-permute-done | bytes 122912 | tf_op jit(solution)/shard_map/ppermute | solution.py:65
  (42 shorter events, 7.9 us)
Async XLA Ops:
  1.7 6.5 %collective-permute-start = (bf16[264,512]{1,0:T(8,128)(2,1)S(1)}, bf16[264,512]{1,0:T(8,128)(2,1)S(1)}, u32[]{:S(2)}, u32[]{:S(2)}) collective-permute-start(bf16[264,512]{1,0:T(8,128)(2,1)S(1)} %message.1), channel_id=1, source_target_pairs={{0,128},{1,33},{2,130},{3,35},{32,160},{33,1},{34,162},{35,3},{64,... | collective-permute-start | bytes 811016 | tf_op jit(solution)/shard_map/ppermute | solution.py:39
  2.6 10.9 %collective-permute-start.3 = (bf16[264,512]{1,0:T(8,128)(2,1)S(1)}, bf16[264,512]{1,0:T(8,128)(2,1)S(1)}, u32[]{:S(2)}, u32[]{:S(2)}) collective-permute-start(bf16[264,512]{1,0:T(8,128)(2,1)S(1)} %message.1), channel_id=1, source_target_pairs={{0,130},{1,97},{2,128},{3,99},{32,162},{33,65},{34,160},{35,67},{6... | collective-permute-start | bytes 811016 | tf_op jit(solution)/shard_map/ppermute | solution.py:39
  4.0 9.4 %collective-permute-start.2 = (bf16[264,512]{1,0:T(8,128)(2,1)S(1)}, bf16[264,512]{1,0:T(8,128)(2,1)S(1)}, u32[]{:S(2)}, u32[]{:S(2)}) collective-permute-start(bf16[264,512]{1,0:T(8,128)(2,1)S(1)} %message.1), channel_id=1, source_target_pairs={{0,2},{1,65},{2,0},{3,67},{32,34},{33,97},{34,32},{35,99},{64,66},... | collective-permute-start | bytes 811016 | tf_op jit(solution)/shard_map/ppermute | solution.py:39
  8.3 8.7 %collective-permute-start.11 = (bf16[2,264,512]{2,1,0:T(8,128)(2,1)S(1)}, bf16[2,264,512]{2,1,0:T(8,128)(2,1)S(1)}, u32[]{:S(2)}, u32[]{:S(2)}) collective-permute-start(bf16[2,264,512]{2,1,0:T(8,128)(2,1)S(1)} %pad_maximum_fusion.own0.own_low), channel_id=1, source_target_pairs={{0,1},{1,0},{2,3},{3,2},{4,5},{5,4},{6,7},{7,6},{8,9},{9,8},{10,11... | collective-permute-start | bytes 1622024 | tf_op jit(solution)/shard_map/ppermute | solution.py:47
  8.4 10.7 %collective-permute-start.5 = (bf16[2,264,512]{2,1,0:T(8,128)(2,1)S(1)}, bf16[2,264,512]{2,1,0:T(8,128)(2,1)S(1)}, u32[]{:S(2)}, u32[]{:S(2)}) collective-permute-start(bf16[2,264,512]{2,1,0:T(8,128)(2,1)S(1)} %pad_maximum_fusion.own0.own_low), channel_id=1, source_target_pairs={{0,96},{1,131},{2,98},{3,129},{32,64},{33,163},{34,66},{35,161},{6... | collective-permute-start | bytes 1622024 | tf_op jit(solution)/shard_map/ppermute | solution.py:39
  11.5 9.4 %collective-permute-start.1 = (bf16[2,264,512]{2,1,0:T(8,128)(2,1)S(1)}, bf16[2,264,512]{2,1,0:T(8,128)(2,1)S(1)}, u32[]{:S(2)}, u32[]{:S(2)}) collective-permute-start(bf16[2,264,512]{2,1,0:T(8,128)(2,1)S(1)} %pad_maximum_fusion.own0.own_low), channel_id=1, source_target_pairs={{0,32},{1,129},{2,34},{3,131},{32,0},{33,161},{34,2},{35,163},{64,... | collective-permute-start | bytes 1622024 | tf_op jit(solution)/shard_map/ppermute | solution.py:39
  13.5 11.3 %collective-permute-start.6 = (bf16[2,264,512]{2,1,0:T(8,128)(2,1)S(1)}, bf16[2,264,512]{2,1,0:T(8,128)(2,1)S(1)}, u32[]{:S(2)}, u32[]{:S(2)}) collective-permute-start(bf16[2,264,512]{2,1,0:T(8,128)(2,1)S(1)} %pad_maximum_fusion.1.own1.own_high), channel_id=1, source_target_pairs={{0,96},{1,131},{2,98},{3,129},{32,64},{33,163},{34,66},{35,161},{6... | collective-permute-start | bytes 1622024 | tf_op jit(solution)/shard_map/ppermute | solution.py:39
  16.8 9.8 %collective-permute-start.4 = (bf16[2,264,512]{2,1,0:T(8,128)(2,1)S(1)}, bf16[2,264,512]{2,1,0:T(8,128)(2,1)S(1)}, u32[]{:S(2)}, u32[]{:S(2)}) collective-permute-start(bf16[2,264,512]{2,1,0:T(8,128)(2,1)S(1)} %pad_maximum_fusion.1.own1.own_high), channel_id=1, source_target_pairs={{0,32},{1,129},{2,34},{3,131},{32,0},{33,161},{34,2},{35,163},{64,... | collective-permute-start | bytes 1622024 | tf_op jit(solution)/shard_map/ppermute | solution.py:39
  16.9 13.1 %collective-permute-start.12 = (bf16[2,264,512]{2,1,0:T(8,128)(2,1)S(1)}, bf16[2,264,512]{2,1,0:T(8,128)(2,1)S(1)}, u32[]{:S(2)}, u32[]{:S(2)}) collective-permute-start(bf16[2,264,512]{2,1,0:T(8,128)(2,1)S(1)} %pad_maximum_fusion.1.own1.own_high), channel_id=1, source_target_pairs={{0,1},{1,0},{2,3},{3,2},{4,5},{5,4},{6,7},{7,6},{8,9},{9,8},{10,11... | collective-permute-start | bytes 1622024 | tf_op jit(solution)/shard_map/ppermute | solution.py:47
  19.0 12.8 %collective-permute-start.9 = (bf16[2,264,512]{2,1,0:T(8,128)(2,1)S(1)}, bf16[2,264,512]{2,1,0:T(8,128)(2,1)S(1)}, u32[]{:S(2)}, u32[]{:S(2)}) collective-permute-start(bf16[2,264,512]{2,1,0:T(8,128)(2,1)S(1)} %collective-permute-done.5.refs_2_), channel_id=1, source_target_pairs={{0,1},{1,0},{2,3},{3,2},{4,5},{5,4},{6,7},{7,6},{8,9},{9,8},{10,11... | collective-permute-start | bytes 1622024 | tf_op jit(solution)/shard_map/ppermute | solution.py:47
  20.8 14.0 %collective-permute-start.7 = (bf16[2,264,512]{2,1,0:T(8,128)(2,1)S(1)}, bf16[2,264,512]{2,1,0:T(8,128)(2,1)S(1)}, u32[]{:S(2)}, u32[]{:S(2)}) collective-permute-start(bf16[2,264,512]{2,1,0:T(8,128)(2,1)S(1)} %collective-permute-done.1.refs_0_), channel_id=1, source_target_pairs={{0,1},{1,0},{2,3},{3,2},{4,5},{5,4},{6,7},{7,6},{8,9},{9,8},{10,11... | collective-permute-start | bytes 1622024 | tf_op jit(solution)/shard_map/ppermute | solution.py:47
  24.8 10.0 %collective-permute-start.10 = (bf16[2,264,512]{2,1,0:T(8,128)(2,1)S(1)}, bf16[2,264,512]{2,1,0:T(8,128)(2,1)S(1)}, u32[]{:S(2)}, u32[]{:S(2)}) collective-permute-start(bf16[2,264,512]{2,1,0:T(8,128)(2,1)S(1)} %collective-permute-done.6.refs_3_), channel_id=1, source_target_pairs={{0,1},{1,0},{2,3},{3,2},{4,5},{5,4},{6,7},{7,6},{8,9},{9,8},{10,11... | collective-permute-start | bytes 1622024 | tf_op jit(solution)/shard_map/ppermute | solution.py:47
  26.6 8.2 %collective-permute-start.8 = (bf16[2,264,512]{2,1,0:T(8,128)(2,1)S(1)}, bf16[2,264,512]{2,1,0:T(8,128)(2,1)S(1)}, u32[]{:S(2)}, u32[]{:S(2)}) collective-permute-start(bf16[2,264,512]{2,1,0:T(8,128)(2,1)S(1)} %collective-permute-done.4.refs_1_), channel_id=1, source_target_pairs={{0,1},{1,0},{2,3},{3,2},{4,5},{5,4},{6,7},{7,6},{8,9},{9,8},{10,11... | collective-permute-start | bytes 1622024 | tf_op jit(solution)/shard_map/ppermute | solution.py:47
  30.0 10.7 %collective-permute-start.13 = (bf16[2,264,512]{2,1,0:T(8,128)(2,1)S(1)}, bf16[2,264,512]{2,1,0:T(8,128)(2,1)S(1)}, u32[]{:S(2)}, u32[]{:S(2)}) collective-permute-start(bf16[2,264,512]{2,1,0:T(8,128)(2,1)S(1)} %collective-permute-done.1.refs_0_), channel_id=1, source_target_pairs={{0,96},{1,131},{2,98},{3,129},{32,64},{33,163},{34,66},{35,161},{6... | collective-permute-start | bytes 1622024 | tf_op jit(solution)/shard_map/ppermute | solution.py:39
  31.9 9.4 %collective-permute-start.14 = (bf16[2,264,512]{2,1,0:T(8,128)(2,1)S(1)}, bf16[2,264,512]{2,1,0:T(8,128)(2,1)S(1)}, u32[]{:S(2)}, u32[]{:S(2)}) collective-permute-start(bf16[2,264,512]{2,1,0:T(8,128)(2,1)S(1)} %collective-permute-done.6.refs_3_), channel_id=1, source_target_pairs={{0,32},{1,129},{2,34},{3,131},{32,0},{33,161},{34,2},{35,163},{64,... | collective-permute-start | bytes 1622024 | tf_op jit(solution)/shard_map/ppermute | solution.py:39
  41.2 17.0 %collective-permute-start.15 = (bf16[2,264,512]{2,1,0:T(8,128)(2,1)S(1)}, bf16[2,264,512]{2,1,0:T(8,128)(2,1)S(1)}, u32[]{:S(2)}, u32[]{:S(2)}) collective-permute-start(bf16[2,264,512]{2,1,0:T(8,128)(2,1)S(1)} %collective-permute-done.13.refs_0_), channel_id=1, source_target_pairs={{0,1},{1,0},{2,3},{3,2},{4,5},{5,4},{6,7},{7,6},{8,9},{9,8},{10,11... | collective-permute-start | bytes 1622024 | tf_op jit(solution)/shard_map/ppermute | solution.py:47
  41.2 17.0 %collective-permute-start.16 = (bf16[2,264,512]{2,1,0:T(8,128)(2,1)S(1)}, bf16[2,264,512]{2,1,0:T(8,128)(2,1)S(1)}, u32[]{:S(2)}, u32[]{:S(2)}) collective-permute-start(bf16[2,264,512]{2,1,0:T(8,128)(2,1)S(1)} %collective-permute-done.14.refs_1_), channel_id=1, source_target_pairs={{0,1},{1,0},{2,3},{3,2},{4,5},{5,4},{6,7},{7,6},{8,9},{9,8},{10,11... | collective-permute-start | bytes 1622024 | tf_op jit(solution)/shard_map/ppermute | solution.py:47
  41.7 8.4 %collective-permute-start.18 = (f32[8,128]{1,0:T(8,128)S(1)}, f32[8,128]{1,0:T(8,128)S(1)}, u32[]{:S(2)}, u32[]{:S(2)}) collective-permute-start(f32[8,128]{1,0:T(8,128)S(1)} %rows.1), channel_id=1, source_target_pairs={{0,12},{1,17},{4,16},{5,21},{8,20},{9,25},{12,24},{13,29},{16,28},... | collective-permute-start | bytes 12296 | tf_op jit(solution)/shard_map/ppermute | solution.py:59
  46.4 4.8 %collective-permute-start.17 = (f32[8,128]{1,0:T(8,128)S(1)}, f32[8,128]{1,0:T(8,128)S(1)}, u32[]{:S(2)}, u32[]{:S(2)}) collective-permute-start(f32[8,128]{1,0:T(8,128)S(1)} %rows.1), channel_id=1, source_target_pairs={{0,4},{1,9},{4,8},{5,13},{8,12},{9,17},{12,16},{13,21},{16,20},{17... | collective-permute-start | bytes 12296 | tf_op jit(solution)/shard_map/ppermute | solution.py:59
  51.3 3.7 %collective-permute-start.20 = (f32[8,128]{1,0:T(8,128)S(1)}, f32[8,128]{1,0:T(8,128)S(1)}, u32[]{:S(2)}, u32[]{:S(2)}) collective-permute-start(f32[8,128]{1,0:T(8,128)S(1)} %part.1.refs_8_), channel_id=1, source_target_pairs={{0,128},{128,0},{1,129},{129,1},{2,130},{130,2},{3,131},{131,3},{4... | collective-permute-start | bytes 12296 | tf_op jit(solution)/shard_map/ppermute | solution.py:43
  52.2 6.1 %collective-permute-start.19 = (f32[8,128]{1,0:T(8,128)S(1)}, f32[8,128]{1,0:T(8,128)S(1)}, u32[]{:S(2)}, u32[]{:S(2)}) collective-permute-start(f32[8,128]{1,0:T(8,128)S(1)} %part.1.refs_8_), channel_id=1, source_target_pairs={{0,1},{1,0},{2,3},{3,2},{4,5},{5,4},{6,7},{7,6},{8,9},{9,8},{10,11... | collective-permute-start | bytes 12296 | tf_op jit(solution)/shard_map/ppermute | solution.py:47
  55.0 3.3 %collective-permute-start.21 = (f32[8,128]{1,0:T(8,128)S(1)}, f32[8,128]{1,0:T(8,128)S(1)}, u32[]{:S(2)}, u32[]{:S(2)}) collective-permute-start(f32[8,128]{1,0:T(8,128)S(1)} %collective-permute-done.20.refs_10_), channel_id=1, source_target_pairs={{0,1},{1,0},{2,3},{3,2},{4,5},{5,4},{6,7},{7,6},{8,9},{9,8},{10,11... | collective-permute-start | bytes 12296 | tf_op jit(solution)/shard_map/ppermute | solution.py:47
  62.9 7.0 %collective-permute-start.22 = (bf16[4,3,32,384]{3,2,1,0:T(8,128)(2,1)S(1)}, bf16[4,3,32,384]{3,2,1,0:T(8,128)(2,1)S(1)}, u32[]{:S(2)}, u32[]{:S(2)}) collective-permute-start(bf16[4,3,32,384]{3,2,1,0:T(8,128)(2,1)S(1)} %get-tuple-element.44), channel_id=1, source_target_pairs={{0,4},{1,29},{4,0},{5,9},{8,12},{9,5},{12,8},{13,17},{16,20},{17,1... | collective-permute-start | bytes 884744 | tf_op jit(solution)/shard_map/ppermute | solution.py:55
  67.6 5.8 %collective-permute-start.25 = (bf16[4,3,32,256]{3,2,1,0:T(8,128)(2,1)S(1)}, bf16[4,3,32,256]{3,2,1,0:T(8,128)(2,1)S(1)}, u32[]{:S(2)}, u32[]{:S(2)}) collective-permute-start(bf16[4,3,32,256]{3,2,1,0:T(8,128)(2,1)S(1)} %get-tuple-element.51), channel_id=1, source_target_pairs={{0,4},{1,29},{4,0},{5,9},{8,12},{9,5},{12,8},{13,17},{16,20},{17,1... | collective-permute-start | bytes 589832 | tf_op jit(solution)/shard_map/ppermute | solution.py:55
  73.4 11.7 %collective-permute-start.26 = (bf16[3,32,256]{2,1,0:T(8,128)(2,1)S(1)}, bf16[3,32,256]{2,1,0:T(8,128)(2,1)S(1)}, u32[]{:S(2)}, u32[]{:S(2)}) collective-permute-start(bf16[3,32,256]{2,1,0:T(8,128)(2,1)S(1)} %get-tuple-element.54), channel_id=1, source_target_pairs={{0,8},{4,12},{8,16},{12,20},{16,24},{20,28},{24,0},{28,4},{1,9},{5... | collective-permute-start | bytes 147464 | tf_op jit(solution)/shard_map/ppermute | solution.py:65
  74.8 10.3 %collective-permute-start.27 = (bf16[3,32,256]{2,1,0:T(8,128)(2,1)S(1)}, bf16[3,32,256]{2,1,0:T(8,128)(2,1)S(1)}, u32[]{:S(2)}, u32[]{:S(2)}) collective-permute-start(bf16[3,32,256]{2,1,0:T(8,128)(2,1)S(1)} %get-tuple-element.55), channel_id=1, source_target_pairs={{0,24},{4,28},{8,0},{12,4},{16,8},{20,12},{24,16},{28,20},{1,25},{... | collective-permute-start | bytes 147464 | tf_op jit(solution)/shard_map/ppermute | solution.py:65
  77.6 7.5 %collective-permute-start.23 = (bf16[3,32,384]{2,1,0:T(8,128)(2,1)S(1)}, bf16[3,32,384]{2,1,0:T(8,128)(2,1)S(1)}, u32[]{:S(2)}, u32[]{:S(2)}) collective-permute-start(bf16[3,32,384]{2,1,0:T(8,128)(2,1)S(1)} %get-tuple-element.46), channel_id=1, source_target_pairs={{0,8},{4,12},{8,16},{12,20},{16,24},{20,28},{24,0},{28,4},{1,9},{5... | collective-permute-start | bytes 221192 | tf_op jit(solution)/shard_map/ppermute | solution.py:65
  77.8 9.0 %collective-permute-start.24 = (bf16[3,32,384]{2,1,0:T(8,128)(2,1)S(1)}, bf16[3,32,384]{2,1,0:T(8,128)(2,1)S(1)}, u32[]{:S(2)}, u32[]{:S(2)}) collective-permute-start(bf16[3,32,384]{2,1,0:T(8,128)(2,1)S(1)} %get-tuple-element.47), channel_id=1, source_target_pairs={{0,24},{4,28},{8,0},{12,4},{16,8},{20,12},{24,16},{28,20},{1,25},{... | collective-permute-start | bytes 221192 | tf_op jit(solution)/shard_map/ppermute | solution.py:65
  81.8 10.8 %collective-permute-start.28 = (bf16[3,32,640]{2,1,0:T(8,128)(2,1)S(1)}, bf16[3,32,640]{2,1,0:T(8,128)(2,1)S(1)}, u32[]{:S(2)}, u32[]{:S(2)}) collective-permute-start(bf16[3,32,640]{2,1,0:T(8,128)(2,1)S(1)} %get-tuple-element.56), channel_id=1, source_target_pairs={{0,16},{4,20},{8,24},{12,28},{16,0},{20,4},{24,8},{28,12},{1,17},{... | collective-permute-start | bytes 368648 | tf_op jit(solution)/shard_map/ppermute | solution.py:65

commit v11 on v10

--- a/solution.py
+++ b/solution.py
@@ -325,10 +325,10 @@
             v = acc[1, p, rows, lower:upper]
             d = acc[2, p, rows, lower:upper] * w
             square = u * u
-            t = jnp.tanh(ROOT_2_PI * (u + CUBIC * (square * u)))
-            cdf = 0.5 * (1.0 + t)
+            t = jnp.tanh(u * (ROOT_2_PI + (ROOT_2_PI * CUBIC) * square))
+            cdf = 0.5 + 0.5 * t
             act = u * cdf
-            slope = cdf + 0.5 * u * (1.0 - t * t) * (ROOT_2_PI * (1.0 + 3.0 * CUBIC * square))
+            slope = cdf + act * (1.0 - t) * (ROOT_2_PI + (3.0 * CUBIC * ROOT_2_PI) * square)
             gates[p, rows, :width] = (d * v * slope).astype(BF16)
             gates[p, rows, width:] = (d * act).astype(BF16)
             hidden[p, rows] = (act * v * w).astype(BF16)

time: 93.7 us -> 93.5 us (level)
  no operation moved by 1% of the time
where the time goes in v11:
time: 93.5 us; the launch traced here: 93 us
  starting transfers between devices  38.8 us (41%)
  waiting for transfers between devices  32.6 us (35%)
  Pallas kernels  19.9 us (21%)
    ppermute x9, waiting for transfers between devices, across(): return lax.ppermute(block, PLANE, route)  17.8 us
    ppermute x9, starting transfers between devices, across(): return lax.ppermute(block, PLANE, route)  12.6 us
    ppermute x5, starting transfers between devices, z_step(): return lax.ppermute(block, 'z', [(z, (z + step) % 8) for z in range(8)])  11.7 us
    ppermute x2, starting transfers between devices, z_shift(): lax.ppermute(block, ('z', 'c'), [(z * 2 + c, (z + step + c) % 8 * 2 + c)...  7.83 us
    pallas_call x3, Pallas kernels, gathered(): pl.pallas_call(kernel, out_shape=STATE, in_specs=[VMEM] * (n + 2 + len(st...  7.75 us
    pallas_call x2, Pallas kernels, finished(): pl.pallas_call(kernel, out_shape=STATE + (jax.ShapeDtypeStruct((4, 3, 32,...  7.58 us
    ppermute x5, waiting for transfers between devices, z_step(): return lax.ppermute(block, 'z', [(z, (z + step) % 8) for z in range(8)])  7.33 us
    ppermute x2, waiting for transfers between devices, z_pair(): lax.ppermute(block, ('z', 'c'), [(z * 2 + c, partner_of(z, c) * 2 + c) fo...  4.73 us
  transfers between devices with their start and end apart: 29, of which 15 were waited for; matrix products, arithmetic and copies ran while one was open for 0% of the time, Pallas kernels for 16%

profile of v11, /device:TPU:6, one launch (start us, length us, event | category | flops | bytes accessed | tf_op | source)
XLA Modules:
  0.0 93.0 jit_solution(6011498966978545159)
XLA Ops:
  2.6 1.5 %collective-permute-start.3 = (bf16[264,512]{1,0:T(8,128)(2,1)S(1)}, bf16[264,512]{1,0:T(8,128)(2,1)S(1)}, u32[]{:S(2)}, u32[]{:S(2)}) collective-permute-start(bf16[264,512]{1,0:T(8,128)(2,1)S(1)} %message.1), channel_id=1, source_target_pairs={{0,130},{1,97},{2,128},{3,99},{32,162},{33,65},{34,160},{35,67},{6... | collective-permute-start | bytes 811016 | tf_op jit(solution)/shard_map/ppermute | solution.py:39
  4.0 1.8 %collective-permute-start.2 = (bf16[264,512]{1,0:T(8,128)(2,1)S(1)}, bf16[264,512]{1,0:T(8,128)(2,1)S(1)}, u32[]{:S(2)}, u32[]{:S(2)}) collective-permute-start(bf16[264,512]{1,0:T(8,128)(2,1)S(1)} %message.1), channel_id=1, source_target_pairs={{0,2},{1,65},{2,0},{3,67},{32,34},{33,97},{34,32},{35,99},{64,66},... | collective-permute-start | bytes 811016 | tf_op jit(solution)/shard_map/ppermute | solution.py:39
  5.8 2.4 %collective-permute-done = bf16[264,512]{1,0:T(8,128)(2,1)S(1)} collective-permute-done((bf16[264,512]{1,0:T(8,128)(2,1)S(1)}, bf16[264,512]{1,0:T(8,128)(2,1)S(1)}, u32[]{:S(2)}, u32[]{:S(2)}) %collective-permute-start) | collective-permute-done | bytes 270368 | tf_op jit(solution)/shard_map/ppermute | solution.py:39
  8.4 3.1 %collective-permute-start.5 = (bf16[2,264,512]{2,1,0:T(8,128)(2,1)S(1)}, bf16[2,264,512]{2,1,0:T(8,128)(2,1)S(1)}, u32[]{:S(2)}, u32[]{:S(2)}) collective-permute-start(bf16[2,264,512]{2,1,0:T(8,128)(2,1)S(1)} %pad_maximum_fusion.own0.own_low), channel_id=1, source_target_pairs={{0,96},{1,131},{2,98},{3,129},{32,64},{33,163},{34,66},{35,161},{6... | collective-permute-start | bytes 1622024 | tf_op jit(solution)/shard_map/ppermute | solution.py:39
  11.6 1.9 %collective-permute-done.3 = bf16[264,512]{1,0:T(8,128)(2,1)S(1)} collective-permute-done((bf16[264,512]{1,0:T(8,128)(2,1)S(1)}, bf16[264,512]{1,0:T(8,128)(2,1)S(1)}, u32[]{:S(2)}, u32[]{:S(2)}) %collective-permute-start.3) | collective-permute-done | bytes 270368 | tf_op jit(solution)/shard_map/ppermute | solution.py:39
  13.5 3.3 %collective-permute-start.6 = (bf16[2,264,512]{2,1,0:T(8,128)(2,1)S(1)}, bf16[2,264,512]{2,1,0:T(8,128)(2,1)S(1)}, u32[]{:S(2)}, u32[]{:S(2)}) collective-permute-start(bf16[2,264,512]{2,1,0:T(8,128)(2,1)S(1)} %pad_maximum_fusion.1.own1.own_high), channel_id=1, source_target_pairs={{0,96},{1,131},{2,98},{3,129},{32,64},{33,163},{34,66},{35,161},{6... | collective-permute-start | bytes 1622024 | tf_op jit(solution)/shard_map/ppermute | solution.py:39
  16.9 2.1 %collective-permute-done.5.refs_2_ = bf16[2,264,512]{2,1,0:T(8,128)(2,1)S(1)} collective-permute-done((bf16[2,264,512]{2,1,0:T(8,128)(2,1)S(1)}, bf16[2,264,512]{2,1,0:T(8,128)(2,1)S(1)}, u32[]{:S(2)}, u32[]{:S(2)}) %collective-permute-start.5) | collective-permute-done | bytes 540704 | tf_op jit(solution)/shard_map/ppermute | solution.py:39
  19.1 1.8 %collective-permute-done.1.refs_0_ = bf16[2,264,512]{2,1,0:T(8,128)(2,1)S(1)} collective-permute-done((bf16[2,264,512]{2,1,0:T(8,128)(2,1)S(1)}, bf16[2,264,512]{2,1,0:T(8,128)(2,1)S(1)}, u32[]{:S(2)}, u32[]{:S(2)}) %collective-permute-start.1) | collective-permute-done | bytes 540704 | tf_op jit(solution)/shard_map/ppermute | solution.py:39
  20.8 4.0 %collective-permute-done.6.refs_3_ = bf16[2,264,512]{2,1,0:T(8,128)(2,1)S(1)} collective-permute-done((bf16[2,264,512]{2,1,0:T(8,128)(2,1)S(1)}, bf16[2,264,512]{2,1,0:T(8,128)(2,1)S(1)}, u32[]{:S(2)}, u32[]{:S(2)}) %collective-permute-start.6) | collective-permute-done | bytes 540704 | tf_op jit(solution)/shard_map/ppermute | solution.py:39
  24.8 1.8 %collective-permute-done.4.refs_1_ = bf16[2,264,512]{2,1,0:T(8,128)(2,1)S(1)} collective-permute-done((bf16[2,264,512]{2,1,0:T(8,128)(2,1)S(1)}, bf16[2,264,512]{2,1,0:T(8,128)(2,1)S(1)}, u32[]{:S(2)}, u32[]{:S(2)}) %collective-permute-start.4) | collective-permute-done | bytes 540704 | tf_op jit(solution)/shard_map/ppermute | solution.py:39
  26.6 3.4 %load.1 = (bf16[2048,1280]{1,0:T(8,128)(2,1)S(1)}, bf16[2048,640]{1,0:T(8,128)(2,1)S(1)}) custom-call(bf16[4,512,640]{2,1,0:T(8,128)(2,1)} %bitcast.10, bf16[4,512,640]{2,1,0:T(8,128)(2,1)} %bitcast.11, bf16[4,512,640]{2,1,0:T(8,128)(2,1)} %bitcast.12), custom_call_target="tpu_custom_call" | custom-call | tf_op jit(solution)/shard_map/load/pallas_call | solution.py:138
  30.0 1.8 %collective-permute-start.13 = (bf16[2,264,512]{2,1,0:T(8,128)(2,1)S(1)}, bf16[2,264,512]{2,1,0:T(8,128)(2,1)S(1)}, u32[]{:S(2)}, u32[]{:S(2)}) collective-permute-start(bf16[2,264,512]{2,1,0:T(8,128)(2,1)S(1)} %collective-permute-done.1.refs_0_), channel_id=1, source_target_pairs={{0,96},{1,131},{2,98},{3,129},{32,64},{33,163},{34,66},{35,161},{6... | collective-permute-start | bytes 1622024 | tf_op jit(solution)/shard_map/ppermute | solution.py:39
  31.9 2.9 %shard_map.82 = (f32[3,8,128,640]{3,2,1,0:T(8,128)S(1)}, bf16[2,8,128,256]{3,2,1,0:T(8,128)(2,1)S(1)}) custom-call(bf16[2,264,512]{2,1,0:T(8,128)(2,1)S(1)} %pad_maximum_fusion.own0.own_low, bf16[2,264,512]{2,1,0:T(8,128)(2,1)S(1)} %pad_maximum_fusion.1.own1.own_high, bf16[2,264,512]{2,1,0:T(8,128)(2,1)S(1)} %collective-permute-done.11.other0.other_low, ...), custom_call_target="tpu_custom_call" | custom-call | flops 2147483648 | bytes 1048576 | tf_op jit(solution)/shard_map/pallas_call | solution.py:268
  34.8 2.4 %shard_map.83 = (f32[3,8,128,640]{3,2,1,0:T(8,128)S(1)}, bf16[2,8,128,256]{3,2,1,0:T(8,128)(2,1)S(1)}) custom-call(bf16[2,264,512]{2,1,0:T(8,128)(2,1)S(1)} %collective-permute-done.1.refs_0_, bf16[2,264,512]{2,1,0:T(8,128)(2,1)S(1)} %collective-permute-done.4.refs_1_, ...), custom_call_target="tpu_custom_call", output_to_operand_aliasing={{0}: (10, {}), {1}: (11, {})} | custom-call | flops 4294967296 | bytes 1048576 | tf_op jit(solution)/shard_map/pallas_call | solution.py:268
  37.3 3.4 %collective-permute-done.13.refs_0_ = bf16[2,264,512]{2,1,0:T(8,128)(2,1)S(1)} collective-permute-done((bf16[2,264,512]{2,1,0:T(8,128)(2,1)S(1)}, bf16[2,264,512]{2,1,0:T(8,128)(2,1)S(1)}, u32[]{:S(2)}, u32[]{:S(2)}) %collective-permute-start.13) | collective-permute-done | bytes 540704 | tf_op jit(solution)/shard_map/ppermute | solution.py:39
  41.7 4.7 %collective-permute-start.18 = (f32[8,128]{1,0:T(8,128)S(1)}, f32[8,128]{1,0:T(8,128)S(1)}, u32[]{:S(2)}, u32[]{:S(2)}) collective-permute-start(f32[8,128]{1,0:T(8,128)S(1)} %rows.1), channel_id=1, source_target_pairs={{0,12},{1,17},{4,16},{5,21},{8,20},{9,25},{12,24},{13,29},{16,28},... | collective-permute-start | bytes 12296 | tf_op jit(solution)/shard_map/ppermute | solution.py:59
  46.4 3.1 %collective-permute-start.17 = (f32[8,128]{1,0:T(8,128)S(1)}, f32[8,128]{1,0:T(8,128)S(1)}, u32[]{:S(2)}, u32[]{:S(2)}) collective-permute-start(f32[8,128]{1,0:T(8,128)S(1)} %rows.1), channel_id=1, source_target_pairs={{0,4},{1,9},{4,8},{5,13},{8,12},{9,17},{12,16},{13,21},{16,20},{17... | collective-permute-start | bytes 12296 | tf_op jit(solution)/shard_map/ppermute | solution.py:59
  50.1 1.1 %collective-permute-done.17.near = f32[8,128]{1,0:T(8,128)S(1)} collective-permute-done((f32[8,128]{1,0:T(8,128)S(1)}, f32[8,128]{1,0:T(8,128)S(1)}, u32[]{:S(2)}, u32[]{:S(2)}) %collective-permute-start.17) | collective-permute-done | bytes 4128 | tf_op jit(solution)/shard_map/ppermute | solution.py:59
  52.2 1.8 %collective-permute-start.19 = (f32[8,128]{1,0:T(8,128)S(1)}, f32[8,128]{1,0:T(8,128)S(1)}, u32[]{:S(2)}, u32[]{:S(2)}) collective-permute-start(f32[8,128]{1,0:T(8,128)S(1)} %part.1.refs_8_), channel_id=1, source_target_pairs={{0,1},{1,0},{2,3},{3,2},{4,5},{5,4},{6,7},{7,6},{8,9},{9,8},{10,11... | collective-permute-start | bytes 12296 | tf_op jit(solution)/shard_map/ppermute | solution.py:47
  53.9 1.0 %collective-permute-done.20.refs_10_ = f32[8,128]{1,0:T(8,128)S(1)} collective-permute-done((f32[8,128]{1,0:T(8,128)S(1)}, f32[8,128]{1,0:T(8,128)S(1)}, u32[]{:S(2)}, u32[]{:S(2)}) %collective-permute-start.20) | collective-permute-done | bytes 4128 | tf_op jit(solution)/shard_map/ppermute | solution.py:43
  55.8 2.4 %shard_map.84 = (f32[3,8,128,640]{3,2,1,0:T(8,128)S(1)}, bf16[2,8,128,256]{3,2,1,0:T(8,128)(2,1)S(1)}) custom-call(bf16[2,264,512]{2,1,0:T(8,128)(2,1)S(1)} %collective-permute-done.1.refs_0_, bf16[2,264,512]{2,1,0:T(8,128)(2,1)S(1)} %collective-permute-done.4.refs_1_, ...), custom_call_target="tpu_custom_call", output_to_operand_aliasing={{0}: (10, {}), {1}: (11, {})} | custom-call | flops 4294967296 | bytes 1048576 | tf_op jit(solution)/shard_map/pallas_call | solution.py:268
  58.3 4.4 %shard_map.85 = (f32[3,8,128,640]{3,2,1,0:T(8,128)S(1)}, bf16[2,8,128,256]{3,2,1,0:T(8,128)(2,1)S(1)}, f32[4,3,32,384]{3,2,1,0:T(8,128)S(1)}, bf16[4,3,32,384]{3,2,1,0:T(8,128)(2,1)S(1)}) custom-call(bf16[2,264,512]{2,1,0:T(8,128)(2,1)S(1)} %collective-permute-done.13.refs_0_, ...), custom_call_target="tpu_custom_call", output_to_operand_aliasing={{0}: (6, {}), {1}: (7, {})} | custom-call | flops 2147483648 | bytes 1048576 | tf_op jit(solution)/shard_map/pallas_call | solution.py:288
  62.6 1.5 %collective-permute-start.22 = (bf16[4,3,32,384]{3,2,1,0:T(8,128)(2,1)S(1)}, bf16[4,3,32,384]{3,2,1,0:T(8,128)(2,1)S(1)}, u32[]{:S(2)}, u32[]{:S(2)}) collective-permute-start(bf16[4,3,32,384]{3,2,1,0:T(8,128)(2,1)S(1)} %get-tuple-element.44), channel_id=1, source_target_pairs={{0,4},{1,29},{4,0},{5,9},{8,12},{9,5},{12,8},{13,17},{16,20},{17,1... | collective-permute-start | bytes 884744 | tf_op jit(solution)/shard_map/ppermute | solution.py:55
  64.1 3.2 %shard_map.87 = (f32[3,8,128,640]{3,2,1,0:T(8,128)S(1)}, bf16[2,8,128,256]{3,2,1,0:T(8,128)(2,1)S(1)}, f32[4,3,32,256]{3,2,1,0:T(8,128)S(1)}, bf16[4,3,32,256]{3,2,1,0:T(8,128)(2,1)S(1)}) custom-call(bf16[2,264,512]{2,1,0:T(8,128)(2,1)S(1)} %collective-permute-done.13.refs_0_, ...), custom_call_target="tpu_custom_call", output_to_operand_aliasing={{0}: (6, {}), {1}: (7, {})} | custom-call | flops 2147483648 | bytes 1048576 | tf_op jit(solution)/shard_map/pallas_call | solution.py:288
  68.3 1.4 %collective-permute-done.22.got = bf16[4,3,32,384]{3,2,1,0:T(8,128)(2,1)S(1)} collective-permute-done((bf16[4,3,32,384]{3,2,1,0:T(8,128)(2,1)S(1)}, bf16[4,3,32,384]{3,2,1,0:T(8,128)(2,1)S(1)}, u32[]{:S(2)}, u32[]{:S(2)}) %collective-permute-start.22) | collective-permute-done | bytes 294944 | tf_op jit(solution)/shard_map/ppermute | solution.py:55
  69.7 3.3 %collective-permute-done.25.got = bf16[4,3,32,256]{3,2,1,0:T(8,128)(2,1)S(1)} collective-permute-done((bf16[4,3,32,256]{3,2,1,0:T(8,128)(2,1)S(1)}, bf16[4,3,32,256]{3,2,1,0:T(8,128)(2,1)S(1)}, u32[]{:S(2)}, u32[]{:S(2)}) %collective-permute-start.25) | collective-permute-done | bytes 196640 | tf_op jit(solution)/shard_map/ppermute | solution.py:55
  73.1 1.4 %collective-permute-start.26 = (bf16[3,32,256]{2,1,0:T(8,128)(2,1)S(1)}, bf16[3,32,256]{2,1,0:T(8,128)(2,1)S(1)}, u32[]{:S(2)}, u32[]{:S(2)}) collective-permute-start(bf16[3,32,256]{2,1,0:T(8,128)(2,1)S(1)} %get-tuple-element.54), channel_id=1, source_target_pairs={{0,8},{4,12},{8,16},{12,20},{16,24},{20,28},{24,0},{28,4},{1,9},{5... | collective-permute-start | bytes 147464 | tf_op jit(solution)/shard_map/ppermute | solution.py:65
  74.6 2.8 %collective-permute-start.27 = (bf16[3,32,256]{2,1,0:T(8,128)(2,1)S(1)}, bf16[3,32,256]{2,1,0:T(8,128)(2,1)S(1)}, u32[]{:S(2)}, u32[]{:S(2)}) collective-permute-start(bf16[3,32,256]{2,1,0:T(8,128)(2,1)S(1)} %get-tuple-element.55), channel_id=1, source_target_pairs={{0,24},{4,28},{8,0},{12,4},{16,8},{20,12},{24,16},{28,20},{1,25},{... | collective-permute-start | bytes 147464 | tf_op jit(solution)/shard_map/ppermute | solution.py:65
  77.5 4.0 %collective-permute-start.24 = (bf16[3,32,384]{2,1,0:T(8,128)(2,1)S(1)}, bf16[3,32,384]{2,1,0:T(8,128)(2,1)S(1)}, u32[]{:S(2)}, u32[]{:S(2)}) collective-permute-start(bf16[3,32,384]{2,1,0:T(8,128)(2,1)S(1)} %get-tuple-element.47), channel_id=1, source_target_pairs={{0,24},{4,28},{8,0},{12,4},{16,8},{20,12},{24,16},{28,20},{1,25},{... | collective-permute-start | bytes 221192 | tf_op jit(solution)/shard_map/ppermute | solution.py:65
  81.5 3.4 %collective-permute-start.28 = (bf16[3,32,640]{2,1,0:T(8,128)(2,1)S(1)}, bf16[3,32,640]{2,1,0:T(8,128)(2,1)S(1)}, u32[]{:S(2)}, u32[]{:S(2)}) collective-permute-start(bf16[3,32,640]{2,1,0:T(8,128)(2,1)S(1)} %get-tuple-element.56), channel_id=1, source_target_pairs={{0,16},{4,20},{8,24},{12,28},{16,0},{20,4},{24,8},{28,12},{1,17},{... | collective-permute-start | bytes 368648 | tf_op jit(solution)/shard_map/ppermute | solution.py:65
  84.9 1.6 %collective-permute-done.24 = bf16[3,32,384]{2,1,0:T(8,128)(2,1)S(1)} collective-permute-done((bf16[3,32,384]{2,1,0:T(8,128)(2,1)S(1)}, bf16[3,32,384]{2,1,0:T(8,128)(2,1)S(1)}, u32[]{:S(2)}, u32[]{:S(2)}) %collective-permute-start.24) | collective-permute-done | bytes 73760 | tf_op jit(solution)/shard_map/ppermute | solution.py:65
  86.6 5.7 %collective-permute-done.28 = bf16[3,32,640]{2,1,0:T(8,128)(2,1)S(1)} collective-permute-done((bf16[3,32,640]{2,1,0:T(8,128)(2,1)S(1)}, bf16[3,32,640]{2,1,0:T(8,128)(2,1)S(1)}, u32[]{:S(2)}, u32[]{:S(2)}) %collective-permute-start.28) | collective-permute-done | bytes 122912 | tf_op jit(solution)/shard_map/ppermute | solution.py:65
  (42 shorter events, 7.9 us)
Async XLA Ops:
  1.7 6.5 %collective-permute-start = (bf16[264,512]{1,0:T(8,128)(2,1)S(1)}, bf16[264,512]{1,0:T(8,128)(2,1)S(1)}, u32[]{:S(2)}, u32[]{:S(2)}) collective-permute-start(bf16[264,512]{1,0:T(8,128)(2,1)S(1)} %message.1), channel_id=1, source_target_pairs={{0,128},{1,33},{2,130},{3,35},{32,160},{33,1},{34,162},{35,3},{64,... | collective-permute-start | bytes 811016 | tf_op jit(solution)/shard_map/ppermute | solution.py:39
  2.6 10.9 %collective-permute-start.3 = (bf16[264,512]{1,0:T(8,128)(2,1)S(1)}, bf16[264,512]{1,0:T(8,128)(2,1)S(1)}, u32[]{:S(2)}, u32[]{:S(2)}) collective-permute-start(bf16[264,512]{1,0:T(8,128)(2,1)S(1)} %message.1), channel_id=1, source_target_pairs={{0,130},{1,97},{2,128},{3,99},{32,162},{33,65},{34,160},{35,67},{6... | collective-permute-start | bytes 811016 | tf_op jit(solution)/shard_map/ppermute | solution.py:39
  4.0 9.4 %collective-permute-start.2 = (bf16[264,512]{1,0:T(8,128)(2,1)S(1)}, bf16[264,512]{1,0:T(8,128)(2,1)S(1)}, u32[]{:S(2)}, u32[]{:S(2)}) collective-permute-start(bf16[264,512]{1,0:T(8,128)(2,1)S(1)} %message.1), channel_id=1, source_target_pairs={{0,2},{1,65},{2,0},{3,67},{32,34},{33,97},{34,32},{35,99},{64,66},... | collective-permute-start | bytes 811016 | tf_op jit(solution)/shard_map/ppermute | solution.py:39
  8.3 8.7 %collective-permute-start.11 = (bf16[2,264,512]{2,1,0:T(8,128)(2,1)S(1)}, bf16[2,264,512]{2,1,0:T(8,128)(2,1)S(1)}, u32[]{:S(2)}, u32[]{:S(2)}) collective-permute-start(bf16[2,264,512]{2,1,0:T(8,128)(2,1)S(1)} %pad_maximum_fusion.own0.own_low), channel_id=1, source_target_pairs={{0,1},{1,0},{2,3},{3,2},{4,5},{5,4},{6,7},{7,6},{8,9},{9,8},{10,11... | collective-permute-start | bytes 1622024 | tf_op jit(solution)/shard_map/ppermute | solution.py:47
  8.4 10.7 %collective-permute-start.5 = (bf16[2,264,512]{2,1,0:T(8,128)(2,1)S(1)}, bf16[2,264,512]{2,1,0:T(8,128)(2,1)S(1)}, u32[]{:S(2)}, u32[]{:S(2)}) collective-permute-start(bf16[2,264,512]{2,1,0:T(8,128)(2,1)S(1)} %pad_maximum_fusion.own0.own_low), channel_id=1, source_target_pairs={{0,96},{1,131},{2,98},{3,129},{32,64},{33,163},{34,66},{35,161},{6... | collective-permute-start | bytes 1622024 | tf_op jit(solution)/shard_map/ppermute | solution.py:39
  11.5 9.4 %collective-permute-start.1 = (bf16[2,264,512]{2,1,0:T(8,128)(2,1)S(1)}, bf16[2,264,512]{2,1,0:T(8,128)(2,1)S(1)}, u32[]{:S(2)}, u32[]{:S(2)}) collective-permute-start(bf16[2,264,512]{2,1,0:T(8,128)(2,1)S(1)} %pad_maximum_fusion.own0.own_low), channel_id=1, source_target_pairs={{0,32},{1,129},{2,34},{3,131},{32,0},{33,161},{34,2},{35,163},{64,... | collective-permute-start | bytes 1622024 | tf_op jit(solution)/shard_map/ppermute | solution.py:39
  13.5 11.3 %collective-permute-start.6 = (bf16[2,264,512]{2,1,0:T(8,128)(2,1)S(1)}, bf16[2,264,512]{2,1,0:T(8,128)(2,1)S(1)}, u32[]{:S(2)}, u32[]{:S(2)}) collective-permute-start(bf16[2,264,512]{2,1,0:T(8,128)(2,1)S(1)} %pad_maximum_fusion.1.own1.own_high), channel_id=1, source_target_pairs={{0,96},{1,131},{2,98},{3,129},{32,64},{33,163},{34,66},{35,161},{6... | collective-permute-start | bytes 1622024 | tf_op jit(solution)/shard_map/ppermute | solution.py:39
  16.8 9.8 %collective-permute-start.4 = (bf16[2,264,512]{2,1,0:T(8,128)(2,1)S(1)}, bf16[2,264,512]{2,1,0:T(8,128)(2,1)S(1)}, u32[]{:S(2)}, u32[]{:S(2)}) collective-permute-start(bf16[2,264,512]{2,1,0:T(8,128)(2,1)S(1)} %pad_maximum_fusion.1.own1.own_high), channel_id=1, source_target_pairs={{0,32},{1,129},{2,34},{3,131},{32,0},{33,161},{34,2},{35,163},{64,... | collective-permute-start | bytes 1622024 | tf_op jit(solution)/shard_map/ppermute | solution.py:39
  16.9 13.1 %collective-permute-start.12 = (bf16[2,264,512]{2,1,0:T(8,128)(2,1)S(1)}, bf16[2,264,512]{2,1,0:T(8,128)(2,1)S(1)}, u32[]{:S(2)}, u32[]{:S(2)}) collective-permute-start(bf16[2,264,512]{2,1,0:T(8,128)(2,1)S(1)} %pad_maximum_fusion.1.own1.own_high), channel_id=1, source_target_pairs={{0,1},{1,0},{2,3},{3,2},{4,5},{5,4},{6,7},{7,6},{8,9},{9,8},{10,11... | collective-permute-start | bytes 1622024 | tf_op jit(solution)/shard_map/ppermute | solution.py:47
  19.0 12.8 %collective-permute-start.9 = (bf16[2,264,512]{2,1,0:T(8,128)(2,1)S(1)}, bf16[2,264,512]{2,1,0:T(8,128)(2,1)S(1)}, u32[]{:S(2)}, u32[]{:S(2)}) collective-permute-start(bf16[2,264,512]{2,1,0:T(8,128)(2,1)S(1)} %collective-permute-done.5.refs_2_), channel_id=1, source_target_pairs={{0,1},{1,0},{2,3},{3,2},{4,5},{5,4},{6,7},{7,6},{8,9},{9,8},{10,11... | collective-permute-start | bytes 1622024 | tf_op jit(solution)/shard_map/ppermute | solution.py:47
  20.8 14.0 %collective-permute-start.7 = (bf16[2,264,512]{2,1,0:T(8,128)(2,1)S(1)}, bf16[2,264,512]{2,1,0:T(8,128)(2,1)S(1)}, u32[]{:S(2)}, u32[]{:S(2)}) collective-permute-start(bf16[2,264,512]{2,1,0:T(8,128)(2,1)S(1)} %collective-permute-done.1.refs_0_), channel_id=1, source_target_pairs={{0,1},{1,0},{2,3},{3,2},{4,5},{5,4},{6,7},{7,6},{8,9},{9,8},{10,11... | collective-permute-start | bytes 1622024 | tf_op jit(solution)/shard_map/ppermute | solution.py:47
  24.8 10.0 %collective-permute-start.10 = (bf16[2,264,512]{2,1,0:T(8,128)(2,1)S(1)}, bf16[2,264,512]{2,1,0:T(8,128)(2,1)S(1)}, u32[]{:S(2)}, u32[]{:S(2)}) collective-permute-start(bf16[2,264,512]{2,1,0:T(8,128)(2,1)S(1)} %collective-permute-done.6.refs_3_), channel_id=1, source_target_pairs={{0,1},{1,0},{2,3},{3,2},{4,5},{5,4},{6,7},{7,6},{8,9},{9,8},{10,11... | collective-permute-start | bytes 1622024 | tf_op jit(solution)/shard_map/ppermute | solution.py:47
  26.6 8.2 %collective-permute-start.8 = (bf16[2,264,512]{2,1,0:T(8,128)(2,1)S(1)}, bf16[2,264,512]{2,1,0:T(8,128)(2,1)S(1)}, u32[]{:S(2)}, u32[]{:S(2)}) collective-permute-start(bf16[2,264,512]{2,1,0:T(8,128)(2,1)S(1)} %collective-permute-done.4.refs_1_), channel_id=1, source_target_pairs={{0,1},{1,0},{2,3},{3,2},{4,5},{5,4},{6,7},{7,6},{8,9},{9,8},{10,11... | collective-permute-start | bytes 1622024 | tf_op jit(solution)/shard_map/ppermute | solution.py:47
  30.0 10.7 %collective-permute-start.13 = (bf16[2,264,512]{2,1,0:T(8,128)(2,1)S(1)}, bf16[2,264,512]{2,1,0:T(8,128)(2,1)S(1)}, u32[]{:S(2)}, u32[]{:S(2)}) collective-permute-start(bf16[2,264,512]{2,1,0:T(8,128)(2,1)S(1)} %collective-permute-done.1.refs_0_), channel_id=1, source_target_pairs={{0,96},{1,131},{2,98},{3,129},{32,64},{33,163},{34,66},{35,161},{6... | collective-permute-start | bytes 1622024 | tf_op jit(solution)/shard_map/ppermute | solution.py:39
  31.9 9.4 %collective-permute-start.14 = (bf16[2,264,512]{2,1,0:T(8,128)(2,1)S(1)}, bf16[2,264,512]{2,1,0:T(8,128)(2,1)S(1)}, u32[]{:S(2)}, u32[]{:S(2)}) collective-permute-start(bf16[2,264,512]{2,1,0:T(8,128)(2,1)S(1)} %collective-permute-done.6.refs_3_), channel_id=1, source_target_pairs={{0,32},{1,129},{2,34},{3,131},{32,0},{33,161},{34,2},{35,163},{64,... | collective-permute-start | bytes 1622024 | tf_op jit(solution)/shard_map/ppermute | solution.py:39
  41.2 17.0 %collective-permute-start.15 = (bf16[2,264,512]{2,1,0:T(8,128)(2,1)S(1)}, bf16[2,264,512]{2,1,0:T(8,128)(2,1)S(1)}, u32[]{:S(2)}, u32[]{:S(2)}) collective-permute-start(bf16[2,264,512]{2,1,0:T(8,128)(2,1)S(1)} %collective-permute-done.13.refs_0_), channel_id=1, source_target_pairs={{0,1},{1,0},{2,3},{3,2},{4,5},{5,4},{6,7},{7,6},{8,9},{9,8},{10,11... | collective-permute-start | bytes 1622024 | tf_op jit(solution)/shard_map/ppermute | solution.py:47
  41.2 17.0 %collective-permute-start.16 = (bf16[2,264,512]{2,1,0:T(8,128)(2,1)S(1)}, bf16[2,264,512]{2,1,0:T(8,128)(2,1)S(1)}, u32[]{:S(2)}, u32[]{:S(2)}) collective-permute-start(bf16[2,264,512]{2,1,0:T(8,128)(2,1)S(1)} %collective-permute-done.14.refs_1_), channel_id=1, source_target_pairs={{0,1},{1,0},{2,3},{3,2},{4,5},{5,4},{6,7},{7,6},{8,9},{9,8},{10,11... | collective-permute-start | bytes 1622024 | tf_op jit(solution)/shard_map/ppermute | solution.py:47
  41.7 8.4 %collective-permute-start.18 = (f32[8,128]{1,0:T(8,128)S(1)}, f32[8,128]{1,0:T(8,128)S(1)}, u32[]{:S(2)}, u32[]{:S(2)}) collective-permute-start(f32[8,128]{1,0:T(8,128)S(1)} %rows.1), channel_id=1, source_target_pairs={{0,12},{1,17},{4,16},{5,21},{8,20},{9,25},{12,24},{13,29},{16,28},... | collective-permute-start | bytes 12296 | tf_op jit(solution)/shard_map/ppermute | solution.py:59
  46.4 4.8 %collective-permute-start.17 = (f32[8,128]{1,0:T(8,128)S(1)}, f32[8,128]{1,0:T(8,128)S(1)}, u32[]{:S(2)}, u32[]{:S(2)}) collective-permute-start(f32[8,128]{1,0:T(8,128)S(1)} %rows.1), channel_id=1, source_target_pairs={{0,4},{1,9},{4,8},{5,13},{8,12},{9,17},{12,16},{13,21},{16,20},{17... | collective-permute-start | bytes 12296 | tf_op jit(solution)/shard_map/ppermute | solution.py:59
  51.3 3.7 %collective-permute-start.20 = (f32[8,128]{1,0:T(8,128)S(1)}, f32[8,128]{1,0:T(8,128)S(1)}, u32[]{:S(2)}, u32[]{:S(2)}) collective-permute-start(f32[8,128]{1,0:T(8,128)S(1)} %part.1.refs_8_), channel_id=1, source_target_pairs={{0,128},{128,0},{1,129},{129,1},{2,130},{130,2},{3,131},{131,3},{4... | collective-permute-start | bytes 12296 | tf_op jit(solution)/shard_map/ppermute | solution.py:43
  52.2 6.1 %collective-permute-start.19 = (f32[8,128]{1,0:T(8,128)S(1)}, f32[8,128]{1,0:T(8,128)S(1)}, u32[]{:S(2)}, u32[]{:S(2)}) collective-permute-start(f32[8,128]{1,0:T(8,128)S(1)} %part.1.refs_8_), channel_id=1, source_target_pairs={{0,1},{1,0},{2,3},{3,2},{4,5},{5,4},{6,7},{7,6},{8,9},{9,8},{10,11... | collective-permute-start | bytes 12296 | tf_op jit(solution)/shard_map/ppermute | solution.py:47
  55.0 3.3 %collective-permute-start.21 = (f32[8,128]{1,0:T(8,128)S(1)}, f32[8,128]{1,0:T(8,128)S(1)}, u32[]{:S(2)}, u32[]{:S(2)}) collective-permute-start(f32[8,128]{1,0:T(8,128)S(1)} %collective-permute-done.20.refs_10_), channel_id=1, source_target_pairs={{0,1},{1,0},{2,3},{3,2},{4,5},{5,4},{6,7},{7,6},{8,9},{9,8},{10,11... | collective-permute-start | bytes 12296 | tf_op jit(solution)/shard_map/ppermute | solution.py:47
  62.6 7.0 %collective-permute-start.22 = (bf16[4,3,32,384]{3,2,1,0:T(8,128)(2,1)S(1)}, bf16[4,3,32,384]{3,2,1,0:T(8,128)(2,1)S(1)}, u32[]{:S(2)}, u32[]{:S(2)}) collective-permute-start(bf16[4,3,32,384]{3,2,1,0:T(8,128)(2,1)S(1)} %get-tuple-element.44), channel_id=1, source_target_pairs={{0,4},{1,29},{4,0},{5,9},{8,12},{9,5},{12,8},{13,17},{16,20},{17,1... | collective-permute-start | bytes 884744 | tf_op jit(solution)/shard_map/ppermute | solution.py:55
  67.3 5.8 %collective-permute-start.25 = (bf16[4,3,32,256]{3,2,1,0:T(8,128)(2,1)S(1)}, bf16[4,3,32,256]{3,2,1,0:T(8,128)(2,1)S(1)}, u32[]{:S(2)}, u32[]{:S(2)}) collective-permute-start(bf16[4,3,32,256]{3,2,1,0:T(8,128)(2,1)S(1)} %get-tuple-element.51), channel_id=1, source_target_pairs={{0,4},{1,29},{4,0},{5,9},{8,12},{9,5},{12,8},{13,17},{16,20},{17,1... | collective-permute-start | bytes 589832 | tf_op jit(solution)/shard_map/ppermute | solution.py:55
  73.1 11.7 %collective-permute-start.26 = (bf16[3,32,256]{2,1,0:T(8,128)(2,1)S(1)}, bf16[3,32,256]{2,1,0:T(8,128)(2,1)S(1)}, u32[]{:S(2)}, u32[]{:S(2)}) collective-permute-start(bf16[3,32,256]{2,1,0:T(8,128)(2,1)S(1)} %get-tuple-element.54), channel_id=1, source_target_pairs={{0,8},{4,12},{8,16},{12,20},{16,24},{20,28},{24,0},{28,4},{1,9},{5... | collective-permute-start | bytes 147464 | tf_op jit(solution)/shard_map/ppermute | solution.py:65
  74.6 10.3 %collective-permute-start.27 = (bf16[3,32,256]{2,1,0:T(8,128)(2,1)S(1)}, bf16[3,32,256]{2,1,0:T(8,128)(2,1)S(1)}, u32[]{:S(2)}, u32[]{:S(2)}) collective-permute-start(bf16[3,32,256]{2,1,0:T(8,128)(2,1)S(1)} %get-tuple-element.55), channel_id=1, source_target_pairs={{0,24},{4,28},{8,0},{12,4},{16,8},{20,12},{24,16},{28,20},{1,25},{... | collective-permute-start | bytes 147464 | tf_op jit(solution)/shard_map/ppermute | solution.py:65
  77.4 7.5 %collective-permute-start.23 = (bf16[3,32,384]{2,1,0:T(8,128)(2,1)S(1)}, bf16[3,32,384]{2,1,0:T(8,128)(2,1)S(1)}, u32[]{:S(2)}, u32[]{:S(2)}) collective-permute-start(bf16[3,32,384]{2,1,0:T(8,128)(2,1)S(1)} %get-tuple-element.46), channel_id=1, source_target_pairs={{0,8},{4,12},{8,16},{12,20},{16,24},{20,28},{24,0},{28,4},{1,9},{5... | collective-permute-start | bytes 221192 | tf_op jit(solution)/shard_map/ppermute | solution.py:65
  77.5 9.0 %collective-permute-start.24 = (bf16[3,32,384]{2,1,0:T(8,128)(2,1)S(1)}, bf16[3,32,384]{2,1,0:T(8,128)(2,1)S(1)}, u32[]{:S(2)}, u32[]{:S(2)}) collective-permute-start(bf16[3,32,384]{2,1,0:T(8,128)(2,1)S(1)} %get-tuple-element.47), channel_id=1, source_target_pairs={{0,24},{4,28},{8,0},{12,4},{16,8},{20,12},{24,16},{28,20},{1,25},{... | collective-permute-start | bytes 221192 | tf_op jit(solution)/shard_map/ppermute | solution.py:65
  81.5 10.8 %collective-permute-start.28 = (bf16[3,32,640]{2,1,0:T(8,128)(2,1)S(1)}, bf16[3,32,640]{2,1,0:T(8,128)(2,1)S(1)}, u32[]{:S(2)}, u32[]{:S(2)}) collective-permute-start(bf16[3,32,640]{2,1,0:T(8,128)(2,1)S(1)} %get-tuple-element.56), channel_id=1, source_target_pairs={{0,16},{4,20},{8,24},{12,28},{16,0},{20,4},{24,8},{28,12},{1,17},{... | collective-permute-start | bytes 368648 | tf_op jit(solution)/shard_map/ppermute | solution.py:65
